TPU v7x, 32 devices: a whole 2x2x4 slice. The times are simulated.
32 devices in a mesh: dp: 4 (over y, x), frame: 2 (over core), tensor: 4 (over z).
Axes of the slice: x: 2, y: 2, z: 4, core: 2. Of those that a mesh axis runs over, the one named last changes fastest.
Arguments:
- tokens: bfloat16 [8, 8, 256, 1024], P('dp', ('frame', 'tensor')), may hold values from -6 to 6
- out_grad: bfloat16 [8, 8, 256, 1024], P('dp', ('frame', 'tensor')), may hold values from -6 to 6
- noise_index: int32 [8, 8], P('dp', 'frame'), may hold values from 0 to 999, as said below
- qkv_weight: bfloat16 [1024, 3, 1024], P(('dp', 'frame'), None, 'tensor'), may hold values from -0.1875 to 0.1875
- out_weight: bfloat16 [1024, 1024], P(('dp', 'frame'), 'tensor'), may hold values from -0.75 to 0.75
- up_weight: bfloat16 [1024, 4096], P(('dp', 'frame'), 'tensor'), may hold values from -0.1875 to 0.1875
- down_weight: bfloat16 [1024, 4096], P(('dp', 'frame'), 'tensor'), may hold values from -0.09375 to 0.09375
- ada_weight: bfloat16 [1024, 6, 1024], P(('dp', 'frame'), None, 'tensor'), may hold values from -0.25 to 0.25
Outputs:
- result: bfloat16 [8, 8, 256, 1024], P('dp', ('frame', 'tensor'))
- input_grad: bfloat16 [8, 8, 256, 1024], P('dp', ('frame', 'tensor'))
- qkv_grad: float32 [1024, 3, 1024], P(('dp', 'frame'), None, 'tensor')
- out_weight_grad: float32 [1024, 1024], P(('dp', 'frame'), 'tensor')
- up_grad: float32 [1024, 4096], P(('dp', 'frame'), 'tensor')
- down_grad: float32 [1024, 4096], P(('dp', 'frame'), 'tensor')
- ada_grad: float32 [1024, 6, 1024], P(('dp', 'frame'), None, 'tensor')
Inputs may be any that keep to these rules, and one draw needn't show every extreme that they name: `noise_index`: each frame's noise level, most often near 1000 - 1.
All inputs are finite; a program needn't handle non-finite values.
Results may differ from a plain program's by a relative error of at most 0.018.
Values may be sent and summed in bfloat16 or wider, within the bound.
A program may use at most 192 MiB of HBM per device.

v0:
```python
import math

import jax
import jax.numpy as jnp
from jax import lax
from jax.sharding import PartitionSpec as P

HEAD_DIM = 64


epsilon = 1e-06
highest = lax.Precision.HIGHEST


def normalize(values):
    center = values - jnp.mean(values, axis=-1, keepdims=True)
    spread = jnp.mean(center * center, axis=-1, keepdims=True)
    inverse = lax.rsqrt(spread + epsilon)
    return (center * inverse, inverse)


def norm_back(upstream, normed, inverse):
    upstream_mean = jnp.mean(upstream, axis=-1, keepdims=True)
    product_mean = jnp.mean(upstream * normed, axis=-1, keepdims=True)
    return inverse * (upstream - upstream_mean - normed * product_mean)


def level_embedding(levels, model_width):
    halfway = model_width // 2
    frequency = jnp.exp(-math.log(10000.0) * jnp.arange(halfway, dtype=jnp.float32) / halfway)
    angles = levels.astype(jnp.float32)[..., None] * frequency
    return jnp.concatenate([jnp.cos(angles), jnp.sin(angles)], axis=-1)


def gelu_tanh(values):
    return jax.nn.gelu(values, approximate=True)


def on_device(
    tokens, out_grad, noise_index, qkv_weight, out_weight, up_weight, down_weight, ada_weight
):
    model_width = tokens.shape[-1]
    patches_here = tokens.shape[2]
    local_width = qkv_weight.shape[2]
    hidden_local = up_weight.shape[1]
    heads_here = local_width // HEAD_DIM
    scaling = HEAD_DIM ** (-0.5)
    shards = (qkv_weight, out_weight, up_weight, down_weight, ada_weight)

    def fetch_weights():
        fetched = (
            lax.all_gather(shards[0], ("dp", "frame"), axis=0, tiled=True),
            lax.all_gather(shards[1], ("dp", "frame"), axis=0, tiled=True),
            lax.all_gather(shards[2], ("dp", "frame"), axis=0, tiled=True),
            lax.all_gather(shards[3], ("dp", "frame"), axis=0, tiled=True),
            lax.all_gather(shards[4], ("dp", "frame"), axis=0, tiled=True),
        )
        return fetched

    def one_clip(totals, inputs, weights):
        clip_tokens, clip_cotangent, clip_levels = inputs
        joint_weight, mixer_weight, upward_weight, downward_weight, adaptive_weight = weights
        condition = jax.nn.silu(level_embedding(clip_levels, model_width)).astype(jnp.bfloat16)
        columns = jnp.einsum(
            "fd,dkc->fkc", condition, adaptive_weight, preferred_element_type=jnp.float32
        )
        modulation = lax.all_to_all(columns, "tensor", split_axis=0, concat_axis=2, tiled=True)[
            :, :, None, :
        ]
        residual = clip_tokens.astype(jnp.float32)
        normed_one, inverse_one = normalize(residual)
        entering_one = (normed_one * (1.0 + modulation[:, 1]) + modulation[:, 0]).astype(
            jnp.bfloat16
        )
        gathered_one = lax.all_gather(entering_one, "tensor", axis=0, tiled=True)
        token_count = gathered_one.shape[0] * patches_here
        flat_one = gathered_one.reshape(token_count, model_width)
        projected = jnp.einsum(
            "rd,dkc->rkc", flat_one, joint_weight, preferred_element_type=jnp.float32
        ).astype(jnp.bfloat16)
        keys_all, values_all = (
            lax.all_gather(projected[:, 1], "frame", axis=0, tiled=True),
            lax.all_gather(projected[:, 2], "frame", axis=0, tiled=True),
        )
        key_heads = keys_all.reshape(-1, heads_here, HEAD_DIM)
        value_heads = values_all.reshape(-1, heads_here, HEAD_DIM)
        block_rows = min(512, token_count)
        block_count = token_count // block_rows
        query_blocks = projected[:, 0].reshape(block_count, block_rows, heads_here, HEAD_DIM)

        def attend(query_block):
            scores = (
                jnp.einsum(
                    "qhe,khe->hqk", query_block, key_heads, preferred_element_type=jnp.float32
                )
                * scaling
            )
            largest = jnp.max(scores, axis=-1, keepdims=True)
            raised = jnp.exp(scores - largest)
            totals_row = jnp.sum(raised, axis=-1, keepdims=True)
            probs_low = (raised / totals_row).astype(jnp.bfloat16)
            outputs = jnp.einsum(
                "hqk,khe->qhe", probs_low, value_heads, preferred_element_type=jnp.float32
            )
            return (outputs.astype(jnp.bfloat16), (largest + jnp.log(totals_row))[..., 0])

        attended_blocks, log_totals = lax.map(attend, query_blocks)
        attended = attended_blocks.reshape(token_count, local_width)
        partial_one = jnp.einsum(
            "rc,oc->ro", attended, mixer_weight, preferred_element_type=jnp.float32
        )
        branch_one = lax.psum_scatter(
            partial_one.reshape(-1, patches_here, model_width),
            "tensor",
            scatter_dimension=0,
            tiled=True,
        )
        middle = residual + modulation[:, 2] * branch_one
        normed_two, inverse_two = normalize(middle)
        entering_two = (normed_two * (1.0 + modulation[:, 4]) + modulation[:, 3]).astype(
            jnp.bfloat16
        )
        upstream = clip_cotangent.astype(jnp.float32)
        flat_two = lax.all_gather(entering_two, "tensor", axis=0, tiled=True).reshape(
            token_count, model_width
        )
        up_values = jnp.dot(flat_two, upward_weight, preferred_element_type=jnp.float32)
        hidden = gelu_tanh(up_values).astype(jnp.bfloat16)
        partial_two = jnp.einsum(
            "rf,of->ro", hidden, downward_weight, preferred_element_type=jnp.float32
        )
        branch_two = lax.psum_scatter(
            partial_two.reshape(-1, patches_here, model_width).astype(jnp.bfloat16),
            "tensor",
            scatter_dimension=0,
            tiled=True,
        ).astype(jnp.float32)
        grad_branch_two = (modulation[:, 5] * upstream).astype(jnp.bfloat16)
        grad_two_all = lax.all_gather(grad_branch_two, "tensor", axis=0, tiled=True).reshape(
            token_count, model_width
        )
        output = (middle + modulation[:, 5] * branch_two).astype(jnp.bfloat16)
        grad_gate_two = jnp.sum(upstream * branch_two, axis=1)
        grad_hidden = jnp.dot(grad_two_all, downward_weight, preferred_element_type=jnp.float32)
        down_total = jnp.einsum(
            "ro,rf->of", grad_two_all, hidden, preferred_element_type=jnp.float32
        )
        _, gelu_pullback = jax.vjp(gelu_tanh, up_values)
        grad_up = gelu_pullback(grad_hidden)[0].astype(jnp.bfloat16)
        up_total = jnp.einsum("rd,rf->df", flat_two, grad_up, preferred_element_type=jnp.float32)
        partial_back_two = jnp.einsum(
            "rf,df->rd", grad_up, upward_weight, preferred_element_type=jnp.float32
        ).reshape(-1, patches_here, model_width)
        grad_entering_two = lax.psum_scatter(
            partial_back_two.astype(jnp.bfloat16), "tensor", scatter_dimension=0, tiled=True
        ).astype(jnp.float32)
        grad_shift_two = jnp.sum(grad_entering_two, axis=1)
        grad_scale_two = jnp.sum(grad_entering_two * normed_two, axis=1)
        grad_middle = upstream + norm_back(
            grad_entering_two * (1.0 + modulation[:, 4]), normed_two, inverse_two
        )
        grad_gate_one = jnp.sum(grad_middle * branch_one, axis=1)
        grad_branch_one = (modulation[:, 2] * grad_middle).astype(jnp.bfloat16)
        grad_one_all = lax.all_gather(grad_branch_one, "tensor", axis=0, tiled=True).reshape(
            token_count, model_width
        )
        grad_attended = jnp.dot(
            grad_one_all, mixer_weight, preferred_element_type=jnp.float32
        ).astype(jnp.bfloat16)
        mixer_total = jnp.einsum(
            "ro,rc->oc", grad_one_all, attended, preferred_element_type=jnp.float32
        )
        grad_blocks = grad_attended.reshape(block_count, block_rows, heads_here, HEAD_DIM)

        def attend_back(carried, pieces):
            key_sum, value_sum = carried
            query_block, grad_block, log_block = pieces
            scores = (
                jnp.einsum(
                    "qhe,khe->hqk", query_block, key_heads, preferred_element_type=jnp.float32
                )
                * scaling
            )
            probs = jnp.exp(scores - log_block[..., None])
            grad_probs = jnp.einsum(
                "qhe,khe->hqk", grad_block, value_heads, preferred_element_type=jnp.float32
            )
            value_sum = value_sum + jnp.einsum(
                "hqk,qhe->khe",
                probs.astype(jnp.bfloat16),
                grad_block,
                preferred_element_type=jnp.float32,
            )
            row_terms = jnp.sum(probs * grad_probs, axis=-1, keepdims=True)
            grad_scores = (probs * (grad_probs - row_terms)).astype(jnp.bfloat16)
            grad_queries = (
                jnp.einsum(
                    "hqk,khe->qhe", grad_scores, key_heads, preferred_element_type=jnp.float32
                )
                * scaling
            )
            key_sum = (
                key_sum
                + jnp.einsum(
                    "hqk,qhe->khe", grad_scores, query_block, preferred_element_type=jnp.float32
                )
                * scaling
            )
            return ((key_sum, value_sum), grad_queries)

        zeros_keys = jnp.zeros(key_heads.shape, jnp.float32)
        (key_grads, value_grads), query_grads = lax.scan(
            attend_back, (zeros_keys, zeros_keys), (query_blocks, grad_blocks, log_totals)
        )
        key_own, value_own = (
            lax.psum_scatter(
                key_grads.reshape(-1, local_width).astype(jnp.bfloat16),
                "frame",
                scatter_dimension=0,
                tiled=True,
            ).astype(jnp.float32),
            lax.psum_scatter(
                value_grads.reshape(-1, local_width).astype(jnp.bfloat16),
                "frame",
                scatter_dimension=0,
                tiled=True,
            ).astype(jnp.float32),
        )
        grad_projected = jnp.stack(
            [query_grads.reshape(token_count, local_width), key_own, value_own], axis=1
        ).astype(jnp.bfloat16)
        joint_total = jnp.einsum(
            "rd,rkc->dkc", flat_one, grad_projected, preferred_element_type=jnp.float32
        )
        partial_back_one = jnp.einsum(
            "rkc,dkc->rd", grad_projected, joint_weight, preferred_element_type=jnp.float32
        )
        grad_entering_one = lax.psum_scatter(
            partial_back_one.reshape(-1, patches_here, model_width).astype(jnp.bfloat16),
            "tensor",
            scatter_dimension=0,
            tiled=True,
        ).astype(jnp.float32)
        grad_shift_one = jnp.sum(grad_entering_one, axis=1)
        grad_scale_one = jnp.sum(grad_entering_one * normed_one, axis=1)
        grad_input = grad_middle + norm_back(
            grad_entering_one * (1.0 + modulation[:, 1]), normed_one, inverse_one
        )
        grad_modulation = jnp.stack(
            [
                grad_shift_one,
                grad_scale_one,
                grad_gate_one,
                grad_shift_two,
                grad_scale_two,
                grad_gate_two,
            ],
            axis=1,
        )
        grad_columns = lax.all_to_all(
            grad_modulation, "tensor", split_axis=2, concat_axis=0, tiled=True
        )
        adaptive_total = jnp.einsum(
            "fd,fkc->dkc", condition.astype(jnp.float32), grad_columns, precision=highest
        )
        updates = (joint_total, mixer_total, up_total, down_total, adaptive_total)
        totals = tuple((total + update for total, update in zip(totals, updates)))
        return (totals, (output, grad_input.astype(jnp.bfloat16)))

    initial = (
        jnp.zeros((model_width, 3, local_width), jnp.float32),
        jnp.zeros((model_width, local_width), jnp.float32),
        jnp.zeros((model_width, hidden_local), jnp.float32),
        jnp.zeros((model_width, hidden_local), jnp.float32),
        jnp.zeros((model_width, 6, local_width), jnp.float32),
    )

    def micro_step(totals, inputs):
        return one_clip(totals, inputs, fetch_weights())

    totals, (result, input_grad) = lax.scan(micro_step, initial, (tokens, out_grad, noise_index))
    summed = (
        lax.psum_scatter(
            totals[0].astype(jnp.bfloat16), ("dp", "frame"), scatter_dimension=0, tiled=True
        ).astype(jnp.float32),
        lax.psum_scatter(
            totals[1].astype(jnp.bfloat16), ("dp", "frame"), scatter_dimension=0, tiled=True
        ).astype(jnp.float32),
        lax.psum_scatter(
            totals[2].astype(jnp.bfloat16), ("dp", "frame"), scatter_dimension=0, tiled=True
        ).astype(jnp.float32),
        lax.psum_scatter(
            totals[3].astype(jnp.bfloat16), ("dp", "frame"), scatter_dimension=0, tiled=True
        ).astype(jnp.float32),
        lax.psum_scatter(
            totals[4].astype(jnp.bfloat16), ("dp", "frame"), scatter_dimension=0, tiled=True
        ).astype(jnp.float32),
    )
    return (result, input_grad, summed[0], summed[1], summed[2], summed[3], summed[4])


def solution(mesh):
    return jax.shard_map(
        on_device,
        mesh=mesh,
        in_specs=(
            P("dp", ("frame", "tensor"), None, None),
            P("dp", ("frame", "tensor"), None, None),
            P("dp", "frame"),
            P(("dp", "frame"), None, "tensor"),
            P(("dp", "frame"), "tensor"),
            P(("dp", "frame"), "tensor"),
            P(("dp", "frame"), "tensor"),
            P(("dp", "frame"), None, "tensor"),
        ),
        out_specs=(
            P("dp", ("frame", "tensor"), None, None),
            P("dp", ("frame", "tensor"), None, None),
            P(("dp", "frame"), None, "tensor"),
            P(("dp", "frame"), "tensor"),
            P(("dp", "frame"), "tensor"),
            P(("dp", "frame"), "tensor"),
            P(("dp", "frame"), None, "tensor"),
        ),
        check_vma=False,
    )
```

profile of v0, /device:TPU:0, one launch (start us, length us, event | category | flops | bytes accessed | tf_op | source)
XLA Modules:
  0.0 1683.6 jit_solution(13666818316146468677)
XLA Ops:
  8.1 1450.2 %while.83 = (s32[]{:T(128)}, f32[1024,3,256]{2,0,1:T(8,128)}, f32[1024,256]{1,0:T(8,128)}, f32[1024,1024]{1,0:T(8,128)}, f32[1024,1024]{1,0:T(8,128)}, /*index=5...) while((s32[]{:T(128)}, f32[1024,3,256]{2,0,1:T(8,128)}, ...), condition=%wide.region_28.29_spmd.clone, body=%wide.region_0.28_spmd.clone.sunk | while | flops 23346327552 | bytes 683999296 | solution.py:281
  13.4 32.8 %all-gather.19.cloned.1.call-done = bf16[1024,6,256]{2,0,1:T(8,128)(2,1)} async-done(((bf16[128,6,256]{2,0,1:T(8,128)(2,1)}), bf16[1024,6,256]{2,0,1:T(8,128)(2,1)}) %all-gather.19.cloned.1.call-update) | async-done | bytes 3145744 | tf_op jit(solution)/shard_map/while/body/eval_jaxpr/all_gather | solution.py:56
  61.9 11.8 all-gather.23.cloned.1.call-done
  73.7 47.8 %all-gather.21.cloned.1.call-done = bf16[4,256,1024]{2,1,0:T(8,128)(2,1)} async-done(((bf16[1,256,1024]{2,1,0:T(8,128)(2,1)}), bf16[4,256,1024]{2,1,0:T(8,128)(2,1)}) %all-gather.21.cloned.1.call-update) | async-done | bytes 2097168 | tf_op jit(solution)/shard_map/while/body/eval_jaxpr/all_gather | solution.py:75
  127.2 10.8 all_gather.87
  148.3 20.5 %while.84 = (s32[]{:T(128)}, bf16[2,512,4,64]{1,3,2,0:T(8,128)(2,1)S(1)}, f32[2,4,512]{2,1,0:T(4,128)S(1)}, bf16[2,512,4,64]{1,3,2,0:T(8,128)(2,1)S(1)}, bf16[20...) while((s32[]{:T(128)}, bf16[2,512,4,64]{1,3,2,0:T(8,128)(2,1)S(1)}, ...), condition=%wide.region_6.6_spmd, body=%wide.region_3.5_spmd.sunk | while | flops 1111619584 | bytes 53018720 | solution.py:107
  180.6 74.6 %reduce-scatter.22.cloned.1.call-done = f32[1,256,1024]{2,1,0:T(8,128)} async-done(((f32[4,256,1024]{2,1,0:T(8,128)}), f32[1,256,1024]{2,1,0:T(8,128)}) %reduce-scatter.22.cloned.1.call-update) | async-done | bytes 1048592 | tf_op jit(solution)/shard_map/while/body/eval_jaxpr/reduce_scatter | solution.py:112
  259.0 26.3 %all-gather.31.cloned.1.call-done = bf16[1024,1024]{1,0:T(8,128)(2,1)} async-done(((bf16[128,1024]{1,0:T(8,128)(2,1)}), bf16[1024,1024]{1,0:T(8,128)(2,1)}) %all-gather.31.cloned.1.call-update) | async-done | bytes 2097168 | tf_op jit(solution)/shard_map/while/body/eval_jaxpr/all_gather | solution.py:55
  285.3 47.8 %all-gather.29.cloned.1.call-done = bf16[4,256,1024]{2,1,0:T(8,128)(2,1)} async-done(((bf16[1,256,1024]{2,1,0:T(8,128)(2,1)}), bf16[4,256,1024]{2,1,0:T(8,128)(2,1)}) %all-gather.29.cloned.1.call-update) | async-done | bytes 2097168 | tf_op jit(solution)/shard_map/while/body/eval_jaxpr/all_gather | solution.py:139
  339.7 22.0 %all-gather.35.cloned.1.call-done = bf16[1024,1024]{1,0:T(8,128)(2,1)} async-done(((bf16[128,1024]{1,0:T(8,128)(2,1)}), bf16[1024,1024]{1,0:T(8,128)(2,1)}) %all-gather.35.cloned.1.call-update) | async-done | bytes 2097168 | tf_op jit(solution)/shard_map/while/body/eval_jaxpr/all_gather | solution.py:54
  361.7 47.7 %all-gather.33.cloned.1.call-done = bf16[4,256,1024]{2,1,0:T(8,128)(2,1)} async-done(((bf16[1,256,1024]{2,1,0:T(8,128)(2,1)}), bf16[4,256,1024]{2,1,0:T(8,128)(2,1)}) %all-gather.33.cloned.1.call-update) | async-done | bytes 2097168 | tf_op jit(solution)/shard_map/while/body/eval_jaxpr/all_gather | solution.py:124
  409.3 10.0 fusion.215
  430.1 35.5 %reduce-scatter.24.cloned.1.call-done = bf16[1,256,1024]{2,1,0:T(8,128)(2,1)} async-done(((bf16[4,256,1024]{2,1,0:T(8,128)(2,1)}), bf16[1,256,1024]{2,1,0:T(8,128)(2,1)}) %reduce-scatter.24.cloned.1.call-update) | async-done | bytes 524304 | tf_op jit(solution)/shard_map/while/body/eval_jaxpr/reduce_scatter | solution.py:154
  468.2 42.5 %reduce-scatter.26.cloned.1.call-done = bf16[1,256,1024]{2,1,0:T(8,128)(2,1)} async-done(((bf16[4,256,1024]{2,1,0:T(8,128)(2,1)}), bf16[1,256,1024]{2,1,0:T(8,128)(2,1)}) %reduce-scatter.26.cloned.1.call-update) | async-done | bytes 524304 | tf_op jit(solution)/shard_map/while/body/eval_jaxpr/reduce_scatter | solution.py:132
  516.1 44.7 %all-gather.37.cloned.1.call-done = bf16[4,256,1024]{2,1,0:T(8,128)(2,1)} async-done(((bf16[1,256,1024]{2,1,0:T(8,128)(2,1)}), bf16[4,256,1024]{2,1,0:T(8,128)(2,1)}) %all-gather.37.cloned.1.call-update) | async-done | bytes 2097168 | tf_op jit(solution)/shard_map/while/body/eval_jaxpr/all_gather | solution.py:164
  568.2 72.0 %while.85 = (s32[]{:T(128)}, f32[2048,4,64]{0,2,1:T(8,128)}, f32[2048,4,64]{0,2,1:T(8,128)}, bf16[2,512,4,64]{1,3,2,0:T(8,128)(2,1)}, bf16[2,512,4,64]{1,3,2,0:T...) while((s32[]{:T(128)}, f32[2048,4,64]{0,2,1:T(8,128)}, ...), condition=%wide.region_15.15_spmd.clone, body=%wide.region_13.14_spmd.clone.sunk | while | flops 2737436672 | bytes 176742640 | solution.py:212
  575.1 8.0 multiply_reduce_fusion.11
  583.1 10.5 multiply_convert_fusion.12
  610.8 8.0 multiply_reduce_fusion.11
  618.8 10.5 multiply_convert_fusion.12
  650.7 11.7 reduce-scatter.28.cloned.1.call-done
  686.2 25.7 %reduce-scatter.32.cloned.1.call-done = bf16[1,256,1024]{2,1,0:T(8,128)(2,1)} async-done(((bf16[4,256,1024]{2,1,0:T(8,128)(2,1)}), bf16[1,256,1024]{2,1,0:T(8,128)(2,1)}) %reduce-scatter.32.cloned.1.call-update) | async-done | bytes 524304 | tf_op jit(solution)/shard_map/while/body/eval_jaxpr/reduce_scatter | solution.py:238
  738.3 28.3 %all-gather.19.cloned.1.call-done = bf16[1024,6,256]{2,0,1:T(8,128)(2,1)} async-done(((bf16[128,6,256]{2,0,1:T(8,128)(2,1)}), bf16[1024,6,256]{2,0,1:T(8,128)(2,1)}) %all-gather.19.cloned.1.call-update) | async-done | bytes 3145744 | tf_op jit(solution)/shard_map/while/body/eval_jaxpr/all_gather | solution.py:56
  782.3 11.7 all-gather.23.cloned.1.call-done
  794.0 47.8 %all-gather.21.cloned.1.call-done = bf16[4,256,1024]{2,1,0:T(8,128)(2,1)} async-done(((bf16[1,256,1024]{2,1,0:T(8,128)(2,1)}), bf16[4,256,1024]{2,1,0:T(8,128)(2,1)}) %all-gather.21.cloned.1.call-update) | async-done | bytes 2097168 | tf_op jit(solution)/shard_map/while/body/eval_jaxpr/all_gather | solution.py:75
  847.6 10.8 all_gather.87
  868.7 20.5 %while.84 = (s32[]{:T(128)}, bf16[2,512,4,64]{1,3,2,0:T(8,128)(2,1)S(1)}, f32[2,4,512]{2,1,0:T(4,128)S(1)}, bf16[2,512,4,64]{1,3,2,0:T(8,128)(2,1)S(1)}, bf16[20...) while((s32[]{:T(128)}, bf16[2,512,4,64]{1,3,2,0:T(8,128)(2,1)S(1)}, ...), condition=%wide.region_6.6_spmd, body=%wide.region_3.5_spmd.sunk | while | flops 1111619584 | bytes 53018720 | solution.py:107
  901.0 74.6 %reduce-scatter.22.cloned.1.call-done = f32[1,256,1024]{2,1,0:T(8,128)} async-done(((f32[4,256,1024]{2,1,0:T(8,128)}), f32[1,256,1024]{2,1,0:T(8,128)}) %reduce-scatter.22.cloned.1.call-update) | async-done | bytes 1048592 | tf_op jit(solution)/shard_map/while/body/eval_jaxpr/reduce_scatter | solution.py:112
  979.6 26.1 %all-gather.31.cloned.1.call-done = bf16[1024,1024]{1,0:T(8,128)(2,1)} async-done(((bf16[128,1024]{1,0:T(8,128)(2,1)}), bf16[1024,1024]{1,0:T(8,128)(2,1)}) %all-gather.31.cloned.1.call-update) | async-done | bytes 2097168 | tf_op jit(solution)/shard_map/while/body/eval_jaxpr/all_gather | solution.py:55
  1005.7 47.7 %all-gather.29.cloned.1.call-done = bf16[4,256,1024]{2,1,0:T(8,128)(2,1)} async-done(((bf16[1,256,1024]{2,1,0:T(8,128)(2,1)}), bf16[4,256,1024]{2,1,0:T(8,128)(2,1)}) %all-gather.29.cloned.1.call-update) | async-done | bytes 2097168 | tf_op jit(solution)/shard_map/while/body/eval_jaxpr/all_gather | solution.py:139
  1060.0 22.0 %all-gather.35.cloned.1.call-done = bf16[1024,1024]{1,0:T(8,128)(2,1)} async-done(((bf16[128,1024]{1,0:T(8,128)(2,1)}), bf16[1024,1024]{1,0:T(8,128)(2,1)}) %all-gather.35.cloned.1.call-update) | async-done | bytes 2097168 | tf_op jit(solution)/shard_map/while/body/eval_jaxpr/all_gather | solution.py:54
  1081.9 47.7 %all-gather.33.cloned.1.call-done = bf16[4,256,1024]{2,1,0:T(8,128)(2,1)} async-done(((bf16[1,256,1024]{2,1,0:T(8,128)(2,1)}), bf16[4,256,1024]{2,1,0:T(8,128)(2,1)}) %all-gather.33.cloned.1.call-update) | async-done | bytes 2097168 | tf_op jit(solution)/shard_map/while/body/eval_jaxpr/all_gather | solution.py:124
  1129.6 10.0 fusion.215
  1150.4 35.5 %reduce-scatter.24.cloned.1.call-done = bf16[1,256,1024]{2,1,0:T(8,128)(2,1)} async-done(((bf16[4,256,1024]{2,1,0:T(8,128)(2,1)}), bf16[1,256,1024]{2,1,0:T(8,128)(2,1)}) %reduce-scatter.24.cloned.1.call-update) | async-done | bytes 524304 | tf_op jit(solution)/shard_map/while/body/eval_jaxpr/reduce_scatter | solution.py:154
  1188.5 42.6 %reduce-scatter.26.cloned.1.call-done = bf16[1,256,1024]{2,1,0:T(8,128)(2,1)} async-done(((bf16[4,256,1024]{2,1,0:T(8,128)(2,1)}), bf16[1,256,1024]{2,1,0:T(8,128)(2,1)}) %reduce-scatter.26.cloned.1.call-update) | async-done | bytes 524304 | tf_op jit(solution)/shard_map/while/body/eval_jaxpr/reduce_scatter | solution.py:132
  1236.5 44.8 %all-gather.37.cloned.1.call-done = bf16[4,256,1024]{2,1,0:T(8,128)(2,1)} async-done(((bf16[1,256,1024]{2,1,0:T(8,128)(2,1)}), bf16[4,256,1024]{2,1,0:T(8,128)(2,1)}) %all-gather.37.cloned.1.call-update) | async-done | bytes 2097168 | tf_op jit(solution)/shard_map/while/body/eval_jaxpr/all_gather | solution.py:164
  1288.7 72.0 %while.85 = (s32[]{:T(128)}, f32[2048,4,64]{0,2,1:T(8,128)}, f32[2048,4,64]{0,2,1:T(8,128)}, bf16[2,512,4,64]{1,3,2,0:T(8,128)(2,1)}, bf16[2,512,4,64]{1,3,2,0:T...) while((s32[]{:T(128)}, f32[2048,4,64]{0,2,1:T(8,128)}, ...), condition=%wide.region_15.15_spmd.clone, body=%wide.region_13.14_spmd.clone.sunk | while | flops 2737436672 | bytes 176742640 | solution.py:212
  1295.5 8.0 multiply_reduce_fusion.11
  1303.5 10.5 multiply_convert_fusion.12
  1331.2 8.0 multiply_reduce_fusion.11
  1339.2 10.5 multiply_convert_fusion.12
  1371.1 11.9 reduce-scatter.28.cloned.1.call-done
  1410.1 22.5 %reduce-scatter.32.cloned.1.call-done = bf16[1,256,1024]{2,1,0:T(8,128)(2,1)} async-done(((bf16[4,256,1024]{2,1,0:T(8,128)(2,1)}), bf16[1,256,1024]{2,1,0:T(8,128)(2,1)}) %reduce-scatter.32.cloned.1.call-update) | async-done | bytes 524304 | tf_op jit(solution)/shard_map/while/body/eval_jaxpr/reduce_scatter | solution.py:238
  1476.5 18.3 %reduce-scatter.14.cloned.1.call-done = bf16[128,256]{1,0:T(8,128)(2,1)} async-done(((bf16[1024,256]{1,0:T(8,128)(2,1)}), bf16[128,256]{1,0:T(8,128)(2,1)}) %reduce-scatter.14.cloned.1.call-update) | async-done | bytes 65552 | tf_op jit(solution)/shard_map/reduce_scatter | solution.py:286
  1496.3 39.9 %reduce-scatter.12.cloned.1.call-done = bf16[128,3,256]{2,0,1:T(8,128)(2,1)} async-done(((bf16[1024,3,256]{2,0,1:T(8,128)(2,1)}), bf16[128,3,256]{2,0,1:T(8,128)(2,1)}) %reduce-scatter.12.cloned.1.call-update) | async-done | bytes 196624 | tf_op jit(solution)/shard_map/reduce_scatter | solution.py:283
  1538.0 42.4 %reduce-scatter.16.cloned.1.call-done = bf16[128,1024]{1,0:T(8,128)(2,1)} async-done(((bf16[1024,1024]{1,0:T(8,128)(2,1)}), bf16[128,1024]{1,0:T(8,128)(2,1)}) %reduce-scatter.16.cloned.1.call-update) | async-done | bytes 262160 | tf_op jit(solution)/shard_map/reduce_scatter | solution.py:289
  1582.2 42.5 %reduce-scatter.18.cloned.1.call-done = bf16[128,1024]{1,0:T(8,128)(2,1)} async-done(((bf16[1024,1024]{1,0:T(8,128)(2,1)}), bf16[128,1024]{1,0:T(8,128)(2,1)}) %reduce-scatter.18.cloned.1.call-update) | async-done | bytes 262160 | tf_op jit(solution)/shard_map/reduce_scatter | solution.py:292
  1626.5 47.5 %reduce-scatter.20.cloned.1.call-done = bf16[128,6,256]{2,0,1:T(8,128)(2,1)} async-done(((bf16[1024,6,256]{2,0,1:T(8,128)(2,1)}), bf16[128,6,256]{2,0,1:T(8,128)(2,1)}) %reduce-scatter.20.cloned.1.call-update) | async-done | bytes 393232 | tf_op jit(solution)/shard_map/reduce_scatter | solution.py:295
  (503 shorter events, 422.4 us)
Async XLA Ops:
  8.5 37.7 %all-gather.19.cloned.1.call-start = ((), (), s32[]{:S(2)}) async-start(), calls=%async_computation.18 | async-start | bytes 3538944 | tf_op jit(solution)/shard_map/while/body/eval_jaxpr/all_gather | solution.py:56
  9.3 64.4 %all-gather.23.cloned.1.call-start = ((), (), s32[]{:S(2)}) async-start(), calls=%async_computation.20 | async-start | bytes 1769472 | tf_op jit(solution)/shard_map/while/body/eval_jaxpr/all_gather | solution.py:52
  11.9 113.4 %copy-start.32 = (f32[256]{0:T(256)}, f32[256]{0:T(256)S(1)}, u32[]{:S(2)}) copy-start(f32[256]{0:T(256)S(1)} %broadcast_multiply_fusion.11) | copy-start | bytes 3076 | tf_op jit(solution)/shard_map/while
  49.2 10.3 all-to-all-start
  53.8 67.7 %all-gather.21.cloned.1.call-start = ((), (), s32[]{:S(2)}) async-start(), calls=%async_computation.19 | async-start | bytes 2621440 | tf_op jit(solution)/shard_map/while/body/eval_jaxpr/all_gather | solution.py:75
  61.9 77.2 %all-gather.25.cloned.1.call-start = ((), (), s32[]{:S(2)}) async-start(), calls=%async_computation.21 | async-start | bytes 1572864 | tf_op jit(solution)/shard_map/while/body/eval_jaxpr/all_gather | solution.py:82
  126.5 20.3 %all-gather.27.cloned.1.call-start = ((), (), s32[]{:S(2)}) async-start(), calls=%async_computation.22 | async-start | bytes 1572864 | tf_op jit(solution)/shard_map/while/body/eval_jaxpr/all_gather | solution.py:83
  127.1 128.0 %reduce-scatter.22.cloned.1.call-start = ((), (), s32[]{:S(2)}) async-start(), calls=%async_computation.23 | async-start | bytes 5242880 | tf_op jit(solution)/shard_map/while/body/eval_jaxpr/reduce_scatter | solution.py:112
  177.0 80.8 %copy-start.38 = (f32[1,1,1,1024]{3,0,1,2:T(1,128)S(1)}, f32[1,1,1,1024]{3,0,1,2:T(1,128)}, u32[]{:S(2)}) copy-start(f32[1,1,1,1024]{3,0,1,2:T(1,128)} %get-tuple-element.818) | copy-start | bytes 12292 | tf_op jit(solution)/shard_map/while
  177.0 108.3 %all-gather.31.cloned.1.call-start = ((), (), s32[]{:S(2)}) async-start(), calls=%async_computation.25 | async-start | bytes 2359296 | tf_op jit(solution)/shard_map/while/body/eval_jaxpr/all_gather | solution.py:55
  177.7 155.4 %all-gather.29.cloned.1.call-start = ((), (), s32[]{:S(2)}) async-start(), calls=%async_computation.24 | async-start | bytes 2621440 | tf_op jit(solution)/shard_map/while/body/eval_jaxpr/all_gather | solution.py:139
  179.8 181.9 %all-gather.35.cloned.1.call-start = ((), (), s32[]{:S(2)}) async-start(), calls=%async_computation.27 | async-start | bytes 2359296 | tf_op jit(solution)/shard_map/while/body/eval_jaxpr/all_gather | solution.py:54
  180.5 228.8 %all-gather.33.cloned.1.call-start = ((), (), s32[]{:S(2)}) async-start(), calls=%async_computation.26 | async-start | bytes 2621440 | tf_op jit(solution)/shard_map/while/body/eval_jaxpr/all_gather | solution.py:124
  258.8 206.9 %reduce-scatter.24.cloned.1.call-start = ((), (), s32[]{:S(2)}) async-start(), calls=%async_computation.28 | async-start | bytes 2621440 | tf_op jit(solution)/shard_map/while/body/eval_jaxpr/reduce_scatter | solution.py:154
  423.1 87.6 %reduce-scatter.26.cloned.1.call-start = ((), (), s32[]{:S(2)}) async-start(), calls=%async_computation.29 | async-start | bytes 2621440 | tf_op jit(solution)/shard_map/while/body/eval_jaxpr/reduce_scatter | solution.py:132
  430.1 130.7 %copy-start.11 = (bf16[1024,256]{1,0:T(8,128)(2,1)S(1)}, bf16[1024,256]{1,0:T(8,128)(2,1)}, u32[]{:S(2)}) copy-start(bf16[1024,256]{1,0:T(8,128)(2,1)} %all_gather.87) | copy-start | bytes 1572868 | tf_op jit(solution)/shard_map/while
  430.1 130.7 %all-gather.37.cloned.1.call-start = ((), (), s32[]{:S(2)}) async-start(), calls=%async_computation.30 | async-start | bytes 2621440 | tf_op jit(solution)/shard_map/while/body/eval_jaxpr/all_gather | solution.py:164
  515.8 134.9 %reduce-scatter.30.cloned.1.call-start = ((), (), s32[]{:S(2)}) async-start(), calls=%async_computation.32 | async-start | bytes 1572864 | tf_op jit(solution)/shard_map/while/body/eval_jaxpr/reduce_scatter | solution.py:216
  643.4 19.1 %reduce-scatter.28.cloned.1.call-start = ((), (), s32[]{:S(2)}) async-start(), calls=%async_computation.31 | async-start | bytes 1572864 | tf_op jit(solution)/shard_map/while/body/eval_jaxpr/reduce_scatter | solution.py:222
  646.7 65.3 %reduce-scatter.32.cloned.1.call-start = ((), (), s32[]{:S(2)}) async-start(), calls=%async_computation.33 | async-start | bytes 2621440 | tf_op jit(solution)/shard_map/while/body/eval_jaxpr/reduce_scatter | solution.py:238
  717.6 8.9 all-to-all-start.1
  733.7 32.9 %all-gather.19.cloned.1.call-start = ((), (), s32[]{:S(2)}) async-start(), calls=%async_computation.18 | async-start | bytes 3538944 | tf_op jit(solution)/shard_map/while/body/eval_jaxpr/all_gather | solution.py:56
  734.3 59.7 %all-gather.23.cloned.1.call-start = ((), (), s32[]{:S(2)}) async-start(), calls=%async_computation.20 | async-start | bytes 1769472 | tf_op jit(solution)/shard_map/while/body/eval_jaxpr/all_gather | solution.py:52
  736.8 108.9 %copy-start.32 = (f32[256]{0:T(256)}, f32[256]{0:T(256)S(1)}, u32[]{:S(2)}) copy-start(f32[256]{0:T(256)S(1)} %broadcast_multiply_fusion.11) | copy-start | bytes 3076 | tf_op jit(solution)/shard_map/while
  769.7 10.3 all-to-all-start
  774.3 67.6 %all-gather.21.cloned.1.call-start = ((), (), s32[]{:S(2)}) async-start(), calls=%async_computation.19 | async-start | bytes 2621440 | tf_op jit(solution)/shard_map/while/body/eval_jaxpr/all_gather | solution.py:75
  782.3 77.2 %all-gather.25.cloned.1.call-start = ((), (), s32[]{:S(2)}) async-start(), calls=%async_computation.21 | async-start | bytes 1572864 | tf_op jit(solution)/shard_map/while/body/eval_jaxpr/all_gather | solution.py:82
  846.8 20.4 %all-gather.27.cloned.1.call-start = ((), (), s32[]{:S(2)}) async-start(), calls=%async_computation.22 | async-start | bytes 1572864 | tf_op jit(solution)/shard_map/while/body/eval_jaxpr/all_gather | solution.py:83
  847.5 128.0 %reduce-scatter.22.cloned.1.call-start = ((), (), s32[]{:S(2)}) async-start(), calls=%async_computation.23 | async-start | bytes 5242880 | tf_op jit(solution)/shard_map/while/body/eval_jaxpr/reduce_scatter | solution.py:112
  897.4 80.8 %copy-start.27 = (f32[1,1,1,1024]{3,0,1,2:T(1,128)S(1)}, f32[1,1,1,1024]{3,0,1,2:T(1,128)}, u32[]{:S(2)}) copy-start(f32[1,1,1,1024]{3,0,1,2:T(1,128)} %get-tuple-element.819) | copy-start | bytes 12292 | tf_op jit(solution)/shard_map/while
  897.4 80.8 %copy-start.38 = (f32[1,1,1,1024]{3,0,1,2:T(1,128)S(1)}, f32[1,1,1,1024]{3,0,1,2:T(1,128)}, u32[]{:S(2)}) copy-start(f32[1,1,1,1024]{3,0,1,2:T(1,128)} %get-tuple-element.818) | copy-start | bytes 12292 | tf_op jit(solution)/shard_map/while
  897.4 108.3 %all-gather.31.cloned.1.call-start = ((), (), s32[]{:S(2)}) async-start(), calls=%async_computation.25 | async-start | bytes 2359296 | tf_op jit(solution)/shard_map/while/body/eval_jaxpr/all_gather | solution.py:55
  898.1 155.3 %all-gather.29.cloned.1.call-start = ((), (), s32[]{:S(2)}) async-start(), calls=%async_computation.24 | async-start | bytes 2621440 | tf_op jit(solution)/shard_map/while/body/eval_jaxpr/all_gather | solution.py:139
  900.2 181.8 %all-gather.35.cloned.1.call-start = ((), (), s32[]{:S(2)}) async-start(), calls=%async_computation.27 | async-start | bytes 2359296 | tf_op jit(solution)/shard_map/while/body/eval_jaxpr/all_gather | solution.py:54
  900.9 228.7 %all-gather.33.cloned.1.call-start = ((), (), s32[]{:S(2)}) async-start(), calls=%async_computation.26 | async-start | bytes 2621440 | tf_op jit(solution)/shard_map/while/body/eval_jaxpr/all_gather | solution.py:124
  979.2 206.8 %reduce-scatter.24.cloned.1.call-start = ((), (), s32[]{:S(2)}) async-start(), calls=%async_computation.28 | async-start | bytes 2621440 | tf_op jit(solution)/shard_map/while/body/eval_jaxpr/reduce_scatter | solution.py:154
  1143.4 87.7 %reduce-scatter.26.cloned.1.call-start = ((), (), s32[]{:S(2)}) async-start(), calls=%async_computation.29 | async-start | bytes 2621440 | tf_op jit(solution)/shard_map/while/body/eval_jaxpr/reduce_scatter | solution.py:132
  1150.3 130.9 %copy-start.11 = (bf16[1024,256]{1,0:T(8,128)(2,1)S(1)}, bf16[1024,256]{1,0:T(8,128)(2,1)}, u32[]{:S(2)}) copy-start(bf16[1024,256]{1,0:T(8,128)(2,1)} %all_gather.87) | copy-start | bytes 1572868 | tf_op jit(solution)/shard_map/while
  1150.4 130.9 %all-gather.37.cloned.1.call-start = ((), (), s32[]{:S(2)}) async-start(), calls=%async_computation.30 | async-start | bytes 2621440 | tf_op jit(solution)/shard_map/while/body/eval_jaxpr/all_gather | solution.py:164
  1236.2 134.9 %reduce-scatter.30.cloned.1.call-start = ((), (), s32[]{:S(2)}) async-start(), calls=%async_computation.32 | async-start | bytes 1572864 | tf_op jit(solution)/shard_map/while/body/eval_jaxpr/reduce_scatter | solution.py:216
  1363.8 19.2 %reduce-scatter.28.cloned.1.call-start = ((), (), s32[]{:S(2)}) async-start(), calls=%async_computation.31 | async-start | bytes 1572864 | tf_op jit(solution)/shard_map/while/body/eval_jaxpr/reduce_scatter | solution.py:222
  1367.1 65.4 %reduce-scatter.32.cloned.1.call-start = ((), (), s32[]{:S(2)}) async-start(), calls=%async_computation.33 | async-start | bytes 2621440 | tf_op jit(solution)/shard_map/while/body/eval_jaxpr/reduce_scatter | solution.py:238
  1438.4 8.9 all-to-all-start.1
  1458.3 36.5 %reduce-scatter.14.cloned.1.call-start = ((), (), s32[]{:S(2)}) async-start(), calls=%async_computation.14 | async-start | bytes 589824 | tf_op jit(solution)/shard_map/reduce_scatter | solution.py:286
  1460.4 75.8 %reduce-scatter.12.cloned.1.call-start = ((), (), s32[]{:S(2)}) async-start(), calls=%async_computation.13 | async-start | bytes 1769472 | tf_op jit(solution)/shard_map/reduce_scatter | solution.py:283
  1463.7 116.7 %reduce-scatter.16.cloned.1.call-start = ((), (), s32[]{:S(2)}) async-start(), calls=%async_computation.15 | async-start | bytes 2359296 | tf_op jit(solution)/shard_map/reduce_scatter | solution.py:289
  1467.7 157.1 %reduce-scatter.18.cloned.1.call-start = ((), (), s32[]{:S(2)}) async-start(), calls=%async_computation.16 | async-start | bytes 2359296 | tf_op jit(solution)/shard_map/reduce_scatter | solution.py:292
  1471.6 202.4 %reduce-scatter.20.cloned.1.call-start = ((), (), s32[]{:S(2)}) async-start(), calls=%async_computation.17 | async-start | bytes 3538944 | tf_op jit(solution)/shard_map/reduce_scatter | solution.py:295
  (103 other events, 1691.1 us)
Sparse Core Ops, SparseCore 0:
  11.3 34.8 all-gather.18
  48.1 25.5 all-gather.22
  75.8 45.6 all-gather.20
  126.6 7.8 all-gather.24
  136.4 10.3 all-gather.26
  177.1 77.9 reduce-scatter.21
  257.0 28.2 all-gather.30
  287.5 45.6 all-gather.28
  335.0 26.5 all-gather.34
  363.6 45.6 all-gather.32
  423.2 42.4 reduce-scatter.23
  467.8 42.8 reduce-scatter.25
  515.9 44.8 all-gather.36
  643.5 7.1 reduce-scatter.29
  652.8 9.5 reduce-scatter.27
  667.0 44.8 reduce-scatter.31
  736.1 30.4 all-gather.18
  768.4 25.5 all-gather.22
  796.1 45.6 all-gather.20
  846.9 7.8 all-gather.24
  856.9 10.2 all-gather.26
  897.5 77.9 reduce-scatter.21
  977.4 28.2 all-gather.30
  1007.7 45.6 all-gather.28
  1055.3 26.5 all-gather.34
  1083.9 45.6 all-gather.32
  1143.5 42.4 reduce-scatter.23
  1188.2 42.8 reduce-scatter.25
  1236.3 44.8 all-gather.36
  1363.9 7.1 reduce-scatter.29
  1373.4 9.5 reduce-scatter.27
  1387.6 44.8 reduce-scatter.31
Sparse Core Ops, SparseCore 1:
  1462.4 32.3 reduce-scatter.13
  1498.0 38.2 reduce-scatter.11
  1539.4 40.9 reduce-scatter.15
  1583.7 41.0 reduce-scatter.17
  1628.1 45.9 reduce-scatter.19
where the time goes:
time: 1690 us; the launch traced here: 1680 us
  waiting for transfers between devices  1170 us (69%)
  matrix products  263 us (16%)
  other arithmetic  136 us (8%)
  local copies, waits for them, and re-layouts  58.1 us (3%)
  blocking collectives  21.7 us (1%)
  starting transfers between devices  18.2 us (1%)
    reduce_scatter x2, waiting for transfers between devices, one_clip(): lax.psum_scatter(partial_one.reshape(-1, patches_here, model_width), 'ten...  149 us
    all_gather x2, waiting for transfers between devices, one_clip(): gathered_one = lax.all_gather(entering_one, 'tensor', axis=0, tiled=True)  95.7 us
    all_gather x2, waiting for transfers between devices, one_clip(): lax.all_gather(grad_branch_two, 'tensor', axis=0, tiled=True)  95.5 us
    all_gather x2, waiting for transfers between devices, one_clip(): lax.all_gather(entering_two, 'tensor', axis=0, tiled=True)  95.4 us
    all_gather x2, waiting for transfers between devices, one_clip(): lax.all_gather(grad_branch_one, 'tensor', axis=0, tiled=True)  89.5 us
    reduce_scatter x2, waiting for transfers between devices, one_clip(): lax.psum_scatter(partial_two.reshape(-1, patches_here, model_width).astyp...  85.1 us
    reduce_scatter x2, waiting for transfers between devices, one_clip(): lax.psum_scatter(partial_back_two.astype(jnp.bfloat16), 'tensor', scatter...  71.1 us
    all_gather x2, waiting for transfers between devices, fetch_weights(): lax.all_gather(shards[4], ('dp', 'frame'), axis=0, tiled=True)  61.1 us
  transfers between devices with their start and end apart: 41, of which 39 were waited for; matrix products, arithmetic and copies ran while one was open for 8% of the time, Pallas kernels for 0%

commit v1 on v0

v1 whole, which is shorter than its diff:
```python
import math

import jax
import jax.numpy as jnp
from jax import lax
from jax.sharding import PartitionSpec as P

HEAD_DIM = 64


epsilon = 1e-06
highest = lax.Precision.HIGHEST


def normalize(values):
    center = values - jnp.mean(values, axis=-1, keepdims=True)
    spread = jnp.mean(center * center, axis=-1, keepdims=True)
    inverse = lax.rsqrt(spread + epsilon)
    return (center * inverse, inverse)


def norm_back(upstream, normed, inverse):
    upstream_mean = jnp.mean(upstream, axis=-1, keepdims=True)
    product_mean = jnp.mean(upstream * normed, axis=-1, keepdims=True)
    return inverse * (upstream - upstream_mean - normed * product_mean)


def level_embedding(levels, model_width):
    halfway = model_width // 2
    frequency = jnp.exp(-math.log(10000.0) * jnp.arange(halfway, dtype=jnp.float32) / halfway)
    angles = levels.astype(jnp.float32)[..., None] * frequency
    return jnp.concatenate([jnp.cos(angles), jnp.sin(angles)], axis=-1)


def gelu_tanh(values):
    return jax.nn.gelu(values, approximate=True)


def on_device(
    tokens, out_grad, noise_index, qkv_weight, out_weight, up_weight, down_weight, ada_weight
):
    clips = tokens.shape[0]
    patches = tokens.shape[2]
    model_width = tokens.shape[-1]
    local_width = qkv_weight.shape[2]
    rows_here = qkv_weight.shape[0]
    heads_here = local_width // HEAD_DIM
    scaling = HEAD_DIM ** (-0.5)
    groups = lax.axis_size("tensor")
    halves = lax.axis_size("frame")
    replicas = lax.axis_size("dp")

    with jax.named_scope("modulation"):
        levels_all = lax.all_gather(noise_index, ("dp", "frame"), axis=0, tiled=True)
        levels_all = levels_all.reshape(replicas * halves, clips, groups)
        condition_all = jax.nn.silu(level_embedding(levels_all, model_width)).astype(jnp.bfloat16)
        row_block = lax.axis_index("dp") * halves + lax.axis_index("frame")
        my_condition = lax.dynamic_slice_in_dim(
            condition_all, row_block * rows_here, rows_here, axis=3
        )
        partial_mod = jnp.einsum(
            "acgd,dkw->acgkw", my_condition, ada_weight, preferred_element_type=jnp.float32
        )
        summed_mod = lax.psum_scatter(
            partial_mod, ("dp", "frame"), scatter_dimension=0, tiled=True
        )[0]
        modulation = lax.all_to_all(summed_mod, "tensor", 1, 3, tiled=True)
        modulation = modulation.reshape(clips, 6, 1, model_width)

    with jax.named_scope("weights"):
        joint_weight, mixer_weight, upward_weight, downward_weight = (
            lax.all_gather(w, ("dp", "frame"), axis=0, tiled=True)
            for w in (qkv_weight, out_weight, up_weight, down_weight)
        )

    residual = tokens[:, 0].astype(jnp.float32)
    upstream = out_grad[:, 0].astype(jnp.float32)
    shift1, scale1, gate1 = modulation[:, 0], modulation[:, 1], modulation[:, 2]
    shift2, scale2, gate2 = modulation[:, 3], modulation[:, 4], modulation[:, 5]

    def gather_tokens(values):
        return lax.all_gather(values, "tensor", axis=1, tiled=True)

    def scatter_tokens(values):
        return lax.psum_scatter(
            values.astype(jnp.bfloat16), "tensor", scatter_dimension=1, tiled=True
        ).astype(jnp.float32)

    with jax.named_scope("forward"):
        normed_one, inverse_one = normalize(residual)
        entering_one = (normed_one * (1.0 + scale1) + shift1).astype(jnp.bfloat16)
        flat_one = gather_tokens(entering_one)
        token_count = flat_one.shape[1]
        projected = jnp.einsum(
            "crd,dkh->crkh", flat_one, joint_weight, preferred_element_type=jnp.float32
        ).astype(jnp.bfloat16)
        queries = projected[:, :, 0]
        keys_all = lax.all_gather(projected[:, :, 1], "frame", axis=1, tiled=True)
        values_all = lax.all_gather(projected[:, :, 2], "frame", axis=1, tiled=True)
        key_heads = keys_all.reshape(clips, -1, heads_here, HEAD_DIM)
        value_heads = values_all.reshape(clips, -1, heads_here, HEAD_DIM)
        block_rows = min(512, token_count)
        block_count = token_count // block_rows
        query_blocks = jnp.moveaxis(
            queries.reshape(clips, block_count, block_rows, heads_here, HEAD_DIM), 1, 0
        )

        def attend(query_block):
            scores = (
                jnp.einsum(
                    "cqhe,ckhe->chqk", query_block, key_heads, preferred_element_type=jnp.float32
                )
                * scaling
            )
            largest = jnp.max(scores, axis=-1, keepdims=True)
            raised = jnp.exp(scores - largest)
            totals_row = jnp.sum(raised, axis=-1, keepdims=True)
            probs_low = (raised / totals_row).astype(jnp.bfloat16)
            outputs = jnp.einsum(
                "chqk,ckhe->cqhe", probs_low, value_heads, preferred_element_type=jnp.float32
            )
            return (outputs.astype(jnp.bfloat16), (largest + jnp.log(totals_row))[..., 0])

        attended_blocks, log_totals = lax.map(attend, query_blocks)
        attended = jnp.moveaxis(attended_blocks, 0, 1).reshape(clips, token_count, local_width)
        partial_one = jnp.einsum(
            "crh,oh->cro", attended, mixer_weight, preferred_element_type=jnp.float32
        )
        branch_one = scatter_tokens(partial_one)
        middle = residual + gate1 * branch_one
        normed_two, inverse_two = normalize(middle)
        entering_two = (normed_two * (1.0 + scale2) + shift2).astype(jnp.bfloat16)
        flat_two = gather_tokens(entering_two)
        up_values = jnp.einsum(
            "crd,df->crf", flat_two, upward_weight, preferred_element_type=jnp.float32
        )
        hidden = gelu_tanh(up_values).astype(jnp.bfloat16)
        partial_two = jnp.einsum(
            "crf,of->cro", hidden, downward_weight, preferred_element_type=jnp.float32
        )
        branch_two = scatter_tokens(partial_two)
        output = (middle + gate2 * branch_two).astype(jnp.bfloat16)

    with jax.named_scope("backward_ffn"):
        grad_gate_two = jnp.sum(upstream * branch_two, axis=1)
        grad_branch_two = (gate2 * upstream).astype(jnp.bfloat16)
        grad_two_all = gather_tokens(grad_branch_two)
        grad_hidden = jnp.einsum(
            "cro,of->crf", grad_two_all, downward_weight, preferred_element_type=jnp.float32
        )
        down_total = jnp.einsum(
            "cro,crf->of", grad_two_all, hidden, preferred_element_type=jnp.float32
        )
        _, gelu_pullback = jax.vjp(gelu_tanh, up_values)
        grad_up = gelu_pullback(grad_hidden)[0].astype(jnp.bfloat16)
        up_total = jnp.einsum(
            "crd,crf->df", flat_two, grad_up, preferred_element_type=jnp.float32
        )
        partial_back_two = jnp.einsum(
            "crf,df->crd", grad_up, upward_weight, preferred_element_type=jnp.float32
        )
        grad_entering_two = scatter_tokens(partial_back_two)
        grad_shift_two = jnp.sum(grad_entering_two, axis=1)
        grad_scale_two = jnp.sum(grad_entering_two * normed_two, axis=1)
        grad_middle = upstream + norm_back(
            grad_entering_two * (1.0 + scale2), normed_two, inverse_two
        )
        grad_gate_one = jnp.sum(grad_middle * branch_one, axis=1)

    with jax.named_scope("backward_attention"):
        grad_branch_one = (gate1 * grad_middle).astype(jnp.bfloat16)
        grad_one_all = gather_tokens(grad_branch_one)
        grad_attended = jnp.einsum(
            "cro,oh->crh", grad_one_all, mixer_weight, preferred_element_type=jnp.float32
        ).astype(jnp.bfloat16)
        mixer_total = jnp.einsum(
            "cro,crh->oh", grad_one_all, attended, preferred_element_type=jnp.float32
        )
        grad_blocks = jnp.moveaxis(
            grad_attended.reshape(clips, block_count, block_rows, heads_here, HEAD_DIM), 1, 0
        )

        def attend_back(carried, pieces):
            key_sum, value_sum = carried
            query_block, grad_block, log_block = pieces
            scores = (
                jnp.einsum(
                    "cqhe,ckhe->chqk", query_block, key_heads, preferred_element_type=jnp.float32
                )
                * scaling
            )
            probs = jnp.exp(scores - log_block[..., None])
            grad_probs = jnp.einsum(
                "cqhe,ckhe->chqk", grad_block, value_heads, preferred_element_type=jnp.float32
            )
            value_sum = value_sum + jnp.einsum(
                "chqk,cqhe->ckhe",
                probs.astype(jnp.bfloat16),
                grad_block,
                preferred_element_type=jnp.float32,
            )
            row_terms = jnp.sum(probs * grad_probs, axis=-1, keepdims=True)
            grad_scores = (probs * (grad_probs - row_terms)).astype(jnp.bfloat16)
            grad_queries = (
                jnp.einsum(
                    "chqk,ckhe->cqhe", grad_scores, key_heads, preferred_element_type=jnp.float32
                )
                * scaling
            )
            key_sum = (
                key_sum
                + jnp.einsum(
                    "chqk,cqhe->ckhe", grad_scores, query_block, preferred_element_type=jnp.float32
                )
                * scaling
            )
            return ((key_sum, value_sum), grad_queries)

        zeros_keys = jnp.zeros(key_heads.shape, jnp.float32)
        (key_grads, value_grads), query_grads = lax.scan(
            attend_back, (zeros_keys, zeros_keys), (query_blocks, grad_blocks, log_totals)
        )
        query_grads = jnp.moveaxis(query_grads, 0, 1).reshape(clips, token_count, local_width)
        key_own, value_own = (
            lax.psum_scatter(
                grads.reshape(clips, -1, local_width).astype(jnp.bfloat16),
                "frame",
                scatter_dimension=1,
                tiled=True,
            ).astype(jnp.float32)
            for grads in (key_grads, value_grads)
        )
        grad_projected = jnp.stack([query_grads, key_own, value_own], axis=2).astype(
            jnp.bfloat16
        )
        joint_total = jnp.einsum(
            "crd,crkh->dkh", flat_one, grad_projected, preferred_element_type=jnp.float32
        )
        partial_back_one = jnp.einsum(
            "crkh,dkh->crd", grad_projected, joint_weight, preferred_element_type=jnp.float32
        )
        grad_entering_one = scatter_tokens(partial_back_one)
        grad_shift_one = jnp.sum(grad_entering_one, axis=1)
        grad_scale_one = jnp.sum(grad_entering_one * normed_one, axis=1)
        grad_input = grad_middle + norm_back(
            grad_entering_one * (1.0 + scale1), normed_one, inverse_one
        )

    with jax.named_scope("ada_grad"):
        grad_modulation = jnp.stack(
            [
                grad_shift_one,
                grad_scale_one,
                grad_gate_one,
                grad_shift_two,
                grad_scale_two,
                grad_gate_two,
            ],
            axis=1,
        )
        grad_columns = lax.all_to_all(
            grad_modulation.reshape(clips, 1, 6, model_width), "tensor", 3, 1, tiled=True
        )
        grad_all = lax.all_gather(grad_columns, ("dp", "frame"), axis=0, tiled=True)
        grad_all = grad_all.reshape(replicas * halves, clips, groups, 6, local_width)
        adaptive_total = jnp.einsum(
            "acgd,acgkw->dkw",
            my_condition.astype(jnp.float32),
            grad_all,
            precision=highest,
        )

    with jax.named_scope("weight_grads"):
        summed = tuple(
            lax.psum_scatter(
                total.astype(jnp.bfloat16), ("dp", "frame"), scatter_dimension=0, tiled=True
            ).astype(jnp.float32)
            for total in (joint_total, mixer_total, up_total, down_total)
        )
    result = output[:, None]
    input_grad = grad_input.astype(jnp.bfloat16)[:, None]
    return (result, input_grad, summed[0], summed[1], summed[2], summed[3], adaptive_total)


def solution(mesh):
    return jax.shard_map(
        on_device,
        mesh=mesh,
        in_specs=(
            P("dp", ("frame", "tensor"), None, None),
            P("dp", ("frame", "tensor"), None, None),
            P("dp", "frame"),
            P(("dp", "frame"), None, "tensor"),
            P(("dp", "frame"), "tensor"),
            P(("dp", "frame"), "tensor"),
            P(("dp", "frame"), "tensor"),
            P(("dp", "frame"), None, "tensor"),
        ),
        out_specs=(
            P("dp", ("frame", "tensor"), None, None),
            P("dp", ("frame", "tensor"), None, None),
            P(("dp", "frame"), None, "tensor"),
            P(("dp", "frame"), "tensor"),
            P(("dp", "frame"), "tensor"),
            P(("dp", "frame"), "tensor"),
            P(("dp", "frame"), None, "tensor"),
        ),
        check_vma=False,
    )
```

time: 1690 us -> 1420 us (0.84)
  waiting for transfers between devices: 1170 us -> 874 us
  matrix products: 263 us -> 302 us
    all_gather x20 -> x9, waiting for transfers between devices: 569 us -> 383 us  [the longest x4 329 us: gather_tokens(): return lax.all_gather(values, 'tensor', axis=1, tiled=True)]
    reduce_scatter x17 -> x10, waiting for transfers between devices: 572 us -> 430 us  [the longest x4 309 us: scatter_tokens(): lax.psum_scatter(values.astype(jnp.bfloat16), 'tensor', scatter_dimension...]
    unnamed x5 -> x21, waiting for transfers between devices: 0.08 us -> 53.7 us
    dot_general x56 -> x28, matrix products: 263 us -> 302 us  [the longest x2 47.7 us: attend_back(): jnp.einsum('cqhe,ckhe->chqk', grad_block, value_heads, preferred_element_...]
    while x234 -> x5, local copies, waits for them, and re-layouts: 24.4 us -> 3.23 us
    convert_element_type x22 -> x11, other arithmetic: 43.6 us -> 22.7 us  [the longest x4 6.79 us: on_device(): summed = tuple((lax.psum_scatter(total.astype(jnp.bfloat16), ('dp', 'fram...]
    convert_element_type x4 -> x2, other arithmetic: 42.1 us -> 55.8 us  [attend_back(): grad_scores = (probs * (grad_probs - row_terms)).astype(jnp.bfloat16)]
  transfers between devices with their start and end apart: 41 -> 22, of which waited for: 39 -> 19; matrix products, arithmetic and copies ran while one was open for 8% -> 8% of each run, Pallas kernels for 0% -> 0%
where the time goes in v1:
time: 1420 us
  waiting for transfers between devices  874 us (62%)
  matrix products  302 us (21%)
  other arithmetic  129 us (9%)
  local copies, waits for them, and re-layouts  53.9 us (4%)
  blocking collectives  31.3 us (2%)
  between operations  15.2 us (1%)
    all_gather x4, waiting for transfers between devices, gather_tokens(): return lax.all_gather(values, 'tensor', axis=1, tiled=True)  329 us
    reduce_scatter x4, waiting for transfers between devices, scatter_tokens(): lax.psum_scatter(values.astype(jnp.bfloat16), 'tensor', scatter_dimension...  309 us
    reduce_scatter x4, waiting for transfers between devices, on_device(): lax.psum_scatter(total.astype(jnp.bfloat16), ('dp', 'frame'), scatter_dim...  121 us
    convert_element_type x2, other arithmetic, attend_back(): grad_scores = (probs * (grad_probs - row_terms)).astype(jnp.bfloat16)  55.8 us
    unnamed x21, waiting for transfers between devices  53.7 us
    all_gather x3, waiting for transfers between devices, on_device(): lax.all_gather(w, ('dp', 'frame'), axis=0, tiled=True)  49.6 us
    dot_general x2, matrix products, attend_back(): jnp.einsum('cqhe,ckhe->chqk', grad_block, value_heads, preferred_element_...  47.7 us
    dot_general x2, matrix products, attend_back(): jnp.einsum('chqk,cqhe->ckhe', probs.astype(jnp.bfloat16), grad_block, pre...  33.3 us
  transfers between devices with their start and end apart: 22, of which 19 were waited for; matrix products, arithmetic and copies ran while one was open for 8% of the time, Pallas kernels for 0%

profile of v1, /device:TPU:0, one launch (start us, length us, event | category | flops | bytes accessed | tf_op | source)
XLA Modules:
  0.0 1416.2 jit_solution(16636748688124716342)
XLA Ops:
  7.3 10.7 all-gather.3
  24.1 50.8 %all-reduce.3.cloned.1.call-done = f32[8,2,4,6,256]{4,2,3,1,0:T(4,128)} async-done(((f32[8,2,4,6,256]{4,2,3,1,0:T(4,128)}), f32[8,2,4,6,256]{4,2,3,1,0:T(4,128)}) %all-reduce.3.cloned.1.call-update) | async-done | bytes 393232
  89.4 12.3 all-gather.16.cloned.1.call-done
  101.8 82.9 %all-gather.14.cloned.1.call-done = bf16[2,1024,1024]{2,1,0:T(8,128)(2,1)} async-done(((bf16[2,256,1024]{2,1,0:T(8,128)(2,1)}), bf16[2,1024,1024]{2,1,0:T(8,128)(2,1)}) %all-gather.14.cloned.1.call-update) | async-done | bytes 4194320 | tf_op jit(solution)/shard_map/forward/all_gather | solution.py:82
  184.7 6.1 fusion.57
  193.1 11.0 all_gather.41
  217.8 87.8 %while.27 = (s32[]{:T(128)}, bf16[2,2,512,4,64]{2,4,3,1,0:T(8,128)(2,1)}, f32[2,2,4,512]{3,2,1,0:T(4,128)S(1)}, bf16[2,2,512,4,64]{2,4,3,1,0:T(8,128)(2,1)}, bf1...) while((s32[]{:T(128)}, bf16[2,2,512,4,64]{2,4,3,1,0:T(8,128)(2,1)}, ...), condition=%wide.region_6.7_spmd, body=%wide.region_3.6_spmd.sunk | while | flops 2223239168 | bytes 106037344 | solution.py:124
  217.8 14.3 %multiply_reduce_fusion.5 = (f32[2,4,512]{2,1,0:T(4,128)S(1)}, f32[2,4,512,2048]{3,2,1,0:T(8,128)}) fusion(bf16[2,2048,4,64]{1,3,2,0:T(8,128)(2,1)S(1)} %get-tuple-element.435, bf16[2,2,512,4,64]{2,4,3,1,0:T(8,128)(2,1)} %get-tuple-element.434, s32[]{:T(128)S(6)} %copy.212), kind=kOutput, calls=%fused_computation.2.clone.1 | convolution fusion | flops 1090514944 | bytes 36192260 | tf_op jit(solution)/shard_map/forward/while/body/eval_jaxpr/cqhe,ckhe->chqk/dot_general | solution.py:110
  232.1 14.0 fusion.138
  246.1 15.5 %fusion.139 = bf16[2,2,512,4,64]{2,4,3,1,0:T(8,128)(2,1)} fusion(bf16[2,2,512,4,64]{2,4,3,1,0:T(8,128)(2,1)} %get-tuple-element.425, s32[]{:T(128)S(6)} %copy.212, bf16[2,2048,4,64]{1,3,2,0:T(8,128)(2,1)} %get-tuple-element.436, f32[2,4,512,2048]{3,2,1,0:T(8,128)} %get-tuple-element.404, f32[2,4,512]{2,1,0:T(4,128)S(1)} %fusion.138, ...), kind=kOutput, calls=%fused_computation.7.clone.1 | convolution fusion | flops 1107558400 | bytes 36208644 | tf_op jit(solution)/shard_map/forward/while/body/eval_jaxpr/chqk,ckhe->cqhe/dot_general | solution.py:119
  261.7 14.3 %multiply_reduce_fusion.5 = (f32[2,4,512]{2,1,0:T(4,128)S(1)}, f32[2,4,512,2048]{3,2,1,0:T(8,128)}) fusion(bf16[2,2048,4,64]{1,3,2,0:T(8,128)(2,1)S(1)} %get-tuple-element.435, bf16[2,2,512,4,64]{2,4,3,1,0:T(8,128)(2,1)} %get-tuple-element.434, s32[]{:T(128)S(6)} %copy.212), kind=kOutput, calls=%fused_computation.2.clone.1 | convolution fusion | flops 1090514944 | bytes 36192260 | tf_op jit(solution)/shard_map/forward/while/body/eval_jaxpr/cqhe,ckhe->chqk/dot_general | solution.py:110
  276.0 14.0 fusion.138
  290.0 15.5 %fusion.139 = bf16[2,2,512,4,64]{2,4,3,1,0:T(8,128)(2,1)} fusion(bf16[2,2,512,4,64]{2,4,3,1,0:T(8,128)(2,1)} %get-tuple-element.425, s32[]{:T(128)S(6)} %copy.212, bf16[2,2048,4,64]{1,3,2,0:T(8,128)(2,1)} %get-tuple-element.436, f32[2,4,512,2048]{3,2,1,0:T(8,128)} %get-tuple-element.404, f32[2,4,512]{2,1,0:T(4,128)S(1)} %fusion.138, ...), kind=kOutput, calls=%fused_computation.7.clone.1 | convolution fusion | flops 1107558400 | bytes 36208644 | tf_op jit(solution)/shard_map/forward/while/body/eval_jaxpr/chqk,ckhe->cqhe/dot_general | solution.py:119
  317.2 76.9 %reduce-scatter.11.cloned.1.call-done = bf16[2,256,1024]{2,1,0:T(8,128)(2,1)} async-done(((bf16[2,1024,1024]{2,1,0:T(8,128)(2,1)}), bf16[2,256,1024]{2,1,0:T(8,128)(2,1)}) %reduce-scatter.11.cloned.1.call-update) | async-done | bytes 1048592 | tf_op jit(solution)/shard_map/forward/reduce_scatter | solution.py:85
  404.6 19.7 %all-gather.20.cloned.1.call-done = bf16[1024,1024]{1,0:T(8,128)(2,1)} async-done(((bf16[128,1024]{1,0:T(8,128)(2,1)}), bf16[1024,1024]{1,0:T(8,128)(2,1)}) %all-gather.20.cloned.1.call-update) | async-done | bytes 2097168 | tf_op jit(solution)/shard_map/weights/all_gather | solution.py:72
  424.3 82.9 %all-gather.18.cloned.1.call-done = bf16[2,1024,1024]{2,1,0:T(8,128)(2,1)} async-done(((bf16[2,256,1024]{2,1,0:T(8,128)(2,1)}), bf16[2,1024,1024]{2,1,0:T(8,128)(2,1)}) %all-gather.18.cloned.1.call-update) | async-done | bytes 4194320 | tf_op jit(solution)/shard_map/forward/all_gather | solution.py:82
  507.2 10.6 fusion.81
  517.9 17.6 %all-gather.22.cloned.1.call-done = bf16[1024,1024]{1,0:T(8,128)(2,1)} async-done(((bf16[128,1024]{1,0:T(8,128)(2,1)}), bf16[1024,1024]{1,0:T(8,128)(2,1)}) %all-gather.22.cloned.1.call-update) | async-done | bytes 2097168 | tf_op jit(solution)/shard_map/weights/all_gather | solution.py:72
  535.4 82.2 %all-gather.24.cloned.1.call-done = bf16[2,1024,1024]{2,1,0:T(8,128)(2,1)} async-done(((bf16[2,256,1024]{2,1,0:T(8,128)(2,1)}), bf16[2,1024,1024]{2,1,0:T(8,128)(2,1)}) %all-gather.24.cloned.1.call-update) | async-done | bytes 4194320 | tf_op jit(solution)/shard_map/backward_ffn/all_gather | solution.py:82
  617.6 12.5 fusion.40
  632.1 6.3 convolution_convert_fusion
  638.7 75.2 %reduce-scatter.15.cloned.1.call-done = bf16[2,256,1024]{2,1,0:T(8,128)(2,1)} async-done(((bf16[2,1024,1024]{2,1,0:T(8,128)(2,1)}), bf16[2,256,1024]{2,1,0:T(8,128)(2,1)}) %reduce-scatter.15.cloned.1.call-update) | async-done | bytes 1048592 | tf_op jit(solution)/shard_map/backward_ffn/reduce_scatter | solution.py:85
  721.0 81.3 %all-gather.26.cloned.1.call-done = bf16[2,1024,1024]{2,1,0:T(8,128)(2,1)} async-done(((bf16[2,256,1024]{2,1,0:T(8,128)(2,1)}), bf16[2,1024,1024]{2,1,0:T(8,128)(2,1)}) %all-gather.26.cloned.1.call-update) | async-done | bytes 4194320 | tf_op jit(solution)/shard_map/backward_attention/all_gather | solution.py:82
  814.1 200.8 %while.28 = (s32[]{:T(128)}, f32[2,2048,4,64]{1,3,2,0:T(8,128)}, f32[2,2048,4,64]{1,3,2,0:T(8,128)}, bf16[2,2,512,4,64]{2,4,3,1,0:T(8,128)(2,1)}, bf16[2,2,512,4...) while((s32[]{:T(128)}, f32[2,2048,4,64]{1,3,2,0:T(8,128)}, ...), condition=%wide.region_16.17_spmd.clone, body=%wide.region_14.16_spmd.clone.sunk | while | flops 5474873344 | bytes 345096384 | solution.py:220
  814.1 14.3 %fusion.149 = f32[2,4,512,2048]{3,2,1,0:T(8,128)} fusion(bf16[2,2048,4,64]{1,3,2,0:T(8,128)(2,1)S(1)} %get-tuple-element.465, bf16[2,2,512,4,64]{2,4,3,1,0:T(8,128)(2,1)} %get-tuple-element.464, s32[]{:T(128)S(6)} %copy.222), kind=kOutput, calls=%fused_computation.30.clone.1 | convolution fusion | flops 1073741824 | bytes 36175876 | tf_op jit(solution)/shard_map/backward_attention/while/body/eval_jaxpr/cqhe,ckhe->chqk/dot_general | solution.py:187
  828.4 16.1 %bitcast_add_fusion.5 = f32[2,2048,4,64]{1,3,2,0:T(8,128)} fusion(f32[2,2048,4,64]{1,3,2,0:T(8,128)} %get-tuple-element.451, f32[2,4,512,2048]{3,2,1,0:T(8,128)} %fusion.149, f32[2,4,512]{2,1,0:T(4,128)S(1)} %dynamic-slice_bitcast_fusion.3, pred[]{:T(512)S(6)} %compare.3, bf16[2,2,512,4,64]{2,4,3,1,0:T(8,128)(2,1)} %get-tuple-element.467, s32[]{:T(128)S(6)} %copy.222), kind=kOutput, calls=%fused_computation.21.clone.1 | convolution fusion | flops 1101004800 | bytes 42483716 | tf_op jit(solution)/shard_map/backward_attention/while/body/eval_jaxpr/chqk,cqhe->ckhe/dot_general | solution.py:196
  844.4 23.8 %multiply_reduce_fusion.6 = (f32[2,4,512]{2,1,0:T(4,128)S(1)}, f32[2,4,512,2048]{3,2,1,0:T(8,128)}) fusion(f32[2,4,512,2048]{3,2,1,0:T(8,128)} %fusion.149, f32[2,4,512]{2,1,0:T(4,128)S(1)} %dynamic-slice_bitcast_fusion.3, bf16[2,2048,4,64]{1,3,2,0:T(8,128)(2,1)} %get-tuple-element.468, bf16[2,2,512,4,64]{2,4,3,1,0:T(8,128)(2,1)} %get-tuple-element.467, ...), kind=kOutput, calls=%fused_computation.15.clone.1 | convolution fusion | flops 1107292160 | bytes 69763072 | tf_op jit(solution)/shard_map/backward_attention/while/body/eval_jaxpr/cqhe,ckhe->chqk/dot_general | solution.py:193
  868.2 27.9 %multiply_convert_fusion.7 = bf16[2,4,512,2048]{3,2,1,0:T(8,128)(2,1)} fusion(f32[2,4,512,2048]{3,2,1,0:T(8,128)} %get-tuple-element.415, f32[2,4,512,2048]{3,2,1,0:T(8,128)} %fusion.149, f32[2,4,512]{2,1,0:T(4,128)S(1)} %get-tuple-element.416, f32[2,4,512]{2,1,0:T(4,128)S(1)} %dynamic-slice_bitcast_fusion.3), kind=kLoop, calls=%fused_computation.14.clone.1 | loop fusion | flops 41943040 | bytes 83918848 | tf_op jit(solution)/shard_map/backward_attention/while/body/eval_jaxpr/convert_element_type | solution.py:203
  896.2 9.7 fusion.150
  906.9 6.1 bitcast_add_fusion.4
  913.0 14.3 %fusion.149 = f32[2,4,512,2048]{3,2,1,0:T(8,128)} fusion(bf16[2,2048,4,64]{1,3,2,0:T(8,128)(2,1)S(1)} %get-tuple-element.465, bf16[2,2,512,4,64]{2,4,3,1,0:T(8,128)(2,1)} %get-tuple-element.464, s32[]{:T(128)S(6)} %copy.222), kind=kOutput, calls=%fused_computation.30.clone.1 | convolution fusion | flops 1073741824 | bytes 36175876 | tf_op jit(solution)/shard_map/backward_attention/while/body/eval_jaxpr/cqhe,ckhe->chqk/dot_general | solution.py:187
  927.3 17.2 %bitcast_add_fusion.5 = f32[2,2048,4,64]{1,3,2,0:T(8,128)} fusion(f32[2,2048,4,64]{1,3,2,0:T(8,128)} %get-tuple-element.451, f32[2,4,512,2048]{3,2,1,0:T(8,128)} %fusion.149, f32[2,4,512]{2,1,0:T(4,128)S(1)} %dynamic-slice_bitcast_fusion.3, pred[]{:T(512)S(6)} %compare.3, bf16[2,2,512,4,64]{2,4,3,1,0:T(8,128)(2,1)} %get-tuple-element.467, s32[]{:T(128)S(6)} %copy.222), kind=kOutput, calls=%fused_computation.21.clone.1 | convolution fusion | flops 1101004800 | bytes 42483716 | tf_op jit(solution)/shard_map/backward_attention/while/body/eval_jaxpr/chqk,cqhe->ckhe/dot_general | solution.py:196
  944.6 23.9 %multiply_reduce_fusion.6 = (f32[2,4,512]{2,1,0:T(4,128)S(1)}, f32[2,4,512,2048]{3,2,1,0:T(8,128)}) fusion(f32[2,4,512,2048]{3,2,1,0:T(8,128)} %fusion.149, f32[2,4,512]{2,1,0:T(4,128)S(1)} %dynamic-slice_bitcast_fusion.3, bf16[2,2048,4,64]{1,3,2,0:T(8,128)(2,1)} %get-tuple-element.468, bf16[2,2,512,4,64]{2,4,3,1,0:T(8,128)(2,1)} %get-tuple-element.467, ...), kind=kOutput, calls=%fused_computation.15.clone.1 | convolution fusion | flops 1107292160 | bytes 69763072 | tf_op jit(solution)/shard_map/backward_attention/while/body/eval_jaxpr/cqhe,ckhe->chqk/dot_general | solution.py:193
  968.4 27.9 %multiply_convert_fusion.7 = bf16[2,4,512,2048]{3,2,1,0:T(8,128)(2,1)} fusion(f32[2,4,512,2048]{3,2,1,0:T(8,128)} %get-tuple-element.415, f32[2,4,512,2048]{3,2,1,0:T(8,128)} %fusion.149, f32[2,4,512]{2,1,0:T(4,128)S(1)} %get-tuple-element.416, f32[2,4,512]{2,1,0:T(4,128)S(1)} %dynamic-slice_bitcast_fusion.3), kind=kLoop, calls=%fused_computation.14.clone.1 | loop fusion | flops 41943040 | bytes 83918848 | tf_op jit(solution)/shard_map/backward_attention/while/body/eval_jaxpr/convert_element_type | solution.py:203
  996.3 9.7 fusion.150
  1007.1 7.4 bitcast_add_fusion.4
  1025.2 11.2 bitcast_convert_fusion.1
  1036.4 10.1 bitcast_convert_fusion.2
  1056.7 7.7 bitcast_convert_fusion.3
  1064.5 11.8 convolution_convert_fusion.1
  1077.8 6.7 bitcast_convert_fusion
  1089.0 42.5 %reduce-scatter.27.cloned.1.call-done = bf16[128,1024]{1,0:T(8,128)(2,1)} async-done(((bf16[1024,1024]{1,0:T(8,128)(2,1)}), bf16[128,1024]{1,0:T(8,128)(2,1)}) %reduce-scatter.27.cloned.1.call-update) | async-done | bytes 262160 | tf_op jit(solution)/shard_map/weight_grads/reduce_scatter | solution.py:275
  1133.3 35.9 %reduce-scatter.25.cloned.1.call-done = bf16[128,256]{1,0:T(8,128)(2,1)} async-done(((bf16[1024,256]{1,0:T(8,128)(2,1)}), bf16[128,256]{1,0:T(8,128)(2,1)}) %reduce-scatter.25.cloned.1.call-update) | async-done | bytes 65552 | tf_op jit(solution)/shard_map/weight_grads/reduce_scatter | solution.py:275
  1170.7 40.0 %reduce-scatter.23.cloned.1.call-done = bf16[128,3,256]{2,0,1:T(8,128)(2,1)} async-done(((bf16[1024,3,256]{2,0,1:T(8,128)(2,1)}), bf16[128,3,256]{2,0,1:T(8,128)(2,1)}) %reduce-scatter.23.cloned.1.call-update) | async-done | bytes 196624 | tf_op jit(solution)/shard_map/weight_grads/reduce_scatter | solution.py:275
  1212.4 77.4 %reduce-scatter.13.cloned.1.call-done = bf16[2,256,1024]{2,1,0:T(8,128)(2,1)} async-done(((bf16[2,1024,1024]{2,1,0:T(8,128)(2,1)}), bf16[2,256,1024]{2,1,0:T(8,128)(2,1)}) %reduce-scatter.13.cloned.1.call-update) | async-done | bytes 1048592 | tf_op jit(solution)/shard_map/forward/reduce_scatter | solution.py:85
  1289.8 79.5 %reduce-scatter.21.cloned.1.call-done = bf16[2,256,1024]{2,1,0:T(8,128)(2,1)} async-done(((bf16[2,1024,1024]{2,1,0:T(8,128)(2,1)}), bf16[2,256,1024]{2,1,0:T(8,128)(2,1)}) %reduce-scatter.21.cloned.1.call-update) | async-done | bytes 1048592 | tf_op jit(solution)/shard_map/backward_attention/reduce_scatter | solution.py:85
  1369.4 5.7 fusion.74
  1397.4 9.5 all-gather.2
  (205 shorter events, 137.4 us)
Async XLA Ops:
  7.2 12.1 copy-start
  7.2 16.5 %copy-start.3 = (bf16[2,1,256,1024]{3,2,1,0:T(8,128)(2,1)S(1)}, bf16[2,1,256,1024]{3,2,1,0:T(8,128)(2,1)}, u32[]{:S(2)}) copy-start(bf16[2,1,256,1024]{3,2,1,0:T(8,128)(2,1)} %param.12) | copy-start | bytes 3145732
  7.2 67.7 %all-reduce.3.cloned.1.call-start = ((), (), s32[]{:S(2)}) async-start(), calls=%async_computation.31 | async-start | bytes 786432
  20.2 81.6 %all-gather.16.cloned.1.call-start = ((), (), s32[]{:S(2)}) async-start(), calls=%async_computation.13 | async-start | bytes 1769472 | tf_op jit(solution)/shard_map/weights/all_gather | solution.py:72
  23.7 161.0 %copy-start.26 = (f32[2,256]{1,0:T(2,128)}, f32[2,256]{1,0:T(2,128)S(1)}, u32[]{:S(2)}) copy-start(f32[2,256]{1,0:T(2,128)S(1)} %broadcast_multiply_fusion.5) | copy-start | bytes 6148
  77.0 10.2 all-to-all-start
  81.5 103.1 %all-gather.14.cloned.1.call-start = ((), (), s32[]{:S(2)}) async-start(), calls=%async_computation.12 | async-start | bytes 5242880 | tf_op jit(solution)/shard_map/forward/all_gather | solution.py:82
  81.6 103.1 %copy-start.33 = (f32[2,256]{1,0:T(2,128)}, f32[2,256]{1,0:T(2,128)S(1)}, u32[]{:S(2)}) copy-start(f32[2,256]{1,0:T(2,128)S(1)} %add_rsqrt_fusion.1) | copy-start | bytes 6148
  87.9 102.9 %copy-start.17 = (f32[2,1024]{1,0:T(2,128)}, f32[2,1024]{1,0:T(2,128)S(1)}, u32[]{:S(2)}) copy-start(f32[2,1024]{1,0:T(2,128)S(1)} %get-tuple-element.311) | copy-start | bytes 24580
  89.4 117.2 %all-gather.30.cloned.1.call-start = ((), (), s32[]{:S(2)}) async-start(), calls=%async_computation.30 | async-start | bytes 3145728 | tf_op jit(solution)/shard_map/forward/all_gather | solution.py:99
  192.4 22.4 %all-gather.28.cloned.1.call-start = ((), (), s32[]{:S(2)}) async-start(), calls=%async_computation.29 | async-start | bytes 3145728 | tf_op jit(solution)/shard_map/forward/all_gather | solution.py:98
  193.0 201.1 %reduce-scatter.11.cloned.1.call-start = ((), (), s32[]{:S(2)}) async-start(), calls=%async_computation.14 | async-start | bytes 5242880 | tf_op jit(solution)/shard_map/forward/reduce_scatter | solution.py:85
  316.0 78.2 %copy-start.12 = (f32[2,1024]{1,0:T(2,128)S(1)}, f32[2,1024]{1,0:T(2,128)}, u32[]{:S(2)}) copy-start(f32[2,1024]{1,0:T(2,128)} %get-tuple-element.312) | copy-start | bytes 24580
  316.0 82.3 %copy-start.14 = (f32[2,1024]{1,0:T(2,128)S(1)}, f32[2,1024]{1,0:T(2,128)}, u32[]{:S(2)}) copy-start(f32[2,1024]{1,0:T(2,128)} %get-tuple-element.309) | copy-start | bytes 24580
  316.0 82.3 %copy-start.32 = (f32[2,1024]{1,0:T(2,128)S(1)}, f32[2,1024]{1,0:T(2,128)}, u32[]{:S(2)}) copy-start(f32[2,1024]{1,0:T(2,128)} %get-tuple-element.308) | copy-start | bytes 24580
  316.0 108.3 %all-gather.20.cloned.1.call-start = ((), (), s32[]{:S(2)}) async-start(), calls=%async_computation.16 | async-start | bytes 2359296 | tf_op jit(solution)/shard_map/weights/all_gather | solution.py:72
  316.8 190.5 %all-gather.18.cloned.1.call-start = ((), (), s32[]{:S(2)}) async-start(), calls=%async_computation.15 | async-start | bytes 5242880 | tf_op jit(solution)/shard_map/forward/all_gather | solution.py:82
  396.2 320.6 %copy-start.19 = (f32[2,256]{1,0:T(2,128)}, f32[2,256]{1,0:T(2,128)S(1)}, u32[]{:S(2)}) copy-start(f32[2,256]{1,0:T(2,128)S(1)} %broadcast_multiply_fusion.4) | copy-start | bytes 6148
  398.3 318.4 %copy-start.21 = (f32[2,256]{1,0:T(2,128)}, f32[2,256]{1,0:T(2,128)S(1)}, u32[]{:S(2)}) copy-start(f32[2,256]{1,0:T(2,128)S(1)} %add_rsqrt_fusion) | copy-start | bytes 6148
  401.2 134.2 %all-gather.22.cloned.1.call-start = ((), (), s32[]{:S(2)}) async-start(), calls=%async_computation.17 | async-start | bytes 2359296 | tf_op jit(solution)/shard_map/weights/all_gather | solution.py:72
  402.0 215.7 %all-gather.24.cloned.1.call-start = ((), (), s32[]{:S(2)}) async-start(), calls=%async_computation.19 | async-start | bytes 5242880 | tf_op jit(solution)/shard_map/backward_ffn/all_gather | solution.py:82
  404.6 309.3 %reduce-scatter.15.cloned.1.call-start = ((), (), s32[]{:S(2)}) async-start(), calls=%async_computation.20 | async-start | bytes 5242880 | tf_op jit(solution)/shard_map/backward_ffn/reduce_scatter | solution.py:85
  617.6 14.5 %copy-start.35 = (bf16[1024,1024]{1,0:T(8,128)(2,1)S(1)}, bf16[1024,1024]{1,0:T(8,128)(2,1)}, u32[]{:S(2)}) copy-start(bf16[1024,1024]{1,0:T(8,128)(2,1)} %all-gather.20.cloned.1.call-done) | copy-start | bytes 6291460
  638.5 163.8 %all-gather.26.cloned.1.call-start = ((), (), s32[]{:S(2)}) async-start(), calls=%async_computation.21 | async-start | bytes 5242880 | tf_op jit(solution)/shard_map/backward_attention/all_gather | solution.py:82
  720.9 335.7 %reduce-scatter.17.cloned.1.call-start = ((), (), s32[]{:S(2)}) async-start(), calls=%async_computation.22 | async-start | bytes 3145728 | tf_op jit(solution)/shard_map/backward_attention/reduce_scatter | solution.py:225
  896.2 10.7 copy-start.2
  1020.0 36.7 %reduce-scatter.19.cloned.1.call-start = ((), (), s32[]{:S(2)}) async-start(), calls=%async_computation.23 | async-start | bytes 3145728 | tf_op jit(solution)/shard_map/backward_attention/reduce_scatter | solution.py:225
  1025.1 62.1 %reduce-scatter.29.cloned.1.call-start = ((), (), s32[]{:S(2)}) async-start(), calls=%async_computation.28 | async-start | bytes 2359296 | tf_op jit(solution)/shard_map/weight_grads/reduce_scatter | solution.py:275
  1036.4 95.1 %reduce-scatter.27.cloned.1.call-start = ((), (), s32[]{:S(2)}) async-start(), calls=%async_computation.27 | async-start | bytes 2359296 | tf_op jit(solution)/shard_map/weight_grads/reduce_scatter | solution.py:275
  1046.5 122.6 %reduce-scatter.25.cloned.1.call-start = ((), (), s32[]{:S(2)}) async-start(), calls=%async_computation.26 | async-start | bytes 589824 | tf_op jit(solution)/shard_map/weight_grads/reduce_scatter | solution.py:275
  1056.6 154.1 %reduce-scatter.23.cloned.1.call-start = ((), (), s32[]{:S(2)}) async-start(), calls=%async_computation.25 | async-start | bytes 1769472 | tf_op jit(solution)/shard_map/weight_grads/reduce_scatter | solution.py:275
  1064.5 225.4 %reduce-scatter.13.cloned.1.call-start = ((), (), s32[]{:S(2)}) async-start(), calls=%async_computation.18 | async-start | bytes 5242880 | tf_op jit(solution)/shard_map/forward/reduce_scatter | solution.py:85
  1076.3 293.0 %reduce-scatter.21.cloned.1.call-start = ((), (), s32[]{:S(2)}) async-start(), calls=%async_computation.24 | async-start | bytes 5242880 | tf_op jit(solution)/shard_map/backward_attention/reduce_scatter | solution.py:85
  1084.5 284.8 %copy-start.4 = (bf16[2,1,256,1024]{3,2,1,0:T(8,128)(2,1)S(1)}, bf16[2,1,256,1024]{3,2,1,0:T(8,128)(2,1)}, u32[]{:S(2)}) copy-start(bf16[2,1,256,1024]{3,2,1,0:T(8,128)(2,1)} %param.12) | copy-start | bytes 3145732
  1084.5 284.8 %copy-start.6 = (bf16[2,256,1024]{2,1,0:T(8,128)(2,1)S(1)}, bf16[2,256,1024]{2,1,0:T(8,128)(2,1)}, u32[]{:S(2)}) copy-start(bf16[2,256,1024]{2,1,0:T(8,128)(2,1)} %reduce-scatter.11.cloned.1.call-done) | copy-start | bytes 3145732
  1084.5 284.8 %copy-start.8 = (bf16[2,256,1024]{2,1,0:T(8,128)(2,1)S(1)}, bf16[2,256,1024]{2,1,0:T(8,128)(2,1)}, u32[]{:S(2)}) copy-start(bf16[2,256,1024]{2,1,0:T(8,128)(2,1)} %reduce-scatter.15.cloned.1.call-done) | copy-start | bytes 3145732
  1084.5 284.8 %copy-start.13 = (f32[2,1024]{1,0:T(2,128)S(1)}, f32[2,1024]{1,0:T(2,128)}, u32[]{:S(2)}) copy-start(f32[2,1024]{1,0:T(2,128)} %get-tuple-element.312) | copy-start | bytes 24580
  1084.5 284.8 %copy-start.15 = (f32[2,1024]{1,0:T(2,128)S(1)}, f32[2,1024]{1,0:T(2,128)}, u32[]{:S(2)}) copy-start(f32[2,1024]{1,0:T(2,128)} %get-tuple-element.309) | copy-start | bytes 24580
  1084.5 284.8 %copy-start.18 = (f32[2,1024]{1,0:T(2,128)S(1)}, f32[2,1024]{1,0:T(2,128)}, u32[]{:S(2)}) copy-start(f32[2,1024]{1,0:T(2,128)} %copy-done.17) | copy-start | bytes 24580
  1084.5 284.8 %copy-start.20 = (f32[2,256]{1,0:T(2,128)S(1)}, f32[2,256]{1,0:T(2,128)}, u32[]{:S(2)}) copy-start(f32[2,256]{1,0:T(2,128)} %copy-done.19) | copy-start | bytes 6148
  1084.5 284.8 %copy-start.22 = (f32[2,256]{1,0:T(2,128)S(1)}, f32[2,256]{1,0:T(2,128)}, u32[]{:S(2)}) copy-start(f32[2,256]{1,0:T(2,128)} %copy-done.21) | copy-start | bytes 6148
  1084.5 284.8 %copy-start.24 = (f32[2,1024]{1,0:T(2,128)S(1)}, f32[2,1024]{1,0:T(2,128)}, u32[]{:S(2)}) copy-start(f32[2,1024]{1,0:T(2,128)} %get-tuple-element.307) | copy-start | bytes 24580
  1084.5 284.8 %copy-start.27 = (f32[2,256]{1,0:T(2,128)S(1)}, f32[2,256]{1,0:T(2,128)}, u32[]{:S(2)}) copy-start(f32[2,256]{1,0:T(2,128)} %copy-done.26) | copy-start | bytes 6148
  1084.6 284.8 %copy-start.29 = (f32[2,256]{1,0:T(2,128)S(1)}, f32[2,256]{1,0:T(2,128)}, u32[]{:S(2)}) copy-start(f32[2,256]{1,0:T(2,128)} %copy-done.28) | copy-start | bytes 6148
  1084.6 284.8 %copy-start.31 = (f32[2,256]{1,0:T(2,128)S(1)}, f32[2,256]{1,0:T(2,128)}, u32[]{:S(2)}) copy-start(f32[2,256]{1,0:T(2,128)} %copy-done.30) | copy-start | bytes 6148
  1084.6 284.8 %copy-start.34 = (f32[2,256]{1,0:T(2,128)S(1)}, f32[2,256]{1,0:T(2,128)}, u32[]{:S(2)}) copy-start(f32[2,256]{1,0:T(2,128)} %copy-done.33) | copy-start | bytes 6148
  1383.3 10.0 all-to-all-start.1
  1387.5 21.7 %copy-start.1 = (bf16[128,6,256]{2,0,1:T(8,128)(2,1)S(1)}, bf16[128,6,256]{2,0,1:T(8,128)(2,1)}, u32[]{:S(2)}) copy-start(bf16[128,6,256]{2,0,1:T(8,128)(2,1)} %param.19) | copy-start | bytes 1179652
  (14 other events, 55.6 us)
Sparse Core Ops, SparseCore 0:
  20.3 54.5 all-reduce.2
  76.8 24.9 all-gather.15
  103.9 80.7 all-gather.13
  192.5 9.1 all-gather.29
  203.1 11.7 all-gather.27
  316.1 77.9 reduce-scatter.10
  396.0 28.2 all-gather.19
  426.5 80.7 all-gather.17
  509.1 26.2 all-gather.21
  536.9 80.7 all-gather.23
  638.6 75.2 reduce-scatter.14
  721.0 81.2 all-gather.25
  1020.1 8.3 reduce-scatter.16
  1030.6 11.0 reduce-scatter.18
  1044.8 42.3 reduce-scatter.28
  1090.3 41.1 reduce-scatter.26
  1135.0 34.1 reduce-scatter.24
  1172.3 38.3 reduce-scatter.22
  1213.0 76.7 reduce-scatter.12
  1292.0 77.2 reduce-scatter.20

commit v2 on v1

v2 whole, which is shorter than its diff:
```python
import math

import jax
import jax.numpy as jnp
from jax import lax
from jax.sharding import PartitionSpec as P

HEAD_DIM = 64


epsilon = 1e-06
highest = lax.Precision.HIGHEST


def normalize(values):
    center = values - jnp.mean(values, axis=-1, keepdims=True)
    spread = jnp.mean(center * center, axis=-1, keepdims=True)
    inverse = lax.rsqrt(spread + epsilon)
    return (center * inverse, inverse)


def norm_back(upstream, normed, inverse):
    upstream_mean = jnp.mean(upstream, axis=-1, keepdims=True)
    product_mean = jnp.mean(upstream * normed, axis=-1, keepdims=True)
    return inverse * (upstream - upstream_mean - normed * product_mean)


def level_embedding(levels, model_width):
    halfway = model_width // 2
    frequency = jnp.exp(-math.log(10000.0) * jnp.arange(halfway, dtype=jnp.float32) / halfway)
    angles = levels.astype(jnp.float32)[..., None] * frequency
    return jnp.concatenate([jnp.cos(angles), jnp.sin(angles)], axis=-1)


def gelu_tanh(values):
    return jax.nn.gelu(values, approximate=True)


def on_device(
    tokens, out_grad, noise_index, qkv_weight, out_weight, up_weight, down_weight, ada_weight
):
    clips = tokens.shape[0]
    patches = tokens.shape[2]
    model_width = tokens.shape[-1]
    local_width = qkv_weight.shape[2]
    rows_here = qkv_weight.shape[0]
    heads_here = local_width // HEAD_DIM
    scaling = HEAD_DIM ** (-0.5)
    groups = lax.axis_size("tensor")
    halves = lax.axis_size("frame")
    replicas = lax.axis_size("dp")

    with jax.named_scope("modulation"):
        levels_all = lax.all_gather(noise_index, ("dp", "frame"), axis=0, tiled=True)
        levels_all = levels_all.reshape(replicas * halves, clips, groups)
        condition_all = jax.nn.silu(level_embedding(levels_all, model_width)).astype(jnp.bfloat16)
        row_block = lax.axis_index("dp") * halves + lax.axis_index("frame")
        my_condition = lax.dynamic_slice_in_dim(
            condition_all, row_block * rows_here, rows_here, axis=3
        )
        partial_mod = jnp.einsum(
            "acgd,dkw->acgkw", my_condition, ada_weight, preferred_element_type=jnp.float32
        )
        summed_mod = lax.psum_scatter(
            partial_mod, ("dp", "frame"), scatter_dimension=0, tiled=True
        )[0]
        modulation = lax.all_to_all(summed_mod, "tensor", 1, 3, tiled=True)
        modulation = modulation.reshape(clips, 6, 1, model_width)

    with jax.named_scope("weights"):
        joint_weight, mixer_weight, upward_weight, downward_weight = (
            lax.all_gather(w, ("dp", "frame"), axis=0, tiled=True)
            for w in (qkv_weight, out_weight, up_weight, down_weight)
        )

    residual = tokens[:, 0].astype(jnp.float32)
    upstream = out_grad[:, 0].astype(jnp.float32)
    def clip_pass(residual, upstream, modulation):
        clips = residual.shape[0]
        shift1, scale1, gate1 = modulation[:, 0], modulation[:, 1], modulation[:, 2]
        shift2, scale2, gate2 = modulation[:, 3], modulation[:, 4], modulation[:, 5]
        def gather_tokens(values):
            return lax.all_gather(values, "tensor", axis=1, tiled=True)

        def scatter_tokens(values):
            return lax.psum_scatter(
                values.astype(jnp.bfloat16), "tensor", scatter_dimension=1, tiled=True
            ).astype(jnp.float32)

        with jax.named_scope("forward"):
            normed_one, inverse_one = normalize(residual)
            entering_one = (normed_one * (1.0 + scale1) + shift1).astype(jnp.bfloat16)
            flat_one = gather_tokens(entering_one)
            token_count = flat_one.shape[1]
            projected = jnp.einsum(
                "crd,dkh->crkh", flat_one, joint_weight, preferred_element_type=jnp.float32
            ).astype(jnp.bfloat16)
            queries = projected[:, :, 0]
            keys_all = lax.all_gather(projected[:, :, 1], "frame", axis=1, tiled=True)
            values_all = lax.all_gather(projected[:, :, 2], "frame", axis=1, tiled=True)
            key_heads = keys_all.reshape(clips, -1, heads_here, HEAD_DIM)
            value_heads = values_all.reshape(clips, -1, heads_here, HEAD_DIM)
            block_rows = min(512, token_count)
            block_count = token_count // block_rows
            query_blocks = jnp.moveaxis(
                queries.reshape(clips, block_count, block_rows, heads_here, HEAD_DIM), 1, 0
            )

            def attend(query_block):
                scores = (
                    jnp.einsum(
                        "cqhe,ckhe->chqk", query_block, key_heads, preferred_element_type=jnp.float32
                    )
                    * scaling
                )
                largest = jnp.max(scores, axis=-1, keepdims=True)
                raised = jnp.exp(scores - largest)
                totals_row = jnp.sum(raised, axis=-1, keepdims=True)
                probs_low = (raised / totals_row).astype(jnp.bfloat16)
                outputs = jnp.einsum(
                    "chqk,ckhe->cqhe", probs_low, value_heads, preferred_element_type=jnp.float32
                )
                return (outputs.astype(jnp.bfloat16), (largest + jnp.log(totals_row))[..., 0])

            attended_blocks, log_totals = lax.map(attend, query_blocks)
            attended = jnp.moveaxis(attended_blocks, 0, 1).reshape(clips, token_count, local_width)
            partial_one = jnp.einsum(
                "crh,oh->cro", attended, mixer_weight, preferred_element_type=jnp.float32
            )
            branch_one = scatter_tokens(partial_one)
            middle = residual + gate1 * branch_one
            normed_two, inverse_two = normalize(middle)
            entering_two = (normed_two * (1.0 + scale2) + shift2).astype(jnp.bfloat16)
            flat_two = gather_tokens(entering_two)
            up_values = jnp.einsum(
                "crd,df->crf", flat_two, upward_weight, preferred_element_type=jnp.float32
            )
            hidden = gelu_tanh(up_values).astype(jnp.bfloat16)
            partial_two = jnp.einsum(
                "crf,of->cro", hidden, downward_weight, preferred_element_type=jnp.float32
            )
            branch_two = scatter_tokens(partial_two)
            output = (middle + gate2 * branch_two).astype(jnp.bfloat16)

        with jax.named_scope("backward_ffn"):
            grad_gate_two = jnp.sum(upstream * branch_two, axis=1)
            grad_branch_two = (gate2 * upstream).astype(jnp.bfloat16)
            grad_two_all = gather_tokens(grad_branch_two)
            grad_hidden = jnp.einsum(
                "cro,of->crf", grad_two_all, downward_weight, preferred_element_type=jnp.float32
            )
            down_total = jnp.einsum(
                "cro,crf->of", grad_two_all, hidden, preferred_element_type=jnp.float32
            )
            _, gelu_pullback = jax.vjp(gelu_tanh, up_values)
            grad_up = gelu_pullback(grad_hidden)[0].astype(jnp.bfloat16)
            up_total = jnp.einsum(
                "crd,crf->df", flat_two, grad_up, preferred_element_type=jnp.float32
            )
            partial_back_two = jnp.einsum(
                "crf,df->crd", grad_up, upward_weight, preferred_element_type=jnp.float32
            )
            grad_entering_two = scatter_tokens(partial_back_two)
            grad_shift_two = jnp.sum(grad_entering_two, axis=1)
            grad_scale_two = jnp.sum(grad_entering_two * normed_two, axis=1)
            grad_middle = upstream + norm_back(
                grad_entering_two * (1.0 + scale2), normed_two, inverse_two
            )
            grad_gate_one = jnp.sum(grad_middle * branch_one, axis=1)

        with jax.named_scope("backward_attention"):
            grad_branch_one = (gate1 * grad_middle).astype(jnp.bfloat16)
            grad_one_all = gather_tokens(grad_branch_one)
            grad_attended = jnp.einsum(
                "cro,oh->crh", grad_one_all, mixer_weight, preferred_element_type=jnp.float32
            ).astype(jnp.bfloat16)
            mixer_total = jnp.einsum(
                "cro,crh->oh", grad_one_all, attended, preferred_element_type=jnp.float32
            )
            grad_blocks = jnp.moveaxis(
                grad_attended.reshape(clips, block_count, block_rows, heads_here, HEAD_DIM), 1, 0
            )

            def attend_back(carried, pieces):
                key_sum, value_sum = carried
                query_block, grad_block, log_block = pieces
                scores = (
                    jnp.einsum(
                        "cqhe,ckhe->chqk", query_block, key_heads, preferred_element_type=jnp.float32
                    )
                    * scaling
                )
                probs = jnp.exp(scores - log_block[..., None])
                grad_probs = jnp.einsum(
                    "cqhe,ckhe->chqk", grad_block, value_heads, preferred_element_type=jnp.float32
                )
                value_sum = value_sum + jnp.einsum(
                    "chqk,cqhe->ckhe",
                    probs.astype(jnp.bfloat16),
                    grad_block,
                    preferred_element_type=jnp.float32,
                )
                row_terms = jnp.sum(probs * grad_probs, axis=-1, keepdims=True)
                grad_scores = (probs * (grad_probs - row_terms)).astype(jnp.bfloat16)
                grad_queries = (
                    jnp.einsum(
                        "chqk,ckhe->cqhe", grad_scores, key_heads, preferred_element_type=jnp.float32
                    )
                    * scaling
                )
                key_sum = (
                    key_sum
                    + jnp.einsum(
                        "chqk,cqhe->ckhe", grad_scores, query_block, preferred_element_type=jnp.float32
                    )
                    * scaling
                )
                return ((key_sum, value_sum), grad_queries)

            zeros_keys = jnp.zeros(key_heads.shape, jnp.float32)
            (key_grads, value_grads), query_grads = lax.scan(
                attend_back, (zeros_keys, zeros_keys), (query_blocks, grad_blocks, log_totals)
            )
            query_grads = jnp.moveaxis(query_grads, 0, 1).reshape(clips, token_count, local_width)
            key_own, value_own = (
                lax.psum_scatter(
                    grads.reshape(clips, -1, local_width).astype(jnp.bfloat16),
                    "frame",
                    scatter_dimension=1,
                    tiled=True,
                ).astype(jnp.float32)
                for grads in (key_grads, value_grads)
            )
            grad_projected = jnp.stack([query_grads, key_own, value_own], axis=2).astype(
                jnp.bfloat16
            )
            joint_total = jnp.einsum(
                "crd,crkh->dkh", flat_one, grad_projected, preferred_element_type=jnp.float32
            )
            partial_back_one = jnp.einsum(
                "crkh,dkh->crd", grad_projected, joint_weight, preferred_element_type=jnp.float32
            )
            grad_entering_one = scatter_tokens(partial_back_one)
            grad_shift_one = jnp.sum(grad_entering_one, axis=1)
            grad_scale_one = jnp.sum(grad_entering_one * normed_one, axis=1)
            grad_input = grad_middle + norm_back(
                grad_entering_one * (1.0 + scale1), normed_one, inverse_one
            )


        grad_modulation = jnp.stack(
            [grad_shift_one, grad_scale_one, grad_gate_one, grad_shift_two, grad_scale_two, grad_gate_two],
            axis=1,
        )
        totals = (joint_total, mixer_total, up_total, down_total)
        return output, grad_input.astype(jnp.bfloat16), grad_modulation, totals

    pieces = [
        clip_pass(residual[i : i + 1], upstream[i : i + 1], modulation[i : i + 1])
        for i in range(clips)
    ]
    output = jnp.concatenate([p[0] for p in pieces], axis=0)
    grad_input_low = jnp.concatenate([p[1] for p in pieces], axis=0)
    grad_modulation = jnp.concatenate([p[2] for p in pieces], axis=0)
    joint_total, mixer_total, up_total, down_total = (
        sum(p[3][k] for p in pieces[1:]) + pieces[0][3][k] for k in range(4)
    )
    with jax.named_scope("ada_grad"):
        grad_columns = lax.all_to_all(
            grad_modulation.reshape(clips, 1, 6, model_width), "tensor", 3, 1, tiled=True
        )
        grad_all = lax.all_gather(grad_columns, ("dp", "frame"), axis=0, tiled=True)
        grad_all = grad_all.reshape(replicas * halves, clips, groups, 6, local_width)
        adaptive_total = jnp.einsum(
            "acgd,acgkw->dkw",
            my_condition.astype(jnp.float32),
            grad_all,
            precision=highest,
        )

    with jax.named_scope("weight_grads"):
        summed = tuple(
            lax.psum_scatter(
                total.astype(jnp.bfloat16), ("dp", "frame"), scatter_dimension=0, tiled=True
            ).astype(jnp.float32)
            for total in (joint_total, mixer_total, up_total, down_total)
        )
    result = output[:, None]
    input_grad = grad_input_low[:, None]
    return (result, input_grad, summed[0], summed[1], summed[2], summed[3], adaptive_total)


def solution(mesh):
    return jax.shard_map(
        on_device,
        mesh=mesh,
        in_specs=(
            P("dp", ("frame", "tensor"), None, None),
            P("dp", ("frame", "tensor"), None, None),
            P("dp", "frame"),
            P(("dp", "frame"), None, "tensor"),
            P(("dp", "frame"), "tensor"),
            P(("dp", "frame"), "tensor"),
            P(("dp", "frame"), "tensor"),
            P(("dp", "frame"), None, "tensor"),
        ),
        out_specs=(
            P("dp", ("frame", "tensor"), None, None),
            P("dp", ("frame", "tensor"), None, None),
            P(("dp", "frame"), None, "tensor"),
            P(("dp", "frame"), "tensor"),
            P(("dp", "frame"), "tensor"),
            P(("dp", "frame"), "tensor"),
            P(("dp", "frame"), None, "tensor"),
        ),
        check_vma=False,
    )
```

time: 1420 us -> 1310 us (0.923)
  matrix products: 302 us -> 241 us
  waiting for transfers between devices: 874 us -> 836 us
  other arithmetic: 129 us -> 107 us
    all_gather x4 -> x8, waiting for transfers between devices: 329 us -> 280 us  [gather_tokens(): return lax.all_gather(values, 'tensor', axis=1, tiled=True)]
    dot_general x2 -> x4, matrix products: 28.6 us -> 9.89 us  [attend(): jnp.einsum('cqhe,ckhe->chqk', query_block, key_heads, preferred_element_t...]
    dot_general x2 -> x4, matrix products: 28.6 us -> 11.5 us  [attend_back(): jnp.einsum('cqhe,ckhe->chqk', query_block, key_heads, preferred_element_t...]
    dot_general x2 -> x4, matrix products: 33.3 us -> 17.7 us  [attend_back(): jnp.einsum('chqk,cqhe->ckhe', probs.astype(jnp.bfloat16), grad_block, pre...]
    reduce_sum x2 -> x4, other arithmetic: 28 us -> 13.1 us  [attend(): totals_row = jnp.sum(raised, axis=-1, keepdims=True)]
    convert_element_type x2 -> x4, other arithmetic: 55.8 us -> 42.4 us  [attend_back(): grad_scores = (probs * (grad_probs - row_terms)).astype(jnp.bfloat16)]
    dot_general x2 -> x4, matrix products: 47.7 us -> 35 us  [attend_back(): jnp.einsum('cqhe,ckhe->chqk', grad_block, value_heads, preferred_element_...]
    dot_general x2 -> x4, matrix products: 31.1 us -> 20.5 us  [attend(): jnp.einsum('chqk,ckhe->cqhe', probs_low, value_heads, preferred_element_t...]
  transfers between devices with their start and end apart: 22 -> 34, of which waited for: 19 -> 26; matrix products, arithmetic and copies ran while one was open for 8% -> 28% of each run, Pallas kernels for 0% -> 0%
where the time goes in v2:
time: 1310 us; the launch traced here: 1300 us
  waiting for transfers between devices  836 us (64%)
  matrix products  241 us (18%)
  other arithmetic  107 us (8%)
  local copies, waits for them, and re-layouts  60.6 us (5%)
  blocking collectives  31.1 us (2%)
  between operations  15.6 us (1%)
    reduce_scatter x8, waiting for transfers between devices, scatter_tokens(): lax.psum_scatter(values.astype(jnp.bfloat16), 'tensor', scatter_dimension...  303 us
    all_gather x8, waiting for transfers between devices, gather_tokens(): return lax.all_gather(values, 'tensor', axis=1, tiled=True)  280 us
    reduce_scatter x4, waiting for transfers between devices, on_device(): lax.psum_scatter(total.astype(jnp.bfloat16), ('dp', 'frame'), scatter_dim...  129 us
    all_gather x3, waiting for transfers between devices, on_device(): lax.all_gather(w, ('dp', 'frame'), axis=0, tiled=True)  57.8 us
    unnamed x33, waiting for transfers between devices  54.6 us
    convert_element_type x4, other arithmetic, attend_back(): grad_scores = (probs * (grad_probs - row_terms)).astype(jnp.bfloat16)  42.4 us
    dot_general x4, matrix products, attend_back(): jnp.einsum('cqhe,ckhe->chqk', grad_block, value_heads, preferred_element_...  35 us
  transfers between devices with their start and end apart: 34, of which 26 were waited for; matrix products, arithmetic and copies ran while one was open for 28% of the time, Pallas kernels for 0%

profile of v2, /device:TPU:0, one launch (start us, length us, event | category | flops | bytes accessed | tf_op | source)
XLA Modules:
  0.0 1303.8 jit_solution(12212397972172722211)
XLA Ops:
  7.3 10.7 all-gather.5
  23.7 51.2 %all-reduce.3.cloned.1.call-done = f32[8,2,4,6,256]{4,2,3,1,0:T(4,128)} async-done(((f32[8,2,4,6,256]{4,2,3,1,0:T(4,128)}), f32[8,2,4,6,256]{4,2,3,1,0:T(4,128)}) %all-reduce.3.cloned.1.call-update) | async-done | bytes 393232
  90.7 11.1 all-gather.24.cloned.1.call-done
  101.8 47.8 %all-gather.22.cloned.1.call-done = bf16[1,1024,1024]{2,1,0:T(8,128)(2,1)} async-done(((bf16[1,256,1024]{2,1,0:T(8,128)(2,1)}), bf16[1,1024,1024]{2,1,0:T(8,128)(2,1)}) %all-gather.22.cloned.1.call-update) | async-done | bytes 2097168 | tf_op jit(solution)/shard_map/forward/all_gather | solution.py:83
  155.2 40.9 %all-gather.32.cloned.1.call-done = bf16[1,1024,1024]{2,1,0:T(8,128)(2,1)} async-done(((bf16[1,256,1024]{2,1,0:T(8,128)(2,1)}), bf16[1,1024,1024]{2,1,0:T(8,128)(2,1)}) %all-gather.32.cloned.1.call-update) | async-done | bytes 2097168 | tf_op jit(solution)/shard_map/forward/all_gather | solution.py:83
  200.6 10.8 all_gather.59
  220.5 22.1 %while.54 = (s32[]{:T(128)}, bf16[2,1,512,4,64]{2,4,3,1,0:T(8,128)(2,1)}, f32[2,1,4,512]{3,2,1,0:T(4,128)S(1)}, bf16[2,1,512,4,64]{2,4,3,1,0:T(8,128)(2,1)S(1)},...) while((s32[]{:T(128)}, bf16[2,1,512,4,64]{2,4,3,1,0:T(8,128)(2,1)}, ...), condition=%wide.region_6.7_spmd, body=%wide.region_3.6_spmd.sunk | while | flops 1111619584 | bytes 57213080 | solution.py:125
  252.9 23.1 %while.55 = (s32[]{:T(128)}, bf16[2,1,512,4,64]{2,4,3,1,0:T(8,128)(2,1)}, f32[2,1,4,512]{3,2,1,0:T(4,128)S(1)}, bf16[2,1,512,4,64]{2,4,3,1,0:T(8,128)(2,1)S(1)},...) while((s32[]{:T(128)}, bf16[2,1,512,4,64]{2,4,3,1,0:T(8,128)(2,1)}, ...), condition=%wide.region_16.17_spmd, body=%wide.region_13.16_spmd.sunk | while | flops 1111619584 | bytes 53018720 | solution.py:125
  270.2 5.8 fusion.302
  282.6 10.0 reduce-scatter.17.cloned.1.call-done
  292.6 45.0 %reduce-scatter.21.cloned.1.call-done = bf16[1,256,1024]{2,1,0:T(8,128)(2,1)} async-done(((bf16[1,1024,1024]{2,1,0:T(8,128)(2,1)}), bf16[1,256,1024]{2,1,0:T(8,128)(2,1)}) %reduce-scatter.21.cloned.1.call-update) | async-done | bytes 524304 | tf_op jit(solution)/shard_map/forward/reduce_scatter | solution.py:86
  348.1 18.4 %all-gather.28.cloned.1.call-done = bf16[1024,1024]{1,0:T(8,128)(2,1)} async-done(((bf16[128,1024]{1,0:T(8,128)(2,1)}), bf16[1024,1024]{1,0:T(8,128)(2,1)}) %all-gather.28.cloned.1.call-update) | async-done | bytes 2097168 | tf_op jit(solution)/shard_map/weights/all_gather | solution.py:72
  366.5 47.7 %all-gather.34.cloned.1.call-done = bf16[1,1024,1024]{2,1,0:T(8,128)(2,1)} async-done(((bf16[1,256,1024]{2,1,0:T(8,128)(2,1)}), bf16[1,1024,1024]{2,1,0:T(8,128)(2,1)}) %all-gather.34.cloned.1.call-update) | async-done | bytes 2097168 | tf_op jit(solution)/shard_map/forward/all_gather | solution.py:83
  414.2 6.6 fusion.126
  420.8 40.0 %all-gather.40.cloned.1.call-done = bf16[1,1024,1024]{2,1,0:T(8,128)(2,1)} async-done(((bf16[1,256,1024]{2,1,0:T(8,128)(2,1)}), bf16[1,1024,1024]{2,1,0:T(8,128)(2,1)}) %all-gather.40.cloned.1.call-update) | async-done | bytes 2097168 | tf_op jit(solution)/shard_map/backward_ffn/all_gather | solution.py:83
  460.8 28.4 %all-gather.30.cloned.1.call-done = bf16[1024,1024]{1,0:T(8,128)(2,1)} async-done(((bf16[128,1024]{1,0:T(8,128)(2,1)}), bf16[1024,1024]{1,0:T(8,128)(2,1)}) %all-gather.30.cloned.1.call-update) | async-done | bytes 2097168 | tf_op jit(solution)/shard_map/weights/all_gather | solution.py:72
  489.2 7.9 fusion.103
  502.3 6.9 convert_bitcast_fusion.2
  509.5 27.4 %all-gather.26.cloned.1.call-done = bf16[1,1024,1024]{2,1,0:T(8,128)(2,1)} async-done(((bf16[1,256,1024]{2,1,0:T(8,128)(2,1)}), bf16[1,1024,1024]{2,1,0:T(8,128)(2,1)}) %all-gather.26.cloned.1.call-update) | async-done | bytes 2097168 | tf_op jit(solution)/shard_map/forward/all_gather | solution.py:83
  547.0 34.5 %reduce-scatter.33.cloned.1.call-done = bf16[1,256,1024]{2,1,0:T(8,128)(2,1)} async-done(((bf16[1,1024,1024]{2,1,0:T(8,128)(2,1)}), bf16[1,256,1024]{2,1,0:T(8,128)(2,1)}) %reduce-scatter.33.cloned.1.call-update) | async-done | bytes 524304 | tf_op jit(solution)/shard_map/backward_ffn/reduce_scatter | solution.py:86
  583.6 42.8 %reduce-scatter.23.cloned.1.call-done = bf16[1,256,1024]{2,1,0:T(8,128)(2,1)} async-done(((bf16[1,1024,1024]{2,1,0:T(8,128)(2,1)}), bf16[1,256,1024]{2,1,0:T(8,128)(2,1)}) %reduce-scatter.23.cloned.1.call-update) | async-done | bytes 524304 | tf_op jit(solution)/shard_map/forward/reduce_scatter | solution.py:86
  626.5 45.0 %reduce-scatter.19.cloned.1.call-done = bf16[1,256,1024]{2,1,0:T(8,128)(2,1)} async-done(((bf16[1,1024,1024]{2,1,0:T(8,128)(2,1)}), bf16[1,256,1024]{2,1,0:T(8,128)(2,1)}) %reduce-scatter.19.cloned.1.call-update) | async-done | bytes 524304 | tf_op jit(solution)/shard_map/forward/reduce_scatter | solution.py:86
  677.1 43.8 %all-gather.36.cloned.1.call-done = bf16[1,1024,1024]{2,1,0:T(8,128)(2,1)} async-done(((bf16[1,256,1024]{2,1,0:T(8,128)(2,1)}), bf16[1,1024,1024]{2,1,0:T(8,128)(2,1)}) %all-gather.36.cloned.1.call-update) | async-done | bytes 2097168 | tf_op jit(solution)/shard_map/backward_ffn/all_gather | solution.py:83
  720.9 8.0 fusion.96
  734.6 32.9 %all-gather.42.cloned.1.call-done = bf16[1,1024,1024]{2,1,0:T(8,128)(2,1)} async-done(((bf16[1,256,1024]{2,1,0:T(8,128)(2,1)}), bf16[1,1024,1024]{2,1,0:T(8,128)(2,1)}) %all-gather.42.cloned.1.call-update) | async-done | bytes 2097168 | tf_op jit(solution)/shard_map/backward_attention/all_gather | solution.py:83
  775.7 36.5 %reduce-scatter.25.cloned.1.call-done = bf16[1,256,1024]{2,1,0:T(8,128)(2,1)} async-done(((bf16[1,1024,1024]{2,1,0:T(8,128)(2,1)}), bf16[1,256,1024]{2,1,0:T(8,128)(2,1)}) %reduce-scatter.25.cloned.1.call-update) | async-done | bytes 524304 | tf_op jit(solution)/shard_map/backward_ffn/reduce_scatter | solution.py:86
  821.4 74.9 %while.57 = (s32[]{:T(128)}, f32[1,2048,4,64]{1,3,2,0:T(8,128)}, f32[1,2048,4,64]{1,3,2,0:T(8,128)S(1)}, bf16[2,1,512,4,64]{2,4,3,1,0:T(8,128)(2,1)}, bf16[2,1,5...) while((s32[]{:T(128)}, f32[1,2048,4,64]{1,3,2,0:T(8,128)}, ...), condition=%wide.region_37.38_spmd.clone, body=%wide.region_35.37_spmd.clone.sunk | while | flops 2737436672 | bytes 180937008 | solution.py:221
  828.7 9.5 multiply_reduce_fusion.15
  838.2 10.7 multiply_convert_fusion.16
  848.8 6.2 fusion.326
  865.3 9.4 multiply_reduce_fusion.15
  874.8 10.6 multiply_convert_fusion.16
  885.4 6.2 fusion.326
  907.6 72.4 %while.56 = (s32[]{:T(128)}, f32[1,2048,4,64]{1,3,2,0:T(8,128)}, f32[1,2048,4,64]{1,3,2,0:T(8,128)}, bf16[2,1,512,4,64]{2,4,3,1,0:T(8,128)(2,1)}, bf16[2,1,512,4...) while((s32[]{:T(128)}, f32[1,2048,4,64]{1,3,2,0:T(8,128)}, ...), condition=%wide.region_26.27_spmd.clone, body=%wide.region_24.26_spmd.clone.sunk | while | flops 2737436672 | bytes 176742640 | solution.py:221
  914.5 8.0 multiply_reduce_fusion.14
  922.6 10.6 multiply_convert_fusion.15
  933.2 6.2 fusion.314
  950.4 8.0 multiply_reduce_fusion.14
  958.4 10.6 multiply_convert_fusion.15
  969.0 6.2 fusion.314
  1019.2 6.0 add_convert_fusion.2
  1035.0 13.8 %reduce-scatter.47.cloned.1.call-done = bf16[128,1024]{1,0:T(8,128)(2,1)} async-done(((bf16[1024,1024]{1,0:T(8,128)(2,1)}), bf16[128,1024]{1,0:T(8,128)(2,1)}) %reduce-scatter.47.cloned.1.call-update) | async-done | bytes 262160 | tf_op jit(solution)/shard_map/weight_grads/reduce_scatter | solution.py:283
  1050.6 42.6 %reduce-scatter.45.cloned.1.call-done = bf16[128,1024]{1,0:T(8,128)(2,1)} async-done(((bf16[1024,1024]{1,0:T(8,128)(2,1)}), bf16[128,1024]{1,0:T(8,128)(2,1)}) %reduce-scatter.45.cloned.1.call-update) | async-done | bytes 262160 | tf_op jit(solution)/shard_map/weight_grads/reduce_scatter | solution.py:283
  1097.3 33.1 %reduce-scatter.43.cloned.1.call-done = bf16[128,256]{1,0:T(8,128)(2,1)} async-done(((bf16[1024,256]{1,0:T(8,128)(2,1)}), bf16[128,256]{1,0:T(8,128)(2,1)}) %reduce-scatter.43.cloned.1.call-update) | async-done | bytes 65552 | tf_op jit(solution)/shard_map/weight_grads/reduce_scatter | solution.py:283
  1131.9 40.0 %reduce-scatter.41.cloned.1.call-done = bf16[128,3,256]{2,0,1:T(8,128)(2,1)} async-done(((bf16[1024,3,256]{2,0,1:T(8,128)(2,1)}), bf16[128,3,256]{2,0,1:T(8,128)(2,1)}) %reduce-scatter.41.cloned.1.call-update) | async-done | bytes 196624 | tf_op jit(solution)/shard_map/weight_grads/reduce_scatter | solution.py:283
  1173.6 44.3 %reduce-scatter.39.cloned.1.call-done = bf16[1,256,1024]{2,1,0:T(8,128)(2,1)} async-done(((bf16[1,1024,1024]{2,1,0:T(8,128)(2,1)}), bf16[1,256,1024]{2,1,0:T(8,128)(2,1)}) %reduce-scatter.39.cloned.1.call-update) | async-done | bytes 524304 | tf_op jit(solution)/shard_map/backward_attention/reduce_scatter | solution.py:86
  1217.9 45.2 %reduce-scatter.31.cloned.1.call-done = bf16[1,256,1024]{2,1,0:T(8,128)(2,1)} async-done(((bf16[1,1024,1024]{2,1,0:T(8,128)(2,1)}), bf16[1,256,1024]{2,1,0:T(8,128)(2,1)}) %reduce-scatter.31.cloned.1.call-update) | async-done | bytes 524304 | tf_op jit(solution)/shard_map/backward_attention/reduce_scatter | solution.py:86
  1286.1 9.5 all-gather.4
  (433 shorter events, 291.3 us)
Async XLA Ops:
  7.2 67.7 %all-reduce.3.cloned.1.call-start = ((), (), s32[]{:S(2)}) async-start(), calls=%async_computation.49 | async-start | bytes 786432
  20.2 81.6 %all-gather.24.cloned.1.call-start = ((), (), s32[]{:S(2)}) async-start(), calls=%async_computation.19 | async-start | bytes 1769472 | tf_op jit(solution)/shard_map/weights/all_gather | solution.py:72
  77.0 10.2 all-to-all-start
  81.5 68.1 %all-gather.22.cloned.1.call-start = ((), (), s32[]{:S(2)}) async-start(), calls=%async_computation.18 | async-start | bytes 2621440 | tf_op jit(solution)/shard_map/forward/all_gather | solution.py:83
  90.1 106.0 %all-gather.32.cloned.1.call-start = ((), (), s32[]{:S(2)}) async-start(), calls=%async_computation.25 | async-start | bytes 2621440 | tf_op jit(solution)/shard_map/forward/all_gather | solution.py:83
  90.6 124.0 %all-gather.46.cloned.1.call-start = ((), (), s32[]{:S(2)}) async-start(), calls=%async_computation.46 | async-start | bytes 1572864 | tf_op jit(solution)/shard_map/forward/all_gather | solution.py:100
  154.6 63.5 %all-gather.44.cloned.1.call-start = ((), (), s32[]{:S(2)}) async-start(), calls=%async_computation.45 | async-start | bytes 1572864 | tf_op jit(solution)/shard_map/forward/all_gather | solution.py:99
  155.2 93.0 %all-gather.50.cloned.1.call-start = ((), (), s32[]{:S(2)}) async-start(), calls=%async_computation.48 | async-start | bytes 1572864 | tf_op jit(solution)/shard_map/forward/all_gather | solution.py:100
  200.6 49.9 %all-gather.48.cloned.1.call-start = ((), (), s32[]{:S(2)}) async-start(), calls=%async_computation.47 | async-start | bytes 1572864 | tf_op jit(solution)/shard_map/forward/all_gather | solution.py:99
  214.3 78.3 %reduce-scatter.17.cloned.1.call-start = ((), (), s32[]{:S(2)}) async-start(), calls=%async_computation.20 | async-start | bytes 2621440 | tf_op jit(solution)/shard_map/forward/reduce_scatter | solution.py:86
  247.6 90.0 %reduce-scatter.21.cloned.1.call-start = ((), (), s32[]{:S(2)}) async-start(), calls=%async_computation.26 | async-start | bytes 2621440 | tf_op jit(solution)/shard_map/forward/reduce_scatter | solution.py:86
  281.8 84.7 %all-gather.28.cloned.1.call-start = ((), (), s32[]{:S(2)}) async-start(), calls=%async_computation.22 | async-start | bytes 2359296 | tf_op jit(solution)/shard_map/weights/all_gather | solution.py:72
  282.5 131.7 %all-gather.34.cloned.1.call-start = ((), (), s32[]{:S(2)}) async-start(), calls=%async_computation.27 | async-start | bytes 2621440 | tf_op jit(solution)/shard_map/forward/all_gather | solution.py:83
  342.1 118.7 %all-gather.40.cloned.1.call-start = ((), (), s32[]{:S(2)}) async-start(), calls=%async_computation.35 | async-start | bytes 2621440 | tf_op jit(solution)/shard_map/backward_ffn/all_gather | solution.py:83
  345.9 143.3 %all-gather.30.cloned.1.call-start = ((), (), s32[]{:S(2)}) async-start(), calls=%async_computation.23 | async-start | bytes 2359296 | tf_op jit(solution)/shard_map/weights/all_gather | solution.py:72
  346.5 190.4 %all-gather.26.cloned.1.call-start = ((), (), s32[]{:S(2)}) async-start(), calls=%async_computation.21 | async-start | bytes 2621440 | tf_op jit(solution)/shard_map/forward/all_gather | solution.py:83
  347.9 233.5 %reduce-scatter.33.cloned.1.call-start = ((), (), s32[]{:S(2)}) async-start(), calls=%async_computation.36 | async-start | bytes 2621440 | tf_op jit(solution)/shard_map/backward_ffn/reduce_scatter | solution.py:86
  502.3 124.2 %reduce-scatter.23.cloned.1.call-start = ((), (), s32[]{:S(2)}) async-start(), calls=%async_computation.28 | async-start | bytes 2621440 | tf_op jit(solution)/shard_map/forward/reduce_scatter | solution.py:86
  509.2 162.3 %reduce-scatter.19.cloned.1.call-start = ((), (), s32[]{:S(2)}) async-start(), calls=%async_computation.24 | async-start | bytes 2621440 | tf_op jit(solution)/shard_map/forward/reduce_scatter | solution.py:86
  546.9 174.0 %all-gather.36.cloned.1.call-start = ((), (), s32[]{:S(2)}) async-start(), calls=%async_computation.29 | async-start | bytes 2621440 | tf_op jit(solution)/shard_map/backward_ffn/all_gather | solution.py:83
  675.9 91.5 %all-gather.42.cloned.1.call-start = ((), (), s32[]{:S(2)}) async-start(), calls=%async_computation.37 | async-start | bytes 2621440 | tf_op jit(solution)/shard_map/backward_attention/all_gather | solution.py:83
  677.1 135.1 %reduce-scatter.25.cloned.1.call-start = ((), (), s32[]{:S(2)}) async-start(), calls=%async_computation.30 | async-start | bytes 2621440 | tf_op jit(solution)/shard_map/backward_ffn/reduce_scatter | solution.py:86
  734.0 167.3 %all-gather.38.cloned.1.call-start = ((), (), s32[]{:S(2)}) async-start(), calls=%async_computation.31 | async-start | bytes 2621440 | tf_op jit(solution)/shard_map/backward_attention/all_gather | solution.py:83
  820.6 191.7 %reduce-scatter.35.cloned.1.call-start = ((), (), s32[]{:S(2)}) async-start(), calls=%async_computation.38 | async-start | bytes 1572864 | tf_op jit(solution)/shard_map/backward_attention/reduce_scatter | solution.py:226
  899.5 112.8 %reduce-scatter.37.cloned.1.call-start = ((), (), s32[]{:S(2)}) async-start(), calls=%async_computation.39 | async-start | bytes 1572864 | tf_op jit(solution)/shard_map/backward_attention/reduce_scatter | solution.py:226
  901.1 118.1 %reduce-scatter.27.cloned.1.call-start = ((), (), s32[]{:S(2)}) async-start(), calls=%async_computation.32 | async-start | bytes 1572864 | tf_op jit(solution)/shard_map/backward_attention/reduce_scatter | solution.py:226
  983.1 36.1 %reduce-scatter.29.cloned.1.call-start = ((), (), s32[]{:S(2)}) async-start(), calls=%async_computation.33 | async-start | bytes 1572864 | tf_op jit(solution)/shard_map/backward_attention/reduce_scatter | solution.py:226
  986.3 62.4 %reduce-scatter.47.cloned.1.call-start = ((), (), s32[]{:S(2)}) async-start(), calls=%async_computation.44 | async-start | bytes 2359296 | tf_op jit(solution)/shard_map/weight_grads/reduce_scatter | solution.py:283
  996.0 97.1 %reduce-scatter.45.cloned.1.call-start = ((), (), s32[]{:S(2)}) async-start(), calls=%async_computation.43 | async-start | bytes 2359296 | tf_op jit(solution)/shard_map/weight_grads/reduce_scatter | solution.py:283
  1004.2 126.2 %reduce-scatter.43.cloned.1.call-start = ((), (), s32[]{:S(2)}) async-start(), calls=%async_computation.42 | async-start | bytes 589824 | tf_op jit(solution)/shard_map/weight_grads/reduce_scatter | solution.py:283
  1012.2 159.7 %reduce-scatter.41.cloned.1.call-start = ((), (), s32[]{:S(2)}) async-start(), calls=%async_computation.41 | async-start | bytes 1769472 | tf_op jit(solution)/shard_map/weight_grads/reduce_scatter | solution.py:283
  1025.3 192.6 %reduce-scatter.39.cloned.1.call-start = ((), (), s32[]{:S(2)}) async-start(), calls=%async_computation.40 | async-start | bytes 2621440 | tf_op jit(solution)/shard_map/backward_attention/reduce_scatter | solution.py:86
  1030.0 233.0 %reduce-scatter.31.cloned.1.call-start = ((), (), s32[]{:S(2)}) async-start(), calls=%async_computation.34 | async-start | bytes 2621440 | tf_op jit(solution)/shard_map/backward_attention/reduce_scatter | solution.py:86
  1034.8 228.2 %copy-start.43 = (f32[1,1,1,1024]{3,2,1,0:T(1,128)S(1)}, f32[1,1,1,1024]{3,2,1,0:T(1,128)}, u32[]{:S(2)}) copy-start(f32[1,1,1,1024]{3,2,1,0:T(1,128)} %copy-done.42) | copy-start | bytes 12292
  1034.8 228.2 %copy-start.45 = (f32[1,1,1,1024]{3,2,1,0:T(1,128)S(1)}, f32[1,1,1,1024]{3,2,1,0:T(1,128)}, u32[]{:S(2)}) copy-start(f32[1,1,1,1024]{3,2,1,0:T(1,128)} %copy-done.44) | copy-start | bytes 12292
  1034.8 228.2 %copy-start.54 = (f32[256]{0:T(256)S(1)}, f32[256]{0:T(256)}, u32[]{:S(2)}) copy-start(f32[256]{0:T(256)} %copy-done.53) | copy-start | bytes 3076
  1034.8 228.2 %copy-start.56 = (f32[256]{0:T(256)S(1)}, f32[256]{0:T(256)}, u32[]{:S(2)}) copy-start(f32[256]{0:T(256)} %copy-done.55) | copy-start | bytes 3076
  1034.8 228.2 %copy-start.58 = (f32[256]{0:T(256)S(1)}, f32[256]{0:T(256)}, u32[]{:S(2)}) copy-start(f32[256]{0:T(256)} %copy-done.57) | copy-start | bytes 3076
  1034.9 228.2 %copy-start.60 = (f32[256]{0:T(256)S(1)}, f32[256]{0:T(256)}, u32[]{:S(2)}) copy-start(f32[256]{0:T(256)} %copy-done.59) | copy-start | bytes 3076
  1034.9 232.6 %copy-start.65 = (f32[1024]{0:T(1024)S(1)}, f32[1024]{0:T(1024)}, u32[]{:S(2)}) copy-start(f32[1024]{0:T(1024)} %get-tuple-element.467) | copy-start | bytes 12292
  1034.9 232.6 %copy-start.66 = (f32[1024]{0:T(1024)S(1)}, f32[1024]{0:T(1024)}, u32[]{:S(2)}) copy-start(f32[1024]{0:T(1024)} %get-tuple-element.475) | copy-start | bytes 12292
  1034.9 232.6 %copy-start.67 = (f32[1024]{0:T(1024)S(1)}, f32[1024]{0:T(1024)}, u32[]{:S(2)}) copy-start(f32[1024]{0:T(1024)} %get-tuple-element.484) | copy-start | bytes 12292
  1034.9 232.6 %copy-start.68 = (f32[1024]{0:T(1024)S(1)}, f32[1024]{0:T(1024)}, u32[]{:S(2)}) copy-start(f32[1024]{0:T(1024)} %get-tuple-element.547) | copy-start | bytes 12292
  1034.9 232.6 %copy-start.61 = (f32[1024]{0:T(1024)S(1)}, f32[1024]{0:T(1024)}, u32[]{:S(2)}) copy-start(f32[1024]{0:T(1024)} %get-tuple-element.477) | copy-start | bytes 12292
  1034.9 232.6 %copy-start.62 = (f32[1024]{0:T(1024)S(1)}, f32[1024]{0:T(1024)}, u32[]{:S(2)}) copy-start(f32[1024]{0:T(1024)} %get-tuple-element.486) | copy-start | bytes 12292
  1034.9 232.6 %copy-start.63 = (f32[1024]{0:T(1024)S(1)}, f32[1024]{0:T(1024)}, u32[]{:S(2)}) copy-start(f32[1024]{0:T(1024)} %get-tuple-element.468) | copy-start | bytes 12292
  1035.0 232.6 %copy-start.64 = (f32[1024]{0:T(1024)S(1)}, f32[1024]{0:T(1024)}, u32[]{:S(2)}) copy-start(f32[1024]{0:T(1024)} %get-tuple-element.563) | copy-start | bytes 12292
  1272.3 9.7 all-to-all-start.1
  (86 other events, 2150.2 us)
Sparse Core Ops, SparseCore 0:
  20.3 54.5 all-reduce.2
  76.8 24.9 all-gather.23
  103.9 45.6 all-gather.21
  151.6 44.4 all-gather.31
  198.1 7.8 all-gather.45
  207.9 10.1 all-gather.43
  220.3 10.2 all-gather.49
  232.6 10.1 all-gather.47
  247.7 44.7 reduce-scatter.16
  294.7 42.8 reduce-scatter.20
  339.5 26.9 all-gather.27
  368.5 45.6 all-gather.33
  416.3 44.4 all-gather.39
  462.6 26.5 all-gather.29
  491.2 45.6 all-gather.25
  539.0 42.4 reduce-scatter.32
  583.6 42.8 reduce-scatter.22
  628.6 42.8 reduce-scatter.18
  676.1 44.8 all-gather.35
  722.9 44.4 all-gather.41
  769.7 42.4 reduce-scatter.24
  820.7 44.8 all-gather.37
  899.6 7.5 reduce-scatter.34
  909.3 9.5 reduce-scatter.36
  983.2 7.6 reduce-scatter.26
  993.6 9.6 reduce-scatter.28
  1006.4 42.3 reduce-scatter.46
  1052.0 41.0 reduce-scatter.44
  1096.2 34.1 reduce-scatter.42
  1133.5 38.3 reduce-scatter.40
  1174.2 43.6 reduce-scatter.38
  1220.2 42.8 reduce-scatter.30

commit v3 on v2

--- a/solution.py
+++ b/solution.py
@@ -61,9 +61,9 @@
         partial_mod = jnp.einsum(
             "acgd,dkw->acgkw", my_condition, ada_weight, preferred_element_type=jnp.float32
         )
-        summed_mod = lax.psum_scatter(
-            partial_mod, ("dp", "frame"), scatter_dimension=0, tiled=True
-        )[0]
+        summed_mod = jnp.sum(
+            lax.all_to_all(partial_mod, ("dp", "frame"), 0, 0, tiled=True), axis=0
+        )
         modulation = lax.all_to_all(summed_mod, "tensor", 1, 3, tiled=True)
         modulation = modulation.reshape(clips, 6, 1, model_width)
 
@@ -75,6 +75,22 @@
 
     residual = tokens[:, 0].astype(jnp.float32)
     upstream = out_grad[:, 0].astype(jnp.float32)
+    def gather_halves(values):
+        if halves != 2:
+            return lax.all_gather(values, "frame", axis=1, tiled=True)
+        other = lax.ppermute(values, "frame", [(0, 1), (1, 0)])
+        return jnp.concatenate([values, other], axis=1)
+
+    def scatter_halves(values):
+        if halves != 2:
+            return lax.psum_scatter(
+                values.astype(jnp.bfloat16), "frame", scatter_dimension=1, tiled=True
+            ).astype(jnp.float32)
+        count = values.shape[1] // 2
+        mine = values[:, :count]
+        other = lax.ppermute(values[:, count:].astype(jnp.bfloat16), "frame", [(0, 1), (1, 0)])
+        return mine.astype(jnp.bfloat16).astype(jnp.float32) + other.astype(jnp.float32)
+
     def clip_pass(residual, upstream, modulation):
         clips = residual.shape[0]
         shift1, scale1, gate1 = modulation[:, 0], modulation[:, 1], modulation[:, 2]
@@ -83,9 +99,11 @@
             return lax.all_gather(values, "tensor", axis=1, tiled=True)
 
         def scatter_tokens(values):
-            return lax.psum_scatter(
-                values.astype(jnp.bfloat16), "tensor", scatter_dimension=1, tiled=True
-            ).astype(jnp.float32)
+            parts = values.astype(jnp.bfloat16).reshape(
+                values.shape[0], groups, -1, values.shape[-1]
+            )
+            received = lax.all_to_all(parts, "tensor", 1, 1, tiled=True)
+            return jnp.sum(received.astype(jnp.float32), axis=1)
 
         with jax.named_scope("forward"):
             normed_one, inverse_one = normalize(residual)
@@ -96,8 +114,8 @@
                 "crd,dkh->crkh", flat_one, joint_weight, preferred_element_type=jnp.float32
             ).astype(jnp.bfloat16)
             queries = projected[:, :, 0]
-            keys_all = lax.all_gather(projected[:, :, 1], "frame", axis=1, tiled=True)
-            values_all = lax.all_gather(projected[:, :, 2], "frame", axis=1, tiled=True)
+            keys_all = gather_halves(projected[:, :, 1])
+            values_all = gather_halves(projected[:, :, 2])
             key_heads = keys_all.reshape(clips, -1, heads_here, HEAD_DIM)
             value_heads = values_all.reshape(clips, -1, heads_here, HEAD_DIM)
             block_rows = min(512, token_count)
@@ -223,12 +241,7 @@
             )
             query_grads = jnp.moveaxis(query_grads, 0, 1).reshape(clips, token_count, local_width)
             key_own, value_own = (
-                lax.psum_scatter(
-                    grads.reshape(clips, -1, local_width).astype(jnp.bfloat16),
-                    "frame",
-                    scatter_dimension=1,
-                    tiled=True,
-                ).astype(jnp.float32)
+                scatter_halves(grads.reshape(clips, -1, local_width))
                 for grads in (key_grads, value_grads)
             )
             grad_projected = jnp.stack([query_grads, key_own, value_own], axis=2).astype(

time: 1310 us -> 1090 us (0.83)
  waiting for transfers between devices: 836 us -> 566 us
  starting transfers between devices: 12.3 us -> 53.9 us
  other arithmetic: 107 us -> 127 us
    reduce_scatter x12 -> x0, waiting for transfers between devices: 303 us -> none  [the longest x8 303 us: scatter_tokens(): lax.psum_scatter(values.astype(jnp.bfloat16), 'tensor', scatter_dimension...]
    all_to_all x0 -> x9, waiting for transfers between devices: none -> 191 us  [the longest x8 183 us: scatter_tokens(): received = lax.all_to_all(parts, 'tensor', 1, 1, tiled=True)]
    reduce_scatter x4, waiting for transfers between devices: 129 us -> 47.5 us  [on_device(): lax.psum_scatter(total.astype(jnp.bfloat16), ('dp', 'frame'), scatter_dim...]
    unnamed x33 -> x15, waiting for transfers between devices: 54.6 us -> 1.92 us
    all_to_all x0 -> x9, starting transfers between devices: none -> 40.7 us  [the longest x8 37.2 us: scatter_tokens(): received = lax.all_to_all(parts, 'tensor', 1, 1, tiled=True)]
    all_gather x3, waiting for transfers between devices: 57.8 us -> 21.9 us  [on_device(): lax.all_gather(w, ('dp', 'frame'), axis=0, tiled=True)]
    reduce_sum x0 -> x13, other arithmetic: none -> 23.8 us  [the longest x4 10.8 us: scatter_tokens(): return jnp.sum(received.astype(jnp.float32), axis=1)]
    all_gather x8, waiting for transfers between devices: 280 us -> 297 us  [gather_tokens(): return lax.all_gather(values, 'tensor', axis=1, tiled=True)]
  transfers between devices with their start and end apart: 34 -> 34, of which waited for: 26 -> 16; matrix products, arithmetic and copies ran while one was open for 28% -> 34% of each run, Pallas kernels for 0% -> 0%
where the time goes in v3:
time: 1090 us
  waiting for transfers between devices  566 us (52%)
  matrix products  241 us (22%)
  other arithmetic  127 us (12%)
  local copies, waits for them, and re-layouts  53.9 us (5%)
  starting transfers between devices  53.9 us (5%)
  blocking collectives  30.2 us (3%)
  between operations  15.9 us (1%)
    all_gather x8, waiting for transfers between devices, gather_tokens(): return lax.all_gather(values, 'tensor', axis=1, tiled=True)  297 us
    all_to_all x8, waiting for transfers between devices, scatter_tokens(): received = lax.all_to_all(parts, 'tensor', 1, 1, tiled=True)  183 us
    reduce_scatter x4, waiting for transfers between devices, on_device(): lax.psum_scatter(total.astype(jnp.bfloat16), ('dp', 'frame'), scatter_dim...  47.5 us
    convert_element_type x4, other arithmetic, attend_back(): grad_scores = (probs * (grad_probs - row_terms)).astype(jnp.bfloat16)  42.1 us
    all_to_all x8, starting transfers between devices, scatter_tokens(): received = lax.all_to_all(parts, 'tensor', 1, 1, tiled=True)  37.2 us
    dot_general x4, matrix products, attend_back(): jnp.einsum('cqhe,ckhe->chqk', grad_block, value_heads, preferred_element_...  32.4 us
    unnamed x213, local copies, waits for them, and re-layouts  25.8 us
    dot_general x4, matrix products, attend_back(): jnp.einsum('chqk,ckhe->cqhe', grad_scores, key_heads, preferred_element_t...  25.1 us
  transfers between devices with their start and end apart: 34, of which 16 were waited for; matrix products, arithmetic and copies ran while one was open for 34% of the time, Pallas kernels for 0%

profile of v3, /device:TPU:0, one launch (start us, length us, event | category | flops | bytes accessed | tf_op | source)
XLA Modules:
  0.0 1088.7 jit_solution(5027747888431953231)
XLA Ops:
  9.1 10.6 all-gather.1
  26.2 7.4 all-to-all-done
  34.3 4.9 all-to-all-start.1
  39.3 5.7 all-to-all-done.1
  48.5 10.1 all_gather.45
  58.6 31.6 %all-gather.14.cloned.1.call-done = bf16[1,1024,1024]{2,1,0:T(8,128)(2,1)} async-done(((bf16[1,256,1024]{2,1,0:T(8,128)(2,1)}), bf16[1,1024,1024]{2,1,0:T(8,128)(2,1)}) %all-gather.14.cloned.1.call-update) | async-done | bytes 2097168 | tf_op jit(solution)/shard_map/forward/all_gather | solution.py:99
  95.9 40.9 %all-gather.24.cloned.1.call-done = bf16[1,1024,1024]{2,1,0:T(8,128)(2,1)} async-done(((bf16[1,256,1024]{2,1,0:T(8,128)(2,1)}), bf16[1,1024,1024]{2,1,0:T(8,128)(2,1)}) %all-gather.24.cloned.1.call-update) | async-done | bytes 2097168 | tf_op jit(solution)/shard_map/forward/all_gather | solution.py:99
  147.4 22.1 %while.54 = (s32[]{:T(128)}, bf16[2,1,512,4,64]{2,4,3,1,0:T(8,128)(2,1)}, f32[2,1,4,512]{3,2,1,0:T(4,128)S(1)}, bf16[2,1,512,4,64]{2,4,3,1,0:T(8,128)(2,1)S(1)},...) while((s32[]{:T(128)}, bf16[2,1,512,4,64]{2,4,3,1,0:T(8,128)(2,1)}, ...), condition=%wide.region_6.7_spmd, body=%wide.region_3.6_spmd.sunk | while | flops 1111619584 | bytes 57213080 | solution.py:143
  173.7 4.8 all-to-all-start.2
  181.9 22.1 %while.55 = (s32[]{:T(128)}, bf16[2,1,512,4,64]{2,4,3,1,0:T(8,128)(2,1)}, f32[2,1,4,512]{3,2,1,0:T(4,128)S(1)}, bf16[2,1,512,4,64]{2,4,3,1,0:T(8,128)(2,1)S(1)},...) while((s32[]{:T(128)}, ...), condition=%wide.region_16.17_spmd, body=%wide.region_13.16_spmd.sunk | while | flops 1111619584 | bytes 57213080 | solution.py:143
  209.0 18.3 %all-to-all-done.2 = bf16[1,4,256,1024]{3,2,0,1:T(8,128)(2,1)} async-done(((bf16[1,4,256,1024]{3,2,0,1:T(8,128)(2,1)}), bf16[1,4,256,1024]{3,2,0,1:T(8,128)(2,1)}, u32[]{:S(2)}, u32[]{:S(2)}) %all-to-all-start.2) | async-done | bytes 2097184 | tf_op jit(solution)/shard_map/forward/all_to_all | solution.py:105
  235.6 44.0 %all-to-all-done.4 = bf16[1,4,256,1024]{3,2,0,1:T(8,128)(2,1)} async-done(((bf16[1,4,256,1024]{3,2,0,1:T(8,128)(2,1)}), bf16[1,4,256,1024]{3,2,0,1:T(8,128)(2,1)}, u32[]{:S(2)}, u32[]{:S(2)}) %all-to-all-start.4) | async-done | bytes 2097184 | tf_op jit(solution)/shard_map/forward/all_to_all | solution.py:105
  288.8 41.3 %all-gather.26.cloned.1.call-done = bf16[1,1024,1024]{2,1,0:T(8,128)(2,1)} async-done(((bf16[1,256,1024]{2,1,0:T(8,128)(2,1)}), bf16[1,1024,1024]{2,1,0:T(8,128)(2,1)}) %all-gather.26.cloned.1.call-update) | async-done | bytes 2097168 | tf_op jit(solution)/shard_map/forward/all_gather | solution.py:99
  330.0 6.5 fusion.126
  336.6 21.8 %all-gather.22.cloned.1.call-done = bf16[1024,1024]{1,0:T(8,128)(2,1)} async-done(((bf16[128,1024]{1,0:T(8,128)(2,1)}), bf16[1024,1024]{1,0:T(8,128)(2,1)}) %all-gather.22.cloned.1.call-update) | async-done | bytes 2097168 | tf_op jit(solution)/shard_map/weights/all_gather | solution.py:72
  358.4 6.9 convolution_convert_fusion.2
  365.3 4.7 all-to-all-start.5
  371.4 73.6 %all-gather.32.cloned.1.call-done = bf16[1,1024,1024]{2,1,0:T(8,128)(2,1)} async-done(((bf16[1,256,1024]{2,1,0:T(8,128)(2,1)}), bf16[1,1024,1024]{2,1,0:T(8,128)(2,1)}) %all-gather.32.cloned.1.call-update) | async-done | bytes 2097168 | tf_op jit(solution)/shard_map/backward_ffn/all_gather | solution.py:99
  445.0 8.0 fusion.103
  462.7 64.7 %all-gather.18.cloned.1.call-done = bf16[1,1024,1024]{2,1,0:T(8,128)(2,1)} async-done(((bf16[1,256,1024]{2,1,0:T(8,128)(2,1)}), bf16[1,1024,1024]{2,1,0:T(8,128)(2,1)}) %all-gather.18.cloned.1.call-update) | async-done | bytes 2097168 | tf_op jit(solution)/shard_map/forward/all_gather | solution.py:99
  550.5 39.8 %all-to-all-done.3 = bf16[1,4,256,1024]{3,2,0,1:T(8,128)(2,1)} async-done(((bf16[1,4,256,1024]{3,2,0,1:T(8,128)(2,1)}), bf16[1,4,256,1024]{3,2,0,1:T(8,128)(2,1)}, u32[]{:S(2)}, u32[]{:S(2)}) %all-to-all-start.3) | async-done | bytes 2097184 | tf_op jit(solution)/shard_map/forward/all_to_all | solution.py:105
  597.0 44.7 %all-gather.28.cloned.1.call-done = bf16[1,1024,1024]{2,1,0:T(8,128)(2,1)} async-done(((bf16[1,256,1024]{2,1,0:T(8,128)(2,1)}), bf16[1,1024,1024]{2,1,0:T(8,128)(2,1)}) %all-gather.28.cloned.1.call-update) | async-done | bytes 2097168 | tf_op jit(solution)/shard_map/backward_ffn/all_gather | solution.py:99
  641.7 8.0 fusion.96
  659.1 81.1 %all-to-all-done.6 = bf16[1,4,256,1024]{3,2,0,1:T(8,128)(2,1)} async-done(((bf16[1,4,256,1024]{3,2,0,1:T(8,128)(2,1)}), bf16[1,4,256,1024]{3,2,0,1:T(8,128)(2,1)}, u32[]{:S(2)}, u32[]{:S(2)}) %all-to-all-start.6) | async-done | bytes 2097184 | tf_op jit(solution)/shard_map/backward_ffn/all_to_all | solution.py:105
  748.0 6.8 fusion.124
  762.8 8.1 add_convert_fusion
  772.3 72.6 %while.57 = (s32[]{:T(128)}, f32[1,2048,4,64]{1,3,2,0:T(8,128)}, f32[1,2048,4,64]{1,3,2,0:T(8,128)}, bf16[2,1,512,4,64]{2,4,3,1,0:T(8,128)(2,1)}, bf16[2,1,512,4...) while((s32[]{:T(128)}, f32[1,2048,4,64]{1,3,2,0:T(8,128)}, ...), condition=%wide.region_35.36_spmd.clone, body=%wide.region_33.35_spmd.clone.sunk | while | flops 2737436672 | bytes 176742640 | solution.py:239
  779.1 8.0 multiply_reduce_fusion.23
  787.2 10.5 multiply_convert_fusion.16
  797.7 6.5 fusion.300
  809.6 5.6 fusion.299
  815.2 8.1 multiply_reduce_fusion.23
  823.3 10.5 multiply_convert_fusion.16
  833.9 6.2 fusion.300
  854.1 7.4 add_convert_fusion.1
  880.1 72.3 %while.56 = (s32[]{:T(128)}, f32[1,2048,4,64]{1,3,2,0:T(8,128)}, f32[1,2048,4,64]{1,3,2,0:T(8,128)}, bf16[2,1,512,4,64]{2,4,3,1,0:T(8,128)(2,1)}, bf16[2,1,512,4...) while((s32[]{:T(128)}, f32[1,2048,4,64]{1,3,2,0:T(8,128)}, ...), condition=%wide.region_26.27_spmd.clone, body=%wide.region_24.26_spmd.clone.sunk | while | flops 2737436672 | bytes 176742640 | solution.py:239
  887.0 8.2 multiply_reduce_fusion.22
  895.1 10.5 multiply_convert_fusion.15
  905.7 6.2 fusion.288
  917.2 5.6 fusion.287
  922.9 8.0 multiply_reduce_fusion.22
  930.9 10.5 multiply_convert_fusion.15
  941.4 6.2 fusion.288
  947.6 4.7 fusion.286
  973.9 5.1 all-to-all-start.7
  994.1 7.4 reduce-scatter.7.cloned.1.call-done
  1003.1 40.0 %reduce-scatter.5.cloned.1.call-done = bf16[128,3,256]{2,0,1:T(8,128)(2,1)} async-done(((bf16[1024,3,256]{2,0,1:T(8,128)(2,1)}), bf16[128,3,256]{2,0,1:T(8,128)(2,1)}) %reduce-scatter.5.cloned.1.call-update) | async-done | bytes 196624 | tf_op jit(solution)/shard_map/weight_grads/reduce_scatter | solution.py:296
  1070.7 9.5 all-gather
  (478 shorter events, 293.0 us)
Async XLA Ops:
  7.2 51.4 %all-gather.16.cloned.1.call-start = ((), (), s32[]{:S(2)}) async-start(), calls=%async_computation.16 | async-start | bytes 1769472 | tf_op jit(solution)/shard_map/weights/all_gather | solution.py:72
  21.9 11.7 %all-to-all-start = ((f32[8,2,4,6,256]{4,2,3,1,0:T(4,128)}), f32[8,2,4,6,256]{4,2,3,1,0:T(4,128)S(1)}, u32[]{:S(2)}, u32[]{:S(2)}) async-start(f32[8,2,4,6,256]{4,2,3,1,0:T(4,128)} %fusion.190), calls=%async_computation | async-start | bytes 786432 | tf_op jit(solution)/shard_map/modulation/all_to_all | solution.py:65
  26.2 67.8 %copy-start.84 = (f32[256]{0:T(256)}, f32[256]{0:T(256)S(1)}, u32[]{:S(2)}) copy-start(f32[256]{0:T(256)S(1)} %add_rsqrt_fusion.3) | copy-start | bytes 3076
  34.3 10.6 all-to-all-start.1
  39.2 50.9 %all-gather.14.cloned.1.call-start = ((), (), s32[]{:S(2)}) async-start(), calls=%async_computation.15 | async-start | bytes 2621440 | tf_op jit(solution)/shard_map/forward/all_gather | solution.py:99
  39.2 54.8 %copy-start.86 = (f32[256]{0:T(256)}, f32[256]{0:T(256)S(1)}, u32[]{:S(2)}) copy-start(f32[256]{0:T(256)S(1)} %add_rsqrt_fusion.1) | copy-start | bytes 3076
  45.7 48.4 %copy-start.70 = (f32[1,1,1,1024]{3,2,1,0:T(1,128)}, f32[1,1,1,1024]{3,2,1,0:T(1,128)S(1)}, u32[]{:S(2)}) copy-start(f32[1,1,1,1024]{3,2,1,0:T(1,128)S(1)} %get-tuple-element.598) | copy-start | bytes 12292
  46.3 47.8 %copy-start.72 = (f32[1,1,1,1024]{3,2,1,0:T(1,128)}, f32[1,1,1,1024]{3,2,1,0:T(1,128)S(1)}, u32[]{:S(2)}) copy-start(f32[1,1,1,1024]{3,2,1,0:T(1,128)S(1)} %get-tuple-element.604) | copy-start | bytes 12292
  47.8 89.0 %all-gather.24.cloned.1.call-start = ((), (), s32[]{:S(2)}) async-start(), calls=%async_computation.20 | async-start | bytes 2621440 | tf_op jit(solution)/shard_map/forward/all_gather | solution.py:99
  95.4 48.9 %collective-permute-start = (bf16[1,1024,256]{1,2,0:T(8,128)(2,1)}, bf16[1,1024,256]{1,2,0:T(8,128)(2,1)}, u32[]{:S(2)}, u32[]{:S(2)}) collective-permute-start(bf16[1,1024,256]{1,2,0:T(8,128)(2,1)} %get-tuple-element.574), channel_id=1, source_target_pairs={{0,4},{4,0},{1,5},{5,1},{2,6},{6,2},{3,7},{7,3},{8,12},{12,8},{9,1... | collective-permute-start | bytes 1572872 | tf_op jit(solution)/shard_map/forward/ppermute | solution.py:81
  95.4 50.1 %collective-permute-start.1 = (bf16[1,1024,256]{1,2,0:T(8,128)(2,1)}, bf16[1,1024,256]{1,2,0:T(8,128)(2,1)}, u32[]{:S(2)}, u32[]{:S(2)}) collective-permute-start(bf16[1,1024,256]{1,2,0:T(8,128)(2,1)} %get-tuple-element.575), channel_id=1, source_target_pairs={{0,4},{4,0},{1,5},{5,1},{2,6},{6,2},{3,7},{7,3},{8,12},{12,8},{9,1... | collective-permute-start | bytes 1572872 | tf_op jit(solution)/shard_map/forward/ppermute | solution.py:81
  143.3 35.2 %collective-permute-start.2 = (bf16[1,1024,256]{1,2,0:T(8,128)(2,1)}, bf16[1,1024,256]{1,2,0:T(8,128)(2,1)}, u32[]{:S(2)}, u32[]{:S(2)}) collective-permute-start(bf16[1,1024,256]{1,2,0:T(8,128)(2,1)} %get-tuple-element.579), channel_id=1, source_target_pairs={{0,4},{4,0},{1,5},{5,1},{2,6},{6,2},{3,7},{7,3},{8,12},{12,8},{9,1... | collective-permute-start | bytes 1572872 | tf_op jit(solution)/shard_map/forward/ppermute | solution.py:81
  143.3 36.6 %collective-permute-start.3 = (bf16[1,1024,256]{1,2,0:T(8,128)(2,1)}, bf16[1,1024,256]{1,2,0:T(8,128)(2,1)}, u32[]{:S(2)}, u32[]{:S(2)}) collective-permute-start(bf16[1,1024,256]{1,2,0:T(8,128)(2,1)} %get-tuple-element.580), channel_id=1, source_target_pairs={{0,4},{4,0},{1,5},{5,1},{2,6},{6,2},{3,7},{7,3},{8,12},{12,8},{9,1... | collective-permute-start | bytes 1572872 | tf_op jit(solution)/shard_map/forward/ppermute | solution.py:81
  173.7 53.5 %all-to-all-start.2 = ((bf16[1,4,256,1024]{3,2,0,1:T(8,128)(2,1)}), bf16[1,4,256,1024]{3,2,0,1:T(8,128)(2,1)}, u32[]{:S(2)}, u32[]{:S(2)}) async-start(bf16[1,4,256,1024]{3,2,0,1:T(8,128)(2,1)} %bitcast.579), calls=%async_computation.2 | async-start | bytes 4194304 | tf_op jit(solution)/shard_map/forward/all_to_all | solution.py:105
  227.3 52.3 %all-to-all-start.4 = ((bf16[1,4,256,1024]{3,2,0,1:T(8,128)(2,1)}), bf16[1,4,256,1024]{3,2,0,1:T(8,128)(2,1)}, u32[]{:S(2)}, u32[]{:S(2)}) async-start(bf16[1,4,256,1024]{3,2,0,1:T(8,128)(2,1)} %bitcast.580), calls=%async_computation.4 | async-start | bytes 4194304 | tf_op jit(solution)/shard_map/forward/all_to_all | solution.py:105
  231.8 57.0 %all-gather.20.cloned.1.call-start = ((), (), s32[]{:S(2)}) async-start(), calls=%async_computation.18 | async-start | bytes 2359296 | tf_op jit(solution)/shard_map/weights/all_gather | solution.py:72
  232.3 49.5 %copy-start.7 = (f32[2,1,256,1024]{3,2,1,0:T(8,128)S(1)}, f32[2,1,256,1024]{3,2,1,0:T(8,128)}, u32[]{:S(2)}) copy-start(f32[2,1,256,1024]{3,2,1,0:T(8,128)} %copy-done.6) | copy-start | bytes 6291460
  232.3 49.5 %copy-start.78 = (f32[1,1,1,1024]{3,2,1,0:T(1,128)S(1)}, f32[1,1,1,1024]{3,2,1,0:T(1,128)}, u32[]{:S(2)}) copy-start(f32[1,1,1,1024]{3,2,1,0:T(1,128)} %get-tuple-element.599) | copy-start | bytes 12292
  232.4 49.5 %copy-start.79 = (f32[1,1,1,1024]{3,2,1,0:T(1,128)S(1)}, f32[1,1,1,1024]{3,2,1,0:T(1,128)}, u32[]{:S(2)}) copy-start(f32[1,1,1,1024]{3,2,1,0:T(1,128)} %get-tuple-element.605) | copy-start | bytes 12292
  232.4 97.7 %all-gather.26.cloned.1.call-start = ((), (), s32[]{:S(2)}) async-start(), calls=%async_computation.21 | async-start | bytes 2621440 | tf_op jit(solution)/shard_map/forward/all_gather | solution.py:99
  285.2 73.2 %all-gather.22.cloned.1.call-start = ((), (), s32[]{:S(2)}) async-start(), calls=%async_computation.19 | async-start | bytes 2359296 | tf_op jit(solution)/shard_map/weights/all_gather | solution.py:72
  285.8 159.2 %all-gather.32.cloned.1.call-start = ((), (), s32[]{:S(2)}) async-start(), calls=%async_computation.24 | async-start | bytes 2621440 | tf_op jit(solution)/shard_map/backward_ffn/all_gather | solution.py:99
  365.3 92.9 %all-to-all-start.5 = ((bf16[1,4,256,1024]{3,2,0,1:T(8,128)(2,1)}), bf16[1,4,256,1024]{3,2,0,1:T(8,128)(2,1)}, u32[]{:S(2)}, u32[]{:S(2)}) async-start(bf16[1,4,256,1024]{3,2,0,1:T(8,128)(2,1)} %bitcast.589), calls=%async_computation.5 | async-start | bytes 4194304 | tf_op jit(solution)/shard_map/forward/all_to_all | solution.py:105
  370.0 157.4 %all-gather.18.cloned.1.call-start = ((), (), s32[]{:S(2)}) async-start(), calls=%async_computation.17 | async-start | bytes 2621440 | tf_op jit(solution)/shard_map/forward/all_gather | solution.py:99
  458.2 79.9 %all-to-all-start.8 = ((bf16[1,4,256,1024]{3,2,0,1:T(8,128)(2,1)}), bf16[1,4,256,1024]{3,2,0,1:T(8,128)(2,1)}, u32[]{:S(2)}, u32[]{:S(2)}) async-start(bf16[1,4,256,1024]{3,2,0,1:T(8,128)(2,1)} %bitcast.592), calls=%async_computation.8 | async-start | bytes 4194304 | tf_op jit(solution)/shard_map/backward_ffn/all_to_all | solution.py:105
  538.1 52.2 %all-to-all-start.3 = ((bf16[1,4,256,1024]{3,2,0,1:T(8,128)(2,1)}), bf16[1,4,256,1024]{3,2,0,1:T(8,128)(2,1)}, u32[]{:S(2)}, u32[]{:S(2)}) async-start(bf16[1,4,256,1024]{3,2,0,1:T(8,128)(2,1)} %bitcast.590), calls=%async_computation.3 | async-start | bytes 4194304 | tf_op jit(solution)/shard_map/forward/all_to_all | solution.py:105
  542.6 99.1 %all-gather.28.cloned.1.call-start = ((), (), s32[]{:S(2)}) async-start(), calls=%async_computation.22 | async-start | bytes 2621440 | tf_op jit(solution)/shard_map/backward_ffn/all_gather | solution.py:99
  653.5 86.7 %all-to-all-start.6 = ((bf16[1,4,256,1024]{3,2,0,1:T(8,128)(2,1)}), bf16[1,4,256,1024]{3,2,0,1:T(8,128)(2,1)}, u32[]{:S(2)}, u32[]{:S(2)}) async-start(bf16[1,4,256,1024]{3,2,0,1:T(8,128)(2,1)} %bitcast.591), calls=%async_computation.6 | async-start | bytes 4194304 | tf_op jit(solution)/shard_map/backward_ffn/all_to_all | solution.py:105
  658.1 101.4 %all-gather.34.cloned.1.call-start = ((), (), s32[]{:S(2)}) async-start(), calls=%async_computation.25 | async-start | bytes 2621440 | tf_op jit(solution)/shard_map/backward_attention/all_gather | solution.py:99
  659.0 85.7 %copy-start.32 = (f32[256,1024]{1,0:T(8,128)S(1)}, f32[256,1024]{1,0:T(8,128)}, u32[]{:S(2)}) copy-start(f32[256,1024]{1,0:T(8,128)} %convert_reduce_fusion.11) | copy-start | bytes 3145732
  659.1 214.7 %all-gather.30.cloned.1.call-start = ((), (), s32[]{:S(2)}) async-start(), calls=%async_computation.23 | async-start | bytes 2621440 | tf_op jit(solution)/shard_map/backward_attention/all_gather | solution.py:99
  747.7 239.3 %reduce-scatter.11.cloned.1.call-start = ((), (), s32[]{:S(2)}) async-start(), calls=%async_computation.29 | async-start | bytes 2359296 | tf_op jit(solution)/shard_map/weight_grads/reduce_scatter | solution.py:296
  771.0 217.9 %reduce-scatter.9.cloned.1.call-start = ((), (), s32[]{:S(2)}) async-start(), calls=%async_computation.28 | async-start | bytes 2359296 | tf_op jit(solution)/shard_map/weight_grads/reduce_scatter | solution.py:296
  849.7 13.6 %collective-permute-start.6 = (bf16[1,1024,256]{2,1,0:T(8,128)(2,1)}, bf16[1,1024,256]{2,1,0:T(8,128)(2,1)}, u32[]{:S(2)}, u32[]{:S(2)}) collective-permute-start(bf16[1,1024,256]{2,1,0:T(8,128)(2,1)} %copy.282), channel_id=1, source_target_pairs={{0,4},{4,0},{1,5},{5,1},{2,6},{6,2},{3,7},{7,3},{8,12},{12,8},{9,1... | collective-permute-start | bytes 1572872 | tf_op jit(solution)/shard_map/backward_attention/ppermute | solution.py:91
  853.6 10.9 %collective-permute-start.7 = (bf16[1,1024,256]{2,1,0:T(8,128)(2,1)}, bf16[1,1024,256]{2,1,0:T(8,128)(2,1)}, u32[]{:S(2)}, u32[]{:S(2)}) collective-permute-start(bf16[1,1024,256]{2,1,0:T(8,128)(2,1)} %copy.284), channel_id=1, source_target_pairs={{0,4},{4,0},{1,5},{5,1},{2,6},{6,2},{3,7},{7,3},{8,12},{12,8},{9,1... | collective-permute-start | bytes 1572872 | tf_op jit(solution)/shard_map/backward_attention/ppermute | solution.py:91
  869.0 104.8 %all-to-all-start.9 = ((bf16[1,4,256,1024]{3,2,0,1:T(8,128)(2,1)}), bf16[1,4,256,1024]{3,2,0,1:T(8,128)(2,1)}, u32[]{:S(2)}, u32[]{:S(2)}) async-start(bf16[1,4,256,1024]{3,2,0,1:T(8,128)(2,1)} %bitcast.97), calls=%async_computation.9 | async-start | bytes 4194304 | tf_op jit(solution)/shard_map/backward_attention/all_to_all | solution.py:105
  873.7 127.9 %reduce-scatter.7.cloned.1.call-start = ((), (), s32[]{:S(2)}) async-start(), calls=%async_computation.27 | async-start | bytes 589824 | tf_op jit(solution)/shard_map/weight_grads/reduce_scatter | solution.py:296
  957.3 8.7 collective-permute-start.4
  962.3 5.0 collective-permute-start.5
  973.9 70.9 %all-to-all-start.7 = ((bf16[1,4,256,1024]{3,2,0,1:T(8,128)(2,1)}), bf16[1,4,256,1024]{3,2,0,1:T(8,128)(2,1)}, u32[]{:S(2)}, u32[]{:S(2)}) async-start(bf16[1,4,256,1024]{3,2,0,1:T(8,128)(2,1)} %bitcast.83), calls=%async_computation.7 | async-start | bytes 4194304 | tf_op jit(solution)/shard_map/backward_attention/all_to_all | solution.py:105
  979.0 64.1 %reduce-scatter.5.cloned.1.call-start = ((), (), s32[]{:S(2)}) async-start(), calls=%async_computation.26 | async-start | bytes 1769472 | tf_op jit(solution)/shard_map/weight_grads/reduce_scatter | solution.py:296
  993.3 54.3 %copy-start.71 = (f32[1,1,1,1024]{3,2,1,0:T(1,128)S(1)}, f32[1,1,1,1024]{3,2,1,0:T(1,128)}, u32[]{:S(2)}) copy-start(f32[1,1,1,1024]{3,2,1,0:T(1,128)} %copy-done.70) | copy-start | bytes 12292
  993.4 55.2 %copy-start.8 = (f32[2,1,256,1024]{3,2,1,0:T(8,128)S(1)}, f32[2,1,256,1024]{3,2,1,0:T(8,128)}, u32[]{:S(2)}) copy-start(f32[2,1,256,1024]{3,2,1,0:T(8,128)} %copy-done.6) | copy-start | bytes 6291460
  993.4 55.2 %copy-start.81 = (f32[256]{0:T(256)S(1)}, f32[256]{0:T(256)}, u32[]{:S(2)}) copy-start(f32[256]{0:T(256)} %copy-done.80) | copy-start | bytes 3076
  993.4 55.2 %copy-start.83 = (f32[256]{0:T(256)S(1)}, f32[256]{0:T(256)}, u32[]{:S(2)}) copy-start(f32[256]{0:T(256)} %copy-done.82) | copy-start | bytes 3076
  993.4 55.1 %copy-start.85 = (f32[256]{0:T(256)S(1)}, f32[256]{0:T(256)}, u32[]{:S(2)}) copy-start(f32[256]{0:T(256)} %copy-done.84) | copy-start | bytes 3076
  993.4 55.1 %copy-start.87 = (f32[256]{0:T(256)S(1)}, f32[256]{0:T(256)}, u32[]{:S(2)}) copy-start(f32[256]{0:T(256)} %copy-done.86) | copy-start | bytes 3076
  1056.2 10.4 all-to-all-start.10
  (105 other events, 673.3 us)
Sparse Core Ops, SparseCore 0:
  10.4 29.0 all-gather.15
  47.9 42.2 all-gather.13
  92.3 44.4 all-gather.23
  234.1 29.0 all-gather.19
  285.3 44.6 all-gather.25
  331.8 26.5 all-gather.21
  360.5 84.4 all-gather.31
  447.1 80.2 all-gather.17
  597.2 44.5 all-gather.27
  660.7 74.2 all-gather.33
  747.8 43.7 all-gather.29
  794.8 39.9 reduce-scatter.10
  861.6 39.2 reduce-scatter.8
  966.1 35.4 reduce-scatter.6
  1004.7 38.3 reduce-scatter.4

commit v4 on v3

--- a/solution.py
+++ b/solution.py
@@ -64,8 +64,10 @@
         summed_mod = jnp.sum(
             lax.all_to_all(partial_mod, ("dp", "frame"), 0, 0, tiled=True), axis=0
         )
-        modulation = lax.all_to_all(summed_mod, "tensor", 1, 3, tiled=True)
-        modulation = modulation.reshape(clips, 6, 1, model_width)
+        group_mod = lax.all_gather(summed_mod, "tensor", axis=3, tiled=True)
+        group_mod = jnp.swapaxes(group_mod, 1, 2)[:, :, :, None, :]
+        group_index = lax.axis_index("tensor")
+        modulation = lax.dynamic_index_in_dim(group_mod, group_index, axis=2, keepdims=False)
 
     with jax.named_scope("weights"):
         joint_weight, mixer_weight, upward_weight, downward_weight = (
@@ -75,6 +77,9 @@
 
     residual = tokens[:, 0].astype(jnp.float32)
     upstream = out_grad[:, 0].astype(jnp.float32)
+    with jax.named_scope("group_inputs"):
+        group_tokens = lax.all_gather(tokens[:, 0], "tensor", axis=1, tiled=True)
+        group_upstream = lax.all_gather(out_grad[:, 0], "tensor", axis=1, tiled=True)
     def gather_halves(values):
         if halves != 2:
             return lax.all_gather(values, "frame", axis=1, tiled=True)
@@ -91,8 +96,9 @@
         other = lax.ppermute(values[:, count:].astype(jnp.bfloat16), "frame", [(0, 1), (1, 0)])
         return mine.astype(jnp.bfloat16).astype(jnp.float32) + other.astype(jnp.float32)
 
-    def clip_pass(residual, upstream, modulation):
+    def clip_pass(residual, upstream, modulation, group_tokens, group_upstream, group_mod):
         clips = residual.shape[0]
+        patches = residual.shape[1]
         shift1, scale1, gate1 = modulation[:, 0], modulation[:, 1], modulation[:, 2]
         shift2, scale2, gate2 = modulation[:, 3], modulation[:, 4], modulation[:, 5]
         def gather_tokens(values):
@@ -107,8 +113,14 @@
 
         with jax.named_scope("forward"):
             normed_one, inverse_one = normalize(residual)
-            entering_one = (normed_one * (1.0 + scale1) + shift1).astype(jnp.bfloat16)
-            flat_one = gather_tokens(entering_one)
+            group_normed, _ = normalize(
+                group_tokens.astype(jnp.float32).reshape(clips, groups, patches, model_width)
+            )
+            flat_one = (
+                (group_normed * (1.0 + group_mod[:, 1]) + group_mod[:, 0])
+                .astype(jnp.bfloat16)
+                .reshape(clips, groups * patches, model_width)
+            )
             token_count = flat_one.shape[1]
             projected = jnp.einsum(
                 "crd,dkh->crkh", flat_one, joint_weight, preferred_element_type=jnp.float32
@@ -162,8 +174,14 @@
 
         with jax.named_scope("backward_ffn"):
             grad_gate_two = jnp.sum(upstream * branch_two, axis=1)
-            grad_branch_two = (gate2 * upstream).astype(jnp.bfloat16)
-            grad_two_all = gather_tokens(grad_branch_two)
+            grad_two_all = (
+                (
+                    group_mod[:, 5]
+                    * group_upstream.astype(jnp.float32).reshape(clips, groups, patches, model_width)
+                )
+                .astype(jnp.bfloat16)
+                .reshape(clips, groups * patches, model_width)
+            )
             grad_hidden = jnp.einsum(
                 "cro,of->crf", grad_two_all, downward_weight, preferred_element_type=jnp.float32
             )
@@ -269,7 +287,14 @@
         return output, grad_input.astype(jnp.bfloat16), grad_modulation, totals
 
     pieces = [
-        clip_pass(residual[i : i + 1], upstream[i : i + 1], modulation[i : i + 1])
+        clip_pass(
+            residual[i : i + 1],
+            upstream[i : i + 1],
+            modulation[i : i + 1],
+            group_tokens[i : i + 1],
+            group_upstream[i : i + 1],
+            group_mod[i : i + 1],
+        )
         for i in range(clips)
     ]
     output = jnp.concatenate([p[0] for p in pieces], axis=0)

time: 1090 us -> 1030 us (0.945)
  waiting for transfers between devices: 566 us -> 431 us
  matrix products: 241 us -> 264 us
  blocking collectives: 30.2 us -> 52.3 us
  other arithmetic: 127 us -> 141 us
  local copies, waits for them, and re-layouts: 53.9 us -> 67.7 us
    all_gather x8 -> x4, waiting for transfers between devices: 297 us -> 86.4 us  [gather_tokens(): return lax.all_gather(values, 'tensor', axis=1, tiled=True)]
    all_to_all x8, waiting for transfers between devices: 183 us -> 237 us  [scatter_tokens(): received = lax.all_to_all(parts, 'tensor', 1, 1, tiled=True)]
    all_gather x0 -> x2, waiting for transfers between devices: none -> 36.2 us  [the longest x1 36.2 us: on_device(): group_tokens = lax.all_gather(tokens[:, 0], 'tensor', axis=1, tiled=True)]
    all_gather x0 -> x1, blocking collectives: none -> 19.4 us  [on_device(): group_mod = lax.all_gather(summed_mod, 'tensor', axis=3, tiled=True)]
    dot_general x4, matrix products: 15.4 us -> 27.9 us  [attend_back(): jnp.einsum('chqk,cqhe->ckhe', grad_scores, query_block, preferred_element...]
    unnamed x213 -> x204, local copies, waits for them, and re-layouts: 25.8 us -> 28 us
  transfers between devices with their start and end apart: 34 -> 31, of which waited for: 16 -> 12; matrix products, arithmetic and copies ran while one was open for 34% -> 43% of each run, Pallas kernels for 0% -> 0%
where the time goes in v4:
time: 1030 us; the launch traced here: 1020 us
  waiting for transfers between devices  431 us (42%)
  matrix products  264 us (26%)
  other arithmetic  141 us (14%)
  local copies, waits for them, and re-layouts  67.7 us (7%)
  blocking collectives  52.3 us (5%)
  starting transfers between devices  48.9 us (5%)
  between operations  15.6 us (2%)
    all_to_all x8, waiting for transfers between devices, scatter_tokens(): received = lax.all_to_all(parts, 'tensor', 1, 1, tiled=True)  237 us
    all_gather x4, waiting for transfers between devices, gather_tokens(): return lax.all_gather(values, 'tensor', axis=1, tiled=True)  86.4 us
    reduce_scatter x4, waiting for transfers between devices, on_device(): lax.psum_scatter(total.astype(jnp.bfloat16), ('dp', 'frame'), scatter_dim...  49.6 us
    convert_element_type x4, other arithmetic, attend_back(): grad_scores = (probs * (grad_probs - row_terms)).astype(jnp.bfloat16)  41.9 us
    all_to_all x8, starting transfers between devices, scatter_tokens(): received = lax.all_to_all(parts, 'tensor', 1, 1, tiled=True)  37.4 us
    all_gather x1, waiting for transfers between devices, on_device(): group_tokens = lax.all_gather(tokens[:, 0], 'tensor', axis=1, tiled=True)  36.2 us
    dot_general x4, matrix products, attend_back(): jnp.einsum('cqhe,ckhe->chqk', grad_block, value_heads, preferred_element_...  34.3 us
    dot_general x4, matrix products, attend_back(): jnp.einsum('chqk,ckhe->cqhe', grad_scores, key_heads, preferred_element_t...  30 us
  transfers between devices with their start and end apart: 31, of which 12 were waited for; matrix products, arithmetic and copies ran while one was open for 43% of the time, Pallas kernels for 0%

profile of v4, /device:TPU:0, one launch (start us, length us, event | category | flops | bytes accessed | tf_op | source)
XLA Modules:
  0.0 1021.3 jit_solution(15384394116283009315)
XLA Ops:
  10.5 10.6 %all-gather.3 = s32[8,2,4]{2,1,0:T(2,128)S(1)} all-gather(s32[1,2,4]{2,1,0:T(2,128)} %bitcast.739), channel_id=1, replica_groups=mesh['dp'=4,'frame'=2,'tensor'=4] {'dp','frame'}, dimensions={0}, use_global_device_ids=true | all-gather | bytes 288 | tf_op jit(solution)/shard_map/modulation/all_gather | solution.py:54
  27.3 12.8 %all_gather.43 = bf16[1024,256]{1,0:T(8,128)(2,1)} all-gather(bf16[128,256]{1,0:T(8,128)(2,1)S(1)} %copy-done.71), channel_id=1, replica_groups=mesh['dp'=4,'frame'=2,'tensor'=4] {'dp','frame'}, dimensions={0}, use_global_device_ids=true | all-gather | bytes 589824 | tf_op jit(solution)/shard_map/weights/all_gather | solution.py:74
  40.3 19.4 %all_gather.40 = f32[2,4,6,1024]{3,2,1,0:T(8,128)S(1)} all-gather(f32[2,4,6,256]{3,2,1,0:T(8,128)S(1)} %copy.337), channel_id=1, replica_groups=mesh['dp'=4,'frame'=2,'tensor'=4] {'tensor'}, dimensions={3}, use_global_device_ids=true | all-gather | bytes 245760 | tf_op jit(solution)/shard_map/modulation/all_gather | solution.py:67
  61.0 36.2 %all-gather.28.cloned.1.call-done = bf16[2,1,1024,1024]{3,2,1,0:T(8,128)(2,1)} async-done(((bf16[2,1,256,1024]{3,2,1,0:T(8,128)(2,1)}), bf16[2,1,1024,1024]{3,2,1,0:T(8,128)(2,1)}) %all-gather.28.cloned.1.call-update) | async-done | bytes 4194320 | tf_op jit(solution)/shard_map/group_inputs/all_gather | solution.py:81
  107.5 16.5 %all-gather.14.cloned.1.call-done = bf16[1024,3,256]{0,2,1:T(8,128)(2,1)} async-done(((bf16[128,3,256]{0,2,1:T(8,128)(2,1)}), bf16[1024,3,256]{0,2,1:T(8,128)(2,1)}) %all-gather.14.cloned.1.call-update) | async-done | bytes 1572880 | tf_op jit(solution)/shard_map/weights/all_gather | solution.py:74
  140.7 22.0 %while.55 = (s32[]{:T(128)}, bf16[2,1,512,4,64]{2,4,3,1,0:T(8,128)(2,1)}, f32[2,1,4,512]{3,2,1,0:T(4,128)S(1)}, bf16[2,1,512,4,64]{2,4,3,1,0:T(8,128)(2,1)S(1)},...) while((s32[]{:T(128)}, ...), condition=%wide.region_16.17_spmd, body=%wide.region_13.16_spmd.sunk | while | flops 1111619584 | bytes 53019220 | solution.py:155
  175.0 21.8 %while.54 = (s32[]{:T(128)}, bf16[2,1,512,4,64]{2,4,3,1,0:T(8,128)(2,1)}, f32[2,1,4,512]{3,2,1,0:T(4,128)S(1)}, bf16[2,1,512,4,64]{2,4,3,1,0:T(8,128)(2,1)S(1)},...) while((s32[]{:T(128)}, bf16[2,1,512,4,64]{2,4,3,1,0:T(8,128)(2,1)}, ...), condition=%wide.region_6.7_spmd, body=%wide.region_3.0_spmd.sunk | while | flops 1111619584 | bytes 53019220 | solution.py:155
  191.7 5.1 fusion.280
  201.7 49.1 %all-to-all-done.3 = bf16[1,4,256,1024]{3,2,0,1:T(8,128)(2,1)} async-done(((bf16[1,4,256,1024]{3,2,0,1:T(8,128)(2,1)}), bf16[1,4,256,1024]{3,2,0,1:T(8,128)(2,1)}, u32[]{:S(2)}, u32[]{:S(2)}) %all-to-all-start.3) | async-done | bytes 2097184 | tf_op jit(solution)/shard_map/forward/all_to_all | solution.py:111
  261.7 42.4 %all-to-all-done.1 = bf16[1,4,256,1024]{3,2,0,1:T(8,128)(2,1)} async-done(((bf16[1,4,256,1024]{3,2,0,1:T(8,128)(2,1)}), bf16[1,4,256,1024]{3,2,0,1:T(8,128)(2,1)}, u32[]{:S(2)}, u32[]{:S(2)}) %all-to-all-start.1) | async-done | bytes 2097184 | tf_op jit(solution)/shard_map/forward/all_to_all | solution.py:111
  312.4 5.6 fusion.107
  318.0 6.8 fusion.211
  326.2 30.1 %all-gather.22.cloned.1.call-done = bf16[1,1024,1024]{2,1,0:T(8,128)(2,1)} async-done(((bf16[1,256,1024]{2,1,0:T(8,128)(2,1)}), bf16[1,1024,1024]{2,1,0:T(8,128)(2,1)}) %all-gather.22.cloned.1.call-update) | async-done | bytes 2097168 | tf_op jit(solution)/shard_map/forward/all_gather | solution.py:105
  356.3 10.1 fusion.125
  374.7 6.6 fusion.210
  381.3 56.3 %all-gather.16.cloned.1.call-done = bf16[1,1024,1024]{2,1,0:T(8,128)(2,1)} async-done(((bf16[1,256,1024]{2,1,0:T(8,128)(2,1)}), bf16[1,1024,1024]{2,1,0:T(8,128)(2,1)}) %all-gather.16.cloned.1.call-update) | async-done | bytes 2097168 | tf_op jit(solution)/shard_map/forward/all_gather | solution.py:105
  437.7 10.1 fusion.118
  457.3 6.9 convolution_convert_fusion.2
  464.2 39.3 %all-to-all-done.5 = bf16[1,4,256,1024]{3,2,0,1:T(8,128)(2,1)} async-done(((bf16[1,4,256,1024]{3,2,0,1:T(8,128)(2,1)}), bf16[1,4,256,1024]{3,2,0,1:T(8,128)(2,1)}, u32[]{:S(2)}, u32[]{:S(2)}) %all-to-all-start.5) | async-done | bytes 2097184 | tf_op jit(solution)/shard_map/backward_ffn/all_to_all | solution.py:111
  509.7 6.9 convolution_convert_fusion.4
  516.6 39.3 %all-to-all-done.4 = bf16[1,4,256,1024]{3,2,0,1:T(8,128)(2,1)} async-done(((bf16[1,4,256,1024]{3,2,0,1:T(8,128)(2,1)}), bf16[1,4,256,1024]{3,2,0,1:T(8,128)(2,1)}, u32[]{:S(2)}, u32[]{:S(2)}) %all-to-all-start.4) | async-done | bytes 2097184 | tf_op jit(solution)/shard_map/forward/all_to_all | solution.py:111
  574.5 67.3 %all-to-all-done.2 = bf16[1,4,256,1024]{3,2,0,1:T(8,128)(2,1)} async-done(((bf16[1,4,256,1024]{3,2,0,1:T(8,128)(2,1)}), bf16[1,4,256,1024]{3,2,0,1:T(8,128)(2,1)}, u32[]{:S(2)}, u32[]{:S(2)}) %all-to-all-start.2) | async-done | bytes 2097184 | tf_op jit(solution)/shard_map/forward/all_to_all | solution.py:111
  653.7 5.2 fusion.197
  680.0 87.4 %while.57 = (s32[]{:T(128)}, f32[1,2048,4,64]{1,3,2,0:T(8,128)}, f32[1,2048,4,64]{1,3,2,0:T(8,128)}, bf16[2,1,512,4,64]{2,4,3,1,0:T(8,128)(2,1)}, bf16[2,1,512,4...) while((s32[]{:T(128)}, f32[1,2048,4,64]{1,3,2,0:T(8,128)}, ...), condition=%wide.region_39.40_spmd.clone, body=%wide.region_37.39_spmd.clone.sunk | while | flops 2737436672 | bytes 273212096 | solution.py:257
  682.5 8.6 multiply_reduce_fusion.23
  693.3 10.6 %multiply_convert_fusion.14 = bf16[4,512,2048]{2,1,0:T(8,128)(2,1)} fusion(f32[4,512,2048]{2,1,0:T(8,128)} %get-tuple-element.848, f32[4,512,2048]{2,1,0:T(8,128)S(1)} %fusion.304, f32[4,512]{1,0:T(4,128)S(1)} %get-tuple-element.849, f32[4,512]{1,0:T(4,128)S(1)} %dynamic-slice_bitcast_fusion.7), kind=kLoop, calls=%fused_computation.66.clone.1 | loop fusion | flops 20971520 | bytes 41959424 | tf_op jit(solution)/shard_map/backward_attention/while/body/eval_jaxpr/convert_element_type | solution.py:240
  703.9 6.9 fusion.305
  710.8 7.5 fusion.307
  725.1 8.6 multiply_reduce_fusion.23
  736.0 10.4 %multiply_convert_fusion.14 = bf16[4,512,2048]{2,1,0:T(8,128)(2,1)} fusion(f32[4,512,2048]{2,1,0:T(8,128)} %get-tuple-element.848, f32[4,512,2048]{2,1,0:T(8,128)S(1)} %fusion.304, f32[4,512]{1,0:T(4,128)S(1)} %get-tuple-element.849, f32[4,512]{1,0:T(4,128)S(1)} %dynamic-slice_bitcast_fusion.7), kind=kLoop, calls=%fused_computation.66.clone.1 | loop fusion | flops 20971520 | bytes 41959424 | tf_op jit(solution)/shard_map/backward_attention/while/body/eval_jaxpr/convert_element_type | solution.py:240
  746.4 7.6 fusion.305
  754.0 7.5 fusion.307
  761.5 5.6 fusion.306
  793.7 86.0 %while.56 = (s32[]{:T(128)}, f32[1,2048,4,64]{1,3,2,0:T(8,128)}, f32[1,2048,4,64]{1,3,2,0:T(8,128)}, bf16[2,1,512,4,64]{2,4,3,1,0:T(8,128)(2,1)}, bf16[2,1,512,4...) while((s32[]{:T(128)}, f32[1,2048,4,64]{1,3,2,0:T(8,128)}, ...), condition=%wide.region_28.29_spmd.clone, body=%wide.region_26.28_spmd.clone.sunk | while | flops 2737436672 | bytes 273212096 | solution.py:257
  796.2 8.6 multiply_reduce_fusion.22
  807.0 10.4 %multiply_convert_fusion.13 = bf16[4,512,2048]{2,1,0:T(8,128)(2,1)} fusion(f32[4,512,2048]{2,1,0:T(8,128)} %get-tuple-element.837, f32[4,512,2048]{2,1,0:T(8,128)S(1)} %fusion.292, f32[4,512]{1,0:T(4,128)S(1)} %get-tuple-element.838, f32[4,512]{1,0:T(4,128)S(1)} %dynamic-slice_bitcast_fusion.6), kind=kLoop, calls=%fused_computation.32.clone.1 | loop fusion | flops 20971520 | bytes 41959424 | tf_op jit(solution)/shard_map/backward_attention/while/body/eval_jaxpr/convert_element_type | solution.py:240
  817.5 6.5 fusion.293
  823.9 7.5 fusion.295
  838.2 8.6 multiply_reduce_fusion.22
  849.1 10.4 %multiply_convert_fusion.13 = bf16[4,512,2048]{2,1,0:T(8,128)(2,1)} fusion(f32[4,512,2048]{2,1,0:T(8,128)} %get-tuple-element.837, f32[4,512,2048]{2,1,0:T(8,128)S(1)} %fusion.292, f32[4,512]{1,0:T(4,128)S(1)} %get-tuple-element.838, f32[4,512]{1,0:T(4,128)S(1)} %dynamic-slice_bitcast_fusion.6), kind=kLoop, calls=%fused_computation.32.clone.1 | loop fusion | flops 20971520 | bytes 41959424 | tf_op jit(solution)/shard_map/backward_attention/while/body/eval_jaxpr/convert_element_type | solution.py:240
  859.5 7.0 fusion.293
  866.6 7.5 fusion.295
  874.1 5.6 fusion.294
  908.3 5.1 all-to-all-start.6
  913.5 5.4 add_convert_fusion.2
  923.7 9.4 reduce-scatter.7.cloned.1.call-done
  934.6 40.2 %reduce-scatter.5.cloned.1.call-done = bf16[128,3,256]{2,0,1:T(8,128)(2,1)} async-done(((bf16[1024,3,256]{2,0,1:T(8,128)(2,1)}), bf16[128,3,256]{2,0,1:T(8,128)(2,1)}) %reduce-scatter.5.cloned.1.call-update) | async-done | bytes 196624 | tf_op jit(solution)/shard_map/weight_grads/reduce_scatter | solution.py:321
  1003.6 9.5 all-gather.2
  (452 shorter events, 307.4 us)
Async XLA Ops:
  7.2 20.2 %copy-start.71 = (bf16[128,256]{1,0:T(8,128)(2,1)S(1)}, bf16[128,256]{1,0:T(8,128)(2,1)}, u32[]{:S(2)}) copy-start(bf16[128,256]{1,0:T(8,128)(2,1)} %param.20) | copy-start | bytes 196612
  7.2 90.0 %all-gather.28.cloned.1.call-start = ((), (), s32[]{:S(2)}) async-start(), calls=%async_computation.25 | async-start | bytes 5242880 | tf_op jit(solution)/shard_map/group_inputs/all_gather | solution.py:81
  7.9 116.1 %all-gather.14.cloned.1.call-start = ((), (), s32[]{:S(2)}) async-start(), calls=%async_computation.14 | async-start | bytes 1769472 | tf_op jit(solution)/shard_map/weights/all_gather | solution.py:74
  9.7 302.7 %all-gather.30.cloned.1.call-start = ((), (), s32[]{:S(2)}) async-start(), calls=%async_computation.26 | async-start | bytes 5242880 | tf_op jit(solution)/shard_map/group_inputs/all_gather | solution.py:82
  23.3 16.9 %all-to-all-start = ((f32[8,2,4,6,256]{4,2,3,1,0:T(4,128)}), f32[8,2,4,6,256]{4,2,3,1,0:T(4,128)S(1)}, u32[]{:S(2)}, u32[]{:S(2)}) async-start(f32[8,2,4,6,256]{4,2,3,1,0:T(4,128)} %fusion.183), calls=%async_computation | async-start | bytes 786432 | tf_op jit(solution)/shard_map/modulation/all_to_all | solution.py:65
  26.8 291.2 %all-gather.20.cloned.1.call-start = ((), (), s32[]{:S(2)}) async-start(), calls=%async_computation.17 | async-start | bytes 2359296 | tf_op jit(solution)/shard_map/weights/all_gather | solution.py:74
  59.7 42.9 %copy-start.52 = (f32[2,4,6,1024]{3,2,1,0:T(8,128)}, f32[2,4,6,1024]{3,2,1,0:T(8,128)S(1)}, u32[]{:S(2)}) copy-start(f32[2,4,6,1024]{3,2,1,0:T(8,128)S(1)} %all_gather.40) | copy-start | bytes 589828
  128.5 8.0 collective-permute-start.3
  128.8 9.9 collective-permute-start.2
  134.8 36.9 %collective-permute-start.1 = (bf16[1,1024,256]{1,2,0:T(8,128)(2,1)}, bf16[1,1024,256]{1,2,0:T(8,128)(2,1)}, u32[]{:S(2)}, u32[]{:S(2)}) collective-permute-start(bf16[1,1024,256]{1,2,0:T(8,128)(2,1)} %get-tuple-element.602), channel_id=1, source_target_pairs={{0,4},{4,0},{1,5},{5,1},{2,6},{6,2},{3,7},{7,3},{8,12},{12,8},{9,1... | collective-permute-start | bytes 1572872 | tf_op jit(solution)/shard_map/forward/ppermute | solution.py:86
  135.1 37.9 %collective-permute-start = (bf16[1,1024,256]{1,2,0:T(8,128)(2,1)}, bf16[1,1024,256]{1,2,0:T(8,128)(2,1)}, u32[]{:S(2)}, u32[]{:S(2)}) collective-permute-start(bf16[1,1024,256]{1,2,0:T(8,128)(2,1)} %get-tuple-element.601), channel_id=1, source_target_pairs={{0,4},{4,0},{1,5},{5,1},{2,6},{6,2},{3,7},{7,3},{8,12},{12,8},{9,1... | collective-permute-start | bytes 1572872 | tf_op jit(solution)/shard_map/forward/ppermute | solution.py:86
  140.7 24.1 %copy-start.36 = (bf16[1024,256]{1,0:T(8,128)(2,1)S(1)}, bf16[1024,256]{1,0:T(8,128)(2,1)}, u32[]{:S(2)}) copy-start(bf16[1024,256]{1,0:T(8,128)(2,1)} %all_gather.43) | copy-start | bytes 1572868
  167.0 83.8 %all-to-all-start.3 = ((bf16[1,4,256,1024]{3,2,0,1:T(8,128)(2,1)}), bf16[1,4,256,1024]{3,2,0,1:T(8,128)(2,1)}, u32[]{:S(2)}, u32[]{:S(2)}) async-start(bf16[1,4,256,1024]{3,2,0,1:T(8,128)(2,1)} %bitcast.675), calls=%async_computation.3 | async-start | bytes 4194304 | tf_op jit(solution)/shard_map/forward/all_to_all | solution.py:111
  175.0 24.6 %copy-start.37 = (bf16[1024,256]{1,0:T(8,128)(2,1)S(1)}, bf16[1024,256]{1,0:T(8,128)(2,1)}, u32[]{:S(2)}) copy-start(bf16[1024,256]{1,0:T(8,128)(2,1)} %all_gather.43) | copy-start | bytes 1572868
  196.8 54.0 %copy-start.63 = (f32[2,1,4,512]{3,2,1,0:T(4,128)}, f32[2,1,4,512]{3,2,1,0:T(4,128)S(1)}, u32[]{:S(2)}) copy-start(f32[2,1,4,512]{3,2,1,0:T(4,128)S(1)} %get-tuple-element.898) | copy-start | bytes 49156
  196.8 54.0 %copy-start.6 = (bf16[1,2048,4,64]{1,3,2,0:T(8,128)(2,1)}, bf16[1,2048,4,64]{1,3,2,0:T(8,128)(2,1)S(1)}, u32[]{:S(2)}) copy-start(bf16[1,2048,4,64]{1,3,2,0:T(8,128)(2,1)S(1)} %get-tuple-element.971) | copy-start | bytes 3145732
  196.8 54.0 %copy-start.10 = (bf16[1,2048,4,64]{1,3,2,0:T(8,128)(2,1)}, bf16[1,2048,4,64]{1,3,2,0:T(8,128)(2,1)S(1)}, u32[]{:S(2)}) copy-start(bf16[1,2048,4,64]{1,3,2,0:T(8,128)(2,1)S(1)} %get-tuple-element.973) | copy-start | bytes 3145732
  250.8 53.2 %all-to-all-start.1 = ((bf16[1,4,256,1024]{3,2,0,1:T(8,128)(2,1)}), bf16[1,4,256,1024]{3,2,0,1:T(8,128)(2,1)}, u32[]{:S(2)}, u32[]{:S(2)}) async-start(bf16[1,4,256,1024]{3,2,0,1:T(8,128)(2,1)} %bitcast.676), calls=%async_computation.1 | async-start | bytes 4194304 | tf_op jit(solution)/shard_map/forward/all_to_all | solution.py:111
  255.4 70.8 %all-gather.18.cloned.1.call-start = ((), (), s32[]{:S(2)}) async-start(), calls=%async_computation.16 | async-start | bytes 2359296 | tf_op jit(solution)/shard_map/weights/all_gather | solution.py:74
  256.0 100.2 %all-gather.22.cloned.1.call-start = ((), (), s32[]{:S(2)}) async-start(), calls=%async_computation.18 | async-start | bytes 2621440 | tf_op jit(solution)/shard_map/forward/all_gather | solution.py:105
  257.5 48.6 %copy-start.16 = (f32[2,1,256,1024]{3,2,1,0:T(8,128)}, f32[2,1,256,1024]{3,2,1,0:T(8,128)S(1)}, u32[]{:S(2)}) copy-start(f32[2,1,256,1024]{3,2,1,0:T(8,128)S(1)} %convert_element_type.357) | copy-start | bytes 6291460
  257.8 52.1 %copy-start.72 = (f32[256]{0:T(256)}, f32[256]{0:T(256)S(1)}, u32[]{:S(2)}) copy-start(f32[256]{0:T(256)S(1)} %get-tuple-element.646) | copy-start | bytes 3076
  257.8 52.1 %copy-start.74 = (f32[256]{0:T(256)}, f32[256]{0:T(256)S(1)}, u32[]{:S(2)}) copy-start(f32[256]{0:T(256)S(1)} %get-tuple-element.647) | copy-start | bytes 3076
  311.2 126.4 %all-gather.16.cloned.1.call-start = ((), (), s32[]{:S(2)}) async-start(), calls=%async_computation.15 | async-start | bytes 2621440 | tf_op jit(solution)/shard_map/forward/all_gather | solution.py:105
  370.1 82.8 %all-to-all-start.7 = ((bf16[1,4,256,1024]{3,2,0,1:T(8,128)(2,1)}), bf16[1,4,256,1024]{3,2,0,1:T(8,128)(2,1)}, u32[]{:S(2)}, u32[]{:S(2)}) async-start(bf16[1,4,256,1024]{3,2,0,1:T(8,128)(2,1)} %bitcast.687), calls=%async_computation.7 | async-start | bytes 4194304 | tf_op jit(solution)/shard_map/backward_ffn/all_to_all | solution.py:111
  452.8 50.7 %all-to-all-start.5 = ((bf16[1,4,256,1024]{3,2,0,1:T(8,128)(2,1)}), bf16[1,4,256,1024]{3,2,0,1:T(8,128)(2,1)}, u32[]{:S(2)}, u32[]{:S(2)}) async-start(bf16[1,4,256,1024]{3,2,0,1:T(8,128)(2,1)} %bitcast.689), calls=%async_computation.5 | async-start | bytes 4194304 | tf_op jit(solution)/shard_map/backward_ffn/all_to_all | solution.py:111
  464.2 43.9 %copy-start.40 = (bf16[2,1,256,1024]{3,2,1,0:T(8,128)(2,1)S(1)}, bf16[2,1,256,1024]{3,2,1,0:T(8,128)(2,1)}, u32[]{:S(2)}) copy-start(bf16[2,1,256,1024]{3,2,1,0:T(8,128)(2,1)} %param.17) | copy-start | bytes 3145732
  503.5 52.5 %all-to-all-start.4 = ((bf16[1,4,256,1024]{3,2,0,1:T(8,128)(2,1)}), bf16[1,4,256,1024]{3,2,0,1:T(8,128)(2,1)}, u32[]{:S(2)}, u32[]{:S(2)}) async-start(bf16[1,4,256,1024]{3,2,0,1:T(8,128)(2,1)} %bitcast.688), calls=%async_computation.4 | async-start | bytes 4194304 | tf_op jit(solution)/shard_map/forward/all_to_all | solution.py:111
  556.0 85.9 %all-to-all-start.2 = ((bf16[1,4,256,1024]{3,2,0,1:T(8,128)(2,1)}), bf16[1,4,256,1024]{3,2,0,1:T(8,128)(2,1)}, u32[]{:S(2)}, u32[]{:S(2)}) async-start(bf16[1,4,256,1024]{3,2,0,1:T(8,128)(2,1)} %bitcast.686), calls=%async_computation.2 | async-start | bytes 4194304 | tf_op jit(solution)/shard_map/forward/all_to_all | solution.py:111
  560.4 111.0 %all-gather.26.cloned.1.call-start = ((), (), s32[]{:S(2)}) async-start(), calls=%async_computation.20 | async-start | bytes 2621440 | tf_op jit(solution)/shard_map/backward_attention/all_gather | solution.py:105
  568.0 208.8 %all-gather.24.cloned.1.call-start = ((), (), s32[]{:S(2)}) async-start(), calls=%async_computation.19 | async-start | bytes 2621440 | tf_op jit(solution)/shard_map/backward_attention/all_gather | solution.py:105
  649.3 269.7 %reduce-scatter.11.cloned.1.call-start = ((), (), s32[]{:S(2)}) async-start(), calls=%async_computation.24 | async-start | bytes 2359296 | tf_op jit(solution)/shard_map/weight_grads/reduce_scatter | solution.py:321
  663.1 257.8 %reduce-scatter.9.cloned.1.call-start = ((), (), s32[]{:S(2)}) async-start(), calls=%async_computation.23 | async-start | bytes 2359296 | tf_op jit(solution)/shard_map/weight_grads/reduce_scatter | solution.py:321
  771.3 8.9 collective-permute-start.6
  773.8 7.5 collective-permute-start.7
  788.1 120.2 %all-to-all-start.8 = ((bf16[1,4,256,1024]{3,2,0,1:T(8,128)(2,1)}), bf16[1,4,256,1024]{3,2,0,1:T(8,128)(2,1)}, u32[]{:S(2)}, u32[]{:S(2)}) async-start(bf16[1,4,256,1024]{3,2,0,1:T(8,128)(2,1)} %bitcast.685), calls=%async_computation.8 | async-start | bytes 4194304 | tf_op jit(solution)/shard_map/backward_attention/all_to_all | solution.py:111
  792.8 140.3 %reduce-scatter.7.cloned.1.call-start = ((), (), s32[]{:S(2)}) async-start(), calls=%async_computation.22 | async-start | bytes 589824 | tf_op jit(solution)/shard_map/weight_grads/reduce_scatter | solution.py:321
  882.7 14.7 %collective-permute-start.4 = (bf16[1,1024,256]{2,1,0:T(8,128)(2,1)}, bf16[1,1024,256]{2,1,0:T(8,128)(2,1)}, u32[]{:S(2)}, u32[]{:S(2)}) collective-permute-start(bf16[1,1024,256]{2,1,0:T(8,128)(2,1)} %copy.340), channel_id=1, source_target_pairs={{0,4},{4,0},{1,5},{5,1},{2,6},{6,2},{3,7},{7,3},{8,12},{12,8},{9,1... | collective-permute-start | bytes 1572872 | tf_op jit(solution)/shard_map/backward_attention/ppermute | solution.py:96
  886.3 12.3 %collective-permute-start.5 = (bf16[1,1024,256]{2,1,0:T(8,128)(2,1)}, bf16[1,1024,256]{2,1,0:T(8,128)(2,1)}, u32[]{:S(2)}, u32[]{:S(2)}) collective-permute-start(bf16[1,1024,256]{2,1,0:T(8,128)(2,1)} %copy.342), channel_id=1, source_target_pairs={{0,4},{4,0},{1,5},{5,1},{2,6},{6,2},{3,7},{7,3},{8,12},{12,8},{9,1... | collective-permute-start | bytes 1572872 | tf_op jit(solution)/shard_map/backward_attention/ppermute | solution.py:96
  908.3 71.3 %all-to-all-start.6 = ((bf16[1,4,256,1024]{3,2,0,1:T(8,128)(2,1)}), bf16[1,4,256,1024]{3,2,0,1:T(8,128)(2,1)}, u32[]{:S(2)}, u32[]{:S(2)}) async-start(bf16[1,4,256,1024]{3,2,0,1:T(8,128)(2,1)} %bitcast.93), calls=%async_computation.6 | async-start | bytes 4194304 | tf_op jit(solution)/shard_map/backward_attention/all_to_all | solution.py:111
  913.4 61.3 %reduce-scatter.5.cloned.1.call-start = ((), (), s32[]{:S(2)}) async-start(), calls=%async_computation.21 | async-start | bytes 1769472 | tf_op jit(solution)/shard_map/weight_grads/reduce_scatter | solution.py:321
  919.0 60.4 %copy-start.69 = (f32[1,1,1,1024]{3,1,2,0:T(1,128)S(1)}, f32[1,1,1,1024]{3,1,2,0:T(1,128)}, u32[]{:S(2)}) copy-start(f32[1,1,1,1024]{3,1,2,0:T(1,128)} %get-tuple-element.633) | copy-start | bytes 12292
  919.0 63.5 %copy-start.84 = (f32[256]{0:T(256)}, f32[256]{0:T(256)S(1)}, u32[]{:S(2)}) copy-start(f32[256]{0:T(256)S(1)} %add_rsqrt_fusion.2) | copy-start | bytes 3076
  919.0 63.4 %copy-start.85 = (f32[256]{0:T(256)}, f32[256]{0:T(256)S(1)}, u32[]{:S(2)}) copy-start(f32[256]{0:T(256)S(1)} %add_rsqrt_fusion.3) | copy-start | bytes 3076
  923.7 58.6 %copy-start.70 = (f32[1,1,1,1024]{3,1,2,0:T(1,128)S(1)}, f32[1,1,1,1024]{3,1,2,0:T(1,128)}, u32[]{:S(2)}) copy-start(f32[1,1,1,1024]{3,1,2,0:T(1,128)} %get-tuple-element.629) | copy-start | bytes 12292
  989.1 10.4 %all-to-all-start.9 = ((f32[4,1,3072]{2,1,0:T(1,128)}), f32[4,1,3072]{2,1,0:T(1,128)}, u32[]{:S(2)}, u32[]{:S(2)}) async-start(f32[4,1,3072]{2,1,0:T(1,128)} %reshape.1457), calls=%async_computation.13 | async-start | bytes 98304 | tf_op jit(solution)/shard_map/ada_grad/all_to_all | solution.py:307
  993.7 20.9 %copy-start.1 = (bf16[128,6,256]{2,0,1:T(8,128)(2,1)S(1)}, bf16[128,6,256]{2,0,1:T(8,128)(2,1)}, u32[]{:S(2)}) copy-start(bf16[128,6,256]{2,0,1:T(8,128)(2,1)} %param.23) | copy-start | bytes 1179652
  996.3 16.8 %copy-start.68 = (bf16[8,2,4,128]{3,0,2,1:T(8,128)(2,1)S(1)}, bf16[8,2,4,128]{3,0,2,1:T(8,128)(2,1)}, u32[]{:S(2)}) copy-start(bf16[8,2,4,128]{3,0,2,1:T(8,128)(2,1)} %copy-done.67) | copy-start | bytes 49156
  (85 other events, 504.9 us)
Sparse Core Ops, SparseCore 0:
  9.6 87.6 all-gather.27
  99.7 24.2 all-gather.13
  125.6 119.1 all-gather.29
  246.5 26.3 all-gather.19
  274.6 27.7 all-gather.17
  311.3 44.8 all-gather.21
  358.4 79.1 all-gather.15
  568.1 74.0 all-gather.25
  649.5 43.9 all-gather.23
  696.6 39.9 reduce-scatter.10
  739.8 41.1 reduce-scatter.8
  897.5 35.5 reduce-scatter.6
  936.4 38.3 reduce-scatter.4

commit v5 on v4

--- a/solution.py
+++ b/solution.py
@@ -1,8 +1,11 @@
+import functools
 import math
 
 import jax
 import jax.numpy as jnp
 from jax import lax
+from jax.experimental import pallas as pl
+from jax.experimental.pallas import tpu as pltpu
 from jax.sharding import PartitionSpec as P
 
 HEAD_DIM = 64
@@ -30,6 +33,117 @@
     frequency = jnp.exp(-math.log(10000.0) * jnp.arange(halfway, dtype=jnp.float32) / halfway)
     angles = levels.astype(jnp.float32)[..., None] * frequency
     return jnp.concatenate([jnp.cos(angles), jnp.sin(angles)], axis=-1)
+
+
+def _nt(a, b):
+    return lax.dot_general(a, b, (((1,), (1,)), ((), ())), preferred_element_type=jnp.float32)
+
+
+def _tn(a, b):
+    return lax.dot_general(a, b, (((0,), (0,)), ((), ())), preferred_element_type=jnp.float32)
+
+
+def _forward_kernel(heads, scaling, q_ref, k_ref, v_ref, o_ref, lse_ref):
+    for h in range(heads):
+        cols = slice(h * HEAD_DIM, (h + 1) * HEAD_DIM)
+        scores = _nt(q_ref[:, cols], k_ref[:, cols]) * scaling
+        largest = jnp.max(scores, axis=1, keepdims=True)
+        raised = jnp.exp(scores - largest)
+        total = jnp.sum(raised, axis=1, keepdims=True)
+        probs_low = (raised / total).astype(jnp.bfloat16)
+        out = jnp.dot(probs_low, v_ref[:, cols], preferred_element_type=jnp.float32)
+        o_ref[:, cols] = out.astype(o_ref.dtype)
+        lse_ref[:, h : h + 1] = largest + jnp.log(total)
+
+
+def _backward_kernel(heads, scaling, q_ref, k_ref, v_ref, g_ref, lse_ref, dq_ref, dk_ref, dv_ref):
+    @pl.when(pl.program_id(0) == 0)
+    def _():
+        dk_ref[...] = jnp.zeros_like(dk_ref)
+        dv_ref[...] = jnp.zeros_like(dv_ref)
+
+    for h in range(heads):
+        cols = slice(h * HEAD_DIM, (h + 1) * HEAD_DIM)
+        q = q_ref[:, cols]
+        g = g_ref[:, cols]
+        scores = _nt(q, k_ref[:, cols]) * scaling
+        probs = jnp.exp(scores - lse_ref[:, h : h + 1])
+        grad_probs = _nt(g, v_ref[:, cols])
+        dv_ref[:, cols] += _tn(probs.astype(jnp.bfloat16), g)
+        row_terms = jnp.sum(probs * grad_probs, axis=1, keepdims=True)
+        grad_scores = (probs * (grad_probs - row_terms)).astype(jnp.bfloat16)
+        dq_ref[:, cols] = jnp.dot(grad_scores, k_ref[:, cols], preferred_element_type=jnp.float32) * scaling
+        dk_ref[:, cols] += _tn(grad_scores, q) * scaling
+
+
+def attention_forward(queries, keys, values, block_rows=256):
+    rows, width = queries.shape
+    length = keys.shape[0]
+    heads = width // HEAD_DIM
+    block_rows = min(block_rows, rows)
+    flops = 4 * rows * length * width
+    return pl.pallas_call(
+        functools.partial(_forward_kernel, heads, HEAD_DIM ** (-0.5)),
+        out_shape=(
+            jax.ShapeDtypeStruct((rows, width), jnp.bfloat16),
+            jax.ShapeDtypeStruct((rows, heads), jnp.float32),
+        ),
+        grid=(rows // block_rows,),
+        in_specs=[
+            pl.BlockSpec((block_rows, width), lambda i: (i, 0)),
+            pl.BlockSpec((length, width), lambda i: (0, 0)),
+            pl.BlockSpec((length, width), lambda i: (0, 0)),
+        ],
+        out_specs=[
+            pl.BlockSpec((block_rows, width), lambda i: (i, 0)),
+            pl.BlockSpec((block_rows, heads), lambda i: (i, 0)),
+        ],
+        compiler_params=pltpu.CompilerParams(
+            dimension_semantics=("arbitrary",), vmem_limit_bytes=56 * 1024 * 1024
+        ),
+        cost_estimate=pl.CostEstimate(
+            flops=flops,
+            transcendentals=rows * length * heads,
+            bytes_accessed=2 * (2 * rows * width + 2 * length * width),
+        ),
+    )(queries, keys, values)
+
+
+def attention_backward(queries, keys, values, grad_out, lse, block_rows=256):
+    rows, width = queries.shape
+    length = keys.shape[0]
+    heads = width // HEAD_DIM
+    block_rows = min(block_rows, rows)
+    flops = 10 * rows * length * width
+    return pl.pallas_call(
+        functools.partial(_backward_kernel, heads, HEAD_DIM ** (-0.5)),
+        out_shape=(
+            jax.ShapeDtypeStruct((rows, width), jnp.float32),
+            jax.ShapeDtypeStruct((length, width), jnp.float32),
+            jax.ShapeDtypeStruct((length, width), jnp.float32),
+        ),
+        grid=(rows // block_rows,),
+        in_specs=[
+            pl.BlockSpec((block_rows, width), lambda i: (i, 0)),
+            pl.BlockSpec((length, width), lambda i: (0, 0)),
+            pl.BlockSpec((length, width), lambda i: (0, 0)),
+            pl.BlockSpec((block_rows, width), lambda i: (i, 0)),
+            pl.BlockSpec((block_rows, heads), lambda i: (i, 0)),
+        ],
+        out_specs=[
+            pl.BlockSpec((block_rows, width), lambda i: (i, 0)),
+            pl.BlockSpec((length, width), lambda i: (0, 0)),
+            pl.BlockSpec((length, width), lambda i: (0, 0)),
+        ],
+        compiler_params=pltpu.CompilerParams(
+            dimension_semantics=("arbitrary",), vmem_limit_bytes=56 * 1024 * 1024
+        ),
+        cost_estimate=pl.CostEstimate(
+            flops=flops,
+            transcendentals=rows * length * heads,
+            bytes_accessed=2 * (3 * rows * width + 2 * length * width) + 4 * (rows + 2 * length) * width,
+        ),
+    )(queries, keys, values, grad_out, lse)
 
 
 def gelu_tanh(values):
@@ -128,32 +242,8 @@
             queries = projected[:, :, 0]
             keys_all = gather_halves(projected[:, :, 1])
             values_all = gather_halves(projected[:, :, 2])
-            key_heads = keys_all.reshape(clips, -1, heads_here, HEAD_DIM)
-            value_heads = values_all.reshape(clips, -1, heads_here, HEAD_DIM)
-            block_rows = min(512, token_count)
-            block_count = token_count // block_rows
-            query_blocks = jnp.moveaxis(
-                queries.reshape(clips, block_count, block_rows, heads_here, HEAD_DIM), 1, 0
-            )
-
-            def attend(query_block):
-                scores = (
-                    jnp.einsum(
-                        "cqhe,ckhe->chqk", query_block, key_heads, preferred_element_type=jnp.float32
-                    )
-                    * scaling
-                )
-                largest = jnp.max(scores, axis=-1, keepdims=True)
-                raised = jnp.exp(scores - largest)
-                totals_row = jnp.sum(raised, axis=-1, keepdims=True)
-                probs_low = (raised / totals_row).astype(jnp.bfloat16)
-                outputs = jnp.einsum(
-                    "chqk,ckhe->cqhe", probs_low, value_heads, preferred_element_type=jnp.float32
-                )
-                return (outputs.astype(jnp.bfloat16), (largest + jnp.log(totals_row))[..., 0])
-
-            attended_blocks, log_totals = lax.map(attend, query_blocks)
-            attended = jnp.moveaxis(attended_blocks, 0, 1).reshape(clips, token_count, local_width)
+            attended, log_totals = attention_forward(queries[0], keys_all[0], values_all[0])
+            attended = attended[None]
             partial_one = jnp.einsum(
                 "crh,oh->cro", attended, mixer_weight, preferred_element_type=jnp.float32
             )
@@ -213,51 +303,12 @@
             mixer_total = jnp.einsum(
                 "cro,crh->oh", grad_one_all, attended, preferred_element_type=jnp.float32
             )
-            grad_blocks = jnp.moveaxis(
-                grad_attended.reshape(clips, block_count, block_rows, heads_here, HEAD_DIM), 1, 0
-            )
-
-            def attend_back(carried, pieces):
-                key_sum, value_sum = carried
-                query_block, grad_block, log_block = pieces
-                scores = (
-                    jnp.einsum(
-                        "cqhe,ckhe->chqk", query_block, key_heads, preferred_element_type=jnp.float32
-                    )
-                    * scaling
-                )
-                probs = jnp.exp(scores - log_block[..., None])
-                grad_probs = jnp.einsum(
-                    "cqhe,ckhe->chqk", grad_block, value_heads, preferred_element_type=jnp.float32
-                )
-                value_sum = value_sum + jnp.einsum(
-                    "chqk,cqhe->ckhe",
-                    probs.astype(jnp.bfloat16),
-                    grad_block,
-                    preferred_element_type=jnp.float32,
-                )
-                row_terms = jnp.sum(probs * grad_probs, axis=-1, keepdims=True)
-                grad_scores = (probs * (grad_probs - row_terms)).astype(jnp.bfloat16)
-                grad_queries = (
-                    jnp.einsum(
-                        "chqk,ckhe->cqhe", grad_scores, key_heads, preferred_element_type=jnp.float32
-                    )
-                    * scaling
-                )
-                key_sum = (
-                    key_sum
-                    + jnp.einsum(
-                        "chqk,cqhe->ckhe", grad_scores, query_block, preferred_element_type=jnp.float32
-                    )
-                    * scaling
-                )
-                return ((key_sum, value_sum), grad_queries)
-
-            zeros_keys = jnp.zeros(key_heads.shape, jnp.float32)
-            (key_grads, value_grads), query_grads = lax.scan(
-                attend_back, (zeros_keys, zeros_keys), (query_blocks, grad_blocks, log_totals)
-            )
-            query_grads = jnp.moveaxis(query_grads, 0, 1).reshape(clips, token_count, local_width)
+            query_grads, key_grads, value_grads = attention_backward(
+                queries[0], keys_all[0], values_all[0], grad_attended[0], log_totals
+            )
+            query_grads = query_grads[None]
+            key_grads = key_grads[None]
+            value_grads = value_grads[None]
             key_own, value_own = (
                 scatter_halves(grads.reshape(clips, -1, local_width))
                 for grads in (key_grads, value_grads)

time: 1030 us -> 914 us (0.89)
  matrix products: 264 us -> 110 us
  Pallas kernels: 0 us -> 107 us
  other arithmetic: 141 us -> 74.9 us
  local copies, waits for them, and re-layouts: 67.7 us -> 30.3 us
  waiting for transfers between devices: 431 us -> 467 us
    dot_general x28 -> x0, matrix products: 152 us -> none  [the longest x4 34.3 us: attend_back(): jnp.einsum('cqhe,ckhe->chqk', grad_block, value_heads, preferred_element_...]
    pallas_call x0 -> x4, Pallas kernels: none -> 107 us  [the longest x2 64.7 us: attention_backward(): pl.pallas_call(functools.partial(_backward_kernel, heads, HEAD_DIM ** (-0...]
    all_to_all x8, waiting for transfers between devices: 237 us -> 327 us  [scatter_tokens(): received = lax.all_to_all(parts, 'tensor', 1, 1, tiled=True)]
    all_gather x4, waiting for transfers between devices: 86.4 us -> 34 us  [gather_tokens(): return lax.all_gather(values, 'tensor', axis=1, tiled=True)]
    convert_element_type x4 -> x0, other arithmetic: 41.9 us -> none  [attend_back(): grad_scores = (probs * (grad_probs - row_terms)).astype(jnp.bfloat16)]
    while x20 -> x0, local copies, waits for them, and re-layouts: 14.1 us -> none
    reduce_scatter x4, waiting for transfers between devices: 49.6 us -> 35.6 us  [on_device(): lax.psum_scatter(total.astype(jnp.bfloat16), ('dp', 'frame'), scatter_dim...]
    reduce_sum x4 -> x0, other arithmetic: 13.1 us -> none  [attend(): totals_row = jnp.sum(raised, axis=-1, keepdims=True)]
  transfers between devices with their start and end apart: 31 -> 30, of which waited for: 12 -> 13; matrix products, arithmetic and copies ran while one was open for 43% -> 19% of each run, Pallas kernels for 0% -> 12%
where the time goes in v5:
time: 914 us; the launch traced here: 907 us
  waiting for transfers between devices  467 us (51%)
  matrix products  110 us (12%)
  Pallas kernels  107 us (12%)
  other arithmetic  74.9 us (8%)
  blocking collectives  58.1 us (6%)
  starting transfers between devices  44.5 us (5%)
  local copies, waits for them, and re-layouts  30.3 us (3%)
  between operations  15.5 us (2%)
    all_to_all x8, waiting for transfers between devices, scatter_tokens(): received = lax.all_to_all(parts, 'tensor', 1, 1, tiled=True)  327 us
    pallas_call x2, Pallas kernels, attention_backward(): pl.pallas_call(functools.partial(_backward_kernel, heads, HEAD_DIM ** (-0...  64.7 us
    all_gather x1, waiting for transfers between devices, on_device(): group_tokens = lax.all_gather(tokens[:, 0], 'tensor', axis=1, tiled=True)  47.6 us
    pallas_call x2, Pallas kernels, attention_forward(): pl.pallas_call(functools.partial(_forward_kernel, heads, HEAD_DIM ** (-0....  42.3 us
    reduce_scatter x4, waiting for transfers between devices, on_device(): lax.psum_scatter(total.astype(jnp.bfloat16), ('dp', 'frame'), scatter_dim...  35.6 us
    all_to_all x8, starting transfers between devices, scatter_tokens(): received = lax.all_to_all(parts, 'tensor', 1, 1, tiled=True)  35.5 us
    all_gather x4, waiting for transfers between devices, gather_tokens(): return lax.all_gather(values, 'tensor', axis=1, tiled=True)  34 us
    dot_general x2, matrix products, clip_pass(): jnp.einsum('crd,df->crf', flat_two, upward_weight, preferred_element_type...  19.9 us
  transfers between devices with their start and end apart: 30, of which 13 were waited for; matrix products, arithmetic and copies ran while one was open for 19% of the time, Pallas kernels for 12%

profile of v5, /device:TPU:0, one launch (start us, length us, event | category | flops | bytes accessed | tf_op | source)
XLA Modules:
  0.0 906.7 jit_solution(12265367591908184428)
XLA Ops:
  9.4 10.4 %all-gather.3 = s32[8,2,4]{2,1,0:T(2,128)S(1)} all-gather(s32[1,2,4]{2,1,0:T(2,128)S(1)} %bitcast.497), channel_id=1, replica_groups=mesh['dp'=4,'frame'=2,'tensor'=4] {'dp','frame'}, dimensions={0}, use_global_device_ids=true | all-gather | bytes 288 | tf_op jit(solution)/shard_map/modulation/all_gather | solution.py:168
  21.1 10.9 %all_to_all.63 = f32[8,2,4,6,256]{4,2,3,1,0:T(4,128)S(1)} all-to-all(f32[8,2,4,6,256]{4,2,3,1,0:T(4,128)S(1)} %fusion.93), channel_id=1, replica_groups=mesh['dp'=4,'frame'=2,'tensor'=4] {'dp','frame'}, dimensions={0} | all-to-all | bytes 786432 | tf_op jit(solution)/shard_map/modulation/all_to_all | solution.py:179
  32.1 17.3 %all_gather.40 = f32[2,4,6,1024]{3,2,1,0:T(8,128)S(1)} all-gather(f32[2,4,6,256]{3,2,1,0:T(8,128)S(1)} %copy.137), channel_id=1, replica_groups=mesh['dp'=4,'frame'=2,'tensor'=4] {'tensor'}, dimensions={3}, use_global_device_ids=true | all-gather | bytes 245760 | tf_op jit(solution)/shard_map/modulation/all_gather | solution.py:181
  49.6 47.6 %all-gather.28.cloned.1.call-done = bf16[2,1,1024,1024]{3,2,1,0:T(8,128)(2,1)} async-done(((bf16[2,1,256,1024]{3,2,1,0:T(8,128)(2,1)}), bf16[2,1,1024,1024]{3,2,1,0:T(8,128)(2,1)}) %all-gather.28.cloned.1.call-update) | async-done | bytes 4194320 | tf_op jit(solution)/shard_map/group_inputs/all_gather | solution.py:195
  107.3 15.9 %all-gather.14.cloned.1.call-done = bf16[1024,3,256]{2,0,1:T(8,128)(2,1)} async-done(((bf16[128,3,256]{2,0,1:T(8,128)(2,1)}), bf16[1024,3,256]{2,0,1:T(8,128)(2,1)}) %all-gather.14.cloned.1.call-update) | async-done | bytes 1572880 | tf_op jit(solution)/shard_map/weights/all_gather | solution.py:188
  123.2 3.2 fusion.59
  127.8 10.0 %all_gather.43 = bf16[1024,256]{1,0:T(8,128)(2,1)S(1)} all-gather(bf16[128,256]{1,0:T(8,128)(2,1)S(1)} %copy-done.47), channel_id=1, replica_groups=mesh['dp'=4,'frame'=2,'tensor'=4] {'dp','frame'}, dimensions={0}, use_global_device_ids=true | all-gather | bytes 589824 | tf_op jit(solution)/shard_map/weights/all_gather | solution.py:188
  140.0 21.1 %forward.3 = (bf16[1024,256]{1,0:T(8,128)(2,1)}, f32[1024,4]{1,0:T(8,128)}) custom-call(bf16[1024,256]{1,0:T(8,128)(2,1)} %get-tuple-element.83.q_ref, bf16[2048,256]{1,0:T(8,128)(2,1)} %maximum_bitcast_fusion.2.k_ref, bf16[2048,256]{1,0:T(8,128)(2,1)} %maximum_bitcast_fusion.3.v_ref), custom_call_target="tpu_custom_call" | custom-call | flops 2147483648 | bytes 3145728 | tf_op jit(solution)/shard_map/forward/pallas_call | solution.py:85
  164.3 4.6 all-to-all-start.3
  169.5 3.8 fusion.58
  178.2 21.1 %forward.2 = (bf16[1024,256]{1,0:T(8,128)(2,1)}, f32[1024,4]{1,0:T(8,128)}) custom-call(bf16[1024,256]{1,0:T(8,128)(2,1)} %get-tuple-element.80.q_ref, bf16[2048,256]{1,0:T(8,128)(2,1)} %maximum_bitcast_fusion.k_ref, bf16[2048,256]{1,0:T(8,128)(2,1)} %maximum_bitcast_fusion.1.v_ref), custom_call_target="tpu_custom_call" | custom-call | flops 2147483648 | bytes 3145728 | tf_op jit(solution)/shard_map/forward/pallas_call | solution.py:85
  202.5 47.4 %all-to-all-done.3 = bf16[1,4,256,1024]{3,2,0,1:T(8,128)(2,1)S(1)} async-done(((bf16[1,4,256,1024]{3,2,0,1:T(8,128)(2,1)}), bf16[1,4,256,1024]{3,2,0,1:T(8,128)(2,1)S(1)}, u32[]{:S(2)}, u32[]{:S(2)}) %all-to-all-start.3) | async-done | bytes 2097184 | tf_op jit(solution)/shard_map/forward/all_to_all | solution.py:225
  251.3 4.5 all-to-all-start.1
  262.1 42.5 %all-to-all-done.1 = bf16[1,4,256,1024]{3,2,0,1:T(8,128)(2,1)} async-done(((bf16[1,4,256,1024]{3,2,0,1:T(8,128)(2,1)}), bf16[1,4,256,1024]{3,2,0,1:T(8,128)(2,1)}, u32[]{:S(2)}, u32[]{:S(2)}) %all-to-all-start.1) | async-done | bytes 2097184 | tf_op jit(solution)/shard_map/forward/all_to_all | solution.py:225
  309.7 4.8 fusion.17
  314.5 6.0 fusion.115
  320.6 34.0 %all-gather.22.cloned.1.call-done = bf16[1,1024,1024]{2,1,0:T(8,128)(2,1)} async-done(((bf16[1,256,1024]{2,1,0:T(8,128)(2,1)}), bf16[1,1024,1024]{2,1,0:T(8,128)(2,1)}) %all-gather.22.cloned.1.call-update) | async-done | bytes 2097168 | tf_op jit(solution)/shard_map/forward/all_gather | solution.py:219
  354.5 9.9 %fusion.35 = (bf16[1024,1024]{1,0:T(8,128)(2,1)S(1)}, f32[1024,1024]{1,0:T(8,128)}) fusion(f32[1024,1024]{1,0:T(8,128)} %fusion.115, bf16[1024,1024]{1,0:T(8,128)(2,1)} %all-gather.18.cloned.1.call-done, bf16[1,1024,1024]{2,1,0:T(8,128)(2,1)} %all-gather.22.cloned.1.call-done), kind=kOutput, calls=%fused_computation.55 | convolution fusion | flops 2168455168 | bytes 14680064 | tf_op jit(solution)/shard_map/forward/crd,df->crf/dot_general | solution.py:255
  364.4 3.8 convolution_convert_fusion
  368.2 4.6 all-to-all-start.7
  374.4 6.9 convolution_convert_fusion.2
  381.3 73.5 %all-to-all-done.7 = bf16[1,4,256,1024]{3,2,0,1:T(8,128)(2,1)} async-done(((bf16[1,4,256,1024]{3,2,0,1:T(8,128)(2,1)}), bf16[1,4,256,1024]{3,2,0,1:T(8,128)(2,1)}, u32[]{:S(2)}, u32[]{:S(2)}) %all-to-all-start.7) | async-done | bytes 2097184 | tf_op jit(solution)/shard_map/backward_ffn/all_to_all | solution.py:225
  454.8 4.5 all-to-all-start.4
  459.3 6.6 fusion.114
  465.9 10.1 %fusion.28 = (bf16[1024,1024]{1,0:T(8,128)(2,1)S(1)}, f32[1024,1024]{1,0:T(8,128)}) fusion(f32[1024,1024]{1,0:T(8,128)} %fusion.114, bf16[1024,1024]{1,0:T(8,128)(2,1)} %all-gather.18.cloned.1.call-done, bf16[1,1024,1024]{2,1,0:T(8,128)(2,1)} %all-gather.16.cloned.1.call-done), kind=kOutput, calls=%fused_computation.48 | convolution fusion | flops 2168455168 | bytes 14680064 | tf_op jit(solution)/shard_map/forward/crd,df->crf/dot_general | solution.py:255
  477.2 3.8 convolution_convert_fusion.1
  481.0 26.1 %all-to-all-done.4 = bf16[1,4,256,1024]{3,2,0,1:T(8,128)(2,1)} async-done(((bf16[1,4,256,1024]{3,2,0,1:T(8,128)(2,1)}), bf16[1,4,256,1024]{3,2,0,1:T(8,128)(2,1)}, u32[]{:S(2)}, u32[]{:S(2)}) %all-to-all-start.4) | async-done | bytes 2097184 | tf_op jit(solution)/shard_map/forward/all_to_all | solution.py:225
  507.1 4.8 all-to-all-start.5
  514.3 6.2 convolution_convert_fusion.4
  520.4 39.3 %all-to-all-done.5 = bf16[1,4,256,1024]{3,2,0,1:T(8,128)(2,1)} async-done(((bf16[1,4,256,1024]{3,2,0,1:T(8,128)(2,1)}), bf16[1,4,256,1024]{3,2,0,1:T(8,128)(2,1)}, u32[]{:S(2)}, u32[]{:S(2)}) %all-to-all-start.5) | async-done | bytes 2097184 | tf_op jit(solution)/shard_map/backward_ffn/all_to_all | solution.py:225
  559.7 4.5 all-to-all-start.2
  577.1 68.6 %all-to-all-done.2 = bf16[1,4,256,1024]{3,2,0,1:T(8,128)(2,1)} async-done(((bf16[1,4,256,1024]{3,2,0,1:T(8,128)(2,1)}), bf16[1,4,256,1024]{3,2,0,1:T(8,128)(2,1)}, u32[]{:S(2)}, u32[]{:S(2)}) %all-to-all-start.2) | async-done | bytes 2097184 | tf_op jit(solution)/shard_map/forward/all_to_all | solution.py:225
  657.2 5.2 fusion.107
  662.4 4.1 add_convert_fusion
  668.1 4.2 fusion.48
  672.3 3.9 add_convert_fusion.1
  680.4 32.3 %backward_attention.3 = (f32[1024,256]{1,0:T(8,128)}, f32[2048,256]{1,0:T(8,128)}, f32[2048,256]{1,0:T(8,128)}) custom-call(bf16[1024,256]{1,0:T(8,128)(2,1)} %get-tuple-element.83.q_ref, bf16[2048,256]{1,0:T(8,128)(2,1)} %maximum_bitcast_fusion.2.k_ref, bf16[2048,256]{1,0:T(8,128)(2,1)} %maximum_bitcast_fusion.3.v_ref, bf16[1024,256]{1,0:T(8,128)(2,1)} %fusion.66.g_ref, ...), custom_call_target="tpu_custom_call" | custom-call | flops 5368709120 | bytes 8912896 | tf_op jit(solution)/shard_map/backward_attention/pallas_call | solution.py:118
  720.0 32.4 %backward_attention.2 = (f32[1024,256]{1,0:T(8,128)}, f32[2048,256]{1,0:T(8,128)}, f32[2048,256]{1,0:T(8,128)}) custom-call(bf16[1024,256]{1,0:T(8,128)(2,1)} %get-tuple-element.80.q_ref, bf16[2048,256]{1,0:T(8,128)(2,1)} %maximum_bitcast_fusion.k_ref, bf16[2048,256]{1,0:T(8,128)(2,1)} %maximum_bitcast_fusion.1.v_ref, bf16[1024,256]{1,0:T(8,128)(2,1)} %fusion.63.g_ref, ...), custom_call_target="tpu_custom_call" | custom-call | flops 5368709120 | bytes 8912896 | tf_op jit(solution)/shard_map/backward_attention/pallas_call | solution.py:118
  754.5 3.2 bitcast_convert_fusion
  757.7 3.6 all-to-all-start.8
  773.7 3.5 fusion.88
  780.4 29.4 %all-to-all-done.8 = bf16[1,4,256,1024]{3,2,0,1:T(8,128)(2,1)S(1)} async-done(((bf16[1,4,256,1024]{3,2,0,1:T(8,128)(2,1)}), bf16[1,4,256,1024]{3,2,0,1:T(8,128)(2,1)S(1)}, u32[]{:S(2)}, u32[]{:S(2)}) %all-to-all-start.8) | async-done | bytes 2097184 | tf_op jit(solution)/shard_map/backward_attention/all_to_all | solution.py:225
  809.9 4.6 all-to-all-start.6
  814.9 5.8 add_convert_fusion.2
  826.9 35.6 %reduce-scatter.5.cloned.1.call-done = bf16[128,3,256]{2,0,1:T(8,128)(2,1)} async-done(((bf16[1024,3,256]{2,0,1:T(8,128)(2,1)}), bf16[128,3,256]{2,0,1:T(8,128)(2,1)}) %reduce-scatter.5.cloned.1.call-update) | async-done | bytes 196624 | tf_op jit(solution)/shard_map/weight_grads/reduce_scatter | solution.py:372
  870.7 3.4 reshape.1187
  874.1 4.6 all-to-all-start.9
  888.6 9.5 %all-gather.2 = f32[16,4,1,6,256]{4,1,0,3,2:T(4,128)S(1)} all-gather(f32[2,4,1,6,256]{4,1,0,3,2:T(4,128)S(1)} %bitcast.459), channel_id=4, replica_groups=mesh['dp'=4,'frame'=2,'tensor'=4] {'dp','frame'}, dimensions={0}, use_global_device_ids=true | all-gather | bytes 442368 | tf_op jit(solution)/shard_map/ada_grad/all_gather | solution.py:361
  (302 shorter events, 127.8 us)
Async XLA Ops:
  7.2 13.4 %copy-start = (bf16[128,6,256]{2,0,1:T(8,128)(2,1)S(1)}, bf16[128,6,256]{2,0,1:T(8,128)(2,1)}, u32[]{:S(2)}) copy-start(bf16[128,6,256]{2,0,1:T(8,128)(2,1)} %param.15) | copy-start | bytes 1179652
  7.2 90.0 %all-gather.28.cloned.1.call-start = ((), (), s32[]{:S(2)}) async-start(), calls=%async_computation.25 | async-start | bytes 5242880 | tf_op jit(solution)/shard_map/group_inputs/all_gather | solution.py:195
  7.9 115.3 %all-gather.14.cloned.1.call-start = ((), (), s32[]{:S(2)}) async-start(), calls=%async_computation.14 | async-start | bytes 1769472 | tf_op jit(solution)/shard_map/weights/all_gather | solution.py:188
  8.7 301.0 %all-gather.30.cloned.1.call-start = ((), (), s32[]{:S(2)}) async-start(), calls=%async_computation.26 | async-start | bytes 5242880 | tf_op jit(solution)/shard_map/group_inputs/all_gather | solution.py:196
  107.3 19.1 %copy-start.28 = (bf16[1024,1024,1]{1,0,2:T(8,128)(2,1)}, bf16[1024,1024,1]{1,0,2:T(8,128)(2,1)S(1)}, u32[]{:S(2)}) copy-start(bf16[1024,1024,1]{1,0,2:T(8,128)(2,1)S(1)} %get-tuple-element.68) | copy-start | bytes 6291460
  127.3 10.5 %collective-permute-start.3 = (bf16[1,1024,256]{2,1,0:T(8,128)(2,1)S(1)}, bf16[1,1024,256]{2,1,0:T(8,128)(2,1)S(1)}, u32[]{:S(2)}, u32[]{:S(2)}) collective-permute-start(bf16[1,1024,256]{2,1,0:T(8,128)(2,1)S(1)} %get-tuple-element.81), channel_id=1, source_target_pairs={{0,4},{4,0},{1,5},{5,1},{2,6},{6,2},{3,7},{7,3},{8,12},{12,8},{9,1... | collective-permute-start | bytes 1572872 | tf_op jit(solution)/shard_map/forward/ppermute | solution.py:200
  127.5 11.4 %collective-permute-start.2 = (bf16[1,1024,256]{2,1,0:T(8,128)(2,1)S(1)}, bf16[1,1024,256]{2,1,0:T(8,128)(2,1)S(1)}, u32[]{:S(2)}, u32[]{:S(2)}) collective-permute-start(bf16[1,1024,256]{2,1,0:T(8,128)(2,1)S(1)} %get-tuple-element.82), channel_id=1, source_target_pairs={{0,4},{4,0},{1,5},{5,1},{2,6},{6,2},{3,7},{7,3},{8,12},{12,8},{9,1... | collective-permute-start | bytes 1572872 | tf_op jit(solution)/shard_map/forward/ppermute | solution.py:200
  137.8 61.5 %copy-start.18 = (bf16[1024,256]{1,0:T(8,128)(2,1)}, bf16[1024,256]{1,0:T(8,128)(2,1)S(1)}, u32[]{:S(2)}) copy-start(bf16[1024,256]{1,0:T(8,128)(2,1)S(1)} %all_gather.43) | copy-start | bytes 1572868
  164.3 85.6 %all-to-all-start.3 = ((bf16[1,4,256,1024]{3,2,0,1:T(8,128)(2,1)}), bf16[1,4,256,1024]{3,2,0,1:T(8,128)(2,1)S(1)}, u32[]{:S(2)}, u32[]{:S(2)}) async-start(bf16[1,4,256,1024]{3,2,0,1:T(8,128)(2,1)} %bitcast.448), calls=%async_computation.3 | async-start | bytes 4194304 | tf_op jit(solution)/shard_map/forward/all_to_all | solution.py:225
  168.9 145.6 %all-gather.20.cloned.1.call-start = ((), (), s32[]{:S(2)}) async-start(), calls=%async_computation.17 | async-start | bytes 2359296 | tf_op jit(solution)/shard_map/weights/all_gather | solution.py:188
  174.2 1.9 collective-permute-start.1
  174.3 2.9 collective-permute-start
  251.3 53.3 %all-to-all-start.1 = ((bf16[1,4,256,1024]{3,2,0,1:T(8,128)(2,1)}), bf16[1,4,256,1024]{3,2,0,1:T(8,128)(2,1)}, u32[]{:S(2)}, u32[]{:S(2)}) async-start(bf16[1,4,256,1024]{3,2,0,1:T(8,128)(2,1)} %bitcast.447), calls=%async_computation.1 | async-start | bytes 4194304 | tf_op jit(solution)/shard_map/forward/all_to_all | solution.py:225
  255.7 64.8 %all-gather.18.cloned.1.call-start = ((), (), s32[]{:S(2)}) async-start(), calls=%async_computation.16 | async-start | bytes 2359296 | tf_op jit(solution)/shard_map/weights/all_gather | solution.py:188
  256.3 98.2 %all-gather.22.cloned.1.call-start = ((), (), s32[]{:S(2)}) async-start(), calls=%async_computation.18 | async-start | bytes 2621440 | tf_op jit(solution)/shard_map/forward/all_gather | solution.py:219
  258.3 48.4 %copy-start.2 = (f32[2,1,256,1024]{3,2,1,0:T(8,128)}, f32[2,1,256,1024]{3,2,1,0:T(8,128)S(1)}, u32[]{:S(2)}) copy-start(f32[2,1,256,1024]{3,2,1,0:T(8,128)S(1)} %convert_element_type.309) | copy-start | bytes 6291460
  258.5 48.2 %copy-start.48 = (f32[256]{0:T(256)}, f32[256]{0:T(256)S(1)}, u32[]{:S(2)}) copy-start(f32[256]{0:T(256)S(1)} %get-tuple-element.112) | copy-start | bytes 3076
  258.5 48.2 %copy-start.50 = (f32[256]{0:T(256)}, f32[256]{0:T(256)S(1)}, u32[]{:S(2)}) copy-start(f32[256]{0:T(256)S(1)} %get-tuple-element.113) | copy-start | bytes 3076
  320.6 43.9 %copy-start.57 = (bf16[1024,1024]{1,0:T(8,128)(2,1)S(1)}, bf16[1024,1024]{1,0:T(8,128)(2,1)}, u32[]{:S(2)}) copy-start(bf16[1024,1024]{1,0:T(8,128)(2,1)} %all-gather.18.cloned.1.call-done) | copy-start | bytes 6291460
  368.2 86.7 %all-to-all-start.7 = ((bf16[1,4,256,1024]{3,2,0,1:T(8,128)(2,1)}), bf16[1,4,256,1024]{3,2,0,1:T(8,128)(2,1)}, u32[]{:S(2)}, u32[]{:S(2)}) async-start(bf16[1,4,256,1024]{3,2,0,1:T(8,128)(2,1)} %bitcast.454), calls=%async_computation.7 | async-start | bytes 4194304 | tf_op jit(solution)/shard_map/backward_ffn/all_to_all | solution.py:225
  372.8 93.1 %all-gather.16.cloned.1.call-start = ((), (), s32[]{:S(2)}) async-start(), calls=%async_computation.15 | async-start | bytes 2621440 | tf_op jit(solution)/shard_map/forward/all_gather | solution.py:219
  454.8 52.3 %all-to-all-start.4 = ((bf16[1,4,256,1024]{3,2,0,1:T(8,128)(2,1)}), bf16[1,4,256,1024]{3,2,0,1:T(8,128)(2,1)}, u32[]{:S(2)}, u32[]{:S(2)}) async-start(bf16[1,4,256,1024]{3,2,0,1:T(8,128)(2,1)} %bitcast.455), calls=%async_computation.4 | async-start | bytes 4194304 | tf_op jit(solution)/shard_map/forward/all_to_all | solution.py:225
  465.9 11.4 %copy-start.58 = (bf16[1024,1024]{1,0:T(8,128)(2,1)S(1)}, bf16[1024,1024]{1,0:T(8,128)(2,1)}, u32[]{:S(2)}) copy-start(bf16[1024,1024]{1,0:T(8,128)(2,1)} %all-gather.18.cloned.1.call-done) | copy-start | bytes 6291460
  507.1 52.6 %all-to-all-start.5 = ((bf16[1,4,256,1024]{3,2,0,1:T(8,128)(2,1)}), bf16[1,4,256,1024]{3,2,0,1:T(8,128)(2,1)}, u32[]{:S(2)}, u32[]{:S(2)}) async-start(bf16[1,4,256,1024]{3,2,0,1:T(8,128)(2,1)} %bitcast.456), calls=%async_computation.5 | async-start | bytes 4194304 | tf_op jit(solution)/shard_map/backward_ffn/all_to_all | solution.py:225
  559.7 86.0 %all-to-all-start.2 = ((bf16[1,4,256,1024]{3,2,0,1:T(8,128)(2,1)}), bf16[1,4,256,1024]{3,2,0,1:T(8,128)(2,1)}, u32[]{:S(2)}, u32[]{:S(2)}) async-start(bf16[1,4,256,1024]{3,2,0,1:T(8,128)(2,1)} %bitcast.453), calls=%async_computation.2 | async-start | bytes 4194304 | tf_op jit(solution)/shard_map/forward/all_to_all | solution.py:225
  564.2 112.1 %all-gather.26.cloned.1.call-start = ((), (), s32[]{:S(2)}) async-start(), calls=%async_computation.20 | async-start | bytes 2621440 | tf_op jit(solution)/shard_map/backward_attention/all_gather | solution.py:219
  571.2 145.7 %all-gather.24.cloned.1.call-start = ((), (), s32[]{:S(2)}) async-start(), calls=%async_computation.19 | async-start | bytes 2621440 | tf_op jit(solution)/shard_map/backward_attention/all_gather | solution.py:219
  652.3 168.4 %reduce-scatter.11.cloned.1.call-start = ((), (), s32[]{:S(2)}) async-start(), calls=%async_computation.24 | async-start | bytes 2359296 | tf_op jit(solution)/shard_map/weight_grads/reduce_scatter | solution.py:372
  657.2 5.2 copy-start.62
  666.5 156.0 %reduce-scatter.9.cloned.1.call-start = ((), (), s32[]{:S(2)}) async-start(), calls=%async_computation.23 | async-start | bytes 2359296 | tf_op jit(solution)/shard_map/weight_grads/reduce_scatter | solution.py:372
  715.4 37.1 %collective-permute-start.6 = (bf16[1,1024,256]{2,1,0:T(8,128)(2,1)}, bf16[1,1024,256]{2,1,0:T(8,128)(2,1)S(1)}, u32[]{:S(2)}, u32[]{:S(2)}) collective-permute-start(bf16[1,1024,256]{2,1,0:T(8,128)(2,1)} %slice.241), channel_id=1, source_target_pairs={{0,4},{4,0},{1,5},{5,1},{2,6},{6,2},{3,7},{7,3},{8,12},{12,8},{9,1... | collective-permute-start | bytes 1572872 | tf_op jit(solution)/shard_map/backward_attention/ppermute | solution.py:210
  716.4 36.3 %collective-permute-start.7 = (bf16[1,1024,256]{2,1,0:T(8,128)(2,1)}, bf16[1,1024,256]{2,1,0:T(8,128)(2,1)}, u32[]{:S(2)}, u32[]{:S(2)}) collective-permute-start(bf16[1,1024,256]{2,1,0:T(8,128)(2,1)} %slice.243), channel_id=1, source_target_pairs={{0,4},{4,0},{1,5},{5,1},{2,6},{6,2},{3,7},{7,3},{8,12},{12,8},{9,1... | collective-permute-start | bytes 1572872 | tf_op jit(solution)/shard_map/backward_attention/ppermute | solution.py:210
  720.0 32.4 %copy-start.30 = (f32[1024,256]{1,0:T(8,128)S(1)}, f32[1024,256]{1,0:T(8,128)}, u32[]{:S(2)}) copy-start(f32[1024,256]{1,0:T(8,128)} %get-tuple-element.24) | copy-start | bytes 3145732
  752.5 5.2 copy-start.31
  752.6 5.0 copy-start.33
  757.7 52.2 %all-to-all-start.8 = ((bf16[1,4,256,1024]{3,2,0,1:T(8,128)(2,1)}), bf16[1,4,256,1024]{3,2,0,1:T(8,128)(2,1)S(1)}, u32[]{:S(2)}, u32[]{:S(2)}) async-start(bf16[1,4,256,1024]{3,2,0,1:T(8,128)(2,1)} %bitcast.452), calls=%async_computation.8 | async-start | bytes 4194304 | tf_op jit(solution)/shard_map/backward_attention/all_to_all | solution.py:225
  761.3 64.1 %reduce-scatter.7.cloned.1.call-start = ((), (), s32[]{:S(2)}) async-start(), calls=%async_computation.22 | async-start | bytes 589824 | tf_op jit(solution)/shard_map/weight_grads/reduce_scatter | solution.py:372
  764.3 6.3 collective-permute-start.4
  765.3 7.0 collective-permute-start.5
  770.6 6.7 copy-start.37
  772.3 5.0 copy-start.39
  809.9 4.9 copy-start.40
  809.9 55.6 %all-to-all-start.6 = ((bf16[1,4,256,1024]{3,2,0,1:T(8,128)(2,1)}), bf16[1,4,256,1024]{3,2,0,1:T(8,128)(2,1)}, u32[]{:S(2)}, u32[]{:S(2)}) async-start(bf16[1,4,256,1024]{3,2,0,1:T(8,128)(2,1)} %bitcast.451), calls=%async_computation.6 | async-start | bytes 4194304 | tf_op jit(solution)/shard_map/backward_attention/all_to_all | solution.py:225
  814.5 48.1 %reduce-scatter.5.cloned.1.call-start = ((), (), s32[]{:S(2)}) async-start(), calls=%async_computation.21 | async-start | bytes 1769472 | tf_op jit(solution)/shard_map/weight_grads/reduce_scatter | solution.py:372
  825.4 39.8 %copy-start.46 = (f32[1,1,1,1024]{3,1,2,0:T(1,128)S(1)}, f32[1,1,1,1024]{3,1,2,0:T(1,128)}, u32[]{:S(2)}) copy-start(f32[1,1,1,1024]{3,1,2,0:T(1,128)} %get-tuple-element.99) | copy-start | bytes 12292
  874.1 10.4 %all-to-all-start.9 = ((f32[4,1,3072]{2,1,0:T(1,128)}), f32[4,1,3072]{2,1,0:T(1,128)}, u32[]{:S(2)}, u32[]{:S(2)}) async-start(f32[4,1,3072]{2,1,0:T(1,128)} %reshape.1187), calls=%async_computation.13 | async-start | bytes 98304 | tf_op jit(solution)/shard_map/ada_grad/all_to_all | solution.py:358
  881.2 16.9 %copy-start.45 = (bf16[8,2,4,128]{3,0,2,1:T(8,128)(2,1)S(1)}, bf16[8,2,4,128]{3,0,2,1:T(8,128)(2,1)}, u32[]{:S(2)}) copy-start(bf16[8,2,4,128]{3,0,2,1:T(8,128)(2,1)} %copy-done.44) | copy-start | bytes 49156
  881.2 18.4 %copy-start.1 = (bf16[128,6,256]{2,0,1:T(8,128)(2,1)S(1)}, bf16[128,6,256]{2,0,1:T(8,128)(2,1)}, u32[]{:S(2)}) copy-start(bf16[128,6,256]{2,0,1:T(8,128)(2,1)} %param.15) | copy-start | bytes 1179652
  (48 other events, 132.2 us)
Sparse Core Ops, SparseCore 0:
  9.6 87.5 all-gather.27
  99.1 24.0 all-gather.13
  124.8 119.6 all-gather.29
  246.2 26.0 all-gather.19
  274.0 27.7 all-gather.17
  309.8 44.6 all-gather.21
  375.1 74.3 all-gather.15
  571.3 74.3 all-gather.25
  652.4 43.7 all-gather.23
  699.4 39.9 reduce-scatter.10
  742.6 41.1 reduce-scatter.8
  786.7 34.1 reduce-scatter.6
  824.2 38.3 reduce-scatter.4

commit v6 on v5

--- a/solution.py
+++ b/solution.py
@@ -183,17 +183,51 @@
         group_index = lax.axis_index("tensor")
         modulation = lax.dynamic_index_in_dim(group_mod, group_index, axis=2, keepdims=False)
 
+    frame_index = lax.axis_index("frame")
+
+    def order_by_half(mine, other):
+        both = jnp.stack([mine, other])
+        return jnp.where(frame_index == 0, both, both[::-1])
+
+    def hidden_half(weight):
+        half = weight.shape[1] // halves
+        blocks = weight.reshape(rows_here, halves, half)
+        mine = jnp.take(blocks, frame_index, axis=1)
+        sent = jnp.take(blocks, 1 - frame_index, axis=1)
+        received = lax.ppermute(sent, "frame", [(0, 1), (1, 0)])
+        rows = order_by_half(mine, received).reshape(halves * rows_here, half)
+        gathered = lax.all_gather(rows, ("dp", "tensor"), axis=0, tiled=True)
+        gathered = gathered.reshape(replicas, groups, halves * rows_here, half)
+        return jnp.swapaxes(gathered, 1, 2).reshape(model_width, groups * half)
+
+    def hidden_half_back(total):
+        half = total.shape[1] // groups
+        blocks = total.reshape(replicas, halves * rows_here, groups, half)
+        blocks = jnp.swapaxes(blocks, 1, 2).astype(jnp.bfloat16)
+        summed = lax.psum_scatter(
+            blocks.reshape(replicas * groups, halves * rows_here, half),
+            ("dp", "tensor"),
+            scatter_dimension=0,
+            tiled=True,
+        )[0].reshape(halves, rows_here, half)
+        mine = jnp.take(summed, frame_index, axis=0).astype(jnp.float32)
+        sent = jnp.take(summed, 1 - frame_index, axis=0)
+        received = lax.ppermute(sent, "frame", [(0, 1), (1, 0)]).astype(jnp.float32)
+        return jnp.swapaxes(order_by_half(mine, received), 0, 1).reshape(rows_here, halves * half)
+
     with jax.named_scope("weights"):
-        joint_weight, mixer_weight, upward_weight, downward_weight = (
+        joint_weight, mixer_weight = (
             lax.all_gather(w, ("dp", "frame"), axis=0, tiled=True)
-            for w in (qkv_weight, out_weight, up_weight, down_weight)
-        )
+            for w in (qkv_weight, out_weight)
+        )
+        upward_weight = hidden_half(up_weight)
+        downward_weight = hidden_half(down_weight)
 
     residual = tokens[:, 0].astype(jnp.float32)
     upstream = out_grad[:, 0].astype(jnp.float32)
     with jax.named_scope("group_inputs"):
         group_tokens = lax.all_gather(tokens[:, 0], "tensor", axis=1, tiled=True)
-        group_upstream = lax.all_gather(out_grad[:, 0], "tensor", axis=1, tiled=True)
+        group_upstream = None
     def gather_halves(values):
         if halves != 2:
             return lax.all_gather(values, "frame", axis=1, tiled=True)
@@ -251,7 +285,7 @@
             middle = residual + gate1 * branch_one
             normed_two, inverse_two = normalize(middle)
             entering_two = (normed_two * (1.0 + scale2) + shift2).astype(jnp.bfloat16)
-            flat_two = gather_tokens(entering_two)
+            flat_two = gather_halves(entering_two)
             up_values = jnp.einsum(
                 "crd,df->crf", flat_two, upward_weight, preferred_element_type=jnp.float32
             )
@@ -259,19 +293,12 @@
             partial_two = jnp.einsum(
                 "crf,of->cro", hidden, downward_weight, preferred_element_type=jnp.float32
             )
-            branch_two = scatter_tokens(partial_two)
+            branch_two = scatter_halves(partial_two)
             output = (middle + gate2 * branch_two).astype(jnp.bfloat16)
 
         with jax.named_scope("backward_ffn"):
             grad_gate_two = jnp.sum(upstream * branch_two, axis=1)
-            grad_two_all = (
-                (
-                    group_mod[:, 5]
-                    * group_upstream.astype(jnp.float32).reshape(clips, groups, patches, model_width)
-                )
-                .astype(jnp.bfloat16)
-                .reshape(clips, groups * patches, model_width)
-            )
+            grad_two_all = gather_halves((gate2 * upstream).astype(jnp.bfloat16))
             grad_hidden = jnp.einsum(
                 "cro,of->crf", grad_two_all, downward_weight, preferred_element_type=jnp.float32
             )
@@ -286,7 +313,7 @@
             partial_back_two = jnp.einsum(
                 "crf,df->crd", grad_up, upward_weight, preferred_element_type=jnp.float32
             )
-            grad_entering_two = scatter_tokens(partial_back_two)
+            grad_entering_two = scatter_halves(partial_back_two)
             grad_shift_two = jnp.sum(grad_entering_two, axis=1)
             grad_scale_two = jnp.sum(grad_entering_two * normed_two, axis=1)
             grad_middle = upstream + norm_back(
@@ -343,7 +370,7 @@
             upstream[i : i + 1],
             modulation[i : i + 1],
             group_tokens[i : i + 1],
-            group_upstream[i : i + 1],
+            None,
             group_mod[i : i + 1],
         )
         for i in range(clips)
@@ -368,12 +395,13 @@
         )
 
     with jax.named_scope("weight_grads"):
-        summed = tuple(
+        joint_sum, mixer_sum = (
             lax.psum_scatter(
                 total.astype(jnp.bfloat16), ("dp", "frame"), scatter_dimension=0, tiled=True
             ).astype(jnp.float32)
-            for total in (joint_total, mixer_total, up_total, down_total)
-        )
+            for total in (joint_total, mixer_total)
+        )
+        summed = (joint_sum, mixer_sum, hidden_half_back(up_total), hidden_half_back(down_total))
     result = output[:, None]
     input_grad = grad_input_low[:, None]
     return (result, input_grad, summed[0], summed[1], summed[2], summed[3], adaptive_total)

time: 914 us -> 860 us (0.941)
  waiting for transfers between devices: 467 us -> 419 us
  local copies, waits for them, and re-layouts: 30.3 us -> 68.6 us
  matrix products: 110 us -> 96.1 us
  starting transfers between devices: 44.5 us -> 32.8 us
  other arithmetic: 74.9 us -> 64.3 us
  blocking collectives: 58.1 us -> 48.8 us
    all_to_all x8 -> x4, waiting for transfers between devices: 327 us -> 160 us  [scatter_tokens(): received = lax.all_to_all(parts, 'tensor', 1, 1, tiled=True)]
    reduce_scatter x0 -> x2, waiting for transfers between devices: none -> 84.3 us  [hidden_half_back(): lax.psum_scatter(blocks.reshape(replicas * groups, halves * rows_here, ha...]
    all_gather x1 -> x2, waiting for transfers between devices: 0.02 us -> 73.7 us  [hidden_half(): gathered = lax.all_gather(rows, ('dp', 'tensor'), axis=0, tiled=True)]
    reduce_scatter x4 -> x2, waiting for transfers between devices: 35.6 us -> 0.02 us  [on_device(): lax.psum_scatter(total.astype(jnp.bfloat16), ('dp', 'frame'), scatter_dim...]
    convert_element_type x0 -> x4, local copies, waits for them, and re-layouts: none -> 26 us  [hidden_half_back(): blocks = jnp.swapaxes(blocks, 1, 2).astype(jnp.bfloat16)]
    all_to_all x8 -> x4, starting transfers between devices: 35.5 us -> 18.8 us  [scatter_tokens(): received = lax.all_to_all(parts, 'tensor', 1, 1, tiled=True)]
    dot_general x2, matrix products: 19.9 us -> 6.74 us  [clip_pass(): jnp.einsum('crd,df->crf', flat_two, upward_weight, preferred_element_type...]
    all_to_all x1 -> x0, blocking collectives: 10.9 us -> none  [on_device(): lax.all_to_all(partial_mod, ('dp', 'frame'), 0, 0, tiled=True)]
  transfers between devices with their start and end apart: 30 -> 36, of which waited for: 13 -> 17; matrix products, arithmetic and copies ran while one was open for 19% -> 25% of each run, Pallas kernels for 12% -> 9%
where the time goes in v6:
time: 860 us; the launch traced here: 852 us
  waiting for transfers between devices  419 us (49%)
  Pallas kernels  107 us (12%)
  matrix products  96.1 us (11%)
  local copies, waits for them, and re-layouts  68.6 us (8%)
  other arithmetic  64.3 us (7%)
  blocking collectives  48.8 us (6%)
  starting transfers between devices  32.8 us (4%)
  between operations  15.6 us (2%)
    all_to_all x4, waiting for transfers between devices, scatter_tokens(): received = lax.all_to_all(parts, 'tensor', 1, 1, tiled=True)  160 us
    reduce_scatter x2, waiting for transfers between devices, hidden_half_back(): lax.psum_scatter(blocks.reshape(replicas * groups, halves * rows_here, ha...  84.3 us
    all_gather x2, waiting for transfers between devices, hidden_half(): gathered = lax.all_gather(rows, ('dp', 'tensor'), axis=0, tiled=True)  73.7 us
    pallas_call x2, Pallas kernels, attention_backward(): pl.pallas_call(functools.partial(_backward_kernel, heads, HEAD_DIM ** (-0...  64.5 us
    all_gather x1, waiting for transfers between devices, on_device(): group_tokens = lax.all_gather(tokens[:, 0], 'tensor', axis=1, tiled=True)  42.3 us
    pallas_call x2, Pallas kernels, attention_forward(): pl.pallas_call(functools.partial(_forward_kernel, heads, HEAD_DIM ** (-0....  42.3 us
    all_gather x2, waiting for transfers between devices, gather_tokens(): return lax.all_gather(values, 'tensor', axis=1, tiled=True)  27.6 us
    convert_element_type x4, local copies, waits for them, and re-layouts, hidden_half_back(): blocks = jnp.swapaxes(blocks, 1, 2).astype(jnp.bfloat16)  26 us
  transfers between devices with their start and end apart: 36, of which 17 were waited for; matrix products, arithmetic and copies ran while one was open for 25% of the time, Pallas kernels for 9%

profile of v6, /device:TPU:0, one launch (start us, length us, event | category | flops | bytes accessed | tf_op | source)
XLA Modules:
  0.0 852.1 jit_solution(8941133389790673421)
XLA Ops:
  13.1 10.1 %all-gather.2 = s32[8,2,4]{2,1,0:T(2,128)S(1)} all-gather(s32[1,2,4]{2,1,0:T(2,128)S(1)} %bitcast.484), channel_id=1, replica_groups=mesh['dp'=4,'frame'=2,'tensor'=4] {'dp','frame'}, dimensions={0}, use_global_device_ids=true | all-gather | bytes 288 | tf_op jit(solution)/shard_map/modulation/all_gather | solution.py:168
  24.8 3.5 all-to-all-start
  29.4 7.1 all-to-all-done
  36.6 18.1 %all_gather.31 = f32[2,4,6,1024]{3,2,1,0:T(8,128)S(1)} all-gather(f32[2,4,6,256]{3,2,1,0:T(8,128)S(1)} %copy.231), channel_id=1, replica_groups=mesh['dp'=4,'frame'=2,'tensor'=4] {'tensor'}, dimensions={3}, use_global_device_ids=true | all-gather | bytes 245760 | tf_op jit(solution)/shard_map/modulation/all_gather | solution.py:181
  54.9 42.3 %all-gather.20.cloned.1.call-done = bf16[2,1,1024,1024]{3,2,1,0:T(8,128)(2,1)} async-done(((bf16[2,1,256,1024]{3,2,1,0:T(8,128)(2,1)}), bf16[2,1,1024,1024]{3,2,1,0:T(8,128)(2,1)}) %all-gather.20.cloned.1.call-update) | async-done | bytes 4194320 | tf_op jit(solution)/shard_map/group_inputs/all_gather | solution.py:229
  107.2 16.0 %all-gather.10.cloned.1.call-done = bf16[1024,3,256]{2,0,1:T(8,128)(2,1)} async-done(((bf16[128,3,256]{2,0,1:T(8,128)(2,1)}), bf16[1024,3,256]{2,0,1:T(8,128)(2,1)}) %all-gather.10.cloned.1.call-update) | async-done | bytes 1572880 | tf_op jit(solution)/shard_map/weights/all_gather | solution.py:220
  123.2 3.2 fusion.39
  127.9 10.1 %all_gather.34 = bf16[1024,256]{1,0:T(8,128)(2,1)S(1)} all-gather(bf16[128,256]{1,0:T(8,128)(2,1)S(1)} %copy-done.49), channel_id=1, replica_groups=mesh['dp'=4,'frame'=2,'tensor'=4] {'dp','frame'}, dimensions={0}, use_global_device_ids=true | all-gather | bytes 589824 | tf_op jit(solution)/shard_map/weights/all_gather | solution.py:220
  140.2 21.1 %forward.3 = (bf16[1024,256]{1,0:T(8,128)(2,1)}, f32[1024,4]{1,0:T(8,128)}) custom-call(bf16[1024,256]{1,0:T(8,128)(2,1)} %get-tuple-element.160.q_ref, bf16[2048,256]{1,0:T(8,128)(2,1)} %maximum_bitcast_fusion.3.k_ref, bf16[2048,256]{1,0:T(8,128)(2,1)} %maximum_bitcast_fusion.4.v_ref), custom_call_target="tpu_custom_call" | custom-call | flops 2147483648 | bytes 3145728 | tf_op jit(solution)/shard_map/forward/pallas_call | solution.py:85
  161.3 3.2 convolution_convert_fusion
  164.5 5.1 all-to-all-start.2
  169.6 3.8 fusion.38
  178.3 21.1 %forward.2 = (bf16[1024,256]{1,0:T(8,128)(2,1)}, f32[1024,4]{1,0:T(8,128)}) custom-call(bf16[1024,256]{1,0:T(8,128)(2,1)} %get-tuple-element.157.q_ref, bf16[2048,256]{1,0:T(8,128)(2,1)} %maximum_bitcast_fusion.k_ref, bf16[2048,256]{1,0:T(8,128)(2,1)} %maximum_bitcast_fusion.1.v_ref), custom_call_target="tpu_custom_call" | custom-call | flops 2147483648 | bytes 3145728 | tf_op jit(solution)/shard_map/forward/pallas_call | solution.py:85
  199.4 3.2 convolution_convert_fusion.1
  202.6 38.3 %all-to-all-done.2 = bf16[1,4,256,1024]{3,2,0,1:T(8,128)(2,1)S(1)} async-done(((bf16[1,4,256,1024]{3,2,0,1:T(8,128)(2,1)}), bf16[1,4,256,1024]{3,2,0,1:T(8,128)(2,1)S(1)}, u32[]{:S(2)}, u32[]{:S(2)}) %all-to-all-start.2) | async-done | bytes 2097184 | tf_op jit(solution)/shard_map/forward/all_to_all | solution.py:259
  240.9 4.5 all-to-all-start.1
  253.7 5.4 copy.195
  259.1 3.4 copy.234
  262.5 73.7 %all-gather.14.cloned.1.call-done = bf16[4096,512]{1,0:T(8,128)(2,1)} async-done(((bf16[256,512]{1,0:T(8,128)(2,1)}), bf16[4096,512]{1,0:T(8,128)(2,1)}) %all-gather.14.cloned.1.call-update) | async-done | bytes 4194320 | tf_op jit(solution)/shard_map/weights/all_gather | solution.py:199
  336.2 5.4 copy.199
  341.6 3.3 copy.235
  355.5 6.7 fusion.20
  371.8 4.4 fusion.73
  377.6 8.3 fusion.27
  398.7 22.8 %all-gather.16.cloned.1.call-done = bf16[1,1024,1024]{2,1,0:T(8,128)(2,1)} async-done(((bf16[1,256,1024]{2,1,0:T(8,128)(2,1)}), bf16[1,1024,1024]{2,1,0:T(8,128)(2,1)}) %all-gather.16.cloned.1.call-update) | async-done | bytes 2097168 | tf_op jit(solution)/shard_map/backward_attention/all_gather | solution.py:253
  421.5 3.2 fusion.47.g_ref
  424.7 32.2 %backward_attention.2 = (f32[1024,256]{1,0:T(8,128)}, f32[2048,256]{1,0:T(8,128)}, f32[2048,256]{1,0:T(8,128)}) custom-call(bf16[1024,256]{1,0:T(8,128)(2,1)} %get-tuple-element.157.q_ref, bf16[2048,256]{1,0:T(8,128)(2,1)} %maximum_bitcast_fusion.k_ref, bf16[2048,256]{1,0:T(8,128)(2,1)} %maximum_bitcast_fusion.1.v_ref, bf16[1024,256]{1,0:T(8,128)(2,1)} %fusion.47.g_ref, ...), custom_call_target="tpu_custom_call" | custom-call | flops 5368709120 | bytes 8912896 | tf_op jit(solution)/shard_map/backward_attention/pallas_call | solution.py:118
  462.7 4.7 all-gather.18.cloned.1.call-done
  470.6 32.3 %backward_attention.3 = (f32[1024,256]{1,0:T(8,128)}, f32[2048,256]{1,0:T(8,128)}, f32[2048,256]{1,0:T(8,128)}) custom-call(bf16[1024,256]{1,0:T(8,128)(2,1)} %get-tuple-element.160.q_ref, bf16[2048,256]{1,0:T(8,128)(2,1)} %maximum_bitcast_fusion.3.k_ref, bf16[2048,256]{1,0:T(8,128)(2,1)} %maximum_bitcast_fusion.4.v_ref, bf16[1024,256]{1,0:T(8,128)(2,1)} %fusion.50.g_ref, ...), custom_call_target="tpu_custom_call" | custom-call | flops 5368709120 | bytes 8912896 | tf_op jit(solution)/shard_map/backward_attention/pallas_call | solution.py:118
  518.2 3.2 add_convert_fusion.2
  521.4 5.2 fusion.71
  526.6 5.5 add_convert_fusion
  532.1 7.9 convert_element_type.302
  540.0 5.1 copy.209
  545.2 7.7 fusion.74
  552.9 3.2 bitcast_convert_fusion.1
  556.0 4.6 all-to-all-start.3
  560.9 8.4 add_convert_fusion.1
  569.2 7.9 convert_element_type.299
  577.1 5.1 copy.207
  583.4 4.8 bitcast_convert_fusion
  588.2 46.0 %all-to-all-done.3 = bf16[1,4,256,1024]{3,2,0,1:T(8,128)(2,1)} async-done(((bf16[1,4,256,1024]{3,2,0,1:T(8,128)(2,1)}), bf16[1,4,256,1024]{3,2,0,1:T(8,128)(2,1)}, u32[]{:S(2)}, u32[]{:S(2)}) %all-to-all-start.3) | async-done | bytes 2097184 | tf_op jit(solution)/shard_map/backward_attention/all_to_all | solution.py:259
  634.3 4.6 all-to-all-start.4
  646.1 76.0 %all-to-all-done.4 = bf16[1,4,256,1024]{3,2,0,1:T(8,128)(2,1)} async-done(((bf16[1,4,256,1024]{3,2,0,1:T(8,128)(2,1)}), bf16[1,4,256,1024]{3,2,0,1:T(8,128)(2,1)}, u32[]{:S(2)}, u32[]{:S(2)}) %all-to-all-start.4) | async-done | bytes 2097184 | tf_op jit(solution)/shard_map/backward_attention/all_to_all | solution.py:259
  728.0 3.4 reshape.1120
  731.4 3.3 all-to-all-start.5
  743.6 10.5 %all-gather.1 = f32[16,4,1,6,256]{4,1,0,3,2:T(4,128)S(1)} all-gather(f32[2,4,1,6,256]{4,1,0,3,2:T(4,128)S(1)} %bitcast.444), channel_id=3, replica_groups=mesh['dp'=4,'frame'=2,'tensor'=4] {'dp','frame'}, dimensions={0}, use_global_device_ids=true | all-gather | bytes 442368 | tf_op jit(solution)/shard_map/ada_grad/all_gather | solution.py:388
  757.0 84.3 %reduce-scatter.9.cloned.1.call-done = bf16[1,256,512]{2,1,0:T(8,128)(2,1)} async-done(((bf16[16,256,512]{2,1,0:T(8,128)(2,1)}), bf16[1,256,512]{2,1,0:T(8,128)(2,1)}) %reduce-scatter.9.cloned.1.call-update) | async-done | bytes 262160 | tf_op jit(solution)/shard_map/weight_grads/reduce_scatter | solution.py:207
  (325 shorter events, 123.2 us)
Async XLA Ops:
  7.2 16.7 %copy-start = (bf16[128,6,256]{2,0,1:T(8,128)(2,1)S(1)}, bf16[128,6,256]{2,0,1:T(8,128)(2,1)}, u32[]{:S(2)}) copy-start(bf16[128,6,256]{2,0,1:T(8,128)(2,1)} %param.19) | copy-start | bytes 1179652
  7.2 90.0 %all-gather.20.cloned.1.call-start = ((), (), s32[]{:S(2)}) async-start(), calls=%async_computation.19 | async-start | bytes 5242880 | tf_op jit(solution)/shard_map/group_inputs/all_gather | solution.py:229
  7.9 115.3 %all-gather.10.cloned.1.call-start = ((), (), s32[]{:S(2)}) async-start(), calls=%async_computation.10 | async-start | bytes 1769472 | tf_op jit(solution)/shard_map/weights/all_gather | solution.py:220
  8.7 245.0 %all-gather.12.cloned.1.call-start = ((), (), s32[]{:S(2)}) async-start(), calls=%async_computation.11 | async-start | bytes 4456448 | tf_op jit(solution)/shard_map/weights/all_gather | solution.py:199
  9.9 1.5 collective-permute-start.3
  12.6 15.8 %collective-permute-start.4 = (bf16[128,512]{0,1:T(8,128)(2,1)S(1)}, bf16[128,512]{0,1:T(8,128)(2,1)S(1)}, u32[]{:S(2)}, u32[]{:S(2)}) collective-permute-start(bf16[128,512]{0,1:T(8,128)(2,1)S(1)} %get-tuple-element.173), channel_id=1, source_target_pairs={{0,4},{4,0},{1,5},{5,1},{2,6},{6,2},{3,7},{7,3},{8,12},{12,8},{9,1... | collective-permute-start | bytes 393224 | tf_op jit(solution)/shard_map/weights/ppermute | solution.py:197
  24.8 11.7 %all-to-all-start = ((f32[8,2,4,6,256]{4,2,3,1,0:T(4,128)}), f32[8,2,4,6,256]{4,2,3,1,0:T(4,128)S(1)}, u32[]{:S(2)}, u32[]{:S(2)}) async-start(f32[8,2,4,6,256]{4,2,3,1,0:T(4,128)} %fusion.83), calls=%async_computation | async-start | bytes 786432 | tf_op jit(solution)/shard_map/modulation/all_to_all | solution.py:179
  28.3 307.9 %all-gather.14.cloned.1.call-start = ((), (), s32[]{:S(2)}) async-start(), calls=%async_computation.12 | async-start | bytes 4456448 | tf_op jit(solution)/shard_map/weights/all_gather | solution.py:199
  107.2 16.0 %copy-start.24 = (bf16[1024,1024,1]{1,0,2:T(8,128)(2,1)}, bf16[1024,1024,1]{1,0,2:T(8,128)(2,1)S(1)}, u32[]{:S(2)}) copy-start(bf16[1024,1024,1]{1,0,2:T(8,128)(2,1)S(1)} %get-tuple-element.144) | copy-start | bytes 6291460
  127.4 10.6 %collective-permute-start.7 = (bf16[1,1024,256]{2,1,0:T(8,128)(2,1)S(1)}, bf16[1,1024,256]{2,1,0:T(8,128)(2,1)S(1)}, u32[]{:S(2)}, u32[]{:S(2)}) collective-permute-start(bf16[1,1024,256]{2,1,0:T(8,128)(2,1)S(1)} %get-tuple-element.158), channel_id=1, source_target_pairs={{0,4},{4,0},{1,5},{5,1},{2,6},{6,2},{3,7},{7,3},{8,12},{12,8},{9,1... | collective-permute-start | bytes 1572872 | tf_op jit(solution)/shard_map/forward/ppermute | solution.py:234
  127.6 11.5 %collective-permute-start.6 = (bf16[1,1024,256]{2,1,0:T(8,128)(2,1)S(1)}, bf16[1,1024,256]{2,1,0:T(8,128)(2,1)S(1)}, u32[]{:S(2)}, u32[]{:S(2)}) collective-permute-start(bf16[1,1024,256]{2,1,0:T(8,128)(2,1)S(1)} %get-tuple-element.159), channel_id=1, source_target_pairs={{0,4},{4,0},{1,5},{5,1},{2,6},{6,2},{3,7},{7,3},{8,12},{12,8},{9,1... | collective-permute-start | bytes 1572872 | tf_op jit(solution)/shard_map/forward/ppermute | solution.py:234
  138.0 61.5 %copy-start.11 = (bf16[1024,256]{1,0:T(8,128)(2,1)}, bf16[1024,256]{1,0:T(8,128)(2,1)S(1)}, u32[]{:S(2)}) copy-start(bf16[1024,256]{1,0:T(8,128)(2,1)S(1)} %all_gather.34) | copy-start | bytes 1572868
  164.5 76.5 %all-to-all-start.2 = ((bf16[1,4,256,1024]{3,2,0,1:T(8,128)(2,1)}), bf16[1,4,256,1024]{3,2,0,1:T(8,128)(2,1)S(1)}, u32[]{:S(2)}, u32[]{:S(2)}) async-start(bf16[1,4,256,1024]{3,2,0,1:T(8,128)(2,1)} %bitcast.415), calls=%async_computation.2 | async-start | bytes 4194304 | tf_op jit(solution)/shard_map/forward/all_to_all | solution.py:259
  174.3 1.9 collective-permute-start.1
  174.4 2.9 collective-permute-start
  240.9 105.4 %all-to-all-start.1 = ((bf16[1,4,256,1024]{3,2,0,1:T(8,128)(2,1)}), bf16[1,4,256,1024]{3,2,0,1:T(8,128)(2,1)}, u32[]{:S(2)}, u32[]{:S(2)}) async-start(bf16[1,4,256,1024]{3,2,0,1:T(8,128)(2,1)} %bitcast.414), calls=%async_computation.1 | async-start | bytes 4194304 | tf_op jit(solution)/shard_map/forward/all_to_all | solution.py:259
  245.4 176.1 %all-gather.16.cloned.1.call-start = ((), (), s32[]{:S(2)}) async-start(), calls=%async_computation.13 | async-start | bytes 2621440 | tf_op jit(solution)/shard_map/backward_attention/all_gather | solution.py:253
  252.5 103.0 %collective-permute-start.10 = (bf16[1,256,1024]{2,1,0:T(8,128)(2,1)}, bf16[1,256,1024]{2,1,0:T(8,128)(2,1)}, u32[]{:S(2)}, u32[]{:S(2)}) collective-permute-start(bf16[1,256,1024]{2,1,0:T(8,128)(2,1)} %multiply_convert_fusion.5), channel_id=1, source_target_pairs={{0,4},{4,0},{1,5},{5,1},{2,6},{6,2},{3,7},{7,3},{8,12},{12,8},{9,1... | collective-permute-start | bytes 1572872 | tf_op jit(solution)/shard_map/backward_ffn/ppermute | solution.py:234
  351.1 2.0 collective-permute-start.2
  351.7 20.1 %copy-start.39 = (bf16[1,256,1024]{2,1,0:T(8,128)(2,1)}, bf16[1,256,1024]{2,1,0:T(8,128)(2,1)S(1)}, u32[]{:S(2)}) copy-start(bf16[1,256,1024]{2,1,0:T(8,128)(2,1)S(1)} %add_convert_fusion.10) | copy-start | bytes 1572868
  351.7 20.1 %collective-permute-start.8 = (bf16[1,256,1024]{2,1,0:T(8,128)(2,1)S(1)}, bf16[1,256,1024]{2,1,0:T(8,128)(2,1)S(1)}, u32[]{:S(2)}, u32[]{:S(2)}) collective-permute-start(bf16[1,256,1024]{2,1,0:T(8,128)(2,1)S(1)} %add_convert_fusion.10), channel_id=1, source_target_pairs={{0,4},{4,0},{1,5},{5,1},{2,6},{6,2},{3,7},{7,3},{8,12},{12,8},{9,1... | collective-permute-start | bytes 1572872 | tf_op jit(solution)/shard_map/forward/ppermute | solution.py:234
  355.5 9.4 %copy-start.57 = (f32[512,2048]{1,0:T(8,128)}, f32[512,2048]{1,0:T(8,128)S(1)}, u32[]{:S(2)}) copy-start(f32[512,2048]{1,0:T(8,128)S(1)} %fusion.75) | copy-start | bytes 12582916
  364.7 3.4 collective-permute-start.11
  367.7 2.0 collective-permute-start.5
  371.4 6.2 collective-permute-start.14
  377.1 90.3 %all-gather.18.cloned.1.call-start = ((), (), s32[]{:S(2)}) async-start(), calls=%async_computation.14 | async-start | bytes 2621440 | tf_op jit(solution)/shard_map/backward_attention/all_gather | solution.py:253
  377.6 8.3 copy-start.15
  388.4 4.7 collective-permute-start.15
  392.9 2.0 collective-permute-start.9
  398.5 241.5 %reduce-scatter.7.cloned.1.call-start = ((), (), s32[]{:S(2)}) async-start(), calls=%async_computation.16 | async-start | bytes 589824 | tf_op jit(solution)/shard_map/weight_grads/reduce_scatter | solution.py:399
  458.8 2.0 collective-permute-start.12
  459.2 8.3 copy-start.12
  459.3 2.4 collective-permute-start.13
  505.6 6.8 collective-permute-start.16
  507.5 6.3 collective-permute-start.17
  510.4 134.0 %reduce-scatter.5.cloned.1.call-start = ((), (), s32[]{:S(2)}) async-start(), calls=%async_computation.15 | async-start | bytes 1769472 | tf_op jit(solution)/shard_map/weight_grads/reduce_scatter | solution.py:399
  521.4 232.8 %reduce-scatter.11.cloned.1.call-start = ((), (), s32[]{:S(2)}) async-start(), calls=%async_computation.18 | async-start | bytes 4456448 | tf_op jit(solution)/shard_map/weight_grads/reduce_scatter | solution.py:207
  556.0 78.3 %all-to-all-start.3 = ((bf16[1,4,256,1024]{3,2,0,1:T(8,128)(2,1)}), bf16[1,4,256,1024]{3,2,0,1:T(8,128)(2,1)}, u32[]{:S(2)}, u32[]{:S(2)}) async-start(bf16[1,4,256,1024]{3,2,0,1:T(8,128)(2,1)} %bitcast.429), calls=%async_computation.3 | async-start | bytes 4194304 | tf_op jit(solution)/shard_map/backward_attention/all_to_all | solution.py:259
  560.6 280.7 %reduce-scatter.9.cloned.1.call-start = ((), (), s32[]{:S(2)}) async-start(), calls=%async_computation.17 | async-start | bytes 4456448 | tf_op jit(solution)/shard_map/weight_grads/reduce_scatter | solution.py:207
  588.2 50.7 %copy-start.22 = (bf16[1,256,1024]{2,1,0:T(8,128)(2,1)S(1)}, bf16[1,256,1024]{2,1,0:T(8,128)(2,1)}, u32[]{:S(2)}) copy-start(bf16[1,256,1024]{2,1,0:T(8,128)(2,1)} %get-tuple-element.147) | copy-start | bytes 1572868
  588.2 50.7 %copy-start.28 = (bf16[1,256,1024]{2,1,0:T(8,128)(2,1)S(1)}, bf16[1,256,1024]{2,1,0:T(8,128)(2,1)}, u32[]{:S(2)}) copy-start(bf16[1,256,1024]{2,1,0:T(8,128)(2,1)} %get-tuple-element.161) | copy-start | bytes 1572868
  634.3 9.9 %copy-start.48 = (f32[1,1,1,1024]{3,1,2,0:T(1,128)S(1)}, f32[1,1,1,1024]{3,1,2,0:T(1,128)}, u32[]{:S(2)}) copy-start(f32[1,1,1,1024]{3,1,2,0:T(1,128)} %get-tuple-element.178) | copy-start | bytes 12292
  634.3 87.8 %all-to-all-start.4 = ((bf16[1,4,256,1024]{3,2,0,1:T(8,128)(2,1)}), bf16[1,4,256,1024]{3,2,0,1:T(8,128)(2,1)}, u32[]{:S(2)}, u32[]{:S(2)}) async-start(bf16[1,4,256,1024]{3,2,0,1:T(8,128)(2,1)} %bitcast.428), calls=%async_computation.4 | async-start | bytes 4194304 | tf_op jit(solution)/shard_map/backward_attention/all_to_all | solution.py:259
  640.0 85.8 %copy-start.47 = (f32[1,1,1,1024]{3,1,2,0:T(1,128)S(1)}, f32[1,1,1,1024]{3,1,2,0:T(1,128)}, u32[]{:S(2)}) copy-start(f32[1,1,1,1024]{3,1,2,0:T(1,128)} %get-tuple-element.182) | copy-start | bytes 12292
  731.4 8.9 %all-to-all-start.5 = ((f32[4,1,3072]{2,1,0:T(1,128)}), f32[4,1,3072]{2,1,0:T(1,128)S(1)}, u32[]{:S(2)}, u32[]{:S(2)}) async-start(f32[4,1,3072]{2,1,0:T(1,128)} %reshape.1120), calls=%async_computation.9 | async-start | bytes 98304 | tf_op jit(solution)/shard_map/ada_grad/all_to_all | solution.py:385
  738.6 17.0 %copy-start.46 = (bf16[8,2,4,128]{3,0,2,1:T(8,128)(2,1)S(1)}, bf16[8,2,4,128]{3,0,2,1:T(8,128)(2,1)}, u32[]{:S(2)}) copy-start(bf16[8,2,4,128]{3,0,2,1:T(8,128)(2,1)} %copy-done.45) | copy-start | bytes 49156
  755.2 87.3 %collective-permute-start.19 = (bf16[128,512]{1,0:T(8,128)(2,1)S(1)}, bf16[128,512]{1,0:T(8,128)(2,1)S(1)}, u32[]{:S(2)}, u32[]{:S(2)}) collective-permute-start(bf16[128,512]{1,0:T(8,128)(2,1)S(1)} %get-tuple-element.163), channel_id=1, source_target_pairs={{0,4},{4,0},{1,5},{5,1},{2,6},{6,2},{3,7},{7,3},{8,12},{12,8},{9,1... | collective-permute-start | bytes 393224 | tf_op jit(solution)/shard_map/weight_grads/ppermute | solution.py:215
  842.4 1.4 collective-permute-start.18
  (50 other events, 175.7 us)
Sparse Core Ops, SparseCore 0:
  9.6 87.5 all-gather.19
  99.1 24.0 all-gather.9
  126.0 105.3 all-gather.11
  234.0 102.1 all-gather.13
  377.2 44.2 all-gather.15
  423.0 44.4 all-gather.17
  510.5 32.8 reduce-scatter.6
  546.7 38.3 reduce-scatter.4
  587.4 153.0 reduce-scatter.10
  742.7 98.6 reduce-scatter.8

commit v7 on v6

--- a/solution.py
+++ b/solution.py
@@ -189,44 +189,76 @@
         both = jnp.stack([mine, other])
         return jnp.where(frame_index == 0, both, both[::-1])
 
-    def hidden_half(weight):
-        half = weight.shape[1] // halves
-        blocks = weight.reshape(rows_here, halves, half)
-        mine = jnp.take(blocks, frame_index, axis=1)
-        sent = jnp.take(blocks, 1 - frame_index, axis=1)
-        received = lax.ppermute(sent, "frame", [(0, 1), (1, 0)])
-        rows = order_by_half(mine, received).reshape(halves * rows_here, half)
-        gathered = lax.all_gather(rows, ("dp", "tensor"), axis=0, tiled=True)
-        gathered = gathered.reshape(replicas, groups, halves * rows_here, half)
-        return jnp.swapaxes(gathered, 1, 2).reshape(model_width, groups * half)
-
-    def hidden_half_back(total):
-        half = total.shape[1] // groups
-        blocks = total.reshape(replicas, halves * rows_here, groups, half)
-        blocks = jnp.swapaxes(blocks, 1, 2).astype(jnp.bfloat16)
+    def hidden_half(weights):
+        half = weights[0].shape[1] // halves
+        pieces = []
+        for weight in weights:
+            blocks = weight.reshape(rows_here, halves, half)
+            mine = jnp.take(blocks, frame_index, axis=1)
+            sent = jnp.take(blocks, 1 - frame_index, axis=1)
+            received = lax.ppermute(sent, "frame", [(0, 1), (1, 0)])
+            pieces.append(order_by_half(mine, received).reshape(halves * rows_here, half))
+        joined = jnp.concatenate(pieces, axis=1)
+        gathered = lax.all_gather(joined, ("dp", "tensor"), axis=0, tiled=True)
+        gathered = gathered.reshape(replicas, groups, halves * rows_here, len(weights), half)
+        return tuple(
+            jnp.swapaxes(gathered[:, :, :, k], 1, 2).reshape(model_width, groups * half)
+            for k in range(len(weights))
+        )
+
+    def hidden_half_back(totals):
+        half = totals[0].shape[1] // groups
+        blocks = jnp.concatenate(
+            [
+                jnp.swapaxes(total.reshape(replicas, halves * rows_here, groups, half), 1, 2)
+                for total in totals
+            ],
+            axis=3,
+        ).astype(jnp.bfloat16)
         summed = lax.psum_scatter(
-            blocks.reshape(replicas * groups, halves * rows_here, half),
+            blocks.reshape(replicas * groups, halves * rows_here, len(totals) * half),
             ("dp", "tensor"),
             scatter_dimension=0,
             tiled=True,
-        )[0].reshape(halves, rows_here, half)
+        )[0].reshape(halves, rows_here, len(totals) * half)
         mine = jnp.take(summed, frame_index, axis=0).astype(jnp.float32)
         sent = jnp.take(summed, 1 - frame_index, axis=0)
         received = lax.ppermute(sent, "frame", [(0, 1), (1, 0)]).astype(jnp.float32)
-        return jnp.swapaxes(order_by_half(mine, received), 0, 1).reshape(rows_here, halves * half)
+        ordered = jnp.swapaxes(order_by_half(mine, received), 0, 1)
+        ordered = ordered.reshape(rows_here, halves, len(totals), half)
+        return tuple(
+            ordered[:, :, k].reshape(rows_here, halves * half) for k in range(len(totals))
+        )
+
+    def line_gather(values):
+        if groups == 1:
+            return values[:, None]
+        rightward = [(i, i + 1) for i in range(groups - 1)]
+        leftward = [(i + 1, i) for i in range(groups - 1)]
+        right, left = values, values
+        before, after = [], []
+        for _ in range(groups - 1):
+            right = lax.ppermute(right, "tensor", rightward)
+            left = lax.ppermute(left, "tensor", leftward)
+            before.insert(0, right)
+            after.append(left)
+        stacked = jnp.stack(before + [values] + after, axis=1)
+        start = groups - 1 - lax.axis_index("tensor")
+        return lax.dynamic_slice_in_dim(stacked, start, groups, axis=1)
 
     with jax.named_scope("weights"):
-        joint_weight, mixer_weight = (
-            lax.all_gather(w, ("dp", "frame"), axis=0, tiled=True)
-            for w in (qkv_weight, out_weight)
-        )
-        upward_weight = hidden_half(up_weight)
-        downward_weight = hidden_half(down_weight)
+        attention_shards = jnp.concatenate(
+            [qkv_weight.reshape(rows_here, 3 * local_width), out_weight], axis=1
+        )
+        attention_weights = lax.all_gather(attention_shards, ("dp", "frame"), axis=0, tiled=True)
+        joint_weight = attention_weights[:, : 3 * local_width].reshape(model_width, 3, local_width)
+        mixer_weight = attention_weights[:, 3 * local_width :]
+        upward_weight, downward_weight = hidden_half((up_weight, down_weight))
 
     residual = tokens[:, 0].astype(jnp.float32)
     upstream = out_grad[:, 0].astype(jnp.float32)
     with jax.named_scope("group_inputs"):
-        group_tokens = lax.all_gather(tokens[:, 0], "tensor", axis=1, tiled=True)
+        group_tokens = line_gather(tokens[:, 0]).reshape(clips, groups * patches, model_width)
         group_upstream = None
     def gather_halves(values):
         if halves != 2:
@@ -395,13 +427,16 @@
         )
 
     with jax.named_scope("weight_grads"):
-        joint_sum, mixer_sum = (
-            lax.psum_scatter(
-                total.astype(jnp.bfloat16), ("dp", "frame"), scatter_dimension=0, tiled=True
-            ).astype(jnp.float32)
-            for total in (joint_total, mixer_total)
-        )
-        summed = (joint_sum, mixer_sum, hidden_half_back(up_total), hidden_half_back(down_total))
+        attention_totals = jnp.concatenate(
+            [joint_total.reshape(model_width, 3 * local_width), mixer_total], axis=1
+        )
+        attention_sums = lax.psum_scatter(
+            attention_totals.astype(jnp.bfloat16), ("dp", "frame"), scatter_dimension=0, tiled=True
+        ).astype(jnp.float32)
+        joint_sum = attention_sums[:, : 3 * local_width].reshape(rows_here, 3, local_width)
+        mixer_sum = attention_sums[:, 3 * local_width :]
+        up_sum, down_sum = hidden_half_back((up_total, down_total))
+        summed = (joint_sum, mixer_sum, up_sum, down_sum)
     result = output[:, None]
     input_grad = grad_input_low[:, None]
     return (result, input_grad, summed[0], summed[1], summed[2], summed[3], adaptive_total)

time: 860 us -> 908 us (1.056)
  local copies, waits for them, and re-layouts: 68.6 us -> 117 us
  waiting for transfers between devices: 419 us -> 378 us
  blocking collectives: 48.8 us -> 73.3 us
  starting transfers between devices: 32.8 us -> 49.7 us
    all_gather x4 -> x2, waiting for transfers between devices: 132 us -> 0.01 us  [the longest x1 0.01 us: on_device(): lax.all_gather(attention_shards, ('dp', 'frame'), axis=0, tiled=True)]
    ppermute x0 -> x6, waiting for transfers between devices: none -> 90.1 us  [the longest x3 58.1 us: line_gather(): left = lax.ppermute(left, 'tensor', leftward)]
    all_to_all x4, waiting for transfers between devices: 160 us -> 238 us  [scatter_tokens(): received = lax.all_to_all(parts, 'tensor', 1, 1, tiled=True)]
    reduce_scatter x4 -> x1, waiting for transfers between devices: 84.3 us -> 15.1 us  [hidden_half_back(): lax.psum_scatter(blocks.reshape(replicas * groups, halves * rows_here, le...]
    all_gather x1, blocking collectives: 18.1 us -> 53 us  [on_device(): group_mod = lax.all_gather(summed_mod, 'tensor', axis=3, tiled=True)]
    reshape x2 -> x5, local copies, waits for them, and re-layouts: 10.9 us -> 41 us  [the longest x4 26.5 us: hidden_half_back(): total.reshape(replicas, halves * rows_here, groups, half)]
    convert_element_type x4 -> x0, local copies, waits for them, and re-layouts: 26 us -> none  [hidden_half_back(): blocks = jnp.swapaxes(blocks, 1, 2).astype(jnp.bfloat16)]
    slice x0 -> x5, local copies, waits for them, and re-layouts: none -> 21.7 us  [the longest x1 16.8 us: hidden_half(): gathered[:, :, :, k]]
  transfers between devices with their start and end apart: 36 -> 37, of which waited for: 17 -> 16; matrix products, arithmetic and copies ran while one was open for 25% -> 28% of each run, Pallas kernels for 9% -> 8%
where the time goes in v7:
time: 908 us; the launch traced here: 902 us
  waiting for transfers between devices  378 us (42%)
  local copies, waits for them, and re-layouts  117 us (13%)
  Pallas kernels  107 us (12%)
  matrix products  94.1 us (10%)
  blocking collectives  73.3 us (8%)
  other arithmetic  67.3 us (7%)
  starting transfers between devices  49.7 us (5%)
  between operations  15.8 us (2%)
    all_to_all x4, waiting for transfers between devices, scatter_tokens(): received = lax.all_to_all(parts, 'tensor', 1, 1, tiled=True)  238 us
    pallas_call x2, Pallas kernels, attention_backward(): pl.pallas_call(functools.partial(_backward_kernel, heads, HEAD_DIM ** (-0...  64.6 us
    ppermute x3, waiting for transfers between devices, line_gather(): left = lax.ppermute(left, 'tensor', leftward)  58.1 us
    all_gather x1, blocking collectives, on_device(): group_mod = lax.all_gather(summed_mod, 'tensor', axis=3, tiled=True)  53 us
    pallas_call x2, Pallas kernels, attention_forward(): pl.pallas_call(functools.partial(_forward_kernel, heads, HEAD_DIM ** (-0....  42.2 us
    unnamed x162, local copies, waits for them, and re-layouts  33.9 us
    ppermute x3, waiting for transfers between devices, line_gather(): right = lax.ppermute(right, 'tensor', rightward)  32 us
    all_gather x2, waiting for transfers between devices, gather_tokens(): return lax.all_gather(values, 'tensor', axis=1, tiled=True)  29 us
  transfers between devices with their start and end apart: 37, of which 16 were waited for; matrix products, arithmetic and copies ran while one was open for 28% of the time, Pallas kernels for 8%

profile of v7, /device:TPU:0, one launch (start us, length us, event | category | flops | bytes accessed | tf_op | source)
XLA Modules:
  0.0 901.9 jit_solution(15098407098688375873)
XLA Ops:
  10.1 5.0 collective-permute-start
  20.7 17.1 %collective-permute-done = bf16[2,256,1024]{2,1,0:T(8,128)(2,1)S(1)} collective-permute-done((bf16[2,256,1024]{2,1,0:T(8,128)(2,1)}, bf16[2,256,1024]{2,1,0:T(8,128)(2,1)S(1)}, u32[]{:S(2)}, u32[]{:S(2)}) %collective-permute-start) | collective-permute-done | bytes 1048608 | tf_op jit(solution)/shard_map/group_inputs/ppermute | solution.py:241
  37.8 5.3 collective-permute-start.1
  44.0 8.9 all-gather.1
  55.2 3.5 all-to-all-start
  60.1 14.8 %collective-permute-done.1 = bf16[2,256,1024]{2,1,0:T(8,128)(2,1)} collective-permute-done((bf16[2,256,1024]{2,1,0:T(8,128)(2,1)S(1)}, bf16[2,256,1024]{2,1,0:T(8,128)(2,1)}, u32[]{:S(2)}, u32[]{:S(2)}) %collective-permute-start.1) | collective-permute-done | bytes 1048608 | tf_op jit(solution)/shard_map/group_inputs/ppermute | solution.py:241
  74.9 5.5 collective-permute-start.2
  81.9 53.0 %all_gather.22 = f32[2,4,6,1024]{3,2,1,0:T(8,128)S(1)} all-gather(f32[2,4,6,256]{3,2,1,0:T(8,128)S(1)} %copy.303), channel_id=1, replica_groups=mesh['dp'=4,'frame'=2,'tensor'=4] {'tensor'}, dimensions={3}, use_global_device_ids=true | all-gather | bytes 245760 | tf_op jit(solution)/shard_map/modulation/all_gather | solution.py:181
  140.7 58.1 %collective-permute-done.5 = bf16[2,256,1024]{2,1,0:T(8,128)(2,1)S(1)} collective-permute-done((bf16[2,256,1024]{2,1,0:T(8,128)(2,1)}, bf16[2,256,1024]{2,1,0:T(8,128)(2,1)S(1)}, u32[]{:S(2)}, u32[]{:S(2)}) %collective-permute-start.5) | collective-permute-done | bytes 1048608 | tf_op jit(solution)/shard_map/group_inputs/ppermute | solution.py:242
  200.9 4.5 fusion.11
  214.5 21.1 %forward.2 = (bf16[1024,256]{1,0:T(8,128)(2,1)}, f32[1024,4]{1,0:T(8,128)}) custom-call(bf16[1024,256]{1,0:T(8,128)(2,1)} %get-tuple-element.156.q_ref, bf16[2048,256]{1,0:T(8,128)(2,1)} %maximum_bitcast_fusion.k_ref, bf16[2048,256]{1,0:T(8,128)(2,1)} %maximum_bitcast_fusion.1.v_ref), custom_call_target="tpu_custom_call" | custom-call | flops 2147483648 | bytes 3145728 | tf_op jit(solution)/shard_map/forward/pallas_call | solution.py:85
  235.6 3.3 convolution_convert_fusion.1
  238.9 3.8 all-to-all-start.1
  242.7 3.9 fusion.35
  255.1 21.1 %forward.3 = (bf16[1024,256]{1,0:T(8,128)(2,1)}, f32[1024,4]{1,0:T(8,128)}) custom-call(bf16[1024,256]{1,0:T(8,128)(2,1)} %get-tuple-element.159.q_ref, bf16[2048,256]{1,0:T(8,128)(2,1)} %maximum_bitcast_fusion.3.k_ref, bf16[2048,256]{1,0:T(8,128)(2,1)} %maximum_bitcast_fusion.4.v_ref), custom_call_target="tpu_custom_call" | custom-call | flops 2147483648 | bytes 3145728 | tf_op jit(solution)/shard_map/forward/pallas_call | solution.py:85
  279.5 12.0 %all-to-all-done.1 = bf16[1,4,256,1024]{3,2,0,1:T(8,128)(2,1)S(1)} async-done(((bf16[1,4,256,1024]{3,2,0,1:T(8,128)(2,1)}), bf16[1,4,256,1024]{3,2,0,1:T(8,128)(2,1)S(1)}, u32[]{:S(2)}, u32[]{:S(2)}) %all-to-all-start.1) | async-done | bytes 2097184 | tf_op jit(solution)/shard_map/forward/all_to_all | solution.py:291
  291.5 4.5 all-to-all-start.2
  305.7 38.3 %all-to-all-done.2 = bf16[1,4,256,1024]{3,2,0,1:T(8,128)(2,1)} async-done(((bf16[1,4,256,1024]{3,2,0,1:T(8,128)(2,1)}), bf16[1,4,256,1024]{3,2,0,1:T(8,128)(2,1)}, u32[]{:S(2)}, u32[]{:S(2)}) %all-to-all-start.2) | async-done | bytes 2097184 | tf_op jit(solution)/shard_map/forward/all_to_all | solution.py:291
  348.4 14.5 %reshape.887 = bf16[4,4,256,2,512]{4,3,2,1,0:T(2,128)(2,1)} reshape(bf16[4096,1024]{1,0:T(8,128)(2,1)} %all-gather.9.cloned.1.call-done) | data formatting | bytes 16777216 | tf_op jit(solution)/shard_map/weights/reshape | solution.py:203
  362.9 16.8 %fusion.105 = (bf16[4,4,256,1,512]{4,3,2,1,0:T(2,128)(2,1)S(1)}, bf16[4,4,256,1,512]{4,3,2,1,0:T(2,128)(2,1)S(1)}) fusion(bf16[4,4,256,2,512]{4,3,2,1,0:T(2,128)(2,1)} %reshape.887), kind=kLoop, calls=%fused_computation.268 | loop fusion | bytes 16777216 | tf_op jit(solution)/shard_map/weights/slice | solution.py:205
  379.7 5.3 copy_bitcast_fusion
  385.0 5.4 copy.258
  397.2 4.4 fusion.69
  401.6 6.9 fusion.18
  418.3 5.8 fusion.67
  425.3 8.3 fusion.25
  446.5 23.3 %all-gather.11.cloned.1.call-done = bf16[1,1024,1024]{2,1,0:T(8,128)(2,1)} async-done(((bf16[1,256,1024]{2,1,0:T(8,128)(2,1)}), bf16[1,1024,1024]{2,1,0:T(8,128)(2,1)}) %all-gather.11.cloned.1.call-update) | async-done | bytes 2097168 | tf_op jit(solution)/shard_map/backward_attention/all_gather | solution.py:285
  473.0 32.1 %backward_attention.2 = (f32[1024,256]{1,0:T(8,128)}, f32[2048,256]{1,0:T(8,128)}, f32[2048,256]{1,0:T(8,128)}) custom-call(bf16[1024,256]{1,0:T(8,128)(2,1)} %get-tuple-element.156.q_ref, bf16[2048,256]{1,0:T(8,128)(2,1)} %maximum_bitcast_fusion.k_ref, bf16[2048,256]{1,0:T(8,128)(2,1)} %maximum_bitcast_fusion.1.v_ref, bf16[1024,256]{1,0:T(8,128)(2,1)} %fusion.43.g_ref, ...), custom_call_target="tpu_custom_call" | custom-call | flops 5368709120 | bytes 8912896 | tf_op jit(solution)/shard_map/backward_attention/pallas_call | solution.py:118
  509.9 5.8 all-gather.13.cloned.1.call-done
  518.9 32.5 %backward_attention.3 = (f32[1024,256]{1,0:T(8,128)}, f32[2048,256]{1,0:T(8,128)}, f32[2048,256]{1,0:T(8,128)}) custom-call(bf16[1024,256]{1,0:T(8,128)(2,1)} %get-tuple-element.159.q_ref, bf16[2048,256]{1,0:T(8,128)(2,1)} %maximum_bitcast_fusion.3.k_ref, bf16[2048,256]{1,0:T(8,128)(2,1)} %maximum_bitcast_fusion.4.v_ref, bf16[1024,256]{1,0:T(8,128)(2,1)} %fusion.46.g_ref, ...), custom_call_target="tpu_custom_call" | custom-call | flops 5368709120 | bytes 8912896 | tf_op jit(solution)/shard_map/backward_attention/pallas_call | solution.py:118
  564.5 4.5 fusion.68
  569.0 7.2 fusion.65
  576.2 5.8 add_convert_fusion.1
  582.0 8.2 reshape.901
  590.2 5.3 copy.270
  595.5 6.7 add_convert_fusion
  602.2 7.8 reshape.902
  610.0 5.1 copy.271
  615.2 8.0 pad_maximum_fusion
  627.9 3.7 all-to-all-start.3
  631.6 4.7 bitcast_convert_fusion
  636.4 96.5 %all-to-all-done.3 = bf16[1,4,256,1024]{3,2,0,1:T(8,128)(2,1)S(1)} async-done(((bf16[1,4,256,1024]{3,2,0,1:T(8,128)(2,1)}), bf16[1,4,256,1024]{3,2,0,1:T(8,128)(2,1)S(1)}, u32[]{:S(2)}, u32[]{:S(2)}) %all-to-all-start.3) | async-done | bytes 2097184 | tf_op jit(solution)/shard_map/backward_attention/all_to_all | solution.py:291
  732.9 4.8 all-to-all-start.4
  742.3 91.1 %all-to-all-done.4 = bf16[1,4,256,1024]{3,2,0,1:T(8,128)(2,1)} async-done(((bf16[1,4,256,1024]{3,2,0,1:T(8,128)(2,1)}), bf16[1,4,256,1024]{3,2,0,1:T(8,128)(2,1)}, u32[]{:S(2)}, u32[]{:S(2)}) %all-to-all-start.4) | async-done | bytes 2097184 | tf_op jit(solution)/shard_map/backward_attention/all_to_all | solution.py:291
  839.8 3.4 reshape.1071
  843.1 3.9 all-to-all-start.5
  863.1 11.4 %all-gather = f32[16,4,1,6,256]{4,1,0,3,2:T(4,128)S(1)} all-gather(f32[2,4,1,6,256]{4,1,0,3,2:T(4,128)S(1)} %bitcast.377), channel_id=2, replica_groups=mesh['dp'=4,'frame'=2,'tensor'=4] {'dp','frame'}, dimensions={0}, use_global_device_ids=true | all-gather | bytes 442368 | tf_op jit(solution)/shard_map/ada_grad/all_gather | solution.py:420
  874.5 15.1 %reduce-scatter.5.cloned.1.call-done = bf16[1,256,1024]{2,1,0:T(8,128)(2,1)} async-done(((bf16[16,256,1024]{2,1,0:T(8,128)(2,1)}), bf16[1,256,1024]{2,1,0:T(8,128)(2,1)}) %reduce-scatter.5.cloned.1.call-update) | async-done | bytes 524304 | tf_op jit(solution)/shard_map/weight_grads/reduce_scatter | solution.py:218
  (354 shorter events, 148.4 us)
Async XLA Ops:
  7.2 198.2 %all-gather.7.cloned.1.call-start = ((), (), s32[]{:S(2)}) async-start(), calls=%async_computation.8 | async-start | bytes 2359296 | tf_op jit(solution)/shard_map/weights/all_gather | solution.py:253
  10.1 338.3 %all-gather.9.cloned.1.call-start = ((), (), s32[]{:S(2)}) async-start(), calls=%async_computation.9 | async-start | bytes 8912896 | tf_op jit(solution)/shard_map/weights/all_gather | solution.py:202
  10.1 27.7 %collective-permute-start = (bf16[2,256,1024]{2,1,0:T(8,128)(2,1)}, bf16[2,256,1024]{2,1,0:T(8,128)(2,1)S(1)}, u32[]{:S(2)}, u32[]{:S(2)}) collective-permute-start(bf16[2,256,1024]{2,1,0:T(8,128)(2,1)} %bitcast.341), channel_id=1, source_target_pairs={{0,1},{1,2},{2,3},{4,5},{5,6},{6,7},{8,9},{9,10},{10,11},{12,13},{... | collective-permute-start | bytes 3145736 | tf_op jit(solution)/shard_map/group_inputs/ppermute | solution.py:241
  16.4 3.1 collective-permute-start.9
  16.4 42.2 %collective-permute-start.3 = (bf16[2,256,1024]{2,1,0:T(8,128)(2,1)}, bf16[2,256,1024]{2,1,0:T(8,128)(2,1)S(1)}, u32[]{:S(2)}, u32[]{:S(2)}) collective-permute-start(bf16[2,256,1024]{2,1,0:T(8,128)(2,1)} %bitcast.342), channel_id=1, source_target_pairs={{1,0},{2,1},{3,2},{5,4},{6,5},{7,6},{9,8},{10,9},{11,10},{13,12},{... | collective-permute-start | bytes 3145736 | tf_op jit(solution)/shard_map/group_inputs/ppermute | solution.py:242
  18.9 1.5 collective-permute-start.10
  37.8 37.1 %collective-permute-start.1 = (bf16[2,256,1024]{2,1,0:T(8,128)(2,1)S(1)}, bf16[2,256,1024]{2,1,0:T(8,128)(2,1)}, u32[]{:S(2)}, u32[]{:S(2)}) collective-permute-start(bf16[2,256,1024]{2,1,0:T(8,128)(2,1)S(1)} %collective-permute-done), channel_id=1, source_target_pairs={{0,1},{1,2},{2,3},{4,5},{5,6},{6,7},{8,9},{9,10},{10,11},{12,13},{... | collective-permute-start | bytes 3145736 | tf_op jit(solution)/shard_map/group_inputs/ppermute | solution.py:241
  55.2 25.2 %all-to-all-start = ((f32[8,2,4,6,256]{4,2,3,1,0:T(4,128)}), f32[8,2,4,6,256]{4,2,3,1,0:T(4,128)S(1)}, u32[]{:S(2)}, u32[]{:S(2)}) async-start(f32[8,2,4,6,256]{4,2,3,1,0:T(4,128)} %fusion.75), calls=%async_computation | async-start | bytes 786432 | tf_op jit(solution)/shard_map/modulation/all_to_all | solution.py:179
  58.6 80.6 %copy-start.19 = (bf16[2,1,256,1024]{3,2,1,0:T(8,128)(2,1)S(1)}, bf16[2,1,256,1024]{3,2,1,0:T(8,128)(2,1)}, u32[]{:S(2)}) copy-start(bf16[2,1,256,1024]{3,2,1,0:T(8,128)(2,1)} %param.12) | copy-start | bytes 3145732
  58.7 76.4 %collective-permute-start.4 = (bf16[2,256,1024]{2,1,0:T(8,128)(2,1)S(1)}, bf16[2,256,1024]{2,1,0:T(8,128)(2,1)}, u32[]{:S(2)}, u32[]{:S(2)}) collective-permute-start(bf16[2,256,1024]{2,1,0:T(8,128)(2,1)S(1)} %collective-permute-done.3), channel_id=1, source_target_pairs={{1,0},{2,1},{3,2},{5,4},{6,5},{7,6},{9,8},{10,9},{11,10},{13,12},{... | collective-permute-start | bytes 3145736 | tf_op jit(solution)/shard_map/group_inputs/ppermute | solution.py:242
  74.9 61.6 %collective-permute-start.2 = (bf16[2,256,1024]{2,1,0:T(8,128)(2,1)}, bf16[2,256,1024]{2,1,0:T(8,128)(2,1)}, u32[]{:S(2)}, u32[]{:S(2)}) collective-permute-start(bf16[2,256,1024]{2,1,0:T(8,128)(2,1)} %collective-permute-done.1), channel_id=1, source_target_pairs={{0,1},{1,2},{2,3},{4,5},{5,6},{6,7},{8,9},{9,10},{10,11},{12,13},{... | collective-permute-start | bytes 3145736 | tf_op jit(solution)/shard_map/group_inputs/ppermute | solution.py:241
  135.1 63.7 %collective-permute-start.5 = (bf16[2,256,1024]{2,1,0:T(8,128)(2,1)}, bf16[2,256,1024]{2,1,0:T(8,128)(2,1)S(1)}, u32[]{:S(2)}, u32[]{:S(2)}) collective-permute-start(bf16[2,256,1024]{2,1,0:T(8,128)(2,1)} %collective-permute-done.4), channel_id=1, source_target_pairs={{1,0},{2,1},{3,2},{5,4},{6,5},{7,6},{9,8},{10,9},{11,10},{13,12},{... | collective-permute-start | bytes 3145736 | tf_op jit(solution)/shard_map/group_inputs/ppermute | solution.py:242
  210.5 1.9 collective-permute-start.7
  210.5 2.9 collective-permute-start.6
  238.9 52.6 %all-to-all-start.1 = ((bf16[1,4,256,1024]{3,2,0,1:T(8,128)(2,1)}), bf16[1,4,256,1024]{3,2,0,1:T(8,128)(2,1)S(1)}, u32[]{:S(2)}, u32[]{:S(2)}) async-start(bf16[1,4,256,1024]{3,2,0,1:T(8,128)(2,1)} %bitcast.340), calls=%async_computation.1 | async-start | bytes 4194304 | tf_op jit(solution)/shard_map/forward/all_to_all | solution.py:291
  247.5 3.4 collective-permute-start.13
  247.6 5.3 collective-permute-start.12
  291.5 52.5 %all-to-all-start.2 = ((bf16[1,4,256,1024]{3,2,0,1:T(8,128)(2,1)}), bf16[1,4,256,1024]{3,2,0,1:T(8,128)(2,1)}, u32[]{:S(2)}, u32[]{:S(2)}) async-start(bf16[1,4,256,1024]{3,2,0,1:T(8,128)(2,1)} %bitcast.339), calls=%async_computation.2 | async-start | bytes 4194304 | tf_op jit(solution)/shard_map/forward/all_to_all | solution.py:291
  296.0 173.8 %all-gather.11.cloned.1.call-start = ((), (), s32[]{:S(2)}) async-start(), calls=%async_computation.10 | async-start | bytes 2621440 | tf_op jit(solution)/shard_map/backward_attention/all_gather | solution.py:285
  300.6 101.1 %collective-permute-start.16 = (bf16[1,256,1024]{2,1,0:T(8,128)(2,1)}, bf16[1,256,1024]{2,1,0:T(8,128)(2,1)}, u32[]{:S(2)}, u32[]{:S(2)}) collective-permute-start(bf16[1,256,1024]{2,1,0:T(8,128)(2,1)} %multiply_convert_fusion.5), channel_id=1, source_target_pairs={{0,4},{4,0},{1,5},{5,1},{2,6},{6,2},{3,7},{7,3},{8,12},{12,8},{9,1... | collective-permute-start | bytes 1572872 | tf_op jit(solution)/shard_map/backward_ffn/ppermute | solution.py:266
  305.2 92.0 %collective-permute-start.8 = (bf16[1,256,1024]{2,1,0:T(8,128)(2,1)}, bf16[1,256,1024]{2,1,0:T(8,128)(2,1)}, u32[]{:S(2)}, u32[]{:S(2)}) collective-permute-start(bf16[1,256,1024]{2,1,0:T(8,128)(2,1)} %add_convert_fusion.12), channel_id=1, source_target_pairs={{0,4},{4,0},{1,5},{5,1},{2,6},{6,2},{3,7},{7,3},{8,12},{12,8},{9,1... | collective-permute-start | bytes 1572872 | tf_op jit(solution)/shard_map/forward/ppermute | solution.py:266
  348.4 69.9 %collective-permute-start.14 = (bf16[1,256,1024]{2,1,0:T(8,128)(2,1)}, bf16[1,256,1024]{2,1,0:T(8,128)(2,1)}, u32[]{:S(2)}, u32[]{:S(2)}) collective-permute-start(bf16[1,256,1024]{2,1,0:T(8,128)(2,1)} %add_convert_fusion.10), channel_id=1, source_target_pairs={{0,4},{4,0},{1,5},{5,1},{2,6},{6,2},{3,7},{7,3},{8,12},{12,8},{9,1... | collective-permute-start | bytes 1572872 | tf_op jit(solution)/shard_map/forward/ppermute | solution.py:266
  411.0 3.5 collective-permute-start.17
  414.4 2.0 collective-permute-start.11
  418.1 7.2 collective-permute-start.20
  425.0 90.7 %all-gather.13.cloned.1.call-start = ((), (), s32[]{:S(2)}) async-start(), calls=%async_computation.11 | async-start | bytes 2621440 | tf_op jit(solution)/shard_map/backward_attention/all_gather | solution.py:285
  436.1 4.8 collective-permute-start.21
  440.5 2.0 collective-permute-start.15
  446.1 401.0 %reduce-scatter.7.cloned.1.call-start = ((), (), s32[]{:S(2)}) async-start(), calls=%async_computation.13 | async-start | bytes 2359296
  507.1 2.0 collective-permute-start.18
  507.5 2.2 collective-permute-start.19
  553.3 3.5 collective-permute-start.22
  553.8 3.3 collective-permute-start.23
  564.2 325.4 %reduce-scatter.5.cloned.1.call-start = ((), (), s32[]{:S(2)}) async-start(), calls=%async_computation.12 | async-start | bytes 8912896 | tf_op jit(solution)/shard_map/weight_grads/reduce_scatter | solution.py:218
  627.9 105.0 %all-to-all-start.3 = ((bf16[1,4,256,1024]{3,2,0,1:T(8,128)(2,1)}), bf16[1,4,256,1024]{3,2,0,1:T(8,128)(2,1)S(1)}, u32[]{:S(2)}, u32[]{:S(2)}) async-start(bf16[1,4,256,1024]{3,2,0,1:T(8,128)(2,1)} %bitcast.359), calls=%async_computation.3 | async-start | bytes 4194304 | tf_op jit(solution)/shard_map/backward_attention/all_to_all | solution.py:291
  636.4 101.2 %copy-start.58 = (f32[256]{0:T(256)S(1)}, f32[256]{0:T(256)}, u32[]{:S(2)}) copy-start(f32[256]{0:T(256)} %get-tuple-element.150) | copy-start | bytes 3076
  636.4 101.3 %copy-start.59 = (f32[256]{0:T(256)S(1)}, f32[256]{0:T(256)}, u32[]{:S(2)}) copy-start(f32[256]{0:T(256)} %get-tuple-element.127) | copy-start | bytes 3076
  636.4 101.3 %copy-start.32 = (bf16[1,256,1024]{2,1,0:T(8,128)(2,1)S(1)}, bf16[1,256,1024]{2,1,0:T(8,128)(2,1)}, u32[]{:S(2)}) copy-start(bf16[1,256,1024]{2,1,0:T(8,128)(2,1)} %get-tuple-element.147) | copy-start | bytes 1572868
  636.4 101.3 %copy-start.35 = (bf16[1,256,1024]{2,1,0:T(8,128)(2,1)S(1)}, bf16[1,256,1024]{2,1,0:T(8,128)(2,1)}, u32[]{:S(2)}) copy-start(bf16[1,256,1024]{2,1,0:T(8,128)(2,1)} %get-tuple-element.162) | copy-start | bytes 1572868
  732.9 100.5 %all-to-all-start.4 = ((bf16[1,4,256,1024]{3,2,0,1:T(8,128)(2,1)}), bf16[1,4,256,1024]{3,2,0,1:T(8,128)(2,1)}, u32[]{:S(2)}, u32[]{:S(2)}) async-start(bf16[1,4,256,1024]{3,2,0,1:T(8,128)(2,1)} %bitcast.358), calls=%async_computation.4 | async-start | bytes 4194304 | tf_op jit(solution)/shard_map/backward_attention/all_to_all | solution.py:291
  737.7 98.5 %copy-start.56 = (f32[256]{0:T(256)}, f32[256]{0:T(256)S(1)}, u32[]{:S(2)}) copy-start(f32[256]{0:T(256)S(1)} %add_rsqrt_fusion.2) | copy-start | bytes 3076
  737.7 98.4 %copy-start.57 = (f32[256]{0:T(256)}, f32[256]{0:T(256)S(1)}, u32[]{:S(2)}) copy-start(f32[256]{0:T(256)S(1)} %add_rsqrt_fusion.3) | copy-start | bytes 3076
  738.8 98.3 %copy-start.3 = (f32[2,256,1024]{2,1,0:T(8,128)S(1)}, f32[2,256,1024]{2,1,0:T(8,128)}, u32[]{:S(2)}) copy-start(f32[2,256,1024]{2,1,0:T(8,128)} %copy-done.2) | copy-start | bytes 6291460
  738.8 98.3 %copy-start.50 = (f32[1,1,1,1024]{3,1,2,0:T(1,128)S(1)}, f32[1,1,1,1024]{3,1,2,0:T(1,128)}, u32[]{:S(2)}) copy-start(f32[1,1,1,1024]{3,1,2,0:T(1,128)} %get-tuple-element.181) | copy-start | bytes 12292
  738.8 98.3 %copy-start.53 = (f32[256]{0:T(256)S(1)}, f32[256]{0:T(256)}, u32[]{:S(2)}) copy-start(f32[256]{0:T(256)} %copy-done.52) | copy-start | bytes 3076
  738.8 98.3 %copy-start.55 = (f32[256]{0:T(256)S(1)}, f32[256]{0:T(256)}, u32[]{:S(2)}) copy-start(f32[256]{0:T(256)} %copy-done.54) | copy-start | bytes 3076
  843.1 15.8 %all-to-all-start.5 = ((f32[4,1,3072]{2,1,0:T(1,128)}), f32[4,1,3072]{2,1,0:T(1,128)}, u32[]{:S(2)}, u32[]{:S(2)}) async-start(f32[4,1,3072]{2,1,0:T(1,128)} %reshape.1071), calls=%async_computation.6 | async-start | bytes 98304 | tf_op jit(solution)/shard_map/ada_grad/all_to_all | solution.py:417
  890.9 1.8 collective-permute-start.24
  (58 other events, 431.7 us)
Sparse Core Ops, SparseCore 0:
  10.5 30.8 all-gather.6
  44.7 151.9 all-gather.8
  425.1 44.6 all-gather.10
  471.2 44.4 all-gather.12
  564.3 39.9 reduce-scatter.6
  623.3 266.1 reduce-scatter.4

commit v8 on v7

--- a/solution.py
+++ b/solution.py
@@ -230,35 +230,17 @@
             ordered[:, :, k].reshape(rows_here, halves * half) for k in range(len(totals))
         )
 
-    def line_gather(values):
-        if groups == 1:
-            return values[:, None]
-        rightward = [(i, i + 1) for i in range(groups - 1)]
-        leftward = [(i + 1, i) for i in range(groups - 1)]
-        right, left = values, values
-        before, after = [], []
-        for _ in range(groups - 1):
-            right = lax.ppermute(right, "tensor", rightward)
-            left = lax.ppermute(left, "tensor", leftward)
-            before.insert(0, right)
-            after.append(left)
-        stacked = jnp.stack(before + [values] + after, axis=1)
-        start = groups - 1 - lax.axis_index("tensor")
-        return lax.dynamic_slice_in_dim(stacked, start, groups, axis=1)
-
     with jax.named_scope("weights"):
-        attention_shards = jnp.concatenate(
-            [qkv_weight.reshape(rows_here, 3 * local_width), out_weight], axis=1
-        )
-        attention_weights = lax.all_gather(attention_shards, ("dp", "frame"), axis=0, tiled=True)
-        joint_weight = attention_weights[:, : 3 * local_width].reshape(model_width, 3, local_width)
-        mixer_weight = attention_weights[:, 3 * local_width :]
+        joint_weight, mixer_weight = (
+            lax.all_gather(w, ("dp", "frame"), axis=0, tiled=True)
+            for w in (qkv_weight, out_weight)
+        )
         upward_weight, downward_weight = hidden_half((up_weight, down_weight))
 
     residual = tokens[:, 0].astype(jnp.float32)
     upstream = out_grad[:, 0].astype(jnp.float32)
     with jax.named_scope("group_inputs"):
-        group_tokens = line_gather(tokens[:, 0]).reshape(clips, groups * patches, model_width)
+        group_tokens = lax.all_gather(tokens[:, 0], "tensor", axis=1, tiled=True)
         group_upstream = None
     def gather_halves(values):
         if halves != 2:
@@ -427,14 +409,12 @@
         )
 
     with jax.named_scope("weight_grads"):
-        attention_totals = jnp.concatenate(
-            [joint_total.reshape(model_width, 3 * local_width), mixer_total], axis=1
-        )
-        attention_sums = lax.psum_scatter(
-            attention_totals.astype(jnp.bfloat16), ("dp", "frame"), scatter_dimension=0, tiled=True
-        ).astype(jnp.float32)
-        joint_sum = attention_sums[:, : 3 * local_width].reshape(rows_here, 3, local_width)
-        mixer_sum = attention_sums[:, 3 * local_width :]
+        joint_sum, mixer_sum = (
+            lax.psum_scatter(
+                total.astype(jnp.bfloat16), ("dp", "frame"), scatter_dimension=0, tiled=True
+            ).astype(jnp.float32)
+            for total in (joint_total, mixer_total)
+        )
         up_sum, down_sum = hidden_half_back((up_total, down_total))
         summed = (joint_sum, mixer_sum, up_sum, down_sum)
     result = output[:, None]

time: 908 us -> 884 us (0.974)
  starting transfers between devices: 49.7 us -> 27.2 us
  waiting for transfers between devices: 378 us -> 396 us
  local copies, waits for them, and re-layouts: 117 us -> 99.8 us
  blocking collectives: 73.3 us -> 61.9 us
    ppermute x6 -> x0, waiting for transfers between devices: 90.1 us -> none  [the longest x3 58.1 us: line_gather(): left = lax.ppermute(left, 'tensor', leftward)]
    all_gather x1 -> x2, waiting for transfers between devices: 0.01 us -> 58.2 us  [the longest x1 42.2 us: on_device(): group_tokens = lax.all_gather(tokens[:, 0], 'tensor', axis=1, tiled=True)]
    all_gather x1, blocking collectives: 53 us -> 18.3 us  [on_device(): group_mod = lax.all_gather(summed_mod, 'tensor', axis=3, tiled=True)]
    all_to_all x4, waiting for transfers between devices: 238 us -> 272 us  [scatter_tokens(): received = lax.all_to_all(parts, 'tensor', 1, 1, tiled=True)]
    reduce_scatter x1, waiting for transfers between devices: 15.1 us -> 39.8 us  [hidden_half_back(): lax.psum_scatter(blocks.reshape(replicas * groups, halves * rows_here, le...]
    ppermute x6 -> x0, starting transfers between devices: 19.9 us -> none  [the longest x3 15.7 us: line_gather(): right = lax.ppermute(right, 'tensor', rightward)]
    unnamed x162 -> x147, local copies, waits for them, and re-layouts: 33.9 us -> 18.6 us
    all_to_all x0 -> x1, blocking collectives: none -> 10.9 us  [on_device(): lax.all_to_all(partial_mod, ('dp', 'frame'), 0, 0, tiled=True)]
  transfers between devices with their start and end apart: 37 -> 32, of which waited for: 16 -> 15; matrix products, arithmetic and copies ran while one was open for 28% -> 29% of each run, Pallas kernels for 8% -> 8%
where the time goes in v8:
time: 884 us; the launch traced here: 875 us
  waiting for transfers between devices  396 us (45%)
  Pallas kernels  107 us (12%)
  local copies, waits for them, and re-layouts  99.8 us (11%)
  matrix products  96.9 us (11%)
  other arithmetic  70.7 us (8%)
  blocking collectives  61.9 us (7%)
  starting transfers between devices  27.2 us (3%)
  between operations  15.8 us (2%)
    all_to_all x4, waiting for transfers between devices, scatter_tokens(): received = lax.all_to_all(parts, 'tensor', 1, 1, tiled=True)  272 us
    pallas_call x2, Pallas kernels, attention_backward(): pl.pallas_call(functools.partial(_backward_kernel, heads, HEAD_DIM ** (-0...  64.7 us
    pallas_call x2, Pallas kernels, attention_forward(): pl.pallas_call(functools.partial(_forward_kernel, heads, HEAD_DIM ** (-0....  42.2 us
    all_gather x1, waiting for transfers between devices, on_device(): group_tokens = lax.all_gather(tokens[:, 0], 'tensor', axis=1, tiled=True)  42.2 us
    reduce_scatter x1, waiting for transfers between devices, hidden_half_back(): lax.psum_scatter(blocks.reshape(replicas * groups, halves * rows_here, le...  39.8 us
    reshape x4, local copies, waits for them, and re-layouts, hidden_half_back(): total.reshape(replicas, halves * rows_here, groups, half)  26.2 us
    all_gather x2, waiting for transfers between devices, gather_tokens(): return lax.all_gather(values, 'tensor', axis=1, tiled=True)  19.3 us
    unnamed x147, local copies, waits for them, and re-layouts  18.6 us
  transfers between devices with their start and end apart: 32, of which 15 were waited for; matrix products, arithmetic and copies ran while one was open for 29% of the time, Pallas kernels for 8%

profile of v8, /device:TPU:0, one launch (start us, length us, event | category | flops | bytes accessed | tf_op | source)
XLA Modules:
  0.0 875.5 jit_solution(9307204763049811112)
XLA Ops:
  14.2 10.1 %all-gather.2 = s32[8,2,4]{2,1,0:T(2,128)S(1)} all-gather(s32[1,2,4]{2,1,0:T(2,128)S(1)} %bitcast.477), channel_id=1, replica_groups=mesh['dp'=4,'frame'=2,'tensor'=4] {'dp','frame'}, dimensions={0}, use_global_device_ids=true | all-gather | bytes 288 | tf_op jit(solution)/shard_map/modulation/all_gather | solution.py:168
  25.6 10.9 %all_to_all.43 = f32[8,2,4,6,256]{4,2,3,1,0:T(4,128)S(1)} all-to-all(f32[8,2,4,6,256]{4,2,3,1,0:T(4,128)S(1)} %fusion.81), channel_id=1, replica_groups=mesh['dp'=4,'frame'=2,'tensor'=4] {'dp','frame'}, dimensions={0} | all-to-all | bytes 786432 | tf_op jit(solution)/shard_map/modulation/all_to_all | solution.py:179
  36.5 18.3 %all_gather.28 = f32[2,4,6,1024]{3,2,1,0:T(8,128)S(1)} all-gather(f32[2,4,6,256]{3,2,1,0:T(8,128)S(1)} %copy.233), channel_id=1, replica_groups=mesh['dp'=4,'frame'=2,'tensor'=4] {'tensor'}, dimensions={3}, use_global_device_ids=true | all-gather | bytes 245760 | tf_op jit(solution)/shard_map/modulation/all_gather | solution.py:181
  55.0 42.2 %all-gather.17.cloned.1.call-done = bf16[2,1,1024,1024]{3,2,1,0:T(8,128)(2,1)} async-done(((bf16[2,1,256,1024]{3,2,1,0:T(8,128)(2,1)}), bf16[2,1,1024,1024]{3,2,1,0:T(8,128)(2,1)}) %all-gather.17.cloned.1.call-update) | async-done | bytes 4194320 | tf_op jit(solution)/shard_map/group_inputs/all_gather | solution.py:243
  107.2 16.0 %all-gather.9.cloned.1.call-done = bf16[1024,3,256]{2,0,1:T(8,128)(2,1)} async-done(((bf16[128,3,256]{2,0,1:T(8,128)(2,1)}), bf16[1024,3,256]{2,0,1:T(8,128)(2,1)}) %all-gather.9.cloned.1.call-update) | async-done | bytes 1572880 | tf_op jit(solution)/shard_map/weights/all_gather | solution.py:235
  123.2 3.2 fusion.39
  127.9 10.3 %all_gather.31 = bf16[1024,256]{1,0:T(8,128)(2,1)S(1)} all-gather(bf16[128,256]{1,0:T(8,128)(2,1)S(1)} %copy-done.51), channel_id=1, replica_groups=mesh['dp'=4,'frame'=2,'tensor'=4] {'dp','frame'}, dimensions={0}, use_global_device_ids=true | all-gather | bytes 589824 | tf_op jit(solution)/shard_map/weights/all_gather | solution.py:235
  140.4 21.1 %forward.3 = (bf16[1024,256]{1,0:T(8,128)(2,1)}, f32[1024,4]{1,0:T(8,128)}) custom-call(bf16[1024,256]{1,0:T(8,128)(2,1)} %get-tuple-element.162.q_ref, bf16[2048,256]{1,0:T(8,128)(2,1)} %maximum_bitcast_fusion.3.k_ref, bf16[2048,256]{1,0:T(8,128)(2,1)} %maximum_bitcast_fusion.4.v_ref), custom_call_target="tpu_custom_call" | custom-call | flops 2147483648 | bytes 3145728 | tf_op jit(solution)/shard_map/forward/pallas_call | solution.py:85
  161.6 3.2 convolution_convert_fusion
  164.7 4.8 all-to-all-start.2
  169.5 3.9 fusion.38
  178.3 21.1 %forward.2 = (bf16[1024,256]{1,0:T(8,128)(2,1)}, f32[1024,4]{1,0:T(8,128)}) custom-call(bf16[1024,256]{1,0:T(8,128)(2,1)} %get-tuple-element.159.q_ref, bf16[2048,256]{1,0:T(8,128)(2,1)} %maximum_bitcast_fusion.k_ref, bf16[2048,256]{1,0:T(8,128)(2,1)} %maximum_bitcast_fusion.1.v_ref), custom_call_target="tpu_custom_call" | custom-call | flops 2147483648 | bytes 3145728 | tf_op jit(solution)/shard_map/forward/pallas_call | solution.py:85
  199.4 3.2 convolution_convert_fusion.1
  202.6 55.0 %all-to-all-done.2 = bf16[1,4,256,1024]{3,2,0,1:T(8,128)(2,1)S(1)} async-done(((bf16[1,4,256,1024]{3,2,0,1:T(8,128)(2,1)}), bf16[1,4,256,1024]{3,2,0,1:T(8,128)(2,1)S(1)}, u32[]{:S(2)}, u32[]{:S(2)}) %all-to-all-start.2) | async-done | bytes 2097184 | tf_op jit(solution)/shard_map/forward/all_to_all | solution.py:273
  257.6 4.5 all-to-all-start.1
  263.8 3.6 convert_element_type.249
  272.7 44.7 %all-to-all-done.1 = bf16[1,4,256,1024]{3,2,0,1:T(8,128)(2,1)} async-done(((bf16[1,4,256,1024]{3,2,0,1:T(8,128)(2,1)}), bf16[1,4,256,1024]{3,2,0,1:T(8,128)(2,1)}, u32[]{:S(2)}, u32[]{:S(2)}) %all-to-all-start.1) | async-done | bytes 2097184 | tf_op jit(solution)/shard_map/forward/all_to_all | solution.py:273
  325.4 14.5 %reshape.897 = bf16[4,4,256,2,512]{4,3,2,1,0:T(2,128)(2,1)} reshape(bf16[4096,1024]{1,0:T(8,128)(2,1)} %all-gather.11.cloned.1.call-done) | data formatting | bytes 16777216 | tf_op jit(solution)/shard_map/weights/reshape | solution.py:203
  340.0 16.8 %fusion.107 = (bf16[4,4,256,1,512]{4,3,2,1,0:T(2,128)(2,1)S(1)}, bf16[4,4,256,1,512]{4,3,2,1,0:T(2,128)(2,1)S(1)}) fusion(bf16[4,4,256,2,512]{4,3,2,1,0:T(2,128)(2,1)} %reshape.897), kind=kLoop, calls=%fused_computation.260 | loop fusion | bytes 16777216 | tf_op jit(solution)/shard_map/weights/slice | solution.py:205
  356.8 5.1 copy_bitcast_fusion
  361.9 5.4 copy.197
  369.5 3.2 copy.198
  376.6 7.2 fusion.20
  393.4 5.6 fusion.73
  400.1 8.3 fusion.27
  421.3 8.3 fusion.71
  429.6 14.4 %all-gather.13.cloned.1.call-done = bf16[1,1024,1024]{2,1,0:T(8,128)(2,1)} async-done(((bf16[1,256,1024]{2,1,0:T(8,128)(2,1)}), bf16[1,1024,1024]{2,1,0:T(8,128)(2,1)}) %all-gather.13.cloned.1.call-update) | async-done | bytes 2097168 | tf_op jit(solution)/shard_map/backward_attention/all_gather | solution.py:267
  447.0 32.1 %backward_attention.2 = (f32[1024,256]{1,0:T(8,128)}, f32[2048,256]{1,0:T(8,128)}, f32[2048,256]{1,0:T(8,128)}) custom-call(bf16[1024,256]{1,0:T(8,128)(2,1)} %get-tuple-element.159.q_ref, bf16[2048,256]{1,0:T(8,128)(2,1)} %maximum_bitcast_fusion.k_ref, bf16[2048,256]{1,0:T(8,128)(2,1)} %maximum_bitcast_fusion.1.v_ref, bf16[1024,256]{1,0:T(8,128)(2,1)} %fusion.47.g_ref, ...), custom_call_target="tpu_custom_call" | custom-call | flops 5368709120 | bytes 8912896 | tf_op jit(solution)/shard_map/backward_attention/pallas_call | solution.py:118
  484.9 4.9 all-gather.15.cloned.1.call-done
  493.0 32.6 %backward_attention.3 = (f32[1024,256]{1,0:T(8,128)}, f32[2048,256]{1,0:T(8,128)}, f32[2048,256]{1,0:T(8,128)}) custom-call(bf16[1024,256]{1,0:T(8,128)(2,1)} %get-tuple-element.162.q_ref, bf16[2048,256]{1,0:T(8,128)(2,1)} %maximum_bitcast_fusion.3.k_ref, bf16[2048,256]{1,0:T(8,128)(2,1)} %maximum_bitcast_fusion.4.v_ref, bf16[1024,256]{1,0:T(8,128)(2,1)} %fusion.50.g_ref, ...), custom_call_target="tpu_custom_call" | custom-call | flops 5368709120 | bytes 8912896 | tf_op jit(solution)/shard_map/backward_attention/pallas_call | solution.py:118
  540.5 4.4 fusion.74
  544.9 5.8 add_convert_fusion.1
  550.6 7.8 reshape.909
  558.5 5.2 copy.206
  563.7 6.8 add_convert_fusion
  570.4 7.9 reshape.910
  578.3 5.3 copy.207
  583.6 8.0 pad_maximum_fusion
  591.6 4.6 bitcast_convert_fusion.1
  596.2 4.0 all-to-all-start.3
  600.2 4.8 bitcast_convert_fusion
  605.0 90.0 %all-to-all-done.3 = bf16[1,4,256,1024]{3,2,0,1:T(8,128)(2,1)S(1)} async-done(((bf16[1,4,256,1024]{3,2,0,1:T(8,128)(2,1)}), bf16[1,4,256,1024]{3,2,0,1:T(8,128)(2,1)S(1)}, u32[]{:S(2)}, u32[]{:S(2)}) %all-to-all-start.3) | async-done | bytes 2097184 | tf_op jit(solution)/shard_map/backward_attention/all_to_all | solution.py:273
  695.0 4.6 all-to-all-start.4
  707.1 81.9 %all-to-all-done.4 = bf16[1,4,256,1024]{3,2,0,1:T(8,128)(2,1)} async-done(((bf16[1,4,256,1024]{3,2,0,1:T(8,128)(2,1)}), bf16[1,4,256,1024]{3,2,0,1:T(8,128)(2,1)}, u32[]{:S(2)}, u32[]{:S(2)}) %all-to-all-start.4) | async-done | bytes 2097184 | tf_op jit(solution)/shard_map/backward_attention/all_to_all | solution.py:273
  794.8 3.4 reshape.1087
  798.2 3.3 all-to-all-start.5
  810.9 12.4 %all-gather.1 = f32[16,4,1,6,256]{4,1,0,3,2:T(4,128)S(1)} all-gather(f32[2,4,1,6,256]{4,1,0,3,2:T(4,128)S(1)} %bitcast.437), channel_id=3, replica_groups=mesh['dp'=4,'frame'=2,'tensor'=4] {'dp','frame'}, dimensions={0}, use_global_device_ids=true | all-gather | bytes 442368 | tf_op jit(solution)/shard_map/ada_grad/all_gather | solution.py:402
  823.3 39.8 %reduce-scatter.8.cloned.1.call-done = bf16[1,256,1024]{2,1,0:T(8,128)(2,1)} async-done(((bf16[16,256,1024]{2,1,0:T(8,128)(2,1)}), bf16[1,256,1024]{2,1,0:T(8,128)(2,1)}) %reduce-scatter.8.cloned.1.call-update) | async-done | bytes 524304 | tf_op jit(solution)/shard_map/weight_grads/reduce_scatter | solution.py:218
  (331 shorter events, 125.4 us)
Async XLA Ops:
  7.2 90.0 %all-gather.17.cloned.1.call-start = ((), (), s32[]{:S(2)}) async-start(), calls=%async_computation.16 | async-start | bytes 5242880 | tf_op jit(solution)/shard_map/group_inputs/all_gather | solution.py:243
  7.9 115.3 %all-gather.9.cloned.1.call-start = ((), (), s32[]{:S(2)}) async-start(), calls=%async_computation.9 | async-start | bytes 1769472 | tf_op jit(solution)/shard_map/weights/all_gather | solution.py:235
  8.7 316.8 %all-gather.11.cloned.1.call-start = ((), (), s32[]{:S(2)}) async-start(), calls=%async_computation.10 | async-start | bytes 8912896 | tf_op jit(solution)/shard_map/weights/all_gather | solution.py:202
  9.9 1.8 collective-permute-start.3
  11.6 1.4 collective-permute-start.4
  127.4 10.8 %collective-permute-start.6 = (bf16[1,1024,256]{2,1,0:T(8,128)(2,1)S(1)}, bf16[1,1024,256]{2,1,0:T(8,128)(2,1)S(1)}, u32[]{:S(2)}, u32[]{:S(2)}) collective-permute-start(bf16[1,1024,256]{2,1,0:T(8,128)(2,1)S(1)} %get-tuple-element.161), channel_id=1, source_target_pairs={{0,4},{4,0},{1,5},{5,1},{2,6},{6,2},{3,7},{7,3},{8,12},{12,8},{9,1... | collective-permute-start | bytes 1572872 | tf_op jit(solution)/shard_map/forward/ppermute | solution.py:248
  127.6 11.7 %collective-permute-start.7 = (bf16[1,1024,256]{2,1,0:T(8,128)(2,1)S(1)}, bf16[1,1024,256]{2,1,0:T(8,128)(2,1)S(1)}, u32[]{:S(2)}, u32[]{:S(2)}) collective-permute-start(bf16[1,1024,256]{2,1,0:T(8,128)(2,1)S(1)} %get-tuple-element.160), channel_id=1, source_target_pairs={{0,4},{4,0},{1,5},{5,1},{2,6},{6,2},{3,7},{7,3},{8,12},{12,8},{9,1... | collective-permute-start | bytes 1572872 | tf_op jit(solution)/shard_map/forward/ppermute | solution.py:248
  138.2 61.2 %copy-start.18 = (bf16[1024,256]{1,0:T(8,128)(2,1)}, bf16[1024,256]{1,0:T(8,128)(2,1)S(1)}, u32[]{:S(2)}) copy-start(bf16[1024,256]{1,0:T(8,128)(2,1)S(1)} %all_gather.31) | copy-start | bytes 1572868
  164.7 92.9 %all-to-all-start.2 = ((bf16[1,4,256,1024]{3,2,0,1:T(8,128)(2,1)}), bf16[1,4,256,1024]{3,2,0,1:T(8,128)(2,1)S(1)}, u32[]{:S(2)}, u32[]{:S(2)}) async-start(bf16[1,4,256,1024]{3,2,0,1:T(8,128)(2,1)} %bitcast.413), calls=%async_computation.2 | async-start | bytes 4194304 | tf_op jit(solution)/shard_map/forward/all_to_all | solution.py:273
  174.3 1.9 collective-permute-start
  174.3 2.9 collective-permute-start.1
  257.6 59.8 %all-to-all-start.1 = ((bf16[1,4,256,1024]{3,2,0,1:T(8,128)(2,1)}), bf16[1,4,256,1024]{3,2,0,1:T(8,128)(2,1)}, u32[]{:S(2)}, u32[]{:S(2)}) async-start(bf16[1,4,256,1024]{3,2,0,1:T(8,128)(2,1)} %bitcast.412), calls=%async_computation.1 | async-start | bytes 4194304 | tf_op jit(solution)/shard_map/forward/all_to_all | solution.py:273
  262.1 181.9 %all-gather.13.cloned.1.call-start = ((), (), s32[]{:S(2)}) async-start(), calls=%async_computation.11 | async-start | bytes 2621440 | tf_op jit(solution)/shard_map/backward_attention/all_gather | solution.py:267
  263.8 55.6 %copy-start.2 = (f32[2,1,256,1024]{3,2,1,0:T(8,128)}, f32[2,1,256,1024]{3,2,1,0:T(8,128)S(1)}, u32[]{:S(2)}) copy-start(f32[2,1,256,1024]{3,2,1,0:T(8,128)S(1)} %convert_element_type.280) | copy-start | bytes 6291460
  267.6 54.6 %copy-start.52 = (f32[256]{0:T(256)}, f32[256]{0:T(256)S(1)}, u32[]{:S(2)}) copy-start(f32[256]{0:T(256)S(1)} %get-tuple-element.193) | copy-start | bytes 3076
  267.6 54.6 %copy-start.54 = (f32[256]{0:T(256)}, f32[256]{0:T(256)S(1)}, u32[]{:S(2)}) copy-start(f32[256]{0:T(256)S(1)} %get-tuple-element.194) | copy-start | bytes 3076
  270.1 106.5 %collective-permute-start.10 = (bf16[1,256,1024]{2,1,0:T(8,128)(2,1)}, bf16[1,256,1024]{2,1,0:T(8,128)(2,1)}, u32[]{:S(2)}, u32[]{:S(2)}) collective-permute-start(bf16[1,256,1024]{2,1,0:T(8,128)(2,1)} %multiply_convert_fusion.5), channel_id=1, source_target_pairs={{0,4},{4,0},{1,5},{5,1},{2,6},{6,2},{3,7},{7,3},{8,12},{12,8},{9,1... | collective-permute-start | bytes 1572872 | tf_op jit(solution)/shard_map/backward_ffn/ppermute | solution.py:248
  323.5 50.7 %copy-start.43 = (bf16[1,256,1024]{2,1,0:T(8,128)(2,1)}, bf16[1,256,1024]{2,1,0:T(8,128)(2,1)S(1)}, u32[]{:S(2)}) copy-start(bf16[1,256,1024]{2,1,0:T(8,128)(2,1)S(1)} %add_convert_fusion.12) | copy-start | bytes 1572868
  323.5 50.7 %collective-permute-start.2 = (bf16[1,256,1024]{2,1,0:T(8,128)(2,1)S(1)}, bf16[1,256,1024]{2,1,0:T(8,128)(2,1)S(1)}, u32[]{:S(2)}, u32[]{:S(2)}) collective-permute-start(bf16[1,256,1024]{2,1,0:T(8,128)(2,1)S(1)} %add_convert_fusion.12), channel_id=1, source_target_pairs={{0,4},{4,0},{1,5},{5,1},{2,6},{6,2},{3,7},{7,3},{8,12},{12,8},{9,1... | collective-permute-start | bytes 1572872 | tf_op jit(solution)/shard_map/forward/ppermute | solution.py:248
  324.9 68.5 %collective-permute-start.8 = (bf16[1,256,1024]{2,1,0:T(8,128)(2,1)}, bf16[1,256,1024]{2,1,0:T(8,128)(2,1)}, u32[]{:S(2)}, u32[]{:S(2)}) collective-permute-start(bf16[1,256,1024]{2,1,0:T(8,128)(2,1)} %add_convert_fusion.10), channel_id=1, source_target_pairs={{0,4},{4,0},{1,5},{5,1},{2,6},{6,2},{3,7},{7,3},{8,12},{12,8},{9,1... | collective-permute-start | bytes 1572872 | tf_op jit(solution)/shard_map/forward/ppermute | solution.py:248
  368.8 24.6 %copy-start.22 = (bf16[128,8,4,512]{3,1,2,0:T(8,128)(2,1)}, bf16[128,8,4,512]{3,1,2,0:T(8,128)(2,1)S(1)}, u32[]{:S(2)}) copy-start(bf16[128,8,4,512]{3,1,2,0:T(8,128)(2,1)S(1)} %copy.238) | copy-start | bytes 12582916
  386.3 3.4 collective-permute-start.11
  389.2 2.1 collective-permute-start.5
  393.0 7.2 collective-permute-start.14
  399.9 89.9 %all-gather.15.cloned.1.call-start = ((), (), s32[]{:S(2)}) async-start(), calls=%async_computation.12 | async-start | bytes 2621440 | tf_op jit(solution)/shard_map/backward_attention/all_gather | solution.py:267
  411.0 4.9 collective-permute-start.15
  415.4 2.0 collective-permute-start.9
  421.0 23.0 %copy-start.19 = (bf16[1024,256]{1,0:T(8,128)(2,1)S(1)}, bf16[1024,256]{1,0:T(8,128)(2,1)}, u32[]{:S(2)}) copy-start(bf16[1024,256]{1,0:T(8,128)(2,1)} %copy-done.18) | copy-start | bytes 1572868
  421.0 279.8 %reduce-scatter.6.cloned.1.call-start = ((), (), s32[]{:S(2)}) async-start(), calls=%async_computation.14 | async-start | bytes 589824 | tf_op jit(solution)/shard_map/weight_grads/reduce_scatter | solution.py:413
  481.1 2.0 collective-permute-start.12
  481.5 2.4 collective-permute-start.13
  528.2 4.0 collective-permute-start.16
  529.2 4.5 collective-permute-start.17
  532.1 173.3 %reduce-scatter.4.cloned.1.call-start = ((), (), s32[]{:S(2)}) async-start(), calls=%async_computation.13 | async-start | bytes 1769472 | tf_op jit(solution)/shard_map/weight_grads/reduce_scatter | solution.py:413
  540.2 322.9 %reduce-scatter.8.cloned.1.call-start = ((), (), s32[]{:S(2)}) async-start(), calls=%async_computation.15 | async-start | bytes 8912896 | tf_op jit(solution)/shard_map/weight_grads/reduce_scatter | solution.py:218
  596.2 98.8 %all-to-all-start.3 = ((bf16[1,4,256,1024]{3,2,0,1:T(8,128)(2,1)}), bf16[1,4,256,1024]{3,2,0,1:T(8,128)(2,1)S(1)}, u32[]{:S(2)}, u32[]{:S(2)}) async-start(bf16[1,4,256,1024]{3,2,0,1:T(8,128)(2,1)} %bitcast.426), calls=%async_computation.3 | async-start | bytes 4194304 | tf_op jit(solution)/shard_map/backward_attention/all_to_all | solution.py:273
  605.0 94.6 %copy-start.57 = (f32[256]{0:T(256)S(1)}, f32[256]{0:T(256)}, u32[]{:S(2)}) copy-start(f32[256]{0:T(256)} %get-tuple-element.128) | copy-start | bytes 3076
  605.0 94.7 %copy-start.56 = (f32[256]{0:T(256)S(1)}, f32[256]{0:T(256)}, u32[]{:S(2)}) copy-start(f32[256]{0:T(256)} %get-tuple-element.127) | copy-start | bytes 3076
  605.0 94.7 %copy-start.28 = (bf16[1,256,1024]{2,1,0:T(8,128)(2,1)S(1)}, bf16[1,256,1024]{2,1,0:T(8,128)(2,1)}, u32[]{:S(2)}) copy-start(bf16[1,256,1024]{2,1,0:T(8,128)(2,1)} %get-tuple-element.149) | copy-start | bytes 1572868
  605.0 94.7 %copy-start.34 = (bf16[1,256,1024]{2,1,0:T(8,128)(2,1)S(1)}, bf16[1,256,1024]{2,1,0:T(8,128)(2,1)}, u32[]{:S(2)}) copy-start(bf16[1,256,1024]{2,1,0:T(8,128)(2,1)} %get-tuple-element.165) | copy-start | bytes 1572868
  695.0 93.9 %all-to-all-start.4 = ((bf16[1,4,256,1024]{3,2,0,1:T(8,128)(2,1)}), bf16[1,4,256,1024]{3,2,0,1:T(8,128)(2,1)}, u32[]{:S(2)}, u32[]{:S(2)}) async-start(bf16[1,4,256,1024]{3,2,0,1:T(8,128)(2,1)} %bitcast.425), calls=%async_computation.4 | async-start | bytes 4194304 | tf_op jit(solution)/shard_map/backward_attention/all_to_all | solution.py:273
  700.8 91.9 %copy-start.3 = (f32[2,1,256,1024]{3,2,1,0:T(8,128)S(1)}, f32[2,1,256,1024]{3,2,1,0:T(8,128)}, u32[]{:S(2)}) copy-start(f32[2,1,256,1024]{3,2,1,0:T(8,128)} %copy-done.2) | copy-start | bytes 6291460
  700.8 91.9 %copy-start.49 = (f32[1,1,1,1024]{3,1,2,0:T(1,128)S(1)}, f32[1,1,1,1024]{3,1,2,0:T(1,128)}, u32[]{:S(2)}) copy-start(f32[1,1,1,1024]{3,1,2,0:T(1,128)} %get-tuple-element.184) | copy-start | bytes 12292
  700.8 91.9 %copy-start.53 = (f32[256]{0:T(256)S(1)}, f32[256]{0:T(256)}, u32[]{:S(2)}) copy-start(f32[256]{0:T(256)} %copy-done.52) | copy-start | bytes 3076
  700.8 91.9 %copy-start.55 = (f32[256]{0:T(256)S(1)}, f32[256]{0:T(256)}, u32[]{:S(2)}) copy-start(f32[256]{0:T(256)} %copy-done.54) | copy-start | bytes 3076
  798.2 9.4 %all-to-all-start.5 = ((f32[4,1,3072]{2,1,0:T(1,128)}), f32[4,1,3072]{2,1,0:T(1,128)S(1)}, u32[]{:S(2)}, u32[]{:S(2)}) async-start(f32[4,1,3072]{2,1,0:T(1,128)} %reshape.1087), calls=%async_computation.8 | async-start | bytes 98304 | tf_op jit(solution)/shard_map/ada_grad/all_to_all | solution.py:399
  805.5 59.1 %copy-start.48 = (bf16[8,2,4,128]{3,0,2,1:T(8,128)(2,1)S(1)}, bf16[8,2,4,128]{3,0,2,1:T(8,128)(2,1)}, u32[]{:S(2)}) copy-start(bf16[8,2,4,128]{3,0,2,1:T(8,128)(2,1)} %copy-done.47) | copy-start | bytes 49156
  864.4 1.8 collective-permute-start.18
  (52 other events, 228.6 us)
Sparse Core Ops, SparseCore 0:
  9.6 87.5 all-gather.16
  99.1 24.0 all-gather.8
  126.6 175.2 all-gather.10
  400.0 43.8 all-gather.12
  445.4 44.4 all-gather.14
  532.2 32.9 reduce-scatter.5
  568.5 38.3 reduce-scatter.3
  609.1 254.0 reduce-scatter.7

commit v9 on v8

--- a/solution.py
+++ b/solution.py
@@ -199,7 +199,8 @@
             received = lax.ppermute(sent, "frame", [(0, 1), (1, 0)])
             pieces.append(order_by_half(mine, received).reshape(halves * rows_here, half))
         joined = jnp.concatenate(pieces, axis=1)
-        gathered = lax.all_gather(joined, ("dp", "tensor"), axis=0, tiled=True)
+        gathered = lax.all_gather(joined, "tensor", axis=0, tiled=True)
+        gathered = lax.all_gather(gathered, "dp", axis=0, tiled=True)
         gathered = gathered.reshape(replicas, groups, halves * rows_here, len(weights), half)
         return tuple(
             jnp.swapaxes(gathered[:, :, :, k], 1, 2).reshape(model_width, groups * half)
@@ -217,10 +218,12 @@
         ).astype(jnp.bfloat16)
         summed = lax.psum_scatter(
             blocks.reshape(replicas * groups, halves * rows_here, len(totals) * half),
-            ("dp", "tensor"),
+            "dp",
             scatter_dimension=0,
             tiled=True,
-        )[0].reshape(halves, rows_here, len(totals) * half)
+        )
+        summed = lax.psum_scatter(summed, "tensor", scatter_dimension=0, tiled=True)
+        summed = summed[0].reshape(halves, rows_here, len(totals) * half)
         mine = jnp.take(summed, frame_index, axis=0).astype(jnp.float32)
         sent = jnp.take(summed, 1 - frame_index, axis=0)
         received = lax.ppermute(sent, "frame", [(0, 1), (1, 0)]).astype(jnp.float32)

time: 884 us -> 727 us (0.82)
  waiting for transfers between devices: 396 us -> 241 us
    all_to_all x4, waiting for transfers between devices: 272 us -> 53.1 us  [scatter_tokens(): received = lax.all_to_all(parts, 'tensor', 1, 1, tiled=True)]
    reduce_scatter x2, waiting for transfers between devices: 0.04 us -> 58.6 us  [on_device(): lax.psum_scatter(total.astype(jnp.bfloat16), ('dp', 'frame'), scatter_dim...]
    reduce_scatter x1, waiting for transfers between devices: 39.8 us -> 0.01 us  [hidden_half_back(): lax.psum_scatter(blocks.reshape(replicas * groups, halves * rows_here, le...]
    all_gather x1, waiting for transfers between devices: 42.2 us -> 81.1 us  [on_device(): group_tokens = lax.all_gather(tokens[:, 0], 'tensor', axis=1, tiled=True)]
    all_gather x2, waiting for transfers between devices: 19.3 us -> 0.04 us  [gather_tokens(): return lax.all_gather(values, 'tensor', axis=1, tiled=True)]
    all_gather x1 -> x2, waiting for transfers between devices: 0.01 us -> 11.5 us  [the longest x1 11.5 us: hidden_half(): gathered = lax.all_gather(joined, 'tensor', axis=0, tiled=True)]
    reduce_scatter x0 -> x1, waiting for transfers between devices: none -> 10.5 us  [hidden_half_back(): summed = lax.psum_scatter(summed, 'tensor', scatter_dimension=0, tiled=True)]
    unnamed x147 -> x159, local copies, waits for them, and re-layouts: 18.6 us -> 21.3 us
  transfers between devices with their start and end apart: 32 -> 34, of which waited for: 15 -> 15; matrix products, arithmetic and copies ran while one was open for 29% -> 35% of each run, Pallas kernels for 8% -> 15%
where the time goes in v9:
time: 727 us; the launch traced here: 718 us
  waiting for transfers between devices  241 us (33%)
  Pallas kernels  107 us (15%)
  local copies, waits for them, and re-layouts  102 us (14%)
  matrix products  94.1 us (13%)
  other arithmetic  70.1 us (10%)
  blocking collectives  57.9 us (8%)
  starting transfers between devices  30.2 us (4%)
  between operations  16.1 us (2%)
    all_gather x1, waiting for transfers between devices, on_device(): group_tokens = lax.all_gather(tokens[:, 0], 'tensor', axis=1, tiled=True)  81.1 us
    pallas_call x2, Pallas kernels, attention_backward(): pl.pallas_call(functools.partial(_backward_kernel, heads, HEAD_DIM ** (-0...  64.7 us
    reduce_scatter x2, waiting for transfers between devices, on_device(): lax.psum_scatter(total.astype(jnp.bfloat16), ('dp', 'frame'), scatter_dim...  58.6 us
    all_to_all x4, waiting for transfers between devices, scatter_tokens(): received = lax.all_to_all(parts, 'tensor', 1, 1, tiled=True)  53.1 us
    pallas_call x2, Pallas kernels, attention_forward(): pl.pallas_call(functools.partial(_forward_kernel, heads, HEAD_DIM ** (-0....  42.2 us
    reshape x4, local copies, waits for them, and re-layouts, hidden_half_back(): total.reshape(replicas, halves * rows_here, groups, half)  26 us
    unnamed x159, local copies, waits for them, and re-layouts  21.3 us
    all_to_all x4, starting transfers between devices, scatter_tokens(): received = lax.all_to_all(parts, 'tensor', 1, 1, tiled=True)  18.2 us
  transfers between devices with their start and end apart: 34, of which 15 were waited for; matrix products, arithmetic and copies ran while one was open for 35% of the time, Pallas kernels for 15%

profile of v9, /device:TPU:0, one launch (start us, length us, event | category | flops | bytes accessed | tf_op | source)
XLA Modules:
  0.0 718.5 jit_solution(13675566098494934510)
XLA Ops:
  14.2 10.1 %all-gather.2 = s32[8,2,4]{2,1,0:T(2,128)S(1)} all-gather(s32[1,2,4]{2,1,0:T(2,128)S(1)} %bitcast.477), channel_id=1, replica_groups=mesh['dp'=4,'frame'=2,'tensor'=4] {'dp','frame'}, dimensions={0}, use_global_device_ids=true | all-gather | bytes 288 | tf_op jit(solution)/shard_map/modulation/all_gather | solution.py:168
  25.6 10.9 %all_to_all.43 = f32[8,2,4,6,256]{4,2,3,1,0:T(4,128)S(1)} all-to-all(f32[8,2,4,6,256]{4,2,3,1,0:T(4,128)S(1)} %fusion.81), channel_id=1, replica_groups=mesh['dp'=4,'frame'=2,'tensor'=4] {'dp','frame'}, dimensions={0} | all-to-all | bytes 786432 | tf_op jit(solution)/shard_map/modulation/all_to_all | solution.py:179
  36.6 16.8 %all_gather.31 = f32[2,4,6,1024]{3,2,1,0:T(8,128)S(1)} all-gather(f32[2,4,6,256]{3,2,1,0:T(8,128)S(1)} %copy.233), channel_id=1, replica_groups=mesh['dp'=4,'frame'=2,'tensor'=4] {'tensor'}, dimensions={3}, use_global_device_ids=true | all-gather | bytes 245760 | tf_op jit(solution)/shard_map/modulation/all_gather | solution.py:181
  53.6 11.5 %all-gather.12.cloned.1.call-done = bf16[1024,1024]{1,0:T(8,128)(2,1)} async-done(((bf16[256,1024]{1,0:T(8,128)(2,1)}), bf16[1024,1024]{1,0:T(8,128)(2,1)}) %all-gather.12.cloned.1.call-update) | async-done | bytes 2097168 | tf_op jit(solution)/shard_map/weights/all_gather | solution.py:202
  65.1 81.1 %all-gather.20.cloned.1.call-done = bf16[2,1,1024,1024]{3,2,1,0:T(8,128)(2,1)} async-done(((bf16[2,1,256,1024]{3,2,1,0:T(8,128)(2,1)}), bf16[2,1,1024,1024]{3,2,1,0:T(8,128)(2,1)}) %all-gather.20.cloned.1.call-update) | async-done | bytes 4194320 | tf_op jit(solution)/shard_map/group_inputs/all_gather | solution.py:246
  156.4 15.9 %all-gather.10.cloned.1.call-done = bf16[1024,3,256]{2,0,1:T(8,128)(2,1)} async-done(((bf16[128,3,256]{2,0,1:T(8,128)(2,1)}), bf16[1024,3,256]{2,0,1:T(8,128)(2,1)}) %all-gather.10.cloned.1.call-update) | async-done | bytes 1572880 | tf_op jit(solution)/shard_map/weights/all_gather | solution.py:238
  172.3 3.2 fusion.39
  176.9 10.5 %all_gather.34 = bf16[1024,256]{1,0:T(8,128)(2,1)S(1)} all-gather(bf16[128,256]{1,0:T(8,128)(2,1)S(1)} %copy-done.55), channel_id=1, replica_groups=mesh['dp'=4,'frame'=2,'tensor'=4] {'dp','frame'}, dimensions={0}, use_global_device_ids=true | all-gather | bytes 589824 | tf_op jit(solution)/shard_map/weights/all_gather | solution.py:238
  189.7 21.1 %forward.3 = (bf16[1024,256]{1,0:T(8,128)(2,1)}, f32[1024,4]{1,0:T(8,128)}) custom-call(bf16[1024,256]{1,0:T(8,128)(2,1)} %get-tuple-element.162.q_ref, bf16[2048,256]{1,0:T(8,128)(2,1)} %maximum_bitcast_fusion.3.k_ref, bf16[2048,256]{1,0:T(8,128)(2,1)} %maximum_bitcast_fusion.4.v_ref), custom_call_target="tpu_custom_call" | custom-call | flops 2147483648 | bytes 3145728 | tf_op jit(solution)/shard_map/forward/pallas_call | solution.py:85
  210.8 3.1 convolution_convert_fusion
  213.9 4.8 all-to-all-start.2
  218.8 3.8 fusion.38
  227.5 21.1 %forward.2 = (bf16[1024,256]{1,0:T(8,128)(2,1)}, f32[1024,4]{1,0:T(8,128)}) custom-call(bf16[1024,256]{1,0:T(8,128)(2,1)} %get-tuple-element.159.q_ref, bf16[2048,256]{1,0:T(8,128)(2,1)} %maximum_bitcast_fusion.k_ref, bf16[2048,256]{1,0:T(8,128)(2,1)} %maximum_bitcast_fusion.1.v_ref), custom_call_target="tpu_custom_call" | custom-call | flops 2147483648 | bytes 3145728 | tf_op jit(solution)/shard_map/forward/pallas_call | solution.py:85
  251.7 15.8 %all-to-all-done.2 = bf16[1,4,256,1024]{3,2,0,1:T(8,128)(2,1)S(1)} async-done(((bf16[1,4,256,1024]{3,2,0,1:T(8,128)(2,1)}), bf16[1,4,256,1024]{3,2,0,1:T(8,128)(2,1)S(1)}, u32[]{:S(2)}, u32[]{:S(2)}) %all-to-all-start.2) | async-done | bytes 2097184 | tf_op jit(solution)/shard_map/forward/all_to_all | solution.py:276
  267.5 4.5 all-to-all-start.1
  273.7 3.6 convert_element_type.249
  282.5 37.3 %all-to-all-done.1 = bf16[1,4,256,1024]{3,2,0,1:T(8,128)(2,1)} async-done(((bf16[1,4,256,1024]{3,2,0,1:T(8,128)(2,1)}), bf16[1,4,256,1024]{3,2,0,1:T(8,128)(2,1)}, u32[]{:S(2)}, u32[]{:S(2)}) %all-to-all-start.1) | async-done | bytes 2097184 | tf_op jit(solution)/shard_map/forward/all_to_all | solution.py:276
  327.9 14.5 %reshape.897 = bf16[4,4,256,2,512]{4,3,2,1,0:T(2,128)(2,1)} reshape(bf16[4096,1024]{1,0:T(8,128)(2,1)} %all-gather.14.cloned.1.call-done) | data formatting | bytes 16777216 | tf_op jit(solution)/shard_map/weights/reshape | solution.py:204
  342.5 16.7 %fusion.107 = (bf16[4,4,256,1,512]{4,3,2,1,0:T(2,128)(2,1)S(1)}, bf16[4,4,256,1,512]{4,3,2,1,0:T(2,128)(2,1)S(1)}) fusion(bf16[4,4,256,2,512]{4,3,2,1,0:T(2,128)(2,1)} %reshape.897), kind=kLoop, calls=%fused_computation.260 | loop fusion | bytes 16777216 | tf_op jit(solution)/shard_map/weights/slice | solution.py:206
  359.2 5.3 copy_bitcast_fusion
  364.5 5.4 copy.197
  372.2 3.2 copy.198
  379.3 6.9 fusion.20
  395.8 5.6 fusion.73
  402.6 8.3 %fusion.27 = bf16[512,2048]{1,0:T(8,128)(2,1)S(1)} fusion(f32[512,2048]{1,0:T(8,128)} %fusion.73, bf16[1024,2048]{1,0:T(8,128)(2,1)} %bitcast.417, bf16[1,256,1024]{2,1,0:T(8,128)(2,1)} %collective-permute-done.14, bf16[1,256,1024]{2,1,0:T(8,128)(2,1)} %get-tuple-element.156), kind=kOutput, calls=%fused_computation.42 | convolution fusion | flops 2170552320 | bytes 11534336 | tf_op jit(solution)/shard_map/backward_ffn/cro,of->crf/dot_general | solution.py:319
  424.0 4.5 fusion.74
  428.5 7.1 fusion.71
  435.6 5.8 add_convert_fusion.1
  441.4 7.8 %reshape.909 = bf16[4,256,4,512]{3,2,1,0:T(4,128)(2,1)} reshape(bf16[1024,2048]{1,0:T(8,128)(2,1)} %add_convert_fusion.1) | data formatting | bytes 8388608 | tf_op jit(solution)/shard_map/weight_grads/reshape | solution.py:214
  449.2 5.2 copy.206
  454.4 6.9 add_convert_fusion
  461.3 7.8 %reshape.910 = bf16[4,256,4,512]{3,2,1,0:T(4,128)(2,1)} reshape(bf16[1024,2048]{1,0:T(8,128)(2,1)} %add_convert_fusion) | data formatting | bytes 8388608 | tf_op jit(solution)/shard_map/weight_grads/reshape | solution.py:214
  469.1 5.2 copy.207
  474.2 8.0 %pad_maximum_fusion = bf16[16,256,1024]{2,1,0:T(8,128)(2,1)} fusion(bf16[16,256,512]{2,1,0:T(8,128)(2,1)} %bitcast.411, bf16[16,256,512]{2,1,0:T(8,128)(2,1)} %bitcast.410), kind=kLoop, calls=%fused_computation | loop fusion | flops 16777216 | bytes 16777216 | tf_op jit(solution)/shard_map/weight_grads/concatenate | solution.py:212
  483.3 3.1 fusion.47.g_ref
  486.4 32.3 %backward_attention.2 = (f32[1024,256]{1,0:T(8,128)}, f32[2048,256]{1,0:T(8,128)}, f32[2048,256]{1,0:T(8,128)}) custom-call(bf16[1024,256]{1,0:T(8,128)(2,1)} %get-tuple-element.159.q_ref, bf16[2048,256]{1,0:T(8,128)(2,1)} %maximum_bitcast_fusion.k_ref, bf16[2048,256]{1,0:T(8,128)(2,1)} %maximum_bitcast_fusion.1.v_ref, bf16[1024,256]{1,0:T(8,128)(2,1)} %fusion.47.g_ref, ...), custom_call_target="tpu_custom_call" | custom-call | flops 5368709120 | bytes 8912896 | tf_op jit(solution)/shard_map/backward_attention/pallas_call | solution.py:118
  523.6 3.2 bitcast_convert_fusion.1
  526.8 3.6 all-to-all-start.3
  533.7 32.4 %backward_attention.3 = (f32[1024,256]{1,0:T(8,128)}, f32[2048,256]{1,0:T(8,128)}, f32[2048,256]{1,0:T(8,128)}) custom-call(bf16[1024,256]{1,0:T(8,128)(2,1)} %get-tuple-element.162.q_ref, bf16[2048,256]{1,0:T(8,128)(2,1)} %maximum_bitcast_fusion.3.k_ref, bf16[2048,256]{1,0:T(8,128)(2,1)} %maximum_bitcast_fusion.4.v_ref, bf16[1024,256]{1,0:T(8,128)(2,1)} %fusion.50.g_ref, ...), custom_call_target="tpu_custom_call" | custom-call | flops 5368709120 | bytes 8912896 | tf_op jit(solution)/shard_map/backward_attention/pallas_call | solution.py:118
  581.3 3.2 add_convert_fusion.2
  584.6 4.7 bitcast_convert_fusion
  589.3 5.2 all-to-all-start.4
  596.3 21.3 %reduce-scatter.7.cloned.1.call-done = bf16[128,256]{1,0:T(8,128)(2,1)} async-done(((bf16[1024,256]{1,0:T(8,128)(2,1)}), bf16[128,256]{1,0:T(8,128)(2,1)}) %reduce-scatter.7.cloned.1.call-update) | async-done | bytes 65552 | tf_op jit(solution)/shard_map/weight_grads/reduce_scatter | solution.py:416
  621.9 37.3 %reduce-scatter.5.cloned.1.call-done = bf16[128,3,256]{2,0,1:T(8,128)(2,1)} async-done(((bf16[1024,3,256]{2,0,1:T(8,128)(2,1)}), bf16[128,3,256]{2,0,1:T(8,128)(2,1)}) %reduce-scatter.5.cloned.1.call-update) | async-done | bytes 196624 | tf_op jit(solution)/shard_map/weight_grads/reduce_scatter | solution.py:416
  666.8 3.6 reshape.1087
  670.4 4.9 all-to-all-start.5
  685.8 9.5 %all-gather.1 = f32[16,4,1,6,256]{4,1,0,3,2:T(4,128)S(1)} all-gather(f32[2,4,1,6,256]{4,1,0,3,2:T(4,128)S(1)} %bitcast.437), channel_id=3, replica_groups=mesh['dp'=4,'frame'=2,'tensor'=4] {'dp','frame'}, dimensions={0}, use_global_device_ids=true | all-gather | bytes 442368 | tf_op jit(solution)/shard_map/ada_grad/all_gather | solution.py:405
  695.4 10.5 %reduce-scatter.11.cloned.1.call-done = bf16[1,256,1024]{2,1,0:T(8,128)(2,1)} async-done(((bf16[4,256,1024]{2,1,0:T(8,128)(2,1)}), bf16[1,256,1024]{2,1,0:T(8,128)(2,1)}) %reduce-scatter.11.cloned.1.call-update) | async-done | bytes 524304 | tf_op jit(solution)/shard_map/weight_grads/reduce_scatter | solution.py:225
  (349 shorter events, 127.9 us)
Async XLA Ops:
  7.2 17.9 %copy-start = (bf16[128,6,256]{2,0,1:T(8,128)(2,1)S(1)}, bf16[128,6,256]{2,0,1:T(8,128)(2,1)}, u32[]{:S(2)}) copy-start(bf16[128,6,256]{2,0,1:T(8,128)(2,1)} %param.19) | copy-start | bytes 1179652
  7.2 57.9 %all-gather.12.cloned.1.call-start = ((), (), s32[]{:S(2)}) async-start(), calls=%async_computation.11 | async-start | bytes 2621440 | tf_op jit(solution)/shard_map/weights/all_gather | solution.py:202
  8.4 1.8 collective-permute-start.3
  10.1 1.4 collective-permute-start.4
  12.7 133.6 %all-gather.20.cloned.1.call-start = ((), (), s32[]{:S(2)}) async-start(), calls=%async_computation.19 | async-start | bytes 5242880 | tf_op jit(solution)/shard_map/group_inputs/all_gather | solution.py:246
  13.4 158.8 %all-gather.10.cloned.1.call-start = ((), (), s32[]{:S(2)}) async-start(), calls=%async_computation.10 | async-start | bytes 1769472 | tf_op jit(solution)/shard_map/weights/all_gather | solution.py:238
  14.2 313.8 %all-gather.14.cloned.1.call-start = ((), (), s32[]{:S(2)}) async-start(), calls=%async_computation.12 | async-start | bytes 10485760 | tf_op jit(solution)/shard_map/weights/all_gather | solution.py:203
  156.4 19.1 %copy-start.31 = (bf16[1024,1024,1]{1,0,2:T(8,128)(2,1)}, bf16[1024,1024,1]{1,0,2:T(8,128)(2,1)S(1)}, u32[]{:S(2)}) copy-start(bf16[1024,1024,1]{1,0,2:T(8,128)(2,1)S(1)} %get-tuple-element.146) | copy-start | bytes 6291460
  176.4 11.1 %collective-permute-start.6 = (bf16[1,1024,256]{2,1,0:T(8,128)(2,1)S(1)}, bf16[1,1024,256]{2,1,0:T(8,128)(2,1)S(1)}, u32[]{:S(2)}, u32[]{:S(2)}) collective-permute-start(bf16[1,1024,256]{2,1,0:T(8,128)(2,1)S(1)} %get-tuple-element.161), channel_id=1, source_target_pairs={{0,4},{4,0},{1,5},{5,1},{2,6},{6,2},{3,7},{7,3},{8,12},{12,8},{9,1... | collective-permute-start | bytes 1572872 | tf_op jit(solution)/shard_map/forward/ppermute | solution.py:251
  176.7 12.0 %collective-permute-start.7 = (bf16[1,1024,256]{2,1,0:T(8,128)(2,1)S(1)}, bf16[1,1024,256]{2,1,0:T(8,128)(2,1)S(1)}, u32[]{:S(2)}, u32[]{:S(2)}) collective-permute-start(bf16[1,1024,256]{2,1,0:T(8,128)(2,1)S(1)} %get-tuple-element.160), channel_id=1, source_target_pairs={{0,4},{4,0},{1,5},{5,1},{2,6},{6,2},{3,7},{7,3},{8,12},{12,8},{9,1... | collective-permute-start | bytes 1572872 | tf_op jit(solution)/shard_map/forward/ppermute | solution.py:251
  187.5 61.1 %copy-start.18 = (bf16[1024,256]{1,0:T(8,128)(2,1)}, bf16[1024,256]{1,0:T(8,128)(2,1)S(1)}, u32[]{:S(2)}) copy-start(bf16[1024,256]{1,0:T(8,128)(2,1)S(1)} %all_gather.34) | copy-start | bytes 1572868
  213.9 53.5 %all-to-all-start.2 = ((bf16[1,4,256,1024]{3,2,0,1:T(8,128)(2,1)}), bf16[1,4,256,1024]{3,2,0,1:T(8,128)(2,1)S(1)}, u32[]{:S(2)}, u32[]{:S(2)}) async-start(bf16[1,4,256,1024]{3,2,0,1:T(8,128)(2,1)} %bitcast.413), calls=%async_computation.2 | async-start | bytes 4194304 | tf_op jit(solution)/shard_map/forward/all_to_all | solution.py:276
  223.5 1.9 collective-permute-start
  223.6 2.9 collective-permute-start.1
  267.5 52.4 %all-to-all-start.1 = ((bf16[1,4,256,1024]{3,2,0,1:T(8,128)(2,1)}), bf16[1,4,256,1024]{3,2,0,1:T(8,128)(2,1)}, u32[]{:S(2)}, u32[]{:S(2)}) async-start(bf16[1,4,256,1024]{3,2,0,1:T(8,128)(2,1)} %bitcast.412), calls=%async_computation.1 | async-start | bytes 4194304 | tf_op jit(solution)/shard_map/forward/all_to_all | solution.py:276
  271.9 210.4 %all-gather.16.cloned.1.call-start = ((), (), s32[]{:S(2)}) async-start(), calls=%async_computation.13 | async-start | bytes 2621440 | tf_op jit(solution)/shard_map/backward_attention/all_gather | solution.py:270
  273.7 48.3 %copy-start.2 = (f32[2,1,256,1024]{3,2,1,0:T(8,128)}, f32[2,1,256,1024]{3,2,1,0:T(8,128)S(1)}, u32[]{:S(2)}) copy-start(f32[2,1,256,1024]{3,2,1,0:T(8,128)S(1)} %convert_element_type.280) | copy-start | bytes 6291460
  277.5 47.3 %copy-start.56 = (f32[256]{0:T(256)}, f32[256]{0:T(256)S(1)}, u32[]{:S(2)}) copy-start(f32[256]{0:T(256)S(1)} %get-tuple-element.193) | copy-start | bytes 3076
  277.5 47.3 %copy-start.58 = (f32[256]{0:T(256)}, f32[256]{0:T(256)S(1)}, u32[]{:S(2)}) copy-start(f32[256]{0:T(256)S(1)} %get-tuple-element.194) | copy-start | bytes 3076
  280.0 99.3 %collective-permute-start.10 = (bf16[1,256,1024]{2,1,0:T(8,128)(2,1)}, bf16[1,256,1024]{2,1,0:T(8,128)(2,1)}, u32[]{:S(2)}, u32[]{:S(2)}) collective-permute-start(bf16[1,256,1024]{2,1,0:T(8,128)(2,1)} %multiply_convert_fusion.5), channel_id=1, source_target_pairs={{0,4},{4,0},{1,5},{5,1},{2,6},{6,2},{3,7},{7,3},{8,12},{12,8},{9,1... | collective-permute-start | bytes 1572872 | tf_op jit(solution)/shard_map/backward_ffn/ppermute | solution.py:251
  326.0 50.8 %copy-start.48 = (bf16[1,256,1024]{2,1,0:T(8,128)(2,1)}, bf16[1,256,1024]{2,1,0:T(8,128)(2,1)S(1)}, u32[]{:S(2)}) copy-start(bf16[1,256,1024]{2,1,0:T(8,128)(2,1)S(1)} %add_convert_fusion.12) | copy-start | bytes 1572868
  326.0 50.8 %collective-permute-start.2 = (bf16[1,256,1024]{2,1,0:T(8,128)(2,1)S(1)}, bf16[1,256,1024]{2,1,0:T(8,128)(2,1)S(1)}, u32[]{:S(2)}, u32[]{:S(2)}) collective-permute-start(bf16[1,256,1024]{2,1,0:T(8,128)(2,1)S(1)} %add_convert_fusion.12), channel_id=1, source_target_pairs={{0,4},{4,0},{1,5},{5,1},{2,6},{6,2},{3,7},{7,3},{8,12},{12,8},{9,1... | collective-permute-start | bytes 1572872 | tf_op jit(solution)/shard_map/forward/ppermute | solution.py:251
  327.4 68.3 %collective-permute-start.8 = (bf16[1,256,1024]{2,1,0:T(8,128)(2,1)}, bf16[1,256,1024]{2,1,0:T(8,128)(2,1)}, u32[]{:S(2)}, u32[]{:S(2)}) collective-permute-start(bf16[1,256,1024]{2,1,0:T(8,128)(2,1)} %add_convert_fusion.10), channel_id=1, source_target_pairs={{0,4},{4,0},{1,5},{5,1},{2,6},{6,2},{3,7},{7,3},{8,12},{12,8},{9,1... | collective-permute-start | bytes 1572872 | tf_op jit(solution)/shard_map/forward/ppermute | solution.py:251
  371.4 24.3 %copy-start.23 = (bf16[128,8,4,512]{3,1,2,0:T(8,128)(2,1)}, bf16[128,8,4,512]{3,1,2,0:T(8,128)(2,1)S(1)}, u32[]{:S(2)}) copy-start(bf16[128,8,4,512]{3,1,2,0:T(8,128)(2,1)S(1)} %copy.238) | copy-start | bytes 12582916
  388.7 3.4 collective-permute-start.11
  391.6 2.1 collective-permute-start.5
  395.3 7.3 %collective-permute-start.14 = (bf16[1,256,1024]{2,1,0:T(8,128)(2,1)}, bf16[1,256,1024]{2,1,0:T(8,128)(2,1)}, u32[]{:S(2)}, u32[]{:S(2)}) collective-permute-start(bf16[1,256,1024]{2,1,0:T(8,128)(2,1)} %get-tuple-element.156), channel_id=1, source_target_pairs={{0,4},{4,0},{1,5},{5,1},{2,6},{6,2},{3,7},{7,3},{8,12},{12,8},{9,1... | collective-permute-start | bytes 1572872 | tf_op jit(solution)/shard_map/backward_ffn/ppermute | solution.py:251
  402.3 128.2 %all-gather.18.cloned.1.call-start = ((), (), s32[]{:S(2)}) async-start(), calls=%async_computation.14 | async-start | bytes 2621440 | tf_op jit(solution)/shard_map/backward_attention/all_gather | solution.py:270
  413.4 4.9 collective-permute-start.15
  417.9 2.0 collective-permute-start.9
  423.5 171.1 %reduce-scatter.9.cloned.1.call-start = ((), (), s32[]{:S(2)}) async-start(), calls=%async_computation.17 | async-start | bytes 10485760 | tf_op jit(solution)/shard_map/weight_grads/reduce_scatter | solution.py:219
  520.6 2.1 collective-permute-start.12
  521.3 2.1 collective-permute-start.13
  526.8 62.5 %all-to-all-start.3 = ((bf16[1,4,256,1024]{3,2,0,1:T(8,128)(2,1)}), bf16[1,4,256,1024]{3,2,0,1:T(8,128)(2,1)S(1)}, u32[]{:S(2)}, u32[]{:S(2)}) async-start(bf16[1,4,256,1024]{3,2,0,1:T(8,128)(2,1)} %bitcast.425), calls=%async_computation.3 | async-start | bytes 4194304 | tf_op jit(solution)/shard_map/backward_attention/all_to_all | solution.py:276
  530.5 87.1 %reduce-scatter.7.cloned.1.call-start = ((), (), s32[]{:S(2)}) async-start(), calls=%async_computation.16 | async-start | bytes 589824 | tf_op jit(solution)/shard_map/weight_grads/reduce_scatter | solution.py:416
  568.9 6.6 collective-permute-start.16
  571.2 5.7 collective-permute-start.17
  573.7 85.6 %reduce-scatter.5.cloned.1.call-start = ((), (), s32[]{:S(2)}) async-start(), calls=%async_computation.15 | async-start | bytes 1769472 | tf_op jit(solution)/shard_map/weight_grads/reduce_scatter | solution.py:416
  589.3 71.6 %all-to-all-start.4 = ((bf16[1,4,256,1024]{3,2,0,1:T(8,128)(2,1)}), bf16[1,4,256,1024]{3,2,0,1:T(8,128)(2,1)}, u32[]{:S(2)}, u32[]{:S(2)}) async-start(bf16[1,4,256,1024]{3,2,0,1:T(8,128)(2,1)} %bitcast.426), calls=%async_computation.4 | async-start | bytes 4194304 | tf_op jit(solution)/shard_map/backward_attention/all_to_all | solution.py:276
  594.6 27.2 %copy-start.54 = (f32[1,1,1,1024]{3,1,2,0:T(1,128)S(1)}, f32[1,1,1,1024]{3,1,2,0:T(1,128)}, u32[]{:S(2)}) copy-start(f32[1,1,1,1024]{3,1,2,0:T(1,128)} %get-tuple-element.180) | copy-start | bytes 12292
  594.6 111.3 %reduce-scatter.11.cloned.1.call-start = ((), (), s32[]{:S(2)}) async-start(), calls=%async_computation.18 | async-start | bytes 2621440 | tf_op jit(solution)/shard_map/weight_grads/reduce_scatter | solution.py:225
  596.3 68.4 %copy-start.3 = (f32[2,1,256,1024]{3,2,1,0:T(8,128)S(1)}, f32[2,1,256,1024]{3,2,1,0:T(8,128)}, u32[]{:S(2)}) copy-start(f32[2,1,256,1024]{3,2,1,0:T(8,128)} %copy-done.2) | copy-start | bytes 6291460
  596.3 68.4 %copy-start.53 = (f32[1,1,1,1024]{3,1,2,0:T(1,128)S(1)}, f32[1,1,1,1024]{3,1,2,0:T(1,128)}, u32[]{:S(2)}) copy-start(f32[1,1,1,1024]{3,1,2,0:T(1,128)} %get-tuple-element.184) | copy-start | bytes 12292
  596.3 68.4 %copy-start.57 = (f32[256]{0:T(256)S(1)}, f32[256]{0:T(256)}, u32[]{:S(2)}) copy-start(f32[256]{0:T(256)} %copy-done.56) | copy-start | bytes 3076
  596.3 68.4 %copy-start.59 = (f32[256]{0:T(256)S(1)}, f32[256]{0:T(256)}, u32[]{:S(2)}) copy-start(f32[256]{0:T(256)} %copy-done.58) | copy-start | bytes 3076
  670.4 12.1 %all-to-all-start.5 = ((f32[4,1,3072]{2,1,0:T(1,128)}), f32[4,1,3072]{2,1,0:T(1,128)S(1)}, u32[]{:S(2)}, u32[]{:S(2)}) async-start(f32[4,1,3072]{2,1,0:T(1,128)} %reshape.1087), calls=%async_computation.9 | async-start | bytes 98304 | tf_op jit(solution)/shard_map/ada_grad/all_to_all | solution.py:402
  679.2 27.9 %copy-start.52 = (bf16[8,2,4,128]{3,0,2,1:T(8,128)(2,1)S(1)}, bf16[8,2,4,128]{3,0,2,1:T(8,128)(2,1)}, u32[]{:S(2)}) copy-start(bf16[8,2,4,128]{3,0,2,1:T(8,128)(2,1)} %copy-done.51) | copy-start | bytes 49156
  707.1 1.8 collective-permute-start.18
  (60 other events, 234.5 us)
Sparse Core Ops, SparseCore 0:
  12.8 52.2 all-gather.11
  66.7 79.5 all-gather.19
  148.2 24.0 all-gather.9
  174.0 87.4 all-gather.13
  402.4 43.7 all-gather.15
  447.7 44.4 all-gather.17
  495.2 85.1 reduce-scatter.8
  583.4 34.0 reduce-scatter.6
  620.9 38.3 reduce-scatter.4
  661.4 44.4 reduce-scatter.10

commit v10 on v9

--- a/solution.py
+++ b/solution.py
@@ -198,39 +198,26 @@
             sent = jnp.take(blocks, 1 - frame_index, axis=1)
             received = lax.ppermute(sent, "frame", [(0, 1), (1, 0)])
             pieces.append(order_by_half(mine, received).reshape(halves * rows_here, half))
-        joined = jnp.concatenate(pieces, axis=1)
+        joined = jnp.concatenate(pieces, axis=0)
         gathered = lax.all_gather(joined, "tensor", axis=0, tiled=True)
         gathered = lax.all_gather(gathered, "dp", axis=0, tiled=True)
-        gathered = gathered.reshape(replicas, groups, halves * rows_here, len(weights), half)
+        gathered = gathered.reshape(replicas, groups, len(weights), halves * rows_here, half)
+        return tuple(gathered[:, :, k] for k in range(len(weights)))
+
+    def hidden_half_back(totals):
+        half = totals[0].shape[-1]
+        blocks = jnp.concatenate(totals, axis=2).astype(jnp.bfloat16)
+        summed = lax.psum_scatter(blocks, "dp", scatter_dimension=0, tiled=True)
+        summed = lax.psum_scatter(summed, "tensor", scatter_dimension=1, tiled=True)
+        summed = summed.reshape(len(totals), halves, rows_here, half)
+        mine = jnp.take(summed, frame_index, axis=1).astype(jnp.float32)
+        sent = jnp.take(summed, 1 - frame_index, axis=1)
+        received = lax.ppermute(sent, "frame", [(0, 1), (1, 0)]).astype(jnp.float32)
+        both = jnp.stack([mine, received], axis=1)
+        ordered = jnp.where(frame_index == 0, both, both[:, ::-1])
         return tuple(
-            jnp.swapaxes(gathered[:, :, :, k], 1, 2).reshape(model_width, groups * half)
-            for k in range(len(weights))
-        )
-
-    def hidden_half_back(totals):
-        half = totals[0].shape[1] // groups
-        blocks = jnp.concatenate(
-            [
-                jnp.swapaxes(total.reshape(replicas, halves * rows_here, groups, half), 1, 2)
-                for total in totals
-            ],
-            axis=3,
-        ).astype(jnp.bfloat16)
-        summed = lax.psum_scatter(
-            blocks.reshape(replicas * groups, halves * rows_here, len(totals) * half),
-            "dp",
-            scatter_dimension=0,
-            tiled=True,
-        )
-        summed = lax.psum_scatter(summed, "tensor", scatter_dimension=0, tiled=True)
-        summed = summed[0].reshape(halves, rows_here, len(totals) * half)
-        mine = jnp.take(summed, frame_index, axis=0).astype(jnp.float32)
-        sent = jnp.take(summed, 1 - frame_index, axis=0)
-        received = lax.ppermute(sent, "frame", [(0, 1), (1, 0)]).astype(jnp.float32)
-        ordered = jnp.swapaxes(order_by_half(mine, received), 0, 1)
-        ordered = ordered.reshape(rows_here, halves, len(totals), half)
-        return tuple(
-            ordered[:, :, k].reshape(rows_here, halves * half) for k in range(len(totals))
+            jnp.swapaxes(ordered[k], 0, 1).reshape(rows_here, halves * half)
+            for k in range(len(totals))
         )
 
     with jax.named_scope("weights"):
@@ -303,33 +290,35 @@
             normed_two, inverse_two = normalize(middle)
             entering_two = (normed_two * (1.0 + scale2) + shift2).astype(jnp.bfloat16)
             flat_two = gather_halves(entering_two)
+            blocked_two = flat_two.reshape(clips, -1, replicas, halves * rows_here)
             up_values = jnp.einsum(
-                "crd,df->crf", flat_two, upward_weight, preferred_element_type=jnp.float32
+                "crad,atdj->crtj", blocked_two, upward_weight, preferred_element_type=jnp.float32
             )
             hidden = gelu_tanh(up_values).astype(jnp.bfloat16)
             partial_two = jnp.einsum(
-                "crf,of->cro", hidden, downward_weight, preferred_element_type=jnp.float32
-            )
+                "crtj,atdj->crad", hidden, downward_weight, preferred_element_type=jnp.float32
+            ).reshape(clips, -1, model_width)
             branch_two = scatter_halves(partial_two)
             output = (middle + gate2 * branch_two).astype(jnp.bfloat16)
 
         with jax.named_scope("backward_ffn"):
             grad_gate_two = jnp.sum(upstream * branch_two, axis=1)
             grad_two_all = gather_halves((gate2 * upstream).astype(jnp.bfloat16))
+            blocked_grad = grad_two_all.reshape(clips, -1, replicas, halves * rows_here)
             grad_hidden = jnp.einsum(
-                "cro,of->crf", grad_two_all, downward_weight, preferred_element_type=jnp.float32
+                "crad,atdj->crtj", blocked_grad, downward_weight, preferred_element_type=jnp.float32
             )
             down_total = jnp.einsum(
-                "cro,crf->of", grad_two_all, hidden, preferred_element_type=jnp.float32
+                "crad,crtj->atdj", blocked_grad, hidden, preferred_element_type=jnp.float32
             )
             _, gelu_pullback = jax.vjp(gelu_tanh, up_values)
             grad_up = gelu_pullback(grad_hidden)[0].astype(jnp.bfloat16)
             up_total = jnp.einsum(
-                "crd,crf->df", flat_two, grad_up, preferred_element_type=jnp.float32
+                "crad,crtj->atdj", blocked_two, grad_up, preferred_element_type=jnp.float32
             )
             partial_back_two = jnp.einsum(
-                "crf,df->crd", grad_up, upward_weight, preferred_element_type=jnp.float32
-            )
+                "crtj,atdj->crad", grad_up, upward_weight, preferred_element_type=jnp.float32
+            ).reshape(clips, -1, model_width)
             grad_entering_two = scatter_halves(partial_back_two)
             grad_shift_two = jnp.sum(grad_entering_two, axis=1)
             grad_scale_two = jnp.sum(grad_entering_two * normed_two, axis=1)

time: 727 us -> 793 us (1.091)
  waiting for transfers between devices: 241 us -> 344 us
  local copies, waits for them, and re-layouts: 102 us -> 51.5 us
  other arithmetic: 70.1 us -> 80.5 us
    unnamed x10 -> x11, waiting for transfers between devices: 2.03 us -> 85.3 us
    reshape x5 -> x2, local copies, waits for them, and re-layouts: 40.5 us -> 1.67 us  [hidden_half_back(): jnp.swapaxes(ordered[k], 0, 1).reshape(rows_here, halves * half)]
    transpose x3 -> x0, local copies, waits for them, and re-layouts: 14 us -> none  [hidden_half(): jnp.swapaxes(gathered[:, :, :, k], 1, 2).reshape(model_width, groups * half)]
    slice x2 -> x1, local copies, waits for them, and re-layouts: 16.8 us -> 3.95 us  [hidden_half(): return tuple((gathered[:, :, k] for k in range(len(weights))))]
    reduce_scatter x2, waiting for transfers between devices: 58.6 us -> 70.4 us  [on_device(): lax.psum_scatter(total.astype(jnp.bfloat16), ('dp', 'frame'), scatter_dim...]
    another operation x3 -> x8, local copies, waits for them, and re-layouts: 1.12 us -> 11.8 us  [the longest x1 1.06 us: hidden_half_back(): mine = jnp.take(summed, frame_index, axis=0).astype(jnp.float32)]
    reduce_scatter x2 -> x1, waiting for transfers between devices: 10.5 us -> 20.1 us  [hidden_half_back(): summed = lax.psum_scatter(summed, 'tensor', scatter_dimension=1, tiled=True)]
    unnamed x159 -> x168, local copies, waits for them, and re-layouts: 21.3 us -> 23.3 us
  transfers between devices with their start and end apart: 34 -> 34, of which waited for: 15 -> 14; matrix products, arithmetic and copies ran while one was open for 35% -> 26% of each run, Pallas kernels for 15% -> 14%
where the time goes in v10:
time: 793 us; the launch traced here: 785 us
  waiting for transfers between devices  344 us (43%)
  Pallas kernels  107 us (13%)
  matrix products  100 us (13%)
  other arithmetic  80.5 us (10%)
  blocking collectives  57.8 us (7%)
  local copies, waits for them, and re-layouts  51.5 us (6%)
  starting transfers between devices  27.8 us (4%)
  between operations  15.9 us (2%)
    unnamed x11, waiting for transfers between devices  85.3 us
    all_gather x1, waiting for transfers between devices, on_device(): group_tokens = lax.all_gather(tokens[:, 0], 'tensor', axis=1, tiled=True)  81.1 us
    reduce_scatter x2, waiting for transfers between devices, on_device(): lax.psum_scatter(total.astype(jnp.bfloat16), ('dp', 'frame'), scatter_dim...  70.4 us
    pallas_call x2, Pallas kernels, attention_backward(): pl.pallas_call(functools.partial(_backward_kernel, heads, HEAD_DIM ** (-0...  65.1 us
    all_to_all x4, waiting for transfers between devices, scatter_tokens(): received = lax.all_to_all(parts, 'tensor', 1, 1, tiled=True)  53.3 us
    pallas_call x2, Pallas kernels, attention_forward(): pl.pallas_call(functools.partial(_forward_kernel, heads, HEAD_DIM ** (-0....  42.3 us
    unnamed x168, local copies, waits for them, and re-layouts  23.3 us
    reduce_scatter x1, waiting for transfers between devices, hidden_half_back(): summed = lax.psum_scatter(summed, 'tensor', scatter_dimension=1, tiled=True)  20.1 us
  transfers between devices with their start and end apart: 34, of which 14 were waited for; matrix products, arithmetic and copies ran while one was open for 26% of the time, Pallas kernels for 14%

profile of v10, /device:TPU:0, one launch (start us, length us, event | category | flops | bytes accessed | tf_op | source)
XLA Modules:
  0.0 785.2 jit_solution(15604493255732115751)
XLA Ops:
  14.2 10.1 %all-gather.2 = s32[8,2,4]{2,1,0:T(2,128)S(1)} all-gather(s32[1,2,4]{2,1,0:T(2,128)S(1)} %bitcast.683), channel_id=1, replica_groups=mesh['dp'=4,'frame'=2,'tensor'=4] {'dp','frame'}, dimensions={0}, use_global_device_ids=true | all-gather | bytes 288 | tf_op jit(solution)/shard_map/modulation/all_gather | solution.py:168
  25.6 10.9 %all_to_all.43 = f32[8,2,4,6,256]{4,2,3,1,0:T(4,128)S(1)} all-to-all(f32[8,2,4,6,256]{4,2,3,1,0:T(4,128)S(1)} %fusion.182), channel_id=1, replica_groups=mesh['dp'=4,'frame'=2,'tensor'=4] {'dp','frame'}, dimensions={0} | all-to-all | bytes 786432 | tf_op jit(solution)/shard_map/modulation/all_to_all | solution.py:179
  36.5 16.8 %all_gather.31 = f32[2,4,6,1024]{3,2,1,0:T(8,128)S(1)} all-gather(f32[2,4,6,256]{3,2,1,0:T(8,128)S(1)} %copy.288), channel_id=1, replica_groups=mesh['dp'=4,'frame'=2,'tensor'=4] {'tensor'}, dimensions={3}, use_global_device_ids=true | all-gather | bytes 245760 | tf_op jit(solution)/shard_map/modulation/all_gather | solution.py:181
  53.6 11.5 %all-gather.12.cloned.1.call-done = bf16[2048,512]{1,0:T(8,128)(2,1)} async-done(((bf16[512,512]{1,0:T(8,128)(2,1)}), bf16[2048,512]{1,0:T(8,128)(2,1)}) %all-gather.12.cloned.1.call-update) | async-done | bytes 2097168 | tf_op jit(solution)/shard_map/weights/all_gather | solution.py:202
  65.1 81.1 %all-gather.20.cloned.1.call-done = bf16[2,1,1024,1024]{3,2,1,0:T(8,128)(2,1)} async-done(((bf16[2,1,256,1024]{3,2,1,0:T(8,128)(2,1)}), bf16[2,1,1024,1024]{3,2,1,0:T(8,128)(2,1)}) %all-gather.20.cloned.1.call-update) | async-done | bytes 4194320 | tf_op jit(solution)/shard_map/group_inputs/all_gather | solution.py:233
  146.2 3.0 convert_reduce_fusion.1
  153.5 2.8 fusion.73
  156.3 15.9 %all-gather.10.cloned.1.call-done = bf16[1024,3,256]{2,0,1:T(8,128)(2,1)} async-done(((bf16[128,3,256]{2,0,1:T(8,128)(2,1)}), bf16[1024,3,256]{2,0,1:T(8,128)(2,1)}) %all-gather.10.cloned.1.call-update) | async-done | bytes 1572880 | tf_op jit(solution)/shard_map/weights/all_gather | solution.py:225
  172.2 3.2 fusion.128
  176.9 10.5 %all_gather.34 = bf16[1024,256]{1,0:T(8,128)(2,1)S(1)} all-gather(bf16[128,256]{1,0:T(8,128)(2,1)S(1)} %copy-done.59), channel_id=1, replica_groups=mesh['dp'=4,'frame'=2,'tensor'=4] {'dp','frame'}, dimensions={0}, use_global_device_ids=true | all-gather | bytes 589824 | tf_op jit(solution)/shard_map/weights/all_gather | solution.py:225
  189.6 21.1 %forward.2 = (bf16[1024,256]{1,0:T(8,128)(2,1)}, f32[1024,4]{1,0:T(8,128)}) custom-call(bf16[1024,256]{1,0:T(8,128)(2,1)} %get-tuple-element.159.q_ref, bf16[2048,256]{1,0:T(8,128)(2,1)} %maximum_bitcast_fusion.k_ref, bf16[2048,256]{1,0:T(8,128)(2,1)} %maximum_bitcast_fusion.1.v_ref), custom_call_target="tpu_custom_call" | custom-call | flops 2147483648 | bytes 3145728 | tf_op jit(solution)/shard_map/forward/pallas_call | solution.py:85
  210.7 3.2 convolution_convert_fusion.1
  213.9 4.8 all-to-all-start.1
  218.7 3.8 fusion.129
  227.5 21.1 %forward.3 = (bf16[1024,256]{1,0:T(8,128)(2,1)}, f32[1024,4]{1,0:T(8,128)}) custom-call(bf16[1024,256]{1,0:T(8,128)(2,1)} %get-tuple-element.162.q_ref, bf16[2048,256]{1,0:T(8,128)(2,1)} %maximum_bitcast_fusion.2.k_ref, bf16[2048,256]{1,0:T(8,128)(2,1)} %maximum_bitcast_fusion.3.v_ref), custom_call_target="tpu_custom_call" | custom-call | flops 2147483648 | bytes 3145728 | tf_op jit(solution)/shard_map/forward/pallas_call | solution.py:85
  248.6 3.1 convolution_convert_fusion
  251.8 15.7 %all-to-all-done.1 = bf16[1,4,256,1024]{3,2,0,1:T(8,128)(2,1)S(1)} async-done(((bf16[1,4,256,1024]{3,2,0,1:T(8,128)(2,1)}), bf16[1,4,256,1024]{3,2,0,1:T(8,128)(2,1)S(1)}, u32[]{:S(2)}, u32[]{:S(2)}) %all-to-all-start.1) | async-done | bytes 2097184 | tf_op jit(solution)/shard_map/forward/all_to_all | solution.py:263
  267.4 4.4 all-to-all-start.2
  273.4 3.6 convert_element_type.260
  282.2 37.6 %all-to-all-done.2 = bf16[1,4,256,1024]{3,2,0,1:T(8,128)(2,1)} async-done(((bf16[1,4,256,1024]{3,2,0,1:T(8,128)(2,1)}), bf16[1,4,256,1024]{3,2,0,1:T(8,128)(2,1)}, u32[]{:S(2)}, u32[]{:S(2)}) %all-to-all-start.2) | async-done | bytes 2097184 | tf_op jit(solution)/shard_map/forward/all_to_all | solution.py:263
  321.9 2.8 multiply_reduce_fusion.10
  341.4 3.9 fusion.244
  356.9 4.5 fusion.136
  377.6 7.2 fusion.60
  387.2 9.0 %fusion.139 = bf16[1,512,1024]{2,1,0:T(8,128)(2,1)S(1)} fusion(bf16[1024,512,4]{1,0,2:T(8,128)(2,1)} %bitcast.623, f32[512,4,512,1]{2,0,3,1:T(8,128)} %fusion.60, f32[512,4,512,1]{2,0,3,1:T(8,128)} %copy-done.71), kind=kOutput, calls=%fused_computation.164 | convolution fusion | flops 2168979456 | bytes 13631488 | tf_op jit(solution)/shard_map/backward_ffn/crtj,atdj->crad/dot_general | solution.py:319
  396.4 6.2 fusion.75
  407.9 10.2 %fusion.43 = bf16[4,4,256,512]{3,2,0,1:T(8,128)(2,1)} fusion(f32[4,512,4,256]{1,3,2,0:T(8,128)} %fusion.75, f32[512,4,512,1]{2,0,3,1:T(8,128)} %copy-done.74, bf16[512,4,256]{0,2,1:T(8,128)(2,1)} %copy.253), kind=kOutput, calls=%fused_computation.62 | convolution fusion | flops 2161115136 | bytes 17825792 | tf_op jit(solution)/shard_map/backward_ffn/crad,crtj->atdj/dot_general | solution.py:311
  418.1 6.3 fusion.78
  424.5 8.2 %fusion.42 = bf16[4,4,256,512]{3,2,0,1:T(8,128)(2,1)} fusion(f32[4,512,4,256]{1,3,2,0:T(8,128)} %fusion.78, bf16[512,4,256,1]{0,2,1,3:T(8,128)(2,1)S(1)} %bitcast.633, f32[512,4,512,1]{2,0,3,1:T(8,128)S(1)} %copy-done.77, f32[512,4,512,1]{2,0,3,1:T(8,128)S(1)} %copy-done.75), kind=kOutput, calls=%fused_computation.61 | convolution fusion | flops 2172649472 | bytes 22020096 | tf_op jit(solution)/shard_map/backward_ffn/crad,crtj->atdj/dot_general | solution.py:316
  432.7 7.5 pad_maximum_fusion
  441.2 3.1 fusion.145.g_ref
  444.4 32.5 %backward_attention.2 = (f32[1024,256]{1,0:T(8,128)}, f32[2048,256]{1,0:T(8,128)}, f32[2048,256]{1,0:T(8,128)}) custom-call(bf16[1024,256]{1,0:T(8,128)(2,1)} %get-tuple-element.159.q_ref, bf16[2048,256]{1,0:T(8,128)(2,1)} %maximum_bitcast_fusion.k_ref, bf16[2048,256]{1,0:T(8,128)(2,1)} %maximum_bitcast_fusion.1.v_ref, bf16[1024,256]{1,0:T(8,128)(2,1)} %fusion.145.g_ref, ...), custom_call_target="tpu_custom_call" | custom-call | flops 5368709120 | bytes 8912896 | tf_op jit(solution)/shard_map/backward_attention/pallas_call | solution.py:118
  482.0 3.2 bitcast_convert_fusion.1
  485.2 3.6 all-to-all-start.3
  488.9 3.3 fusion.148.g_ref
  492.1 32.6 %backward_attention.3 = (f32[1024,256]{1,0:T(8,128)}, f32[2048,256]{1,0:T(8,128)}, f32[2048,256]{1,0:T(8,128)}) custom-call(bf16[1024,256]{1,0:T(8,128)(2,1)} %get-tuple-element.162.q_ref, bf16[2048,256]{1,0:T(8,128)(2,1)} %maximum_bitcast_fusion.2.k_ref, bf16[2048,256]{1,0:T(8,128)(2,1)} %maximum_bitcast_fusion.3.v_ref, bf16[1024,256]{1,0:T(8,128)(2,1)} %fusion.148.g_ref, ...), custom_call_target="tpu_custom_call" | custom-call | flops 5368709120 | bytes 8912896 | tf_op jit(solution)/shard_map/backward_attention/pallas_call | solution.py:118
  539.7 3.2 add_convert_fusion.2
  543.0 4.7 bitcast_convert_fusion
  547.7 4.8 all-to-all-start.4
  553.2 83.8 %all-reduce.3.cloned.1.call-done = bf16[4,4,512,512]{3,2,0,1:T(8,128)(2,1)} async-done(((bf16[4,4,512,512]{3,2,0,1:T(8,128)(2,1)}), bf16[4,4,512,512]{3,2,0,1:T(8,128)(2,1)}) %all-reduce.3.cloned.1.call-update) | async-done | bytes 8388624
  636.9 3.7 constant_dynamic-slice_fusion.1
  641.8 33.0 %reduce-scatter.9.cloned.1.call-done = bf16[128,256]{1,0:T(8,128)(2,1)} async-done(((bf16[1024,256]{1,0:T(8,128)(2,1)}), bf16[128,256]{1,0:T(8,128)(2,1)}) %reduce-scatter.9.cloned.1.call-update) | async-done | bytes 65552 | tf_op jit(solution)/shard_map/weight_grads/reduce_scatter | solution.py:405
  679.2 37.3 %reduce-scatter.7.cloned.1.call-done = bf16[128,3,256]{2,0,1:T(8,128)(2,1)} async-done(((bf16[1024,3,256]{2,0,1:T(8,128)(2,1)}), bf16[128,3,256]{2,0,1:T(8,128)(2,1)}) %reduce-scatter.7.cloned.1.call-update) | async-done | bytes 196624 | tf_op jit(solution)/shard_map/weight_grads/reduce_scatter | solution.py:405
  718.3 2.7 convert_reduce_fusion.2
  724.1 3.6 reshape.1147
  727.7 4.8 all-to-all-start.5
  743.1 20.1 %reduce-scatter.11.cloned.1.call-done = bf16[1,1,512,512]{3,2,0,1:T(8,128)(2,1)} async-done(((bf16[1,4,512,512]{3,2,0,1:T(8,128)(2,1)}), bf16[1,1,512,512]{3,2,0,1:T(8,128)(2,1)}) %reduce-scatter.11.cloned.1.call-update) | async-done | bytes 524304 | tf_op jit(solution)/shard_map/weight_grads/reduce_scatter | solution.py:211
  764.2 9.5 %all-gather.1 = f32[16,4,1,6,256]{4,1,0,3,2:T(4,128)S(1)} all-gather(f32[2,4,1,6,256]{4,1,0,3,2:T(4,128)S(1)} %bitcast.643), channel_id=3, replica_groups=mesh['dp'=4,'frame'=2,'tensor'=4] {'dp','frame'}, dimensions={0}, use_global_device_ids=true | all-gather | bytes 442368 | tf_op jit(solution)/shard_map/ada_grad/all_gather | solution.py:394
  (361 shorter events, 129.6 us)
Async XLA Ops:
  7.2 57.9 %all-gather.12.cloned.1.call-start = ((), (), s32[]{:S(2)}) async-start(), calls=%async_computation.10 | async-start | bytes 2621440 | tf_op jit(solution)/shard_map/weights/all_gather | solution.py:202
  8.4 1.8 collective-permute-start.4
  10.1 1.4 collective-permute-start.3
  12.7 133.6 %all-gather.20.cloned.1.call-start = ((), (), s32[]{:S(2)}) async-start(), calls=%async_computation.17 | async-start | bytes 5242880 | tf_op jit(solution)/shard_map/group_inputs/all_gather | solution.py:233
  13.4 158.8 %all-gather.10.cloned.1.call-start = ((), (), s32[]{:S(2)}) async-start(), calls=%async_computation.9 | async-start | bytes 1769472 | tf_op jit(solution)/shard_map/weights/all_gather | solution.py:225
  14.1 327.3 %all-gather.14.cloned.1.call-start = ((), (), s32[]{:S(2)}) async-start(), calls=%async_computation.11 | async-start | bytes 10485760 | tf_op jit(solution)/shard_map/weights/all_gather | solution.py:203
  176.4 11.0 %collective-permute-start = (bf16[1,1024,256]{2,1,0:T(8,128)(2,1)S(1)}, bf16[1,1024,256]{2,1,0:T(8,128)(2,1)S(1)}, u32[]{:S(2)}, u32[]{:S(2)}) collective-permute-start(bf16[1,1024,256]{2,1,0:T(8,128)(2,1)S(1)} %get-tuple-element.158), channel_id=1, source_target_pairs={{0,4},{4,0},{1,5},{5,1},{2,6},{6,2},{3,7},{7,3},{8,12},{12,8},{9,1... | collective-permute-start | bytes 1572872 | tf_op jit(solution)/shard_map/forward/ppermute | solution.py:238
  176.6 11.9 %collective-permute-start.1 = (bf16[1,1024,256]{2,1,0:T(8,128)(2,1)S(1)}, bf16[1,1024,256]{2,1,0:T(8,128)(2,1)S(1)}, u32[]{:S(2)}, u32[]{:S(2)}) collective-permute-start(bf16[1,1024,256]{2,1,0:T(8,128)(2,1)S(1)} %get-tuple-element.157), channel_id=1, source_target_pairs={{0,4},{4,0},{1,5},{5,1},{2,6},{6,2},{3,7},{7,3},{8,12},{12,8},{9,1... | collective-permute-start | bytes 1572872 | tf_op jit(solution)/shard_map/forward/ppermute | solution.py:238
  187.4 61.3 %copy-start.18 = (bf16[1024,256]{1,0:T(8,128)(2,1)}, bf16[1024,256]{1,0:T(8,128)(2,1)S(1)}, u32[]{:S(2)}) copy-start(bf16[1024,256]{1,0:T(8,128)(2,1)S(1)} %all_gather.34) | copy-start | bytes 1572868
  213.9 53.5 %all-to-all-start.1 = ((bf16[1,4,256,1024]{3,2,0,1:T(8,128)(2,1)}), bf16[1,4,256,1024]{3,2,0,1:T(8,128)(2,1)S(1)}, u32[]{:S(2)}, u32[]{:S(2)}) async-start(bf16[1,4,256,1024]{3,2,0,1:T(8,128)(2,1)} %bitcast.621), calls=%async_computation.1 | async-start | bytes 4194304 | tf_op jit(solution)/shard_map/forward/all_to_all | solution.py:263
  223.4 1.9 collective-permute-start.6
  223.5 2.9 collective-permute-start.7
  267.4 52.4 %all-to-all-start.2 = ((bf16[1,4,256,1024]{3,2,0,1:T(8,128)(2,1)}), bf16[1,4,256,1024]{3,2,0,1:T(8,128)(2,1)}, u32[]{:S(2)}, u32[]{:S(2)}) async-start(bf16[1,4,256,1024]{3,2,0,1:T(8,128)(2,1)} %bitcast.620), calls=%async_computation.2 | async-start | bytes 4194304 | tf_op jit(solution)/shard_map/forward/all_to_all | solution.py:263
  271.9 168.4 %all-gather.16.cloned.1.call-start = ((), (), s32[]{:S(2)}) async-start(), calls=%async_computation.12 | async-start | bytes 2621440 | tf_op jit(solution)/shard_map/backward_attention/all_gather | solution.py:257
  273.4 48.5 %copy-start.2 = (f32[2,1,256,1024]{3,2,1,0:T(8,128)}, f32[2,1,256,1024]{3,2,1,0:T(8,128)S(1)}, u32[]{:S(2)}) copy-start(f32[2,1,256,1024]{3,2,1,0:T(8,128)S(1)} %convert_element_type.295) | copy-start | bytes 6291460
  277.2 47.5 %copy-start.60 = (f32[256]{0:T(256)}, f32[256]{0:T(256)S(1)}, u32[]{:S(2)}) copy-start(f32[256]{0:T(256)S(1)} %get-tuple-element.189) | copy-start | bytes 3076
  277.2 47.5 %copy-start.62 = (f32[256]{0:T(256)}, f32[256]{0:T(256)S(1)}, u32[]{:S(2)}) copy-start(f32[256]{0:T(256)S(1)} %get-tuple-element.190) | copy-start | bytes 3076
  279.6 49.0 %collective-permute-start.10 = (bf16[1,256,1024]{2,1,0:T(8,128)(2,1)}, bf16[1,256,1024]{2,1,0:T(8,128)(2,1)}, u32[]{:S(2)}, u32[]{:S(2)}) collective-permute-start(bf16[1,256,1024]{2,1,0:T(8,128)(2,1)} %multiply_convert_fusion.3), channel_id=1, source_target_pairs={{0,4},{4,0},{1,5},{5,1},{2,6},{6,2},{3,7},{7,3},{8,12},{12,8},{9,1... | collective-permute-start | bytes 1572872 | tf_op jit(solution)/shard_map/backward_ffn/ppermute | solution.py:238
  326.8 6.1 collective-permute-start.2
  328.1 7.4 collective-permute-start.8
  356.8 8.2 %collective-permute-start.5 = (bf16[1,256,1024]{2,1,0:T(8,128)(2,1)S(1)}, bf16[1,256,1024]{2,1,0:T(8,128)(2,1)S(1)}, u32[]{:S(2)}, u32[]{:S(2)}) collective-permute-start(bf16[1,256,1024]{2,1,0:T(8,128)(2,1)S(1)} %slice.284), channel_id=1, source_target_pairs={{0,4},{4,0},{1,5},{5,1},{2,6},{6,2},{3,7},{7,3},{8,12},{12,8},{9,1... | collective-permute-start | bytes 1572872 | tf_op jit(solution)/shard_map/forward/ppermute | solution.py:248
  361.5 2.9 collective-permute-start.11
  366.8 5.9 collective-permute-start.14
  371.3 31.9 %collective-permute-start.9 = (bf16[1,256,1024]{2,1,0:T(8,128)(2,1)}, bf16[1,256,1024]{2,1,0:T(8,128)(2,1)}, u32[]{:S(2)}, u32[]{:S(2)}) collective-permute-start(bf16[1,256,1024]{2,1,0:T(8,128)(2,1)} %slice.298), channel_id=1, source_target_pairs={{0,4},{4,0},{1,5},{5,1},{2,6},{6,2},{3,7},{7,3},{8,12},{12,8},{9,1... | collective-permute-start | bytes 1572872 | tf_op jit(solution)/shard_map/forward/ppermute | solution.py:248
  372.7 116.2 %all-gather.18.cloned.1.call-start = ((), (), s32[]{:S(2)}) async-start(), calls=%async_computation.13 | async-start | bytes 2621440 | tf_op jit(solution)/shard_map/backward_attention/all_gather | solution.py:257
  396.3 6.3 collective-permute-start.15
  407.7 229.3 %all-reduce.3.cloned.1.call-start = ((), (), s32[]{:S(2)}) async-start(), calls=%async_computation.18 | async-start | bytes 16777216
  479.1 2.0 collective-permute-start.13
  479.6 2.2 collective-permute-start.12
  485.2 62.5 %all-to-all-start.3 = ((bf16[1,4,256,1024]{3,2,0,1:T(8,128)(2,1)}), bf16[1,4,256,1024]{3,2,0,1:T(8,128)(2,1)S(1)}, u32[]{:S(2)}, u32[]{:S(2)}) async-start(bf16[1,4,256,1024]{3,2,0,1:T(8,128)(2,1)} %bitcast.628), calls=%async_computation.3 | async-start | bytes 4194304 | tf_op jit(solution)/shard_map/backward_attention/all_to_all | solution.py:263
  488.8 186.1 %reduce-scatter.9.cloned.1.call-start = ((), (), s32[]{:S(2)}) async-start(), calls=%async_computation.15 | async-start | bytes 589824 | tf_op jit(solution)/shard_map/weight_grads/reduce_scatter | solution.py:405
  527.4 6.5 collective-permute-start.17
  529.4 6.0 collective-permute-start.16
  532.2 184.3 %reduce-scatter.7.cloned.1.call-start = ((), (), s32[]{:S(2)}) async-start(), calls=%async_computation.14 | async-start | bytes 1769472 | tf_op jit(solution)/shard_map/weight_grads/reduce_scatter | solution.py:405
  547.7 93.0 %copy-start.15 = (bf16[1,4,256,1024]{3,2,0,1:T(8,128)(2,1)}, bf16[1,4,256,1024]{3,2,0,1:T(8,128)(2,1)S(1)}, u32[]{:S(2)}) copy-start(bf16[1,4,256,1024]{3,2,0,1:T(8,128)(2,1)S(1)} %all-to-all-done.3) | copy-start | bytes 6291460
  547.7 170.6 %all-to-all-start.4 = ((bf16[1,4,256,1024]{3,2,0,1:T(8,128)(2,1)}), bf16[1,4,256,1024]{3,2,0,1:T(8,128)(2,1)}, u32[]{:S(2)}, u32[]{:S(2)}) async-start(bf16[1,4,256,1024]{3,2,0,1:T(8,128)(2,1)} %bitcast.629), calls=%async_computation.4 | async-start | bytes 4194304 | tf_op jit(solution)/shard_map/backward_attention/all_to_all | solution.py:263
  552.5 88.2 %copy-start.65 = (f32[256]{0:T(256)S(1)}, f32[256]{0:T(256)}, u32[]{:S(2)}) copy-start(f32[256]{0:T(256)} %get-tuple-element.127) | copy-start | bytes 3076
  552.5 88.2 %copy-start.64 = (f32[256]{0:T(256)S(1)}, f32[256]{0:T(256)}, u32[]{:S(2)}) copy-start(f32[256]{0:T(256)} %get-tuple-element.128) | copy-start | bytes 3076
  552.5 88.2 %copy-start.28 = (bf16[1,256,1024]{2,1,0:T(8,128)(2,1)S(1)}, bf16[1,256,1024]{2,1,0:T(8,128)(2,1)}, u32[]{:S(2)}) copy-start(bf16[1,256,1024]{2,1,0:T(8,128)(2,1)} %get-tuple-element.149) | copy-start | bytes 1572868
  552.5 88.3 %copy-start.34 = (bf16[1,256,1024]{2,1,0:T(8,128)(2,1)S(1)}, bf16[1,256,1024]{2,1,0:T(8,128)(2,1)}, u32[]{:S(2)}) copy-start(bf16[1,256,1024]{2,1,0:T(8,128)(2,1)} %get-tuple-element.165) | copy-start | bytes 1572868
  552.5 210.6 %reduce-scatter.11.cloned.1.call-start = ((), (), s32[]{:S(2)}) async-start(), calls=%async_computation.16 | async-start | bytes 2621440 | tf_op jit(solution)/shard_map/weight_grads/reduce_scatter | solution.py:211
  640.7 38.4 %copy-start.58 = (f32[1,1,1,1024]{3,1,2,0:T(1,128)S(1)}, f32[1,1,1,1024]{3,1,2,0:T(1,128)}, u32[]{:S(2)}) copy-start(f32[1,1,1,1024]{3,1,2,0:T(1,128)} %get-tuple-element.178) | copy-start | bytes 12292
  641.8 80.1 %copy-start.3 = (f32[2,1,256,1024]{3,2,1,0:T(8,128)S(1)}, f32[2,1,256,1024]{3,2,1,0:T(8,128)}, u32[]{:S(2)}) copy-start(f32[2,1,256,1024]{3,2,1,0:T(8,128)} %copy-done.2) | copy-start | bytes 6291460
  641.8 80.1 %copy-start.57 = (f32[1,1,1,1024]{3,1,2,0:T(1,128)S(1)}, f32[1,1,1,1024]{3,1,2,0:T(1,128)}, u32[]{:S(2)}) copy-start(f32[1,1,1,1024]{3,1,2,0:T(1,128)} %get-tuple-element.182) | copy-start | bytes 12292
  641.8 80.1 %copy-start.61 = (f32[256]{0:T(256)S(1)}, f32[256]{0:T(256)}, u32[]{:S(2)}) copy-start(f32[256]{0:T(256)} %copy-done.60) | copy-start | bytes 3076
  641.8 80.1 %copy-start.63 = (f32[256]{0:T(256)S(1)}, f32[256]{0:T(256)}, u32[]{:S(2)}) copy-start(f32[256]{0:T(256)} %copy-done.62) | copy-start | bytes 3076
  727.7 12.1 %all-to-all-start.5 = ((f32[4,1,3072]{2,1,0:T(1,128)}), f32[4,1,3072]{2,1,0:T(1,128)S(1)}, u32[]{:S(2)}, u32[]{:S(2)}) async-start(f32[4,1,3072]{2,1,0:T(1,128)} %reshape.1147), calls=%async_computation.8 | async-start | bytes 98304 | tf_op jit(solution)/shard_map/ada_grad/all_to_all | solution.py:391
  764.1 12.1 %collective-permute-start.18 = (bf16[2,128,512]{2,1,0:T(8,128)(2,1)S(1)}, bf16[2,128,512]{2,1,0:T(8,128)(2,1)S(1)}, u32[]{:S(2)}, u32[]{:S(2)}) collective-permute-start(bf16[2,128,512]{2,1,0:T(8,128)(2,1)S(1)} %select_bitcast_fusion), channel_id=1, source_target_pairs={{0,4},{4,0},{1,5},{5,1},{2,6},{6,2},{3,7},{7,3},{8,12},{12,8},{9,1... | collective-permute-start | bytes 786440 | tf_op jit(solution)/shard_map/weight_grads/ppermute | solution.py:215
  (65 other events, 337.8 us)
Sparse Core Ops, SparseCore 0:
  12.8 52.2 all-gather.11
  66.6 79.5 all-gather.19
  148.1 24.0 all-gather.9
  173.9 87.4 all-gather.13
  372.8 43.7 all-gather.15
  418.0 44.4 all-gather.17
  466.1 170.8 all-reduce.2
  640.0 34.8 reduce-scatter.8
  678.2 38.3 reduce-scatter.6
  718.7 44.4 reduce-scatter.10

commit v11 on v10

--- a/solution.py
+++ b/solution.py
@@ -207,8 +207,9 @@
     def hidden_half_back(totals):
         half = totals[0].shape[-1]
         blocks = jnp.concatenate(totals, axis=2).astype(jnp.bfloat16)
+        blocks = blocks.reshape(replicas * groups, len(totals) * halves * rows_here, half)
         summed = lax.psum_scatter(blocks, "dp", scatter_dimension=0, tiled=True)
-        summed = lax.psum_scatter(summed, "tensor", scatter_dimension=1, tiled=True)
+        summed = lax.psum_scatter(summed, "tensor", scatter_dimension=0, tiled=True)
         summed = summed.reshape(len(totals), halves, rows_here, half)
         mine = jnp.take(summed, frame_index, axis=1).astype(jnp.float32)
         sent = jnp.take(summed, 1 - frame_index, axis=1)

time: 793 us -> 712 us (0.90)
  waiting for transfers between devices: 344 us -> 260 us
    unnamed x11 -> x10, waiting for transfers between devices: 85.3 us -> 2.03 us
    reduce_scatter x1 -> x2, waiting for transfers between devices: 20.1 us -> 25.7 us  [the longest x1 25.7 us: hidden_half_back(): summed = lax.psum_scatter(summed, 'tensor', scatter_dimension=0, tiled=True)]
    unnamed x168 -> x161, local copies, waits for them, and re-layouts: 23.3 us -> 22.3 us
  transfers between devices with their start and end apart: 34 -> 34, of which waited for: 14 -> 12; matrix products, arithmetic and copies ran while one was open for 26% -> 29% of each run, Pallas kernels for 14% -> 15%
where the time goes in v11:
time: 712 us; the launch traced here: 704 us
  waiting for transfers between devices  260 us (37%)
  Pallas kernels  107 us (15%)
  matrix products  98.5 us (14%)
  other arithmetic  82.2 us (12%)
  blocking collectives  57.8 us (8%)
  local copies, waits for them, and re-layouts  54.1 us (8%)
  starting transfers between devices  28.3 us (4%)
  between operations  15.8 us (2%)
    all_gather x1, waiting for transfers between devices, on_device(): group_tokens = lax.all_gather(tokens[:, 0], 'tensor', axis=1, tiled=True)  81.1 us
    reduce_scatter x2, waiting for transfers between devices, on_device(): lax.psum_scatter(total.astype(jnp.bfloat16), ('dp', 'frame'), scatter_dim...  66.3 us
    pallas_call x2, Pallas kernels, attention_backward(): pl.pallas_call(functools.partial(_backward_kernel, heads, HEAD_DIM ** (-0...  64.7 us
    all_to_all x4, waiting for transfers between devices, scatter_tokens(): received = lax.all_to_all(parts, 'tensor', 1, 1, tiled=True)  53.2 us
    pallas_call x2, Pallas kernels, attention_forward(): pl.pallas_call(functools.partial(_forward_kernel, heads, HEAD_DIM ** (-0....  42.2 us
    reduce_scatter x1, waiting for transfers between devices, hidden_half_back(): summed = lax.psum_scatter(summed, 'tensor', scatter_dimension=0, tiled=True)  25.7 us
    unnamed x161, local copies, waits for them, and re-layouts  22.3 us
    all_to_all x4, starting transfers between devices, scatter_tokens(): received = lax.all_to_all(parts, 'tensor', 1, 1, tiled=True)  18 us
  transfers between devices with their start and end apart: 34, of which 12 were waited for; matrix products, arithmetic and copies ran while one was open for 29% of the time, Pallas kernels for 15%

profile of v11, /device:TPU:0, one launch (start us, length us, event | category | flops | bytes accessed | tf_op | source)
XLA Modules:
  0.0 703.7 jit_solution(16313447465994559826)
XLA Ops:
  14.2 10.1 %all-gather.2 = s32[8,2,4]{2,1,0:T(2,128)S(1)} all-gather(s32[1,2,4]{2,1,0:T(2,128)S(1)} %bitcast.677), channel_id=1, replica_groups=mesh['dp'=4,'frame'=2,'tensor'=4] {'dp','frame'}, dimensions={0}, use_global_device_ids=true | all-gather | bytes 288 | tf_op jit(solution)/shard_map/modulation/all_gather | solution.py:168
  25.6 10.9 %all_to_all.43 = f32[8,2,4,6,256]{4,2,3,1,0:T(4,128)S(1)} all-to-all(f32[8,2,4,6,256]{4,2,3,1,0:T(4,128)S(1)} %fusion.182), channel_id=1, replica_groups=mesh['dp'=4,'frame'=2,'tensor'=4] {'dp','frame'}, dimensions={0} | all-to-all | bytes 786432 | tf_op jit(solution)/shard_map/modulation/all_to_all | solution.py:179
  36.5 16.8 %all_gather.31 = f32[2,4,6,1024]{3,2,1,0:T(8,128)S(1)} all-gather(f32[2,4,6,256]{3,2,1,0:T(8,128)S(1)} %copy.301), channel_id=1, replica_groups=mesh['dp'=4,'frame'=2,'tensor'=4] {'tensor'}, dimensions={3}, use_global_device_ids=true | all-gather | bytes 245760 | tf_op jit(solution)/shard_map/modulation/all_gather | solution.py:181
  53.6 11.5 %all-gather.12.cloned.1.call-done = bf16[2048,512]{1,0:T(8,128)(2,1)} async-done(((bf16[512,512]{1,0:T(8,128)(2,1)}), bf16[2048,512]{1,0:T(8,128)(2,1)}) %all-gather.12.cloned.1.call-update) | async-done | bytes 2097168 | tf_op jit(solution)/shard_map/weights/all_gather | solution.py:202
  65.1 81.1 %all-gather.20.cloned.1.call-done = bf16[2,1,1024,1024]{3,2,1,0:T(8,128)(2,1)} async-done(((bf16[2,1,256,1024]{3,2,1,0:T(8,128)(2,1)}), bf16[2,1,1024,1024]{3,2,1,0:T(8,128)(2,1)}) %all-gather.20.cloned.1.call-update) | async-done | bytes 4194320 | tf_op jit(solution)/shard_map/group_inputs/all_gather | solution.py:234
  146.2 3.0 convert_reduce_fusion.1
  153.5 2.8 fusion.73
  156.3 15.9 %all-gather.10.cloned.1.call-done = bf16[1024,3,256]{2,0,1:T(8,128)(2,1)} async-done(((bf16[128,3,256]{2,0,1:T(8,128)(2,1)}), bf16[1024,3,256]{2,0,1:T(8,128)(2,1)}) %all-gather.10.cloned.1.call-update) | async-done | bytes 1572880 | tf_op jit(solution)/shard_map/weights/all_gather | solution.py:226
  172.2 3.2 fusion.128
  176.9 10.5 %all_gather.34 = bf16[1024,256]{1,0:T(8,128)(2,1)S(1)} all-gather(bf16[128,256]{1,0:T(8,128)(2,1)S(1)} %copy-done.57), channel_id=1, replica_groups=mesh['dp'=4,'frame'=2,'tensor'=4] {'dp','frame'}, dimensions={0}, use_global_device_ids=true | all-gather | bytes 589824 | tf_op jit(solution)/shard_map/weights/all_gather | solution.py:226
  189.5 21.1 %forward.2 = (bf16[1024,256]{1,0:T(8,128)(2,1)}, f32[1024,4]{1,0:T(8,128)}) custom-call(bf16[1024,256]{1,0:T(8,128)(2,1)} %get-tuple-element.159.q_ref, bf16[2048,256]{1,0:T(8,128)(2,1)} %maximum_bitcast_fusion.k_ref, bf16[2048,256]{1,0:T(8,128)(2,1)} %maximum_bitcast_fusion.1.v_ref), custom_call_target="tpu_custom_call" | custom-call | flops 2147483648 | bytes 3145728 | tf_op jit(solution)/shard_map/forward/pallas_call | solution.py:85
  210.6 3.2 convolution_convert_fusion.1
  213.8 4.8 all-to-all-start.1
  218.6 3.8 fusion.129
  227.5 21.1 %forward.3 = (bf16[1024,256]{1,0:T(8,128)(2,1)}, f32[1024,4]{1,0:T(8,128)}) custom-call(bf16[1024,256]{1,0:T(8,128)(2,1)} %get-tuple-element.162.q_ref, bf16[2048,256]{1,0:T(8,128)(2,1)} %maximum_bitcast_fusion.2.k_ref, bf16[2048,256]{1,0:T(8,128)(2,1)} %maximum_bitcast_fusion.3.v_ref), custom_call_target="tpu_custom_call" | custom-call | flops 2147483648 | bytes 3145728 | tf_op jit(solution)/shard_map/forward/pallas_call | solution.py:85
  248.6 3.1 convolution_convert_fusion
  251.7 15.6 %all-to-all-done.1 = bf16[1,4,256,1024]{3,2,0,1:T(8,128)(2,1)S(1)} async-done(((bf16[1,4,256,1024]{3,2,0,1:T(8,128)(2,1)}), bf16[1,4,256,1024]{3,2,0,1:T(8,128)(2,1)S(1)}, u32[]{:S(2)}, u32[]{:S(2)}) %all-to-all-start.1) | async-done | bytes 2097184 | tf_op jit(solution)/shard_map/forward/all_to_all | solution.py:264
  267.3 4.4 all-to-all-start.2
  273.3 3.6 convert_element_type.261
  282.1 37.6 %all-to-all-done.2 = bf16[1,4,256,1024]{3,2,0,1:T(8,128)(2,1)} async-done(((bf16[1,4,256,1024]{3,2,0,1:T(8,128)(2,1)}), bf16[1,4,256,1024]{3,2,0,1:T(8,128)(2,1)}, u32[]{:S(2)}, u32[]{:S(2)}) %all-to-all-start.2) | async-done | bytes 2097184 | tf_op jit(solution)/shard_map/forward/all_to_all | solution.py:264
  321.8 2.8 multiply_reduce_fusion.10
  341.4 3.9 fusion.244
  356.9 4.5 fusion.136
  377.6 7.2 %fusion.60 = f32[512,4,512,1]{2,0,3,1:T(8,128)} fusion(bf16[512,4,256]{2,1,0:T(4,128)(2,1)} %reshape.936, bf16[4,4,1,256,512]{4,3,2,1,0:T(8,128)(2,1)} %copy-done.9), kind=kOutput, calls=%fused_computation.91 | convolution fusion | flops 2147483648 | bytes 9437184 | tf_op jit(solution)/shard_map/backward_ffn/crad,atdj->crtj/dot_general | solution.py:309
  387.2 9.0 %fusion.139 = bf16[1,512,1024]{2,1,0:T(8,128)(2,1)S(1)} fusion(bf16[1024,512,4]{1,0,2:T(8,128)(2,1)} %bitcast.618, f32[512,4,512,1]{2,0,3,1:T(8,128)} %fusion.60, f32[512,4,512,1]{2,0,3,1:T(8,128)} %copy-done.68), kind=kOutput, calls=%fused_computation.164 | convolution fusion | flops 2168979456 | bytes 13631488 | tf_op jit(solution)/shard_map/backward_ffn/crtj,atdj->crad/dot_general | solution.py:320
  396.4 6.1 fusion.75
  407.9 8.1 %fusion.43 = bf16[4,4,256,512]{3,2,0,1:T(8,128)(2,1)S(1)} fusion(f32[4,512,4,256]{1,3,2,0:T(8,128)} %fusion.75, f32[512,4,512,1]{2,0,3,1:T(8,128)} %copy-done.71, bf16[512,4,256]{0,2,1:T(8,128)(2,1)} %copy.266), kind=kOutput, calls=%fused_computation.62 | convolution fusion | flops 2161115136 | bytes 17825792 | tf_op jit(solution)/shard_map/backward_ffn/crad,crtj->atdj/dot_general | solution.py:312
  420.1 6.3 fusion.78
  426.4 6.7 fusion.42
  435.4 7.5 %pad_maximum_fusion = bf16[16,512,512]{2,1,0:T(8,128)(2,1)} fusion(bf16[16,256,512]{2,1,0:T(8,128)(2,1)} %bitcast.611, bf16[16,256,512]{2,1,0:T(8,128)(2,1)} %bitcast.613), kind=kLoop, calls=%fused_computation | loop fusion | flops 16777216 | bytes 16777216 | tf_op jit(solution)/shard_map/weight_grads/concatenate | solution.py:209
  443.9 3.1 fusion.145.g_ref
  447.0 32.5 %backward_attention.2 = (f32[1024,256]{1,0:T(8,128)}, f32[2048,256]{1,0:T(8,128)}, f32[2048,256]{1,0:T(8,128)}) custom-call(bf16[1024,256]{1,0:T(8,128)(2,1)} %get-tuple-element.159.q_ref, bf16[2048,256]{1,0:T(8,128)(2,1)} %maximum_bitcast_fusion.k_ref, bf16[2048,256]{1,0:T(8,128)(2,1)} %maximum_bitcast_fusion.1.v_ref, bf16[1024,256]{1,0:T(8,128)(2,1)} %fusion.145.g_ref, ...), custom_call_target="tpu_custom_call" | custom-call | flops 5368709120 | bytes 8912896 | tf_op jit(solution)/shard_map/backward_attention/pallas_call | solution.py:118
  484.5 3.2 bitcast_convert_fusion.1
  487.7 3.6 all-to-all-start.3
  491.4 3.1 fusion.148.g_ref
  494.6 32.3 %backward_attention.3 = (f32[1024,256]{1,0:T(8,128)}, f32[2048,256]{1,0:T(8,128)}, f32[2048,256]{1,0:T(8,128)}) custom-call(bf16[1024,256]{1,0:T(8,128)(2,1)} %get-tuple-element.162.q_ref, bf16[2048,256]{1,0:T(8,128)(2,1)} %maximum_bitcast_fusion.2.k_ref, bf16[2048,256]{1,0:T(8,128)(2,1)} %maximum_bitcast_fusion.3.v_ref, bf16[1024,256]{1,0:T(8,128)(2,1)} %fusion.148.g_ref, ...), custom_call_target="tpu_custom_call" | custom-call | flops 5368709120 | bytes 8912896 | tf_op jit(solution)/shard_map/backward_attention/pallas_call | solution.py:118
  540.3 3.7 fusion.177
  544.1 3.2 add_convert_fusion.2
  547.3 4.8 bitcast_convert_fusion
  552.1 5.1 all-to-all-start.4
  559.0 29.0 %reduce-scatter.7.cloned.1.call-done = bf16[128,256]{1,0:T(8,128)(2,1)} async-done(((bf16[1024,256]{1,0:T(8,128)(2,1)}), bf16[128,256]{1,0:T(8,128)(2,1)}) %reduce-scatter.7.cloned.1.call-update) | async-done | bytes 65552 | tf_op jit(solution)/shard_map/weight_grads/reduce_scatter | solution.py:406
  592.3 37.3 %reduce-scatter.5.cloned.1.call-done = bf16[128,3,256]{2,0,1:T(8,128)(2,1)} async-done(((bf16[1024,3,256]{2,0,1:T(8,128)(2,1)}), bf16[128,3,256]{2,0,1:T(8,128)(2,1)}) %reduce-scatter.5.cloned.1.call-update) | async-done | bytes 196624 | tf_op jit(solution)/shard_map/weight_grads/reduce_scatter | solution.py:406
  631.3 2.7 convert_reduce_fusion.2
  637.2 3.6 reshape.1149
  640.7 4.9 all-to-all-start.5
  647.0 3.5 add_convert_fusion.6
  650.5 25.7 %reduce-scatter.11.cloned.1.call-done = bf16[1,512,512]{2,1,0:T(8,128)(2,1)} async-done(((bf16[4,512,512]{2,1,0:T(8,128)(2,1)}), bf16[1,512,512]{2,1,0:T(8,128)(2,1)}) %reduce-scatter.11.cloned.1.call-update) | async-done | bytes 524304 | tf_op jit(solution)/shard_map/weight_grads/reduce_scatter | solution.py:212
  683.0 9.5 %all-gather.1 = f32[16,4,1,6,256]{4,1,0,3,2:T(4,128)S(1)} all-gather(f32[2,4,1,6,256]{4,1,0,3,2:T(4,128)S(1)} %bitcast.637), channel_id=3, replica_groups=mesh['dp'=4,'frame'=2,'tensor'=4] {'dp','frame'}, dimensions={0}, use_global_device_ids=true | all-gather | bytes 442368 | tf_op jit(solution)/shard_map/ada_grad/all_gather | solution.py:395
  (356 shorter events, 130.7 us)
Async XLA Ops:
  7.2 17.8 %copy-start = (bf16[128,6,256]{2,0,1:T(8,128)(2,1)S(1)}, bf16[128,6,256]{2,0,1:T(8,128)(2,1)}, u32[]{:S(2)}) copy-start(bf16[128,6,256]{2,0,1:T(8,128)(2,1)} %param.19) | copy-start | bytes 1179652
  7.2 57.9 %all-gather.12.cloned.1.call-start = ((), (), s32[]{:S(2)}) async-start(), calls=%async_computation.11 | async-start | bytes 2621440 | tf_op jit(solution)/shard_map/weights/all_gather | solution.py:202
  8.4 1.8 collective-permute-start.4
  10.1 1.4 collective-permute-start.3
  12.7 133.6 %all-gather.20.cloned.1.call-start = ((), (), s32[]{:S(2)}) async-start(), calls=%async_computation.19 | async-start | bytes 5242880 | tf_op jit(solution)/shard_map/group_inputs/all_gather | solution.py:234
  13.4 158.8 %all-gather.10.cloned.1.call-start = ((), (), s32[]{:S(2)}) async-start(), calls=%async_computation.10 | async-start | bytes 1769472 | tf_op jit(solution)/shard_map/weights/all_gather | solution.py:226
  14.1 327.2 %all-gather.14.cloned.1.call-start = ((), (), s32[]{:S(2)}) async-start(), calls=%async_computation.12 | async-start | bytes 10485760 | tf_op jit(solution)/shard_map/weights/all_gather | solution.py:203
  156.3 19.1 %copy-start.29 = (bf16[1024,1024,1]{1,0,2:T(8,128)(2,1)}, bf16[1024,1024,1]{1,0,2:T(8,128)(2,1)S(1)}, u32[]{:S(2)}) copy-start(bf16[1024,1024,1]{1,0,2:T(8,128)(2,1)S(1)} %get-tuple-element.145) | copy-start | bytes 6291460
  176.4 11.0 %collective-permute-start = (bf16[1,1024,256]{2,1,0:T(8,128)(2,1)S(1)}, bf16[1,1024,256]{2,1,0:T(8,128)(2,1)S(1)}, u32[]{:S(2)}, u32[]{:S(2)}) collective-permute-start(bf16[1,1024,256]{2,1,0:T(8,128)(2,1)S(1)} %get-tuple-element.158), channel_id=1, source_target_pairs={{0,4},{4,0},{1,5},{5,1},{2,6},{6,2},{3,7},{7,3},{8,12},{12,8},{9,1... | collective-permute-start | bytes 1572872 | tf_op jit(solution)/shard_map/forward/ppermute | solution.py:239
  176.6 11.9 %collective-permute-start.1 = (bf16[1,1024,256]{2,1,0:T(8,128)(2,1)S(1)}, bf16[1,1024,256]{2,1,0:T(8,128)(2,1)S(1)}, u32[]{:S(2)}, u32[]{:S(2)}) collective-permute-start(bf16[1,1024,256]{2,1,0:T(8,128)(2,1)S(1)} %get-tuple-element.157), channel_id=1, source_target_pairs={{0,4},{4,0},{1,5},{5,1},{2,6},{6,2},{3,7},{7,3},{8,12},{12,8},{9,1... | collective-permute-start | bytes 1572872 | tf_op jit(solution)/shard_map/forward/ppermute | solution.py:239
  187.4 61.2 %copy-start.18 = (bf16[1024,256]{1,0:T(8,128)(2,1)}, bf16[1024,256]{1,0:T(8,128)(2,1)S(1)}, u32[]{:S(2)}) copy-start(bf16[1024,256]{1,0:T(8,128)(2,1)S(1)} %all_gather.34) | copy-start | bytes 1572868
  213.8 53.5 %all-to-all-start.1 = ((bf16[1,4,256,1024]{3,2,0,1:T(8,128)(2,1)}), bf16[1,4,256,1024]{3,2,0,1:T(8,128)(2,1)S(1)}, u32[]{:S(2)}, u32[]{:S(2)}) async-start(bf16[1,4,256,1024]{3,2,0,1:T(8,128)(2,1)} %bitcast.616), calls=%async_computation.1 | async-start | bytes 4194304 | tf_op jit(solution)/shard_map/forward/all_to_all | solution.py:264
  223.4 1.9 collective-permute-start.6
  223.4 2.9 collective-permute-start.7
  267.3 52.4 %all-to-all-start.2 = ((bf16[1,4,256,1024]{3,2,0,1:T(8,128)(2,1)}), bf16[1,4,256,1024]{3,2,0,1:T(8,128)(2,1)}, u32[]{:S(2)}, u32[]{:S(2)}) async-start(bf16[1,4,256,1024]{3,2,0,1:T(8,128)(2,1)} %bitcast.615), calls=%async_computation.2 | async-start | bytes 4194304 | tf_op jit(solution)/shard_map/forward/all_to_all | solution.py:264
  271.8 171.1 %all-gather.16.cloned.1.call-start = ((), (), s32[]{:S(2)}) async-start(), calls=%async_computation.13 | async-start | bytes 2621440 | tf_op jit(solution)/shard_map/backward_attention/all_gather | solution.py:258
  273.3 48.5 %copy-start.2 = (f32[2,1,256,1024]{3,2,1,0:T(8,128)}, f32[2,1,256,1024]{3,2,1,0:T(8,128)S(1)}, u32[]{:S(2)}) copy-start(f32[2,1,256,1024]{3,2,1,0:T(8,128)S(1)} %convert_element_type.296) | copy-start | bytes 6291460
  277.1 47.5 %copy-start.58 = (f32[256]{0:T(256)}, f32[256]{0:T(256)S(1)}, u32[]{:S(2)}) copy-start(f32[256]{0:T(256)S(1)} %get-tuple-element.191) | copy-start | bytes 3076
  277.1 47.5 %copy-start.60 = (f32[256]{0:T(256)}, f32[256]{0:T(256)S(1)}, u32[]{:S(2)}) copy-start(f32[256]{0:T(256)S(1)} %get-tuple-element.192) | copy-start | bytes 3076
  279.6 49.0 %collective-permute-start.10 = (bf16[1,256,1024]{2,1,0:T(8,128)(2,1)}, bf16[1,256,1024]{2,1,0:T(8,128)(2,1)}, u32[]{:S(2)}, u32[]{:S(2)}) collective-permute-start(bf16[1,256,1024]{2,1,0:T(8,128)(2,1)} %multiply_convert_fusion.3), channel_id=1, source_target_pairs={{0,4},{4,0},{1,5},{5,1},{2,6},{6,2},{3,7},{7,3},{8,12},{12,8},{9,1... | collective-permute-start | bytes 1572872 | tf_op jit(solution)/shard_map/backward_ffn/ppermute | solution.py:239
  326.7 6.2 collective-permute-start.2
  328.0 7.4 %collective-permute-start.8 = (bf16[1,256,1024]{2,1,0:T(8,128)(2,1)}, bf16[1,256,1024]{2,1,0:T(8,128)(2,1)}, u32[]{:S(2)}, u32[]{:S(2)}) collective-permute-start(bf16[1,256,1024]{2,1,0:T(8,128)(2,1)} %add_convert_fusion.10), channel_id=1, source_target_pairs={{0,4},{4,0},{1,5},{5,1},{2,6},{6,2},{3,7},{7,3},{8,12},{12,8},{9,1... | collective-permute-start | bytes 1572872 | tf_op jit(solution)/shard_map/forward/ppermute | solution.py:239
  356.7 8.2 %collective-permute-start.5 = (bf16[1,256,1024]{2,1,0:T(8,128)(2,1)S(1)}, bf16[1,256,1024]{2,1,0:T(8,128)(2,1)S(1)}, u32[]{:S(2)}, u32[]{:S(2)}) collective-permute-start(bf16[1,256,1024]{2,1,0:T(8,128)(2,1)S(1)} %slice.284), channel_id=1, source_target_pairs={{0,4},{4,0},{1,5},{5,1},{2,6},{6,2},{3,7},{7,3},{8,12},{12,8},{9,1... | collective-permute-start | bytes 1572872 | tf_op jit(solution)/shard_map/forward/ppermute | solution.py:249
  361.4 2.9 collective-permute-start.11
  366.8 6.0 collective-permute-start.14
  371.2 31.9 %collective-permute-start.9 = (bf16[1,256,1024]{2,1,0:T(8,128)(2,1)}, bf16[1,256,1024]{2,1,0:T(8,128)(2,1)}, u32[]{:S(2)}, u32[]{:S(2)}) collective-permute-start(bf16[1,256,1024]{2,1,0:T(8,128)(2,1)} %slice.298), channel_id=1, source_target_pairs={{0,4},{4,0},{1,5},{5,1},{2,6},{6,2},{3,7},{7,3},{8,12},{12,8},{9,1... | collective-permute-start | bytes 1572872 | tf_op jit(solution)/shard_map/forward/ppermute | solution.py:249
  372.7 118.8 %all-gather.18.cloned.1.call-start = ((), (), s32[]{:S(2)}) async-start(), calls=%async_computation.14 | async-start | bytes 2621440 | tf_op jit(solution)/shard_map/backward_attention/all_gather | solution.py:258
  387.2 9.2 %copy-start.69 = (f32[512,4,512,1]{2,0,3,1:T(8,128)S(1)}, f32[512,4,512,1]{2,0,3,1:T(8,128)}, u32[]{:S(2)}) copy-start(f32[512,4,512,1]{2,0,3,1:T(8,128)} %copy-done.68) | copy-start | bytes 12582916
  396.3 6.2 collective-permute-start.15
  407.7 149.6 %reduce-scatter.9.cloned.1.call-start = ((), (), s32[]{:S(2)}) async-start(), calls=%async_computation.17 | async-start | bytes 10485760 | tf_op jit(solution)/shard_map/weight_grads/reduce_scatter | solution.py:211
  407.9 10.7 %copy-start.75 = (f32[512,4,512,1]{2,0,3,1:T(8,128)S(1)}, f32[512,4,512,1]{2,0,3,1:T(8,128)}, u32[]{:S(2)}) copy-start(f32[512,4,512,1]{2,0,3,1:T(8,128)} %fusion.60) | copy-start | bytes 12582916
  481.6 2.0 collective-permute-start.13
  482.2 2.2 collective-permute-start.12
  487.7 64.4 %all-to-all-start.3 = ((bf16[1,4,256,1024]{3,2,0,1:T(8,128)(2,1)}), bf16[1,4,256,1024]{3,2,0,1:T(8,128)(2,1)S(1)}, u32[]{:S(2)}, u32[]{:S(2)}) async-start(bf16[1,4,256,1024]{3,2,0,1:T(8,128)(2,1)} %bitcast.623), calls=%async_computation.3 | async-start | bytes 4194304 | tf_op jit(solution)/shard_map/backward_attention/all_to_all | solution.py:264
  491.4 96.6 %reduce-scatter.7.cloned.1.call-start = ((), (), s32[]{:S(2)}) async-start(), calls=%async_computation.16 | async-start | bytes 589824 | tf_op jit(solution)/shard_map/weight_grads/reduce_scatter | solution.py:406
  529.5 7.2 %collective-permute-start.17 = (bf16[1,1024,256]{2,1,0:T(8,128)(2,1)}, bf16[1,1024,256]{2,1,0:T(8,128)(2,1)}, u32[]{:S(2)}, u32[]{:S(2)}) collective-permute-start(bf16[1,1024,256]{2,1,0:T(8,128)(2,1)} %slice.313), channel_id=1, source_target_pairs={{0,4},{4,0},{1,5},{5,1},{2,6},{6,2},{3,7},{7,3},{8,12},{12,8},{9,1... | collective-permute-start | bytes 1572872 | tf_op jit(solution)/shard_map/backward_attention/ppermute | solution.py:249
  531.9 6.1 collective-permute-start.16
  536.4 93.2 %reduce-scatter.5.cloned.1.call-start = ((), (), s32[]{:S(2)}) async-start(), calls=%async_computation.15 | async-start | bytes 1769472 | tf_op jit(solution)/shard_map/weight_grads/reduce_scatter | solution.py:406
  552.1 79.2 %all-to-all-start.4 = ((bf16[1,4,256,1024]{3,2,0,1:T(8,128)(2,1)}), bf16[1,4,256,1024]{3,2,0,1:T(8,128)(2,1)}, u32[]{:S(2)}, u32[]{:S(2)}) async-start(bf16[1,4,256,1024]{3,2,0,1:T(8,128)(2,1)} %bitcast.624), calls=%async_computation.4 | async-start | bytes 4194304 | tf_op jit(solution)/shard_map/backward_attention/all_to_all | solution.py:264
  557.2 34.9 %copy-start.56 = (f32[1,1,1,1024]{3,1,2,0:T(1,128)S(1)}, f32[1,1,1,1024]{3,1,2,0:T(1,128)}, u32[]{:S(2)}) copy-start(f32[1,1,1,1024]{3,1,2,0:T(1,128)} %get-tuple-element.180) | copy-start | bytes 12292
  557.2 119.0 %reduce-scatter.11.cloned.1.call-start = ((), (), s32[]{:S(2)}) async-start(), calls=%async_computation.18 | async-start | bytes 2621440 | tf_op jit(solution)/shard_map/weight_grads/reduce_scatter | solution.py:212
  558.9 76.1 %copy-start.3 = (f32[2,1,256,1024]{3,2,1,0:T(8,128)S(1)}, f32[2,1,256,1024]{3,2,1,0:T(8,128)}, u32[]{:S(2)}) copy-start(f32[2,1,256,1024]{3,2,1,0:T(8,128)} %copy-done.2) | copy-start | bytes 6291460
  558.9 76.1 %copy-start.55 = (f32[1,1,1,1024]{3,1,2,0:T(1,128)S(1)}, f32[1,1,1,1024]{3,1,2,0:T(1,128)}, u32[]{:S(2)}) copy-start(f32[1,1,1,1024]{3,1,2,0:T(1,128)} %get-tuple-element.184) | copy-start | bytes 12292
  559.0 76.1 %copy-start.59 = (f32[256]{0:T(256)S(1)}, f32[256]{0:T(256)}, u32[]{:S(2)}) copy-start(f32[256]{0:T(256)} %copy-done.58) | copy-start | bytes 3076
  559.0 76.1 %copy-start.61 = (f32[256]{0:T(256)S(1)}, f32[256]{0:T(256)}, u32[]{:S(2)}) copy-start(f32[256]{0:T(256)} %copy-done.60) | copy-start | bytes 3076
  640.7 38.9 %all-to-all-start.5 = ((f32[4,1,3072]{2,1,0:T(1,128)}), f32[4,1,3072]{2,1,0:T(1,128)S(1)}, u32[]{:S(2)}, u32[]{:S(2)}) async-start(f32[4,1,3072]{2,1,0:T(1,128)} %reshape.1149), calls=%async_computation.9 | async-start | bytes 98304 | tf_op jit(solution)/shard_map/ada_grad/all_to_all | solution.py:392
  650.5 42.0 %copy-start.54 = (bf16[8,2,4,128]{3,0,2,1:T(8,128)(2,1)S(1)}, bf16[8,2,4,128]{3,0,2,1:T(8,128)(2,1)}, u32[]{:S(2)}) copy-start(bf16[8,2,4,128]{3,0,2,1:T(8,128)(2,1)} %copy-done.53) | copy-start | bytes 49156
  677.3 16.7 %collective-permute-start.18 = (bf16[2,128,512]{2,1,0:T(8,128)(2,1)S(1)}, bf16[2,128,512]{2,1,0:T(8,128)(2,1)S(1)}, u32[]{:S(2)}, u32[]{:S(2)}) collective-permute-start(bf16[2,128,512]{2,1,0:T(8,128)(2,1)S(1)} %get-tuple-element.167), channel_id=1, source_target_pairs={{0,4},{4,0},{1,5},{5,1},{2,6},{6,2},{3,7},{7,3},{8,12},{12,8},{9,1... | collective-permute-start | bytes 786440 | tf_op jit(solution)/shard_map/weight_grads/ppermute | solution.py:216
  (62 other events, 250.5 us)
Sparse Core Ops, SparseCore 0:
  12.8 52.2 all-gather.11
  66.6 79.5 all-gather.19
  148.1 24.0 all-gather.9
  173.9 87.4 all-gather.13
  372.8 43.7 all-gather.15
  418.0 44.4 all-gather.17
  465.6 85.1 reduce-scatter.8
  553.8 34.0 reduce-scatter.6
  591.2 38.3 reduce-scatter.4
  631.7 44.4 reduce-scatter.10

commit v12 on v11

--- a/solution.py
+++ b/solution.py
@@ -226,13 +226,17 @@
             lax.all_gather(w, ("dp", "frame"), axis=0, tiled=True)
             for w in (qkv_weight, out_weight)
         )
-        upward_weight, downward_weight = hidden_half((up_weight, down_weight))
 
     residual = tokens[:, 0].astype(jnp.float32)
     upstream = out_grad[:, 0].astype(jnp.float32)
     with jax.named_scope("group_inputs"):
         group_tokens = lax.all_gather(tokens[:, 0], "tensor", axis=1, tiled=True)
         group_upstream = None
+    with jax.named_scope("ffn_weights"):
+        group_tokens, joint_weight, mixer_weight, ffn_shards = lax.optimization_barrier(
+            (group_tokens, joint_weight, mixer_weight, (up_weight, down_weight))
+        )
+        upward_weight, downward_weight = hidden_half(ffn_shards)
     def gather_halves(values):
         if halves != 2:
             return lax.all_gather(values, "frame", axis=1, tiled=True)

time: 712 us -> 714 us (level)
    unnamed x161 -> x159, local copies, waits for them, and re-layouts: 22.3 us -> 20.7 us
  transfers between devices with their start and end apart: 34 -> 34, of which waited for: 12 -> 13; matrix products, arithmetic and copies ran while one was open for 29% -> 29% of each run, Pallas kernels for 15% -> 15%
where the time goes in v12:
time: 714 us; the launch traced here: 709 us
  waiting for transfers between devices  266 us (37%)
  Pallas kernels  107 us (15%)
  matrix products  98.2 us (14%)
  other arithmetic  81.9 us (11%)
  blocking collectives  57.6 us (8%)
  local copies, waits for them, and re-layouts  54.8 us (8%)
  starting transfers between devices  27.5 us (4%)
  between operations  15.9 us (2%)
    all_gather x1, waiting for transfers between devices, on_device(): group_tokens = lax.all_gather(tokens[:, 0], 'tensor', axis=1, tiled=True)  82.3 us
    reduce_scatter x2, waiting for transfers between devices, on_device(): lax.psum_scatter(total.astype(jnp.bfloat16), ('dp', 'frame'), scatter_dim...  66.8 us
    pallas_call x2, Pallas kernels, attention_backward(): pl.pallas_call(functools.partial(_backward_kernel, heads, HEAD_DIM ** (-0...  65 us
    all_to_all x4, waiting for transfers between devices, scatter_tokens(): received = lax.all_to_all(parts, 'tensor', 1, 1, tiled=True)  52.4 us
    pallas_call x2, Pallas kernels, attention_forward(): pl.pallas_call(functools.partial(_forward_kernel, heads, HEAD_DIM ** (-0....  42.2 us
    reduce_scatter x1, waiting for transfers between devices, hidden_half_back(): summed = lax.psum_scatter(summed, 'tensor', scatter_dimension=0, tiled=True)  25.7 us
    unnamed x159, local copies, waits for them, and re-layouts  20.7 us
    all_gather x1, waiting for transfers between devices, on_device(): lax.all_gather(w, ('dp', 'frame'), axis=0, tiled=True)  17.9 us
  transfers between devices with their start and end apart: 34, of which 13 were waited for; matrix products, arithmetic and copies ran while one was open for 29% of the time, Pallas kernels for 15%

profile of v12, /device:TPU:0, one launch (start us, length us, event | category | flops | bytes accessed | tf_op | source)
XLA Modules:
  0.0 709.1 jit_solution(2441077731835844843)
XLA Ops:
  8.7 11.6 %all_gather.34 = bf16[1024,256]{1,0:T(8,128)(2,1)S(1)} all-gather(bf16[128,256]{1,0:T(8,128)(2,1)} %param.16), channel_id=1, replica_groups=mesh['dp'=4,'frame'=2,'tensor'=4] {'dp','frame'}, dimensions={0}, use_global_device_ids=true | all-gather | bytes 589824 | tf_op jit(solution)/shard_map/weights/all_gather | solution.py:226
  20.4 17.9 %all-gather.10.cloned.1.call-done = bf16[1024,3,256]{2,0,1:T(8,128)(2,1)} async-done(((bf16[128,3,256]{2,0,1:T(8,128)(2,1)}), bf16[1024,3,256]{2,0,1:T(8,128)(2,1)}) %all-gather.10.cloned.1.call-update) | async-done | bytes 1572880 | tf_op jit(solution)/shard_map/weights/all_gather | solution.py:226
  38.2 82.3 %all-gather.20.cloned.1.call-done = bf16[2,1,1024,1024]{3,2,1,0:T(8,128)(2,1)} async-done(((bf16[2,1,256,1024]{3,2,1,0:T(8,128)(2,1)}), bf16[2,1,1024,1024]{3,2,1,0:T(8,128)(2,1)}) %all-gather.20.cloned.1.call-update) | async-done | bytes 4194320 | tf_op jit(solution)/shard_map/group_inputs/all_gather | solution.py:233
  121.8 9.0 %all-gather.2 = s32[8,2,4]{2,1,0:T(2,128)S(1)} all-gather(s32[1,2,4]{2,1,0:T(2,128)} %bitcast.645), channel_id=1, replica_groups=mesh['dp'=4,'frame'=2,'tensor'=4] {'dp','frame'}, dimensions={0}, use_global_device_ids=true | all-gather | bytes 288 | tf_op jit(solution)/shard_map/modulation/all_gather | solution.py:168
  135.9 10.7 %all_to_all.43 = f32[8,2,4,6,256]{4,2,3,1,0:T(4,128)S(1)} all-to-all(f32[8,2,4,6,256]{4,2,3,1,0:T(4,128)S(1)} %fusion.180), channel_id=1, replica_groups=mesh['dp'=4,'frame'=2,'tensor'=4] {'dp','frame'}, dimensions={0} | all-to-all | bytes 786432 | tf_op jit(solution)/shard_map/modulation/all_to_all | solution.py:179
  146.7 16.7 %all_gather.31 = f32[2,4,6,1024]{3,2,1,0:T(8,128)S(1)} all-gather(f32[2,4,6,256]{3,2,1,0:T(8,128)S(1)} %copy.301), channel_id=1, replica_groups=mesh['dp'=4,'frame'=2,'tensor'=4] {'tensor'}, dimensions={3}, use_global_device_ids=true | all-gather | bytes 245760 | tf_op jit(solution)/shard_map/modulation/all_gather | solution.py:181
  163.6 2.9 convert_reduce_fusion.5
  168.2 13.8 %all-gather.12.cloned.1.call-done = bf16[2048,512]{1,0:T(8,128)(2,1)} async-done(((bf16[512,512]{1,0:T(8,128)(2,1)}), bf16[2048,512]{1,0:T(8,128)(2,1)}) %all-gather.12.cloned.1.call-update) | async-done | bytes 2097168 | tf_op jit(solution)/shard_map/ffn_weights/all_gather | solution.py:202
  185.4 2.8 fusion.70
  194.9 21.1 %forward.2 = (bf16[1024,256]{1,0:T(8,128)(2,1)}, f32[1024,4]{1,0:T(8,128)}) custom-call(bf16[1024,256]{1,0:T(8,128)(2,1)} %get-tuple-element.169.q_ref, bf16[2048,256]{1,0:T(8,128)(2,1)} %maximum_bitcast_fusion.k_ref, bf16[2048,256]{1,0:T(8,128)(2,1)} %maximum_bitcast_fusion.1.v_ref), custom_call_target="tpu_custom_call" | custom-call | flops 2147483648 | bytes 3145728 | tf_op jit(solution)/shard_map/forward/pallas_call | solution.py:85
  216.0 3.2 convolution_convert_fusion.1
  219.2 3.8 all-to-all-start.1
  223.0 4.8 fusion.127
  232.8 21.1 %forward.3 = (bf16[1024,256]{1,0:T(8,128)(2,1)}, f32[1024,4]{1,0:T(8,128)}) custom-call(bf16[1024,256]{1,0:T(8,128)(2,1)} %get-tuple-element.172.q_ref, bf16[2048,256]{1,0:T(8,128)(2,1)} %maximum_bitcast_fusion.2.k_ref, bf16[2048,256]{1,0:T(8,128)(2,1)} %maximum_bitcast_fusion.3.v_ref), custom_call_target="tpu_custom_call" | custom-call | flops 2147483648 | bytes 3145728 | tf_op jit(solution)/shard_map/forward/pallas_call | solution.py:85
  253.9 3.1 convolution_convert_fusion
  257.0 14.7 %all-to-all-done.1 = bf16[1,4,256,1024]{3,2,0,1:T(8,128)(2,1)S(1)} async-done(((bf16[1,4,256,1024]{3,2,0,1:T(8,128)(2,1)}), bf16[1,4,256,1024]{3,2,0,1:T(8,128)(2,1)S(1)}, u32[]{:S(2)}, u32[]{:S(2)}) %all-to-all-start.1) | async-done | bytes 2097184 | tf_op jit(solution)/shard_map/forward/all_to_all | solution.py:268
  271.7 4.4 all-to-all-start.2
  277.7 3.6 convert_element_type.261
  286.5 37.7 %all-to-all-done.2 = bf16[1,4,256,1024]{3,2,0,1:T(8,128)(2,1)} async-done(((bf16[1,4,256,1024]{3,2,0,1:T(8,128)(2,1)}), bf16[1,4,256,1024]{3,2,0,1:T(8,128)(2,1)}, u32[]{:S(2)}, u32[]{:S(2)}) %all-to-all-start.2) | async-done | bytes 2097184 | tf_op jit(solution)/shard_map/forward/all_to_all | solution.py:268
  326.3 2.8 multiply_reduce_fusion.10
  345.8 3.9 fusion.242
  361.3 4.5 fusion.134
  382.1 7.2 %fusion.58 = f32[512,4,512,1]{2,0,3,1:T(8,128)} fusion(bf16[512,4,256]{2,1,0:T(4,128)(2,1)} %reshape.936, bf16[4,4,1,256,512]{4,3,2,1,0:T(8,128)(2,1)} %copy-done.10), kind=kOutput, calls=%fused_computation.89 | convolution fusion | flops 2147483648 | bytes 9437184 | tf_op jit(solution)/shard_map/backward_ffn/crad,atdj->crtj/dot_general | solution.py:313
  391.7 9.0 %fusion.137 = bf16[1,512,1024]{2,1,0:T(8,128)(2,1)S(1)} fusion(bf16[1024,512,4]{1,0,2:T(8,128)(2,1)} %bitcast.586, f32[512,4,512,1]{2,0,3,1:T(8,128)} %fusion.58, f32[512,4,512,1]{2,0,3,1:T(8,128)} %copy-done.68), kind=kOutput, calls=%fused_computation.162 | convolution fusion | flops 2168979456 | bytes 13631488 | tf_op jit(solution)/shard_map/backward_ffn/crtj,atdj->crad/dot_general | solution.py:324
  400.9 6.1 fusion.73
  412.4 8.1 %fusion.41 = bf16[4,4,256,512]{3,2,0,1:T(8,128)(2,1)S(1)} fusion(f32[4,512,4,256]{1,3,2,0:T(8,128)} %fusion.73, f32[512,4,512,1]{2,0,3,1:T(8,128)} %copy-done.71, bf16[512,4,256]{0,2,1:T(8,128)(2,1)} %copy.266), kind=kOutput, calls=%fused_computation.60 | convolution fusion | flops 2161115136 | bytes 17825792 | tf_op jit(solution)/shard_map/backward_ffn/crad,crtj->atdj/dot_general | solution.py:316
  424.5 6.3 fusion.76
  430.8 6.7 fusion.40
  439.8 7.5 %pad_maximum_fusion = bf16[16,512,512]{2,1,0:T(8,128)(2,1)} fusion(bf16[16,256,512]{2,1,0:T(8,128)(2,1)} %bitcast.579, bf16[16,256,512]{2,1,0:T(8,128)(2,1)} %bitcast.581), kind=kLoop, calls=%fused_computation | loop fusion | flops 16777216 | bytes 16777216 | tf_op jit(solution)/shard_map/weight_grads/concatenate | solution.py:209
  448.4 3.1 fusion.143.g_ref
  451.5 32.6 %backward_attention.2 = (f32[1024,256]{1,0:T(8,128)}, f32[2048,256]{1,0:T(8,128)}, f32[2048,256]{1,0:T(8,128)}) custom-call(bf16[1024,256]{1,0:T(8,128)(2,1)} %get-tuple-element.169.q_ref, bf16[2048,256]{1,0:T(8,128)(2,1)} %maximum_bitcast_fusion.k_ref, bf16[2048,256]{1,0:T(8,128)(2,1)} %maximum_bitcast_fusion.1.v_ref, bf16[1024,256]{1,0:T(8,128)(2,1)} %fusion.143.g_ref, ...), custom_call_target="tpu_custom_call" | custom-call | flops 5368709120 | bytes 8912896 | tf_op jit(solution)/shard_map/backward_attention/pallas_call | solution.py:118
  489.0 3.2 bitcast_convert_fusion.1
  492.2 3.6 all-to-all-start.3
  495.9 3.3 fusion.146.g_ref
  499.2 32.4 %backward_attention.3 = (f32[1024,256]{1,0:T(8,128)}, f32[2048,256]{1,0:T(8,128)}, f32[2048,256]{1,0:T(8,128)}) custom-call(bf16[1024,256]{1,0:T(8,128)(2,1)} %get-tuple-element.172.q_ref, bf16[2048,256]{1,0:T(8,128)(2,1)} %maximum_bitcast_fusion.2.k_ref, bf16[2048,256]{1,0:T(8,128)(2,1)} %maximum_bitcast_fusion.3.v_ref, bf16[1024,256]{1,0:T(8,128)(2,1)} %fusion.146.g_ref, ...), custom_call_target="tpu_custom_call" | custom-call | flops 5368709120 | bytes 8912896 | tf_op jit(solution)/shard_map/backward_attention/pallas_call | solution.py:118
  545.2 3.7 fusion.175
  549.0 3.1 add_convert_fusion.2
  552.2 4.7 bitcast_convert_fusion
  557.0 5.1 all-to-all-start.4
  563.8 29.5 %reduce-scatter.7.cloned.1.call-done = bf16[128,256]{1,0:T(8,128)(2,1)} async-done(((bf16[1024,256]{1,0:T(8,128)(2,1)}), bf16[128,256]{1,0:T(8,128)(2,1)}) %reduce-scatter.7.cloned.1.call-update) | async-done | bytes 65552 | tf_op jit(solution)/shard_map/weight_grads/reduce_scatter | solution.py:410
  594.8 2.7 convert_reduce_fusion.2
  597.7 37.3 %reduce-scatter.5.cloned.1.call-done = bf16[128,3,256]{2,0,1:T(8,128)(2,1)} async-done(((bf16[1024,3,256]{2,0,1:T(8,128)(2,1)}), bf16[128,3,256]{2,0,1:T(8,128)(2,1)}) %reduce-scatter.5.cloned.1.call-update) | async-done | bytes 196624 | tf_op jit(solution)/shard_map/weight_grads/reduce_scatter | solution.py:410
  636.7 2.7 convert_reduce_fusion
  642.6 3.6 reshape.1145
  646.1 4.9 all-to-all-start.5
  652.4 3.5 add_convert_fusion.6
  655.9 25.7 %reduce-scatter.11.cloned.1.call-done = bf16[1,512,512]{2,1,0:T(8,128)(2,1)} async-done(((bf16[4,512,512]{2,1,0:T(8,128)(2,1)}), bf16[1,512,512]{2,1,0:T(8,128)(2,1)}) %reduce-scatter.11.cloned.1.call-update) | async-done | bytes 524304 | tf_op jit(solution)/shard_map/weight_grads/reduce_scatter | solution.py:212
  688.4 9.5 %all-gather.1 = f32[16,4,1,6,256]{4,1,0,3,2:T(4,128)S(1)} all-gather(f32[2,4,1,6,256]{4,1,0,3,2:T(4,128)S(1)} %bitcast.605), channel_id=3, replica_groups=mesh['dp'=4,'frame'=2,'tensor'=4] {'dp','frame'}, dimensions={0}, use_global_device_ids=true | all-gather | bytes 442368 | tf_op jit(solution)/shard_map/ada_grad/all_gather | solution.py:399
  (356 shorter events, 131.5 us)
Async XLA Ops:
  7.2 128.1 %copy-start = (bf16[128,6,256]{2,0,1:T(8,128)(2,1)S(1)}, bf16[128,6,256]{2,0,1:T(8,128)(2,1)}, u32[]{:S(2)}) copy-start(bf16[128,6,256]{2,0,1:T(8,128)(2,1)} %param.19) | copy-start | bytes 1179652
  7.2 31.0 %all-gather.10.cloned.1.call-start = ((), (), s32[]{:S(2)}) async-start(), calls=%async_computation.10 | async-start | bytes 1769472 | tf_op jit(solution)/shard_map/weights/all_gather | solution.py:226
  7.9 112.6 %all-gather.20.cloned.1.call-start = ((), (), s32[]{:S(2)}) async-start(), calls=%async_computation.19 | async-start | bytes 5242880 | tf_op jit(solution)/shard_map/group_inputs/all_gather | solution.py:233
  8.7 173.4 %all-gather.12.cloned.1.call-start = ((), (), s32[]{:S(2)}) async-start(), calls=%async_computation.11 | async-start | bytes 2621440 | tf_op jit(solution)/shard_map/ffn_weights/all_gather | solution.py:202
  20.4 233.5 %copy-start.19 = (bf16[1024,256]{1,0:T(8,128)(2,1)}, bf16[1024,256]{1,0:T(8,128)(2,1)S(1)}, u32[]{:S(2)}) copy-start(bf16[1024,256]{1,0:T(8,128)(2,1)S(1)} %all_gather.34) | copy-start | bytes 1572868
  121.7 10.8 %collective-permute-start.4 = (bf16[128,512]{0,1:T(8,128)(2,1)S(1)}, bf16[128,512]{0,1:T(8,128)(2,1)S(1)}, u32[]{:S(2)}, u32[]{:S(2)}) collective-permute-start(bf16[128,512]{0,1:T(8,128)(2,1)S(1)} %get-tuple-element.185), channel_id=1, source_target_pairs={{0,4},{4,0},{1,5},{5,1},{2,6},{6,2},{3,7},{7,3},{8,12},{12,8},{9,1... | collective-permute-start | bytes 393224 | tf_op jit(solution)/shard_map/ffn_weights/ppermute | solution.py:199
  132.1 1.4 collective-permute-start.3
  134.6 211.2 %all-gather.14.cloned.1.call-start = ((), (), s32[]{:S(2)}) async-start(), calls=%async_computation.12 | async-start | bytes 10485760 | tf_op jit(solution)/shard_map/ffn_weights/all_gather | solution.py:203
  146.7 19.8 %copy-start.4 = (bf16[2,1,1024,1024]{3,2,1,0:T(8,128)(2,1)S(1)}, bf16[2,1,1024,1024]{3,2,1,0:T(8,128)(2,1)}, u32[]{:S(2)}) copy-start(bf16[2,1,1024,1024]{3,2,1,0:T(8,128)(2,1)} %all-gather.20.cloned.1.call-done) | copy-start | bytes 12582916
  190.9 1.9 collective-permute-start
  190.9 2.9 collective-permute-start.1
  219.2 52.6 %all-to-all-start.1 = ((bf16[1,4,256,1024]{3,2,0,1:T(8,128)(2,1)}), bf16[1,4,256,1024]{3,2,0,1:T(8,128)(2,1)S(1)}, u32[]{:S(2)}, u32[]{:S(2)}) async-start(bf16[1,4,256,1024]{3,2,0,1:T(8,128)(2,1)} %bitcast.584), calls=%async_computation.1 | async-start | bytes 4194304 | tf_op jit(solution)/shard_map/forward/all_to_all | solution.py:268
  228.7 1.9 collective-permute-start.6
  228.9 2.7 collective-permute-start.7
  271.7 52.4 %all-to-all-start.2 = ((bf16[1,4,256,1024]{3,2,0,1:T(8,128)(2,1)}), bf16[1,4,256,1024]{3,2,0,1:T(8,128)(2,1)}, u32[]{:S(2)}, u32[]{:S(2)}) async-start(bf16[1,4,256,1024]{3,2,0,1:T(8,128)(2,1)} %bitcast.583), calls=%async_computation.2 | async-start | bytes 4194304 | tf_op jit(solution)/shard_map/forward/all_to_all | solution.py:268
  276.2 171.2 %all-gather.16.cloned.1.call-start = ((), (), s32[]{:S(2)}) async-start(), calls=%async_computation.13 | async-start | bytes 2621440 | tf_op jit(solution)/shard_map/backward_attention/all_gather | solution.py:262
  277.7 48.6 %copy-start.2 = (f32[2,1,256,1024]{3,2,1,0:T(8,128)}, f32[2,1,256,1024]{3,2,1,0:T(8,128)S(1)}, u32[]{:S(2)}) copy-start(f32[2,1,256,1024]{3,2,1,0:T(8,128)S(1)} %convert_element_type.296) | copy-start | bytes 6291460
  281.5 47.5 %copy-start.58 = (f32[256]{0:T(256)}, f32[256]{0:T(256)S(1)}, u32[]{:S(2)}) copy-start(f32[256]{0:T(256)S(1)} %get-tuple-element.201) | copy-start | bytes 3076
  281.5 47.5 %copy-start.60 = (f32[256]{0:T(256)}, f32[256]{0:T(256)S(1)}, u32[]{:S(2)}) copy-start(f32[256]{0:T(256)S(1)} %get-tuple-element.202) | copy-start | bytes 3076
  284.0 49.0 %collective-permute-start.10 = (bf16[1,256,1024]{2,1,0:T(8,128)(2,1)}, bf16[1,256,1024]{2,1,0:T(8,128)(2,1)}, u32[]{:S(2)}, u32[]{:S(2)}) collective-permute-start(bf16[1,256,1024]{2,1,0:T(8,128)(2,1)} %multiply_convert_fusion.3), channel_id=1, source_target_pairs={{0,4},{4,0},{1,5},{5,1},{2,6},{6,2},{3,7},{7,3},{8,12},{12,8},{9,1... | collective-permute-start | bytes 1572872 | tf_op jit(solution)/shard_map/backward_ffn/ppermute | solution.py:243
  331.1 6.2 collective-permute-start.2
  332.5 7.4 %collective-permute-start.8 = (bf16[1,256,1024]{2,1,0:T(8,128)(2,1)}, bf16[1,256,1024]{2,1,0:T(8,128)(2,1)}, u32[]{:S(2)}, u32[]{:S(2)}) collective-permute-start(bf16[1,256,1024]{2,1,0:T(8,128)(2,1)} %add_convert_fusion.10), channel_id=1, source_target_pairs={{0,4},{4,0},{1,5},{5,1},{2,6},{6,2},{3,7},{7,3},{8,12},{12,8},{9,1... | collective-permute-start | bytes 1572872 | tf_op jit(solution)/shard_map/forward/ppermute | solution.py:243
  361.1 8.2 %collective-permute-start.5 = (bf16[1,256,1024]{2,1,0:T(8,128)(2,1)S(1)}, bf16[1,256,1024]{2,1,0:T(8,128)(2,1)S(1)}, u32[]{:S(2)}, u32[]{:S(2)}) collective-permute-start(bf16[1,256,1024]{2,1,0:T(8,128)(2,1)S(1)} %slice.281), channel_id=1, source_target_pairs={{0,4},{4,0},{1,5},{5,1},{2,6},{6,2},{3,7},{7,3},{8,12},{12,8},{9,1... | collective-permute-start | bytes 1572872 | tf_op jit(solution)/shard_map/forward/ppermute | solution.py:253
  365.9 2.9 collective-permute-start.11
  371.2 6.0 collective-permute-start.14
  375.7 31.9 %collective-permute-start.9 = (bf16[1,256,1024]{2,1,0:T(8,128)(2,1)}, bf16[1,256,1024]{2,1,0:T(8,128)(2,1)}, u32[]{:S(2)}, u32[]{:S(2)}) collective-permute-start(bf16[1,256,1024]{2,1,0:T(8,128)(2,1)} %slice.294), channel_id=1, source_target_pairs={{0,4},{4,0},{1,5},{5,1},{2,6},{6,2},{3,7},{7,3},{8,12},{12,8},{9,1... | collective-permute-start | bytes 1572872 | tf_op jit(solution)/shard_map/forward/ppermute | solution.py:253
  377.1 118.8 %all-gather.18.cloned.1.call-start = ((), (), s32[]{:S(2)}) async-start(), calls=%async_computation.14 | async-start | bytes 2621440 | tf_op jit(solution)/shard_map/backward_attention/all_gather | solution.py:262
  391.7 9.2 %copy-start.69 = (f32[512,4,512,1]{2,0,3,1:T(8,128)S(1)}, f32[512,4,512,1]{2,0,3,1:T(8,128)}, u32[]{:S(2)}) copy-start(f32[512,4,512,1]{2,0,3,1:T(8,128)} %copy-done.68) | copy-start | bytes 12582916
  400.8 6.3 collective-permute-start.15
  412.1 150.0 %reduce-scatter.9.cloned.1.call-start = ((), (), s32[]{:S(2)}) async-start(), calls=%async_computation.17 | async-start | bytes 10485760 | tf_op jit(solution)/shard_map/weight_grads/reduce_scatter | solution.py:211
  412.4 10.7 %copy-start.75 = (f32[512,4,512,1]{2,0,3,1:T(8,128)S(1)}, f32[512,4,512,1]{2,0,3,1:T(8,128)}, u32[]{:S(2)}) copy-start(f32[512,4,512,1]{2,0,3,1:T(8,128)} %fusion.58) | copy-start | bytes 12582916
  486.0 2.1 collective-permute-start.13
  486.7 2.1 collective-permute-start.12
  492.2 64.8 %all-to-all-start.3 = ((bf16[1,4,256,1024]{3,2,0,1:T(8,128)(2,1)}), bf16[1,4,256,1024]{3,2,0,1:T(8,128)(2,1)S(1)}, u32[]{:S(2)}, u32[]{:S(2)}) async-start(bf16[1,4,256,1024]{3,2,0,1:T(8,128)(2,1)} %bitcast.591), calls=%async_computation.3 | async-start | bytes 4194304 | tf_op jit(solution)/shard_map/backward_attention/all_to_all | solution.py:268
  495.8 97.5 %reduce-scatter.7.cloned.1.call-start = ((), (), s32[]{:S(2)}) async-start(), calls=%async_computation.16 | async-start | bytes 589824 | tf_op jit(solution)/shard_map/weight_grads/reduce_scatter | solution.py:410
  534.3 7.3 %collective-permute-start.17 = (bf16[1,1024,256]{2,1,0:T(8,128)(2,1)}, bf16[1,1024,256]{2,1,0:T(8,128)(2,1)}, u32[]{:S(2)}, u32[]{:S(2)}) collective-permute-start(bf16[1,1024,256]{2,1,0:T(8,128)(2,1)} %slice.309), channel_id=1, source_target_pairs={{0,4},{4,0},{1,5},{5,1},{2,6},{6,2},{3,7},{7,3},{8,12},{12,8},{9,1... | collective-permute-start | bytes 1572872 | tf_op jit(solution)/shard_map/backward_attention/ppermute | solution.py:253
  536.3 6.6 collective-permute-start.16
  541.3 93.7 %reduce-scatter.5.cloned.1.call-start = ((), (), s32[]{:S(2)}) async-start(), calls=%async_computation.15 | async-start | bytes 1769472 | tf_op jit(solution)/shard_map/weight_grads/reduce_scatter | solution.py:410
  557.0 79.7 %all-to-all-start.4 = ((bf16[1,4,256,1024]{3,2,0,1:T(8,128)(2,1)}), bf16[1,4,256,1024]{3,2,0,1:T(8,128)(2,1)}, u32[]{:S(2)}, u32[]{:S(2)}) async-start(bf16[1,4,256,1024]{3,2,0,1:T(8,128)(2,1)} %bitcast.592), calls=%async_computation.4 | async-start | bytes 4194304 | tf_op jit(solution)/shard_map/backward_attention/all_to_all | solution.py:268
  562.1 35.4 %copy-start.57 = (f32[1,1,1,1024]{3,1,2,0:T(1,128)S(1)}, f32[1,1,1,1024]{3,1,2,0:T(1,128)}, u32[]{:S(2)}) copy-start(f32[1,1,1,1024]{3,1,2,0:T(1,128)} %get-tuple-element.190) | copy-start | bytes 12292
  562.1 119.5 %reduce-scatter.11.cloned.1.call-start = ((), (), s32[]{:S(2)}) async-start(), calls=%async_computation.18 | async-start | bytes 2621440 | tf_op jit(solution)/shard_map/weight_grads/reduce_scatter | solution.py:212
  563.8 76.6 %copy-start.3 = (f32[2,1,256,1024]{3,2,1,0:T(8,128)S(1)}, f32[2,1,256,1024]{3,2,1,0:T(8,128)}, u32[]{:S(2)}) copy-start(f32[2,1,256,1024]{3,2,1,0:T(8,128)} %copy-done.2) | copy-start | bytes 6291460
  563.8 76.6 %copy-start.56 = (f32[1,1,1,1024]{3,1,2,0:T(1,128)S(1)}, f32[1,1,1,1024]{3,1,2,0:T(1,128)}, u32[]{:S(2)}) copy-start(f32[1,1,1,1024]{3,1,2,0:T(1,128)} %get-tuple-element.194) | copy-start | bytes 12292
  563.8 76.6 %copy-start.59 = (f32[256]{0:T(256)S(1)}, f32[256]{0:T(256)}, u32[]{:S(2)}) copy-start(f32[256]{0:T(256)} %copy-done.58) | copy-start | bytes 3076
  563.8 76.6 %copy-start.61 = (f32[256]{0:T(256)S(1)}, f32[256]{0:T(256)}, u32[]{:S(2)}) copy-start(f32[256]{0:T(256)} %copy-done.60) | copy-start | bytes 3076
  646.1 38.9 %all-to-all-start.5 = ((f32[4,1,3072]{2,1,0:T(1,128)}), f32[4,1,3072]{2,1,0:T(1,128)S(1)}, u32[]{:S(2)}, u32[]{:S(2)}) async-start(f32[4,1,3072]{2,1,0:T(1,128)} %reshape.1145), calls=%async_computation.9 | async-start | bytes 98304 | tf_op jit(solution)/shard_map/ada_grad/all_to_all | solution.py:396
  655.9 42.0 %copy-start.55 = (bf16[8,2,4,128]{3,0,2,1:T(8,128)(2,1)S(1)}, bf16[8,2,4,128]{3,0,2,1:T(8,128)(2,1)}, u32[]{:S(2)}) copy-start(bf16[8,2,4,128]{3,0,2,1:T(8,128)(2,1)} %copy-done.54) | copy-start | bytes 49156
  682.7 16.7 %collective-permute-start.18 = (bf16[2,128,512]{2,1,0:T(8,128)(2,1)S(1)}, bf16[2,128,512]{2,1,0:T(8,128)(2,1)S(1)}, u32[]{:S(2)}, u32[]{:S(2)}) collective-permute-start(bf16[2,128,512]{2,1,0:T(8,128)(2,1)S(1)} %get-tuple-element.177), channel_id=1, source_target_pairs={{0,4},{4,0},{1,5},{5,1},{2,6},{6,2},{3,7},{7,3},{8,12},{12,8},{9,1... | collective-permute-start | bytes 786440 | tf_op jit(solution)/shard_map/weight_grads/ppermute | solution.py:216
  (62 other events, 242.6 us)
Sparse Core Ops, SparseCore 0:
  9.9 28.2 all-gather.9
  39.8 80.7 all-gather.19
  134.7 47.3 all-gather.11
  183.8 86.2 all-gather.13
  377.2 44.6 all-gather.15
  423.4 44.4 all-gather.17
  470.9 85.1 reduce-scatter.8
  559.2 34.1 reduce-scatter.6
  596.6 38.3 reduce-scatter.4
  637.1 44.4 reduce-scatter.10

commit v13 on v12

--- a/solution.py
+++ b/solution.py
@@ -165,20 +165,14 @@
     replicas = lax.axis_size("dp")
 
     with jax.named_scope("modulation"):
-        levels_all = lax.all_gather(noise_index, ("dp", "frame"), axis=0, tiled=True)
-        levels_all = levels_all.reshape(replicas * halves, clips, groups)
-        condition_all = jax.nn.silu(level_embedding(levels_all, model_width)).astype(jnp.bfloat16)
-        row_block = lax.axis_index("dp") * halves + lax.axis_index("frame")
-        my_condition = lax.dynamic_slice_in_dim(
-            condition_all, row_block * rows_here, rows_here, axis=3
-        )
-        partial_mod = jnp.einsum(
-            "acgd,dkw->acgkw", my_condition, ada_weight, preferred_element_type=jnp.float32
-        )
-        summed_mod = jnp.sum(
-            lax.all_to_all(partial_mod, ("dp", "frame"), 0, 0, tiled=True), axis=0
-        )
-        group_mod = lax.all_gather(summed_mod, "tensor", axis=3, tiled=True)
+        ada_rows = lax.all_gather(ada_weight, ("dp", "frame"), axis=0, tiled=True)
+        local_condition = jax.nn.silu(level_embedding(noise_index, model_width)).astype(
+            jnp.bfloat16
+        )
+        local_mod = jnp.einsum(
+            "cgd,dkw->cgkw", local_condition, ada_rows, preferred_element_type=jnp.float32
+        )
+        group_mod = lax.all_gather(local_mod, "tensor", axis=3, tiled=True)
         group_mod = jnp.swapaxes(group_mod, 1, 2)[:, :, :, None, :]
         group_index = lax.axis_index("tensor")
         modulation = lax.dynamic_index_in_dim(group_mod, group_index, axis=2, keepdims=False)
@@ -393,6 +387,13 @@
         sum(p[3][k] for p in pieces[1:]) + pieces[0][3][k] for k in range(4)
     )
     with jax.named_scope("ada_grad"):
+        levels_all = lax.all_gather(noise_index, ("dp", "frame"), axis=0, tiled=True)
+        levels_all = levels_all.reshape(replicas * halves, clips, groups)
+        condition_all = jax.nn.silu(level_embedding(levels_all, model_width)).astype(jnp.bfloat16)
+        row_block = lax.axis_index("dp") * halves + lax.axis_index("frame")
+        my_condition = lax.dynamic_slice_in_dim(
+            condition_all, row_block * rows_here, rows_here, axis=3
+        )
         grad_columns = lax.all_to_all(
             grad_modulation.reshape(clips, 1, 6, model_width), "tensor", 3, 1, tiled=True
         )
@@ -406,13 +407,16 @@
         )
 
     with jax.named_scope("weight_grads"):
+        up_sum, down_sum = hidden_half_back((up_total, down_total))
+        joint_total, mixer_total, up_sum, down_sum = lax.optimization_barrier(
+            (joint_total, mixer_total, up_sum, down_sum)
+        )
         joint_sum, mixer_sum = (
             lax.psum_scatter(
                 total.astype(jnp.bfloat16), ("dp", "frame"), scatter_dimension=0, tiled=True
             ).astype(jnp.float32)
             for total in (joint_total, mixer_total)
         )
-        up_sum, down_sum = hidden_half_back((up_total, down_total))
         summed = (joint_sum, mixer_sum, up_sum, down_sum)
     result = output[:, None]
     input_grad = grad_input_low[:, None]

time: 714 us -> 775 us (1.085)
  waiting for transfers between devices: 266 us -> 344 us
  blocking collectives: 57.6 us -> 45.8 us
    all_gather x2, waiting for transfers between devices: 0.04 us -> 77.2 us  [gather_tokens(): return lax.all_gather(values, 'tensor', axis=1, tiled=True)]
    reduce_scatter x2, waiting for transfers between devices: 66.8 us -> 10.1 us  [on_device(): lax.psum_scatter(total.astype(jnp.bfloat16), ('dp', 'frame'), scatter_dim...]
    all_gather x0 -> x1, waiting for transfers between devices: none -> 27.3 us  [on_device(): ada_rows = lax.all_gather(ada_weight, ('dp', 'frame'), axis=0, tiled=True)]
    reduce_scatter x1, waiting for transfers between devices: 25.7 us -> 0.01 us  [hidden_half_back(): summed = lax.psum_scatter(summed, 'tensor', scatter_dimension=0, tiled=True)]
    all_to_all x4, waiting for transfers between devices: 52.4 us -> 76.9 us  [scatter_tokens(): received = lax.all_to_all(parts, 'tensor', 1, 1, tiled=True)]
    reduce_scatter x1, waiting for transfers between devices: 0.01 us -> 16.8 us  [hidden_half_back(): summed = lax.psum_scatter(blocks, 'dp', scatter_dimension=0, tiled=True)]
    all_gather x1, waiting for transfers between devices: 13.8 us -> 27.1 us  [hidden_half(): gathered = lax.all_gather(joined, 'tensor', axis=0, tiled=True)]
    all_to_all x1 -> x0, blocking collectives: 10.7 us -> none  [on_device(): lax.all_to_all(partial_mod, ('dp', 'frame'), 0, 0, tiled=True)]
  transfers between devices with their start and end apart: 34 -> 35, of which waited for: 13 -> 17; matrix products, arithmetic and copies ran while one was open for 29% -> 26% of each run, Pallas kernels for 15% -> 14%
where the time goes in v13:
time: 775 us; the launch traced here: 771 us
  waiting for transfers between devices  344 us (44%)
  Pallas kernels  107 us (14%)
  matrix products  101 us (13%)
  other arithmetic  77.9 us (10%)
  local copies, waits for them, and re-layouts  52.6 us (7%)
  blocking collectives  45.8 us (6%)
  starting transfers between devices  26.9 us (3%)
  between operations  15.6 us (2%)
    all_gather x1, waiting for transfers between devices, on_device(): group_tokens = lax.all_gather(tokens[:, 0], 'tensor', axis=1, tiled=True)  82.3 us
    all_gather x2, waiting for transfers between devices, gather_tokens(): return lax.all_gather(values, 'tensor', axis=1, tiled=True)  77.2 us
    all_to_all x4, waiting for transfers between devices, scatter_tokens(): received = lax.all_to_all(parts, 'tensor', 1, 1, tiled=True)  76.9 us
    pallas_call x2, Pallas kernels, attention_backward(): pl.pallas_call(functools.partial(_backward_kernel, heads, HEAD_DIM ** (-0...  64.4 us
    pallas_call x2, Pallas kernels, attention_forward(): pl.pallas_call(functools.partial(_forward_kernel, heads, HEAD_DIM ** (-0....  42.2 us
    all_gather x1, waiting for transfers between devices, on_device(): ada_rows = lax.all_gather(ada_weight, ('dp', 'frame'), axis=0, tiled=True)  27.3 us
    all_gather x1, waiting for transfers between devices, hidden_half(): gathered = lax.all_gather(joined, 'tensor', axis=0, tiled=True)  27.1 us
    unnamed x152, local copies, waits for them, and re-layouts  20 us
  transfers between devices with their start and end apart: 35, of which 17 were waited for; matrix products, arithmetic and copies ran while one was open for 26% of the time, Pallas kernels for 14%

profile of v13, /device:TPU:0, one launch (start us, length us, event | category | flops | bytes accessed | tf_op | source)
XLA Modules:
  0.0 770.6 jit_solution(2536148791741132362)
XLA Ops:
  9.5 11.6 %all_gather.37 = bf16[1024,256]{1,0:T(8,128)(2,1)S(1)} all-gather(bf16[128,256]{1,0:T(8,128)(2,1)} %param.16), channel_id=1, replica_groups=mesh['dp'=4,'frame'=2,'tensor'=4] {'dp','frame'}, dimensions={0}, use_global_device_ids=true | all-gather | bytes 589824 | tf_op jit(solution)/shard_map/weights/all_gather | solution.py:220
  21.1 17.1 %all-gather.13.cloned.1.call-done = bf16[1024,3,256]{2,0,1:T(8,128)(2,1)} async-done(((bf16[128,3,256]{2,0,1:T(8,128)(2,1)}), bf16[1024,3,256]{2,0,1:T(8,128)(2,1)}) %all-gather.13.cloned.1.call-update) | async-done | bytes 1572880 | tf_op jit(solution)/shard_map/weights/all_gather | solution.py:220
  38.2 82.3 %all-gather.23.cloned.1.call-done = bf16[2,1,1024,1024]{3,2,1,0:T(8,128)(2,1)} async-done(((bf16[2,1,256,1024]{3,2,1,0:T(8,128)(2,1)}), bf16[2,1,1024,1024]{3,2,1,0:T(8,128)(2,1)}) %all-gather.23.cloned.1.call-update) | async-done | bytes 4194320 | tf_op jit(solution)/shard_map/group_inputs/all_gather | solution.py:227
  125.9 27.3 %all-gather.11.cloned.1.call-done = bf16[1024,6,256]{2,0,1:T(8,128)(2,1)} async-done(((bf16[128,6,256]{2,0,1:T(8,128)(2,1)}), bf16[1024,6,256]{2,0,1:T(8,128)(2,1)}) %all-gather.11.cloned.1.call-update) | async-done | bytes 3145744 | tf_op jit(solution)/shard_map/modulation/all_gather | solution.py:168
  155.7 14.9 %all_gather.34 = f32[2,4,6,1024]{3,1,2,0:T(4,128)S(1)} all-gather(f32[2,4,6,256]{3,1,2,0:T(4,128)S(1)} %fusion.66), channel_id=1, replica_groups=mesh['dp'=4,'frame'=2,'tensor'=4] {'tensor'}, dimensions={3}, use_global_device_ids=true | all-gather | bytes 245760 | tf_op jit(solution)/shard_map/modulation/all_gather | solution.py:175
  170.7 2.9 convert_reduce_fusion.5
  175.4 27.1 %all-gather.15.cloned.1.call-done = bf16[2048,512]{1,0:T(8,128)(2,1)} async-done(((bf16[512,512]{1,0:T(8,128)(2,1)}), bf16[2048,512]{1,0:T(8,128)(2,1)}) %all-gather.15.cloned.1.call-update) | async-done | bytes 2097168 | tf_op jit(solution)/shard_map/ffn_weights/all_gather | solution.py:196
  215.2 21.1 %forward.2 = (bf16[1024,256]{1,0:T(8,128)(2,1)}, f32[1024,4]{1,0:T(8,128)}) custom-call(bf16[1024,256]{1,0:T(8,128)(2,1)} %get-tuple-element.177.q_ref, bf16[2048,256]{1,0:T(8,128)(2,1)} %maximum_bitcast_fusion.k_ref, bf16[2048,256]{1,0:T(8,128)(2,1)} %maximum_bitcast_fusion.1.v_ref), custom_call_target="tpu_custom_call" | custom-call | flops 2147483648 | bytes 3145728 | tf_op jit(solution)/shard_map/forward/pallas_call | solution.py:85
  236.3 3.2 convolution_convert_fusion.1
  239.5 3.9 all-to-all-start
  243.4 4.3 fusion.129
  252.7 21.1 %forward.3 = (bf16[1024,256]{1,0:T(8,128)(2,1)}, f32[1024,4]{1,0:T(8,128)}) custom-call(bf16[1024,256]{1,0:T(8,128)(2,1)} %get-tuple-element.180.q_ref, bf16[2048,256]{1,0:T(8,128)(2,1)} %maximum_bitcast_fusion.2.k_ref, bf16[2048,256]{1,0:T(8,128)(2,1)} %maximum_bitcast_fusion.3.v_ref), custom_call_target="tpu_custom_call" | custom-call | flops 2147483648 | bytes 3145728 | tf_op jit(solution)/shard_map/forward/pallas_call | solution.py:85
  273.8 3.1 convolution_convert_fusion
  276.9 15.2 %all-to-all-done = bf16[1,4,256,1024]{3,2,0,1:T(8,128)(2,1)S(1)} async-done(((bf16[1,4,256,1024]{3,2,0,1:T(8,128)(2,1)}), bf16[1,4,256,1024]{3,2,0,1:T(8,128)(2,1)S(1)}, u32[]{:S(2)}, u32[]{:S(2)}) %all-to-all-start) | async-done | bytes 2097184 | tf_op jit(solution)/shard_map/forward/all_to_all | solution.py:262
  292.1 4.4 all-to-all-start.1
  298.6 3.6 convert_element_type.266
  307.5 37.0 %all-to-all-done.1 = bf16[1,4,256,1024]{3,2,0,1:T(8,128)(2,1)} async-done(((bf16[1,4,256,1024]{3,2,0,1:T(8,128)(2,1)}), bf16[1,4,256,1024]{3,2,0,1:T(8,128)(2,1)}, u32[]{:S(2)}, u32[]{:S(2)}) %all-to-all-start.1) | async-done | bytes 2097184 | tf_op jit(solution)/shard_map/forward/all_to_all | solution.py:262
  346.6 2.7 multiply_reduce_fusion.10
  365.6 3.9 fusion.244
  378.2 4.5 fusion.136
  389.8 4.4 fusion.62
  402.5 5.5 fusion.75
  408.0 5.4 fusion.41
  421.2 6.2 fusion.78
  427.5 7.1 fusion.40
  436.9 7.5 pad_maximum_fusion
  444.4 8.9 %fusion.139 = bf16[1,512,1024]{2,1,0:T(8,128)(2,1)S(1)} fusion(bf16[1024,512,4]{1,0,2:T(8,128)(2,1)} %bitcast.585, f32[512,4,512,1]{2,0,3,1:T(8,128)} %copy-done.72, f32[512,4,512,1]{2,0,3,1:T(8,128)} %fusion.62), kind=kOutput, calls=%fused_computation.164 | convolution fusion | flops 2168979456 | bytes 13631488 | tf_op jit(solution)/shard_map/backward_ffn/crtj,atdj->crad/dot_general | solution.py:318
  462.0 9.4 %all-gather.2 = s32[8,2,4]{2,1,0:T(2,128)S(1)} all-gather(s32[1,2,4]{2,1,0:T(2,128)S(1)} %bitcast.640), channel_id=1, replica_groups=mesh['dp'=4,'frame'=2,'tensor'=4] {'dp','frame'}, dimensions={0}, use_global_device_ids=true | all-gather | bytes 288 | tf_op jit(solution)/shard_map/ada_grad/all_gather | solution.py:390
  472.1 3.4 fusion.145.g_ref
  475.5 32.3 %backward_attention.2 = (f32[1024,256]{1,0:T(8,128)}, f32[2048,256]{1,0:T(8,128)}, f32[2048,256]{1,0:T(8,128)}) custom-call(bf16[1024,256]{1,0:T(8,128)(2,1)} %get-tuple-element.177.q_ref, bf16[2048,256]{1,0:T(8,128)(2,1)} %maximum_bitcast_fusion.k_ref, bf16[2048,256]{1,0:T(8,128)(2,1)} %maximum_bitcast_fusion.1.v_ref, bf16[1024,256]{1,0:T(8,128)(2,1)} %fusion.145.g_ref, ...), custom_call_target="tpu_custom_call" | custom-call | flops 5368709120 | bytes 8912896 | tf_op jit(solution)/shard_map/backward_attention/pallas_call | solution.py:118
  512.5 16.8 %reduce-scatter.5.cloned.1.call-done = bf16[4,512,512]{2,1,0:T(8,128)(2,1)} async-done(((bf16[16,512,512]{2,1,0:T(8,128)(2,1)}), bf16[4,512,512]{2,1,0:T(8,128)(2,1)}) %reduce-scatter.5.cloned.1.call-update) | async-done | bytes 2097168 | tf_op jit(solution)/shard_map/weight_grads/reduce_scatter | solution.py:205
  529.3 4.6 bitcast_convert_fusion.1
  533.9 4.9 all-to-all-start.2
  538.9 77.1 %all-gather.21.cloned.1.call-done = bf16[1,1024,1024]{2,1,0:T(8,128)(2,1)} async-done(((bf16[1,256,1024]{2,1,0:T(8,128)(2,1)}), bf16[1,1024,1024]{2,1,0:T(8,128)(2,1)}) %all-gather.21.cloned.1.call-update) | async-done | bytes 2097168 | tf_op jit(solution)/shard_map/backward_attention/all_gather | solution.py:256
  616.0 3.1 fusion.148.g_ref
  619.1 32.1 %backward_attention.3 = (f32[1024,256]{1,0:T(8,128)}, f32[2048,256]{1,0:T(8,128)}, f32[2048,256]{1,0:T(8,128)}) custom-call(bf16[1024,256]{1,0:T(8,128)(2,1)} %get-tuple-element.180.q_ref, bf16[2048,256]{1,0:T(8,128)(2,1)} %maximum_bitcast_fusion.2.k_ref, bf16[2048,256]{1,0:T(8,128)(2,1)} %maximum_bitcast_fusion.3.v_ref, bf16[1024,256]{1,0:T(8,128)(2,1)} %fusion.148.g_ref, ...), custom_call_target="tpu_custom_call" | custom-call | flops 5368709120 | bytes 8912896 | tf_op jit(solution)/shard_map/backward_attention/pallas_call | solution.py:118
  657.8 3.2 bitcast_convert_fusion
  661.0 4.5 all-to-all-start.3
  665.8 3.6 fusion.142
  669.4 5.5 fusion.174
  676.0 5.2 convolution_add_fusion
  685.8 2.8 convert_reduce_fusion.2
  689.4 24.7 %all-to-all-done.3 = bf16[1,4,256,1024]{3,2,0,1:T(8,128)(2,1)} async-done(((bf16[1,4,256,1024]{3,2,0,1:T(8,128)(2,1)}), bf16[1,4,256,1024]{3,2,0,1:T(8,128)(2,1)}, u32[]{:S(2)}, u32[]{:S(2)}) %all-to-all-start.3) | async-done | bytes 2097184 | tf_op jit(solution)/shard_map/backward_attention/all_to_all | solution.py:262
  714.1 2.8 convert_reduce_fusion
  720.5 3.4 reshape.1152
  723.9 3.3 all-to-all-start.4
  737.1 9.8 %all-gather.1 = f32[16,4,1,6,256]{4,1,0,3,2:T(4,128)S(1)} all-gather(f32[2,4,1,6,256]{4,1,0,3,2:T(4,128)S(1)} %bitcast.601), channel_id=3, replica_groups=mesh['dp'=4,'frame'=2,'tensor'=4] {'dp','frame'}, dimensions={0}, use_global_device_ids=true | all-gather | bytes 442368 | tf_op jit(solution)/shard_map/ada_grad/all_gather | solution.py:400
  751.9 10.1 %reduce-scatter.9.cloned.1.call-done = bf16[128,3,256]{2,0,1:T(8,128)(2,1)} async-done(((bf16[1024,3,256]{2,0,1:T(8,128)(2,1)}), bf16[128,3,256]{2,0,1:T(8,128)(2,1)}) %reduce-scatter.9.cloned.1.call-update) | async-done | bytes 196624 | tf_op jit(solution)/shard_map/weight_grads/reduce_scatter | solution.py:415
  (349 shorter events, 136.1 us)
Async XLA Ops:
  7.2 31.0 %all-gather.13.cloned.1.call-start = ((), (), s32[]{:S(2)}) async-start(), calls=%async_computation.10 | async-start | bytes 1769472 | tf_op jit(solution)/shard_map/weights/all_gather | solution.py:220
  7.9 117.7 %copy-start.61 = (s32[2,4]{1,0:T(2,128)S(1)}, s32[2,4]{1,0:T(2,128)}, u32[]{:S(2)}) copy-start(s32[2,4]{1,0:T(2,128)} %param.14) | copy-start | bytes 100
  7.9 112.6 %all-gather.23.cloned.1.call-start = ((), (), s32[]{:S(2)}) async-start(), calls=%async_computation.19 | async-start | bytes 5242880 | tf_op jit(solution)/shard_map/group_inputs/all_gather | solution.py:227
  8.7 144.5 %all-gather.11.cloned.1.call-start = ((), (), s32[]{:S(2)}) async-start(), calls=%async_computation.9 | async-start | bytes 3538944 | tf_op jit(solution)/shard_map/modulation/all_gather | solution.py:168
  9.4 193.1 %all-gather.15.cloned.1.call-start = ((), (), s32[]{:S(2)}) async-start(), calls=%async_computation.11 | async-start | bytes 2621440 | tf_op jit(solution)/shard_map/ffn_weights/all_gather | solution.py:196
  21.1 252.7 %copy-start.18 = (bf16[1024,256]{1,0:T(8,128)(2,1)}, bf16[1024,256]{1,0:T(8,128)(2,1)S(1)}, u32[]{:S(2)}) copy-start(bf16[1024,256]{1,0:T(8,128)(2,1)S(1)} %all_gather.37) | copy-start | bytes 1572868
  121.7 1.8 collective-permute-start.4
  123.0 1.5 collective-permute-start.3
  125.6 240.0 %all-gather.17.cloned.1.call-start = ((), (), s32[]{:S(2)}) async-start(), calls=%async_computation.12 | async-start | bytes 10485760 | tf_op jit(solution)/shard_map/ffn_weights/all_gather | solution.py:197
  125.7 49.7 %copy-start.51 = (f32[512]{0:T(512)}, f32[512]{0:T(512)S(1)}, u32[]{:S(2)}) copy-start(f32[512]{0:T(512)S(1)} %multiply_exponential_fusion) | copy-start | bytes 6148
  211.2 1.9 collective-permute-start
  211.2 2.9 collective-permute-start.1
  239.5 52.6 %all-to-all-start = ((bf16[1,4,256,1024]{3,2,0,1:T(8,128)(2,1)}), bf16[1,4,256,1024]{3,2,0,1:T(8,128)(2,1)S(1)}, u32[]{:S(2)}, u32[]{:S(2)}) async-start(bf16[1,4,256,1024]{3,2,0,1:T(8,128)(2,1)} %bitcast.581), calls=%async_computation | async-start | bytes 4194304 | tf_op jit(solution)/shard_map/forward/all_to_all | solution.py:262
  248.7 1.9 collective-permute-start.6
  248.9 2.8 collective-permute-start.7
  292.1 52.4 %all-to-all-start.1 = ((bf16[1,4,256,1024]{3,2,0,1:T(8,128)(2,1)}), bf16[1,4,256,1024]{3,2,0,1:T(8,128)(2,1)}, u32[]{:S(2)}, u32[]{:S(2)}) async-start(bf16[1,4,256,1024]{3,2,0,1:T(8,128)(2,1)} %bitcast.580), calls=%async_computation.1 | async-start | bytes 4194304 | tf_op jit(solution)/shard_map/forward/all_to_all | solution.py:262
  296.6 175.5 %all-gather.19.cloned.1.call-start = ((), (), s32[]{:S(2)}) async-start(), calls=%async_computation.13 | async-start | bytes 2621440 | tf_op jit(solution)/shard_map/backward_attention/all_gather | solution.py:256
  298.6 48.1 %copy-start = (f32[2,1,256,1024]{3,2,1,0:T(8,128)}, f32[2,1,256,1024]{3,2,1,0:T(8,128)S(1)}, u32[]{:S(2)}) copy-start(f32[2,1,256,1024]{3,2,1,0:T(8,128)S(1)} %convert_element_type.304) | copy-start | bytes 6291460
  302.4 47.0 %copy-start.53 = (f32[256]{0:T(256)}, f32[256]{0:T(256)S(1)}, u32[]{:S(2)}) copy-start(f32[256]{0:T(256)S(1)} %get-tuple-element.213) | copy-start | bytes 3076
  302.4 47.0 %copy-start.55 = (f32[256]{0:T(256)}, f32[256]{0:T(256)S(1)}, u32[]{:S(2)}) copy-start(f32[256]{0:T(256)S(1)} %get-tuple-element.214) | copy-start | bytes 3076
  304.9 48.4 %collective-permute-start.10 = (bf16[1,256,1024]{2,1,0:T(8,128)(2,1)}, bf16[1,256,1024]{2,1,0:T(8,128)(2,1)}, u32[]{:S(2)}, u32[]{:S(2)}) collective-permute-start(bf16[1,256,1024]{2,1,0:T(8,128)(2,1)} %multiply_convert_fusion.3), channel_id=1, source_target_pairs={{0,4},{4,0},{1,5},{5,1},{2,6},{6,2},{3,7},{7,3},{8,12},{12,8},{9,1... | collective-permute-start | bytes 1572872 | tf_op jit(solution)/shard_map/backward_ffn/ppermute | solution.py:237
  351.4 5.7 collective-permute-start.2
  352.8 7.0 collective-permute-start.8
  382.8 3.3 collective-permute-start.11
  385.6 2.1 collective-permute-start.5
  389.3 5.8 collective-permute-start.14
  395.1 134.2 %reduce-scatter.5.cloned.1.call-start = ((), (), s32[]{:S(2)}) async-start(), calls=%async_computation.15 | async-start | bytes 10485760 | tf_op jit(solution)/shard_map/weight_grads/reduce_scatter | solution.py:205
  444.4 171.6 %all-gather.21.cloned.1.call-start = ((), (), s32[]{:S(2)}) async-start(), calls=%async_computation.14 | async-start | bytes 2621440 | tf_op jit(solution)/shard_map/backward_attention/all_gather | solution.py:256
  453.5 3.3 collective-permute-start.15
  456.3 2.0 collective-permute-start.9
  461.9 212.9 %reduce-scatter.7.cloned.1.call-start = ((), (), s32[]{:S(2)}) async-start(), calls=%async_computation.16 | async-start | bytes 2621440 | tf_op jit(solution)/shard_map/weight_grads/reduce_scatter | solution.py:206
  509.7 2.0 collective-permute-start.13
  510.1 2.2 collective-permute-start.12
  533.9 82.1 %copy-start.19 = (bf16[1024,256]{1,0:T(8,128)(2,1)S(1)}, bf16[1024,256]{1,0:T(8,128)(2,1)}, u32[]{:S(2)}) copy-start(bf16[1024,256]{1,0:T(8,128)(2,1)} %copy-done.18) | copy-start | bytes 1572868
  533.9 127.1 %all-to-all-start.2 = ((bf16[1,4,256,1024]{3,2,0,1:T(8,128)(2,1)}), bf16[1,4,256,1024]{3,2,0,1:T(8,128)(2,1)S(1)}, u32[]{:S(2)}, u32[]{:S(2)}) async-start(bf16[1,4,256,1024]{3,2,0,1:T(8,128)(2,1)} %bitcast.589), calls=%async_computation.2 | async-start | bytes 4194304 | tf_op jit(solution)/shard_map/backward_attention/all_to_all | solution.py:262
  653.2 2.9 collective-permute-start.17
  653.6 2.6 collective-permute-start.16
  661.0 53.1 %all-to-all-start.3 = ((bf16[1,4,256,1024]{3,2,0,1:T(8,128)(2,1)}), bf16[1,4,256,1024]{3,2,0,1:T(8,128)(2,1)}, u32[]{:S(2)}, u32[]{:S(2)}) async-start(bf16[1,4,256,1024]{3,2,0,1:T(8,128)(2,1)} %bitcast.588), calls=%async_computation.3 | async-start | bytes 4194304 | tf_op jit(solution)/shard_map/backward_attention/all_to_all | solution.py:262
  665.5 84.9 %reduce-scatter.11.cloned.1.call-start = ((), (), s32[]{:S(2)}) async-start(), calls=%async_computation.18 | async-start | bytes 589824 | tf_op jit(solution)/shard_map/weight_grads/reduce_scatter | solution.py:415
  675.9 5.3 collective-permute-start.18
  684.6 77.3 %reduce-scatter.9.cloned.1.call-start = ((), (), s32[]{:S(2)}) async-start(), calls=%async_computation.17 | async-start | bytes 1769472 | tf_op jit(solution)/shard_map/weight_grads/reduce_scatter | solution.py:415
  684.7 32.2 %copy-start.57 = (f32[256]{0:T(256)}, f32[256]{0:T(256)S(1)}, u32[]{:S(2)}) copy-start(f32[256]{0:T(256)S(1)} %add_rsqrt_fusion.3) | copy-start | bytes 3076
  684.7 32.2 %copy-start.58 = (f32[256]{0:T(256)}, f32[256]{0:T(256)S(1)}, u32[]{:S(2)}) copy-start(f32[256]{0:T(256)S(1)} %add_rsqrt_fusion.2) | copy-start | bytes 3076
  685.8 32.0 %copy-start.1 = (f32[2,1,256,1024]{3,2,1,0:T(8,128)S(1)}, f32[2,1,256,1024]{3,2,1,0:T(8,128)}, u32[]{:S(2)}) copy-start(f32[2,1,256,1024]{3,2,1,0:T(8,128)} %copy-done) | copy-start | bytes 6291460
  685.8 32.0 %copy-start.49 = (f32[1,1,1,1024]{3,0,2,1:T(1,128)S(1)}, f32[1,1,1,1024]{3,0,2,1:T(1,128)}, u32[]{:S(2)}) copy-start(f32[1,1,1,1024]{3,0,2,1:T(1,128)} %get-tuple-element.204) | copy-start | bytes 12292
  685.8 32.0 %copy-start.54 = (f32[256]{0:T(256)S(1)}, f32[256]{0:T(256)}, u32[]{:S(2)}) copy-start(f32[256]{0:T(256)} %copy-done.53) | copy-start | bytes 3076
  685.8 32.0 %copy-start.56 = (f32[256]{0:T(256)S(1)}, f32[256]{0:T(256)}, u32[]{:S(2)}) copy-start(f32[256]{0:T(256)} %copy-done.55) | copy-start | bytes 3076
  723.9 9.8 %all-to-all-start.4 = ((f32[4,1,3072]{2,1,0:T(1,128)}), f32[4,1,3072]{2,1,0:T(1,128)S(1)}, u32[]{:S(2)}, u32[]{:S(2)}) async-start(f32[4,1,3072]{2,1,0:T(1,128)} %reshape.1152), calls=%async_computation.8 | async-start | bytes 98304 | tf_op jit(solution)/shard_map/ada_grad/all_to_all | solution.py:397
  (60 other events, 332.7 us)
Sparse Core Ops, SparseCore 0:
  9.9 28.2 all-gather.12
  39.8 80.7 all-gather.22
  122.5 30.6 all-gather.10
  155.2 47.2 all-gather.14
  204.2 85.3 all-gather.16
  395.2 43.8 all-gather.18
  444.5 84.7 reduce-scatter.4
  530.9 85.0 all-gather.20
  618.3 42.4 reduce-scatter.6
  684.7 34.9 reduce-scatter.10
  723.0 38.8 reduce-scatter.8

commit v14 on v13

--- a/solution.py
+++ b/solution.py
@@ -166,6 +166,11 @@
 
     with jax.named_scope("modulation"):
         ada_rows = lax.all_gather(ada_weight, ("dp", "frame"), axis=0, tiled=True)
+        token_input, ada_rows = lax.optimization_barrier((tokens[:, 0], ada_rows))
+        group_tokens = lax.all_gather(token_input, "tensor", axis=1, tiled=True)
+        group_tokens, qkv_input, out_input = lax.optimization_barrier(
+            (group_tokens, qkv_weight, out_weight)
+        )
         local_condition = jax.nn.silu(level_embedding(noise_index, model_width)).astype(
             jnp.bfloat16
         )
@@ -218,19 +223,17 @@
     with jax.named_scope("weights"):
         joint_weight, mixer_weight = (
             lax.all_gather(w, ("dp", "frame"), axis=0, tiled=True)
-            for w in (qkv_weight, out_weight)
-        )
+            for w in (qkv_input, out_input)
+        )
+        joint_weight, mixer_weight, ffn_shards = lax.optimization_barrier(
+            (joint_weight, mixer_weight, (up_weight, down_weight))
+        )
+        upward_weight, downward_weight = hidden_half(ffn_shards)
 
     residual = tokens[:, 0].astype(jnp.float32)
     upstream = out_grad[:, 0].astype(jnp.float32)
     with jax.named_scope("group_inputs"):
-        group_tokens = lax.all_gather(tokens[:, 0], "tensor", axis=1, tiled=True)
         group_upstream = None
-    with jax.named_scope("ffn_weights"):
-        group_tokens, joint_weight, mixer_weight, ffn_shards = lax.optimization_barrier(
-            (group_tokens, joint_weight, mixer_weight, (up_weight, down_weight))
-        )
-        upward_weight, downward_weight = hidden_half(ffn_shards)
     def gather_halves(values):
         if halves != 2:
             return lax.all_gather(values, "frame", axis=1, tiled=True)
@@ -407,16 +410,13 @@
         )
 
     with jax.named_scope("weight_grads"):
-        up_sum, down_sum = hidden_half_back((up_total, down_total))
-        joint_total, mixer_total, up_sum, down_sum = lax.optimization_barrier(
-            (joint_total, mixer_total, up_sum, down_sum)
-        )
         joint_sum, mixer_sum = (
             lax.psum_scatter(
                 total.astype(jnp.bfloat16), ("dp", "frame"), scatter_dimension=0, tiled=True
             ).astype(jnp.float32)
             for total in (joint_total, mixer_total)
         )
+        up_sum, down_sum = hidden_half_back((up_total, down_total))
         summed = (joint_sum, mixer_sum, up_sum, down_sum)
     result = output[:, None]
     input_grad = grad_input_low[:, None]

time: 775 us -> 736 us (0.950)
  waiting for transfers between devices: 344 us -> 297 us
  other arithmetic: 77.9 us -> 85.7 us
    all_gather x2, waiting for transfers between devices: 77.2 us -> 0.04 us  [gather_tokens(): return lax.all_gather(values, 'tensor', axis=1, tiled=True)]
    reduce_scatter x2, waiting for transfers between devices: 10.1 us -> 56.1 us  [on_device(): lax.psum_scatter(total.astype(jnp.bfloat16), ('dp', 'frame'), scatter_dim...]
    all_to_all x4, waiting for transfers between devices: 76.9 us -> 50.1 us  [scatter_tokens(): received = lax.all_to_all(parts, 'tensor', 1, 1, tiled=True)]
    reduce_scatter x1, waiting for transfers between devices: 0.01 us -> 24 us  [hidden_half_back(): summed = lax.psum_scatter(summed, 'tensor', scatter_dimension=0, tiled=True)]
    reduce_scatter x1, waiting for transfers between devices: 16.8 us -> 0.01 us  [hidden_half_back(): summed = lax.psum_scatter(blocks, 'dp', scatter_dimension=0, tiled=True)]
    all_gather x1, waiting for transfers between devices: 27.3 us -> 36.9 us  [on_device(): ada_rows = lax.all_gather(ada_weight, ('dp', 'frame'), axis=0, tiled=True)]
    unnamed x152 -> x162, local copies, waits for them, and re-layouts: 20 us -> 20.9 us
  transfers between devices with their start and end apart: 35 -> 35, of which waited for: 17 -> 13; matrix products, arithmetic and copies ran while one was open for 26% -> 29% of each run, Pallas kernels for 14% -> 15%
where the time goes in v14:
time: 736 us; the launch traced here: 732 us
  waiting for transfers between devices  297 us (40%)
  Pallas kernels  107 us (15%)
  matrix products  99.6 us (14%)
  other arithmetic  85.7 us (12%)
  local copies, waits for them, and re-layouts  55.1 us (7%)
  blocking collectives  43.8 us (6%)
  starting transfers between devices  27.7 us (4%)
  between operations  15.5 us (2%)
    all_gather x1, waiting for transfers between devices, on_device(): group_tokens = lax.all_gather(token_input, 'tensor', axis=1, tiled=True)  82.3 us
    pallas_call x2, Pallas kernels, attention_backward(): pl.pallas_call(functools.partial(_backward_kernel, heads, HEAD_DIM ** (-0...  64.8 us
    reduce_scatter x2, waiting for transfers between devices, on_device(): lax.psum_scatter(total.astype(jnp.bfloat16), ('dp', 'frame'), scatter_dim...  56.1 us
    all_to_all x4, waiting for transfers between devices, scatter_tokens(): received = lax.all_to_all(parts, 'tensor', 1, 1, tiled=True)  50.1 us
    pallas_call x2, Pallas kernels, attention_forward(): pl.pallas_call(functools.partial(_forward_kernel, heads, HEAD_DIM ** (-0....  42.3 us
    all_gather x1, waiting for transfers between devices, on_device(): ada_rows = lax.all_gather(ada_weight, ('dp', 'frame'), axis=0, tiled=True)  36.9 us
    all_gather x1, waiting for transfers between devices, hidden_half(): gathered = lax.all_gather(joined, 'tensor', axis=0, tiled=True)  26.4 us
    reduce_scatter x1, waiting for transfers between devices, hidden_half_back(): summed = lax.psum_scatter(summed, 'tensor', scatter_dimension=0, tiled=True)  24 us
  transfers between devices with their start and end apart: 35, of which 13 were waited for; matrix products, arithmetic and copies ran while one was open for 29% of the time, Pallas kernels for 15%

profile of v14, /device:TPU:0, one launch (start us, length us, event | category | flops | bytes accessed | tf_op | source)
XLA Modules:
  0.0 731.5 jit_solution(2447310371947378297)
XLA Ops:
  7.9 36.9 %all-gather.10.cloned.1.call-done = bf16[1024,6,256]{2,0,1:T(8,128)(2,1)} async-done(((bf16[128,6,256]{2,0,1:T(8,128)(2,1)}), bf16[1024,6,256]{2,0,1:T(8,128)(2,1)}) %all-gather.10.cloned.1.call-update) | async-done | bytes 3145744 | tf_op jit(solution)/shard_map/modulation/all_gather | solution.py:168
  44.9 82.3 %all-gather.12.cloned.1.call-done = bf16[2,1024,1024]{2,1,0:T(8,128)(2,1)} async-done(((bf16[2,256,1024]{2,1,0:T(8,128)(2,1)}), bf16[2,1024,1024]{2,1,0:T(8,128)(2,1)}) %all-gather.12.cloned.1.call-update) | async-done | bytes 4194320 | tf_op jit(solution)/shard_map/modulation/all_gather | solution.py:170
  127.2 10.1 %all_gather.37 = bf16[1024,256]{1,0:T(8,128)(2,1)S(1)} all-gather(bf16[128,256]{1,0:T(8,128)(2,1)} %param.16), channel_id=1, replica_groups=mesh['dp'=4,'frame'=2,'tensor'=4] {'dp','frame'}, dimensions={0}, use_global_device_ids=true | all-gather | bytes 589824 | tf_op jit(solution)/shard_map/weights/all_gather | solution.py:225
  137.3 15.8 %all-gather.14.cloned.1.call-done = bf16[1024,3,256]{2,0,1:T(8,128)(2,1)} async-done(((bf16[128,3,256]{2,0,1:T(8,128)(2,1)}), bf16[1024,3,256]{2,0,1:T(8,128)(2,1)}) %all-gather.14.cloned.1.call-update) | async-done | bytes 1572880 | tf_op jit(solution)/shard_map/weights/all_gather | solution.py:225
  161.4 15.1 %all_gather.34 = f32[2,4,6,1024]{3,1,2,0:T(4,128)S(1)} all-gather(f32[2,4,6,256]{3,1,2,0:T(4,128)S(1)} %fusion.66), channel_id=1, replica_groups=mesh['dp'=4,'frame'=2,'tensor'=4] {'tensor'}, dimensions={3}, use_global_device_ids=true | all-gather | bytes 245760 | tf_op jit(solution)/shard_map/modulation/all_gather | solution.py:180
  176.6 2.9 convert_reduce_fusion.5
  179.5 26.4 %all-gather.16.cloned.1.call-done = bf16[2048,512]{1,0:T(8,128)(2,1)} async-done(((bf16[512,512]{1,0:T(8,128)(2,1)}), bf16[2048,512]{1,0:T(8,128)(2,1)}) %all-gather.16.cloned.1.call-update) | async-done | bytes 2097168 | tf_op jit(solution)/shard_map/weights/all_gather | solution.py:201
  205.8 3.0 fusion.8
  212.1 2.8 fusion.72
  221.6 21.1 %forward.2 = (bf16[1024,256]{1,0:T(8,128)(2,1)}, f32[1024,4]{1,0:T(8,128)}) custom-call(bf16[1024,256]{1,0:T(8,128)(2,1)} %get-tuple-element.174.q_ref, bf16[2048,256]{1,0:T(8,128)(2,1)} %maximum_bitcast_fusion.k_ref, bf16[2048,256]{1,0:T(8,128)(2,1)} %maximum_bitcast_fusion.1.v_ref), custom_call_target="tpu_custom_call" | custom-call | flops 2147483648 | bytes 3145728 | tf_op jit(solution)/shard_map/forward/pallas_call | solution.py:85
  242.7 3.2 convolution_convert_fusion.1
  245.9 4.0 all-to-all-start
  249.9 3.8 fusion.129
  255.3 2.8 convert_element_type.266
  262.6 21.1 %forward.3 = (bf16[1024,256]{1,0:T(8,128)(2,1)}, f32[1024,4]{1,0:T(8,128)}) custom-call(bf16[1024,256]{1,0:T(8,128)(2,1)} %get-tuple-element.177.q_ref, bf16[2048,256]{1,0:T(8,128)(2,1)} %maximum_bitcast_fusion.2.k_ref, bf16[2048,256]{1,0:T(8,128)(2,1)} %maximum_bitcast_fusion.3.v_ref), custom_call_target="tpu_custom_call" | custom-call | flops 2147483648 | bytes 3145728 | tf_op jit(solution)/shard_map/forward/pallas_call | solution.py:85
  283.7 3.1 convolution_convert_fusion
  286.8 11.8 %all-to-all-done = bf16[1,4,256,1024]{3,2,0,1:T(8,128)(2,1)S(1)} async-done(((bf16[1,4,256,1024]{3,2,0,1:T(8,128)(2,1)}), bf16[1,4,256,1024]{3,2,0,1:T(8,128)(2,1)S(1)}, u32[]{:S(2)}, u32[]{:S(2)}) %all-to-all-start) | async-done | bytes 2097184 | tf_op jit(solution)/shard_map/forward/all_to_all | solution.py:265
  298.6 4.4 all-to-all-start.1
  312.8 38.3 %all-to-all-done.1 = bf16[1,4,256,1024]{3,2,0,1:T(8,128)(2,1)} async-done(((bf16[1,4,256,1024]{3,2,0,1:T(8,128)(2,1)}), bf16[1,4,256,1024]{3,2,0,1:T(8,128)(2,1)}, u32[]{:S(2)}, u32[]{:S(2)}) %all-to-all-start.1) | async-done | bytes 2097184 | tf_op jit(solution)/shard_map/forward/all_to_all | solution.py:265
  368.4 3.9 fusion.245
  384.3 4.5 fusion.136
  404.7 7.1 fusion.58
  414.2 9.0 %fusion.139 = bf16[1,512,1024]{2,1,0:T(8,128)(2,1)S(1)} fusion(bf16[1024,512,4]{1,0,2:T(8,128)(2,1)} %bitcast.556, f32[512,4,512,1]{2,0,3,1:T(8,128)} %fusion.58, f32[512,4,512,1]{2,0,3,1:T(8,128)} %copy-done.70), kind=kOutput, calls=%fused_computation.164 | convolution fusion | flops 2168979456 | bytes 13631488 | tf_op jit(solution)/shard_map/backward_ffn/crtj,atdj->crad/dot_general | solution.py:321
  423.8 6.2 fusion.75
  435.4 8.1 %fusion.41 = bf16[4,4,256,512]{3,2,0,1:T(8,128)(2,1)S(1)} fusion(f32[4,512,4,256]{1,3,2,0:T(8,128)} %fusion.75, f32[512,4,512,1]{2,0,3,1:T(8,128)} %copy-done.73, bf16[512,4,256]{0,2,1:T(8,128)(2,1)} %copy.253), kind=kOutput, calls=%fused_computation.60 | convolution fusion | flops 2161115136 | bytes 17825792 | tf_op jit(solution)/shard_map/backward_ffn/crad,crtj->atdj/dot_general | solution.py:313
  447.5 6.2 fusion.78
  453.8 6.7 fusion.40
  462.8 7.5 %pad_maximum_fusion = bf16[16,512,512]{2,1,0:T(8,128)(2,1)} fusion(bf16[16,256,512]{2,1,0:T(8,128)(2,1)} %bitcast.548, bf16[16,256,512]{2,1,0:T(8,128)(2,1)} %bitcast.550), kind=kLoop, calls=%fused_computation | loop fusion | flops 16777216 | bytes 16777216 | tf_op jit(solution)/shard_map/weight_grads/concatenate | solution.py:208
  471.4 3.1 fusion.145.g_ref
  474.5 32.6 %backward_attention.2 = (f32[1024,256]{1,0:T(8,128)}, f32[2048,256]{1,0:T(8,128)}, f32[2048,256]{1,0:T(8,128)}) custom-call(bf16[1024,256]{1,0:T(8,128)(2,1)} %get-tuple-element.174.q_ref, bf16[2048,256]{1,0:T(8,128)(2,1)} %maximum_bitcast_fusion.k_ref, bf16[2048,256]{1,0:T(8,128)(2,1)} %maximum_bitcast_fusion.1.v_ref, bf16[1024,256]{1,0:T(8,128)(2,1)} %fusion.145.g_ref, ...), custom_call_target="tpu_custom_call" | custom-call | flops 5368709120 | bytes 8912896 | tf_op jit(solution)/shard_map/backward_attention/pallas_call | solution.py:118
  512.0 3.2 bitcast_convert_fusion.1
  515.2 3.6 all-to-all-start.2
  518.9 3.3 fusion.148.g_ref
  522.3 32.3 %backward_attention.3 = (f32[1024,256]{1,0:T(8,128)}, f32[2048,256]{1,0:T(8,128)}, f32[2048,256]{1,0:T(8,128)}) custom-call(bf16[1024,256]{1,0:T(8,128)(2,1)} %get-tuple-element.177.q_ref, bf16[2048,256]{1,0:T(8,128)(2,1)} %maximum_bitcast_fusion.2.k_ref, bf16[2048,256]{1,0:T(8,128)(2,1)} %maximum_bitcast_fusion.3.v_ref, bf16[1024,256]{1,0:T(8,128)(2,1)} %fusion.148.g_ref, ...), custom_call_target="tpu_custom_call" | custom-call | flops 5368709120 | bytes 8912896 | tf_op jit(solution)/shard_map/backward_attention/pallas_call | solution.py:118
  568.1 3.7 fusion.175
  571.9 3.2 add_convert_fusion.2
  575.1 4.8 bitcast_convert_fusion
  579.9 5.1 all-to-all-start.3
  585.8 9.1 %all-gather.1 = s32[8,2,4]{2,1,0:T(2,128)S(1)} all-gather(s32[1,2,4]{2,1,0:T(2,128)S(1)} %bitcast.614), channel_id=1, replica_groups=mesh['dp'=4,'frame'=2,'tensor'=4] {'dp','frame'}, dimensions={0}, use_global_device_ids=true | all-gather | bytes 288 | tf_op jit(solution)/shard_map/ada_grad/all_gather | solution.py:393
  596.6 19.4 %reduce-scatter.7.cloned.1.call-done = bf16[128,256]{1,0:T(8,128)(2,1)} async-done(((bf16[1024,256]{1,0:T(8,128)(2,1)}), bf16[128,256]{1,0:T(8,128)(2,1)}) %reduce-scatter.7.cloned.1.call-update) | async-done | bytes 65552 | tf_op jit(solution)/shard_map/weight_grads/reduce_scatter | solution.py:414
  617.6 2.7 convert_reduce_fusion.2
  620.9 36.6 %reduce-scatter.5.cloned.1.call-done = bf16[128,3,256]{2,0,1:T(8,128)(2,1)} async-done(((bf16[1024,3,256]{2,0,1:T(8,128)(2,1)}), bf16[128,3,256]{2,0,1:T(8,128)(2,1)}) %reduce-scatter.5.cloned.1.call-update) | async-done | bytes 196624 | tf_op jit(solution)/shard_map/weight_grads/reduce_scatter | solution.py:414
  659.3 2.7 convert_reduce_fusion
  665.7 3.4 reshape.1148
  669.1 5.0 all-to-all-start.4
  676.9 3.5 add_convert_fusion.6
  680.4 24.0 %reduce-scatter.11.cloned.1.call-done = bf16[1,512,512]{2,1,0:T(8,128)(2,1)} async-done(((bf16[4,512,512]{2,1,0:T(8,128)(2,1)}), bf16[1,512,512]{2,1,0:T(8,128)(2,1)}) %reduce-scatter.11.cloned.1.call-update) | async-done | bytes 524304 | tf_op jit(solution)/shard_map/weight_grads/reduce_scatter | solution.py:211
  711.1 9.5 %all-gather = f32[16,4,1,6,256]{4,1,0,3,2:T(4,128)S(1)} all-gather(f32[2,4,1,6,256]{4,1,0,3,2:T(4,128)S(1)} %bitcast.575), channel_id=2, replica_groups=mesh['dp'=4,'frame'=2,'tensor'=4] {'dp','frame'}, dimensions={0}, use_global_device_ids=true | all-gather | bytes 442368 | tf_op jit(solution)/shard_map/ada_grad/all_gather | solution.py:403
  (361 shorter events, 136.8 us)
Async XLA Ops:
  7.2 37.7 %all-gather.10.cloned.1.call-start = ((), (), s32[]{:S(2)}) async-start(), calls=%async_computation.9 | async-start | bytes 3538944 | tf_op jit(solution)/shard_map/modulation/all_gather | solution.py:168
  7.9 119.3 %all-gather.12.cloned.1.call-start = ((), (), s32[]{:S(2)}) async-start(), calls=%async_computation.10 | async-start | bytes 5242880 | tf_op jit(solution)/shard_map/modulation/all_gather | solution.py:170
  44.8 113.5 %copy-start.63 = (s32[2,4]{1,0:T(2,128)S(1)}, s32[2,4]{1,0:T(2,128)}, u32[]{:S(2)}) copy-start(s32[2,4]{1,0:T(2,128)} %param.14) | copy-start | bytes 100
  44.8 108.3 %all-gather.14.cloned.1.call-start = ((), (), s32[]{:S(2)}) async-start(), calls=%async_computation.11 | async-start | bytes 1769472 | tf_op jit(solution)/shard_map/weights/all_gather | solution.py:225
  127.2 78.6 %all-gather.16.cloned.1.call-start = ((), (), s32[]{:S(2)}) async-start(), calls=%async_computation.12 | async-start | bytes 2621440 | tf_op jit(solution)/shard_map/weights/all_gather | solution.py:201
  137.3 146.4 %copy-start.17 = (bf16[1024,256]{1,0:T(8,128)(2,1)}, bf16[1024,256]{1,0:T(8,128)(2,1)S(1)}, u32[]{:S(2)}) copy-start(bf16[1024,256]{1,0:T(8,128)(2,1)S(1)} %all_gather.37) | copy-start | bytes 1572868
  154.3 1.8 collective-permute-start.4
  155.8 1.4 collective-permute-start.3
  158.3 210.1 %all-gather.18.cloned.1.call-start = ((), (), s32[]{:S(2)}) async-start(), calls=%async_computation.13 | async-start | bytes 10485760 | tf_op jit(solution)/shard_map/weights/all_gather | solution.py:202
  217.6 1.9 collective-permute-start
  217.6 2.9 collective-permute-start.1
  245.9 52.7 %all-to-all-start = ((bf16[1,4,256,1024]{3,2,0,1:T(8,128)(2,1)}), bf16[1,4,256,1024]{3,2,0,1:T(8,128)(2,1)S(1)}, u32[]{:S(2)}, u32[]{:S(2)}) async-start(bf16[1,4,256,1024]{3,2,0,1:T(8,128)(2,1)} %bitcast.553), calls=%async_computation | async-start | bytes 4194304 | tf_op jit(solution)/shard_map/forward/all_to_all | solution.py:265
  254.8 3.3 collective-permute-start.6
  255.0 5.4 collective-permute-start.7
  298.6 52.4 %all-to-all-start.1 = ((bf16[1,4,256,1024]{3,2,0,1:T(8,128)(2,1)}), bf16[1,4,256,1024]{3,2,0,1:T(8,128)(2,1)}, u32[]{:S(2)}, u32[]{:S(2)}) async-start(bf16[1,4,256,1024]{3,2,0,1:T(8,128)(2,1)} %bitcast.552), calls=%async_computation.1 | async-start | bytes 4194304 | tf_op jit(solution)/shard_map/forward/all_to_all | solution.py:265
  303.1 167.3 %all-gather.20.cloned.1.call-start = ((), (), s32[]{:S(2)}) async-start(), calls=%async_computation.14 | async-start | bytes 2621440 | tf_op jit(solution)/shard_map/backward_attention/all_gather | solution.py:259
  304.8 48.4 %copy-start = (f32[2,256,1024]{2,1,0:T(8,128)}, f32[2,256,1024]{2,1,0:T(8,128)S(1)}, u32[]{:S(2)}) copy-start(f32[2,256,1024]{2,1,0:T(8,128)S(1)} %bitcast_convert_fusion.6) | copy-start | bytes 6291460
  307.7 47.8 %collective-permute-start.10 = (bf16[1,256,1024]{2,1,0:T(8,128)(2,1)}, bf16[1,256,1024]{2,1,0:T(8,128)(2,1)}, u32[]{:S(2)}, u32[]{:S(2)}) collective-permute-start(bf16[1,256,1024]{2,1,0:T(8,128)(2,1)} %multiply_convert_fusion.3), channel_id=1, source_target_pairs={{0,4},{4,0},{1,5},{5,1},{2,6},{6,2},{3,7},{7,3},{8,12},{12,8},{9,1... | collective-permute-start | bytes 1572872 | tf_op jit(solution)/shard_map/backward_ffn/ppermute | solution.py:240
  312.3 47.5 %collective-permute-start.2 = (bf16[1,256,1024]{2,1,0:T(8,128)(2,1)}, bf16[1,256,1024]{2,1,0:T(8,128)(2,1)}, u32[]{:S(2)}, u32[]{:S(2)}) collective-permute-start(bf16[1,256,1024]{2,1,0:T(8,128)(2,1)} %add_convert_fusion.12), channel_id=1, source_target_pairs={{0,4},{4,0},{1,5},{5,1},{2,6},{6,2},{3,7},{7,3},{8,12},{12,8},{9,1... | collective-permute-start | bytes 1572872 | tf_op jit(solution)/shard_map/forward/ppermute | solution.py:240
  355.5 6.9 collective-permute-start.8
  383.7 8.3 %collective-permute-start.5 = (bf16[1,256,1024]{2,1,0:T(8,128)(2,1)S(1)}, bf16[1,256,1024]{2,1,0:T(8,128)(2,1)S(1)}, u32[]{:S(2)}, u32[]{:S(2)}) collective-permute-start(bf16[1,256,1024]{2,1,0:T(8,128)(2,1)S(1)} %slice.279), channel_id=1, source_target_pairs={{0,4},{4,0},{1,5},{5,1},{2,6},{6,2},{3,7},{7,3},{8,12},{12,8},{9,1... | collective-permute-start | bytes 1572872 | tf_op jit(solution)/shard_map/forward/ppermute | solution.py:250
  388.9 2.5 collective-permute-start.11
  393.8 6.0 collective-permute-start.14
  398.7 31.8 %collective-permute-start.9 = (bf16[1,256,1024]{2,1,0:T(8,128)(2,1)}, bf16[1,256,1024]{2,1,0:T(8,128)(2,1)}, u32[]{:S(2)}, u32[]{:S(2)}) collective-permute-start(bf16[1,256,1024]{2,1,0:T(8,128)(2,1)} %slice.292), channel_id=1, source_target_pairs={{0,4},{4,0},{1,5},{5,1},{2,6},{6,2},{3,7},{7,3},{8,12},{12,8},{9,1... | collective-permute-start | bytes 1572872 | tf_op jit(solution)/shard_map/forward/ppermute | solution.py:250
  399.7 119.2 %all-gather.22.cloned.1.call-start = ((), (), s32[]{:S(2)}) async-start(), calls=%async_computation.15 | async-start | bytes 2621440 | tf_op jit(solution)/shard_map/backward_attention/all_gather | solution.py:259
  423.3 6.7 collective-permute-start.15
  435.1 149.9 %reduce-scatter.9.cloned.1.call-start = ((), (), s32[]{:S(2)}) async-start(), calls=%async_computation.18 | async-start | bytes 10485760 | tf_op jit(solution)/shard_map/weight_grads/reduce_scatter | solution.py:210
  509.1 2.0 collective-permute-start.13
  509.7 2.1 collective-permute-start.12
  515.2 64.7 %all-to-all-start.2 = ((bf16[1,4,256,1024]{3,2,0,1:T(8,128)(2,1)}), bf16[1,4,256,1024]{3,2,0,1:T(8,128)(2,1)S(1)}, u32[]{:S(2)}, u32[]{:S(2)}) async-start(bf16[1,4,256,1024]{3,2,0,1:T(8,128)(2,1)} %bitcast.561), calls=%async_computation.2 | async-start | bytes 4194304 | tf_op jit(solution)/shard_map/backward_attention/all_to_all | solution.py:265
  518.8 97.2 %reduce-scatter.7.cloned.1.call-start = ((), (), s32[]{:S(2)}) async-start(), calls=%async_computation.17 | async-start | bytes 589824 | tf_op jit(solution)/shard_map/weight_grads/reduce_scatter | solution.py:414
  557.2 7.2 collective-permute-start.17
  559.2 6.6 collective-permute-start.16
  564.2 93.4 %reduce-scatter.5.cloned.1.call-start = ((), (), s32[]{:S(2)}) async-start(), calls=%async_computation.16 | async-start | bytes 1769472 | tf_op jit(solution)/shard_map/weight_grads/reduce_scatter | solution.py:414
  579.9 15.6 %copy-start.62 = (f32[256]{0:T(256)S(1)}, f32[256]{0:T(256)}, u32[]{:S(2)}) copy-start(f32[256]{0:T(256)} %get-tuple-element.168) | copy-start | bytes 3076
  579.9 15.7 %copy-start.27 = (bf16[1,256,1024]{2,1,0:T(8,128)(2,1)S(1)}, bf16[1,256,1024]{2,1,0:T(8,128)(2,1)}, u32[]{:S(2)}) copy-start(bf16[1,256,1024]{2,1,0:T(8,128)(2,1)} %get-tuple-element.165) | copy-start | bytes 1572868
  579.9 15.7 %copy-start.32 = (bf16[1,256,1024]{2,1,0:T(8,128)(2,1)S(1)}, bf16[1,256,1024]{2,1,0:T(8,128)(2,1)}, u32[]{:S(2)}) copy-start(bf16[1,256,1024]{2,1,0:T(8,128)(2,1)} %get-tuple-element.180) | copy-start | bytes 1572868
  579.9 79.4 %all-to-all-start.3 = ((bf16[1,4,256,1024]{3,2,0,1:T(8,128)(2,1)}), bf16[1,4,256,1024]{3,2,0,1:T(8,128)(2,1)}, u32[]{:S(2)}, u32[]{:S(2)}) async-start(bf16[1,4,256,1024]{3,2,0,1:T(8,128)(2,1)} %bitcast.562), calls=%async_computation.3 | async-start | bytes 4194304 | tf_op jit(solution)/shard_map/backward_attention/all_to_all | solution.py:265
  585.0 35.2 %copy-start.53 = (f32[1,1,1,1024]{3,0,2,1:T(1,128)S(1)}, f32[1,1,1,1024]{3,0,2,1:T(1,128)}, u32[]{:S(2)}) copy-start(f32[1,1,1,1024]{3,0,2,1:T(1,128)} %get-tuple-element.195) | copy-start | bytes 12292
  585.0 119.3 %reduce-scatter.11.cloned.1.call-start = ((), (), s32[]{:S(2)}) async-start(), calls=%async_computation.19 | async-start | bytes 2621440 | tf_op jit(solution)/shard_map/weight_grads/reduce_scatter | solution.py:211
  595.5 66.5 %copy-start.60 = (f32[256]{0:T(256)}, f32[256]{0:T(256)S(1)}, u32[]{:S(2)}) copy-start(f32[256]{0:T(256)S(1)} %add_rsqrt_fusion.3) | copy-start | bytes 3076
  595.5 66.5 %copy-start.61 = (f32[256]{0:T(256)}, f32[256]{0:T(256)S(1)}, u32[]{:S(2)}) copy-start(f32[256]{0:T(256)S(1)} %add_rsqrt_fusion.2) | copy-start | bytes 3076
  596.6 66.4 %copy-start.1 = (f32[2,256,1024]{2,1,0:T(8,128)S(1)}, f32[2,256,1024]{2,1,0:T(8,128)}, u32[]{:S(2)}) copy-start(f32[2,256,1024]{2,1,0:T(8,128)} %copy-done) | copy-start | bytes 6291460
  596.6 66.4 %copy-start.52 = (f32[1,1,1,1024]{3,0,2,1:T(1,128)S(1)}, f32[1,1,1,1024]{3,0,2,1:T(1,128)}, u32[]{:S(2)}) copy-start(f32[1,1,1,1024]{3,0,2,1:T(1,128)} %get-tuple-element.201) | copy-start | bytes 12292
  596.6 66.4 %copy-start.57 = (f32[256]{0:T(256)S(1)}, f32[256]{0:T(256)}, u32[]{:S(2)}) copy-start(f32[256]{0:T(256)} %copy-done.56) | copy-start | bytes 3076
  596.6 66.4 %copy-start.59 = (f32[256]{0:T(256)S(1)}, f32[256]{0:T(256)}, u32[]{:S(2)}) copy-start(f32[256]{0:T(256)} %copy-done.58) | copy-start | bytes 3076
  669.1 38.7 %all-to-all-start.4 = ((f32[4,1,3072]{2,1,0:T(1,128)}), f32[4,1,3072]{2,1,0:T(1,128)S(1)}, u32[]{:S(2)}, u32[]{:S(2)}) async-start(f32[4,1,3072]{2,1,0:T(1,128)} %reshape.1148), calls=%async_computation.8 | async-start | bytes 98304 | tf_op jit(solution)/shard_map/ada_grad/all_to_all | solution.py:400
  705.4 16.6 %collective-permute-start.18 = (bf16[2,128,512]{2,1,0:T(8,128)(2,1)S(1)}, bf16[2,128,512]{2,1,0:T(8,128)(2,1)S(1)}, u32[]{:S(2)}, u32[]{:S(2)}) collective-permute-start(bf16[2,128,512]{2,1,0:T(8,128)(2,1)S(1)} %get-tuple-element.182), channel_id=1, source_target_pairs={{0,4},{4,0},{1,5},{5,1},{2,6},{6,2},{3,7},{7,3},{8,12},{12,8},{9,1... | collective-permute-start | bytes 786440 | tf_op jit(solution)/shard_map/weight_grads/ppermute | solution.py:215
  (65 other events, 293.0 us)
Sparse Core Ops, SparseCore 0:
  9.9 34.8 all-gather.9
  46.4 80.7 all-gather.11
  129.1 24.0 all-gather.13
  158.4 47.3 all-gather.15
  207.5 86.2 all-gather.17
  399.8 44.6 all-gather.19
  446.1 44.4 all-gather.21
  493.7 85.1 reduce-scatter.8
  581.9 34.1 reduce-scatter.6
  619.2 38.3 reduce-scatter.4
  659.9 44.4 reduce-scatter.10

commit v15 on v11

--- a/solution.py
+++ b/solution.py
@@ -402,12 +402,14 @@
         )
 
     with jax.named_scope("weight_grads"):
-        joint_sum, mixer_sum = (
-            lax.psum_scatter(
-                total.astype(jnp.bfloat16), ("dp", "frame"), scatter_dimension=0, tiled=True
-            ).astype(jnp.float32)
-            for total in (joint_total, mixer_total)
-        )
+        attention_totals = jnp.concatenate(
+            [joint_total.reshape(model_width, 3 * local_width), mixer_total], axis=1
+        )
+        attention_sums = lax.psum_scatter(
+            attention_totals.astype(jnp.bfloat16), ("dp", "frame"), scatter_dimension=0, tiled=True
+        ).astype(jnp.float32)
+        joint_sum = attention_sums[:, : 3 * local_width].reshape(rows_here, 3, local_width)
+        mixer_sum = attention_sums[:, 3 * local_width :]
         up_sum, down_sum = hidden_half_back((up_total, down_total))
         summed = (joint_sum, mixer_sum, up_sum, down_sum)
     result = output[:, None]

time: 712 us -> 715 us (level)
  waiting for transfers between devices: 260 us -> 271 us
    reduce_scatter x2 -> x0, waiting for transfers between devices: 66.3 us -> none  [on_device(): lax.psum_scatter(total.astype(jnp.bfloat16), ('dp', 'frame'), scatter_dim...]
    all_to_all x4, waiting for transfers between devices: 53.2 us -> 114 us  [scatter_tokens(): received = lax.all_to_all(parts, 'tensor', 1, 1, tiled=True)]
    reduce_scatter x1, waiting for transfers between devices: 25.7 us -> 0.01 us  [hidden_half_back(): summed = lax.psum_scatter(summed, 'tensor', scatter_dimension=0, tiled=True)]
    reduce_scatter x1, waiting for transfers between devices: 0.01 us -> 24 us  [hidden_half_back(): summed = lax.psum_scatter(blocks, 'dp', scatter_dimension=0, tiled=True)]
    unnamed x10, waiting for transfers between devices: 2.03 us -> 18.3 us
    unnamed x161 -> x168, local copies, waits for them, and re-layouts: 22.3 us -> 27.1 us
  transfers between devices with their start and end apart: 34 -> 33, of which waited for: 12 -> 14; matrix products, arithmetic and copies ran while one was open for 29% -> 28% of each run, Pallas kernels for 15% -> 15%
where the time goes in v15:
time: 715 us; the launch traced here: 708 us
  waiting for transfers between devices  271 us (38%)
  Pallas kernels  107 us (15%)
  matrix products  94.6 us (13%)
  other arithmetic  75.7 us (11%)
  local copies, waits for them, and re-layouts  59.1 us (8%)
  blocking collectives  57.8 us (8%)
  starting transfers between devices  27 us (4%)
  between operations  15.6 us (2%)
    all_to_all x4, waiting for transfers between devices, scatter_tokens(): received = lax.all_to_all(parts, 'tensor', 1, 1, tiled=True)  114 us
    all_gather x1, waiting for transfers between devices, on_device(): group_tokens = lax.all_gather(tokens[:, 0], 'tensor', axis=1, tiled=True)  81.1 us
    pallas_call x2, Pallas kernels, attention_backward(): pl.pallas_call(functools.partial(_backward_kernel, heads, HEAD_DIM ** (-0...  64.8 us
    pallas_call x2, Pallas kernels, attention_forward(): pl.pallas_call(functools.partial(_forward_kernel, heads, HEAD_DIM ** (-0....  42.2 us
    unnamed x168, local copies, waits for them, and re-layouts  27.1 us
    reduce_scatter x1, waiting for transfers between devices, hidden_half_back(): summed = lax.psum_scatter(blocks, 'dp', scatter_dimension=0, tiled=True)  24 us
    unnamed x10, waiting for transfers between devices  18.3 us
    all_to_all x4, starting transfers between devices, scatter_tokens(): received = lax.all_to_all(parts, 'tensor', 1, 1, tiled=True)  17.6 us
  transfers between devices with their start and end apart: 33, of which 14 were waited for; matrix products, arithmetic and copies ran while one was open for 28% of the time, Pallas kernels for 15%

profile of v15, /device:TPU:0, one launch (start us, length us, event | category | flops | bytes accessed | tf_op | source)
XLA Modules:
  0.0 707.5 jit_solution(626304188122786468)
XLA Ops:
  14.2 10.1 %all-gather.2 = s32[8,2,4]{2,1,0:T(2,128)S(1)} all-gather(s32[1,2,4]{2,1,0:T(2,128)S(1)} %bitcast.678), channel_id=1, replica_groups=mesh['dp'=4,'frame'=2,'tensor'=4] {'dp','frame'}, dimensions={0}, use_global_device_ids=true | all-gather | bytes 288 | tf_op jit(solution)/shard_map/modulation/all_gather | solution.py:168
  25.6 10.9 %all_to_all.43 = f32[8,2,4,6,256]{4,2,3,1,0:T(4,128)S(1)} all-to-all(f32[8,2,4,6,256]{4,2,3,1,0:T(4,128)S(1)} %fusion.182), channel_id=1, replica_groups=mesh['dp'=4,'frame'=2,'tensor'=4] {'dp','frame'}, dimensions={0} | all-to-all | bytes 786432 | tf_op jit(solution)/shard_map/modulation/all_to_all | solution.py:179
  36.5 16.8 %all_gather.31 = f32[2,4,6,1024]{3,2,1,0:T(8,128)S(1)} all-gather(f32[2,4,6,256]{3,2,1,0:T(8,128)S(1)} %copy.317), channel_id=1, replica_groups=mesh['dp'=4,'frame'=2,'tensor'=4] {'tensor'}, dimensions={3}, use_global_device_ids=true | all-gather | bytes 245760 | tf_op jit(solution)/shard_map/modulation/all_gather | solution.py:181
  53.6 11.5 %all-gather.12.cloned.1.call-done = bf16[2048,512]{1,0:T(8,128)(2,1)} async-done(((bf16[512,512]{1,0:T(8,128)(2,1)}), bf16[2048,512]{1,0:T(8,128)(2,1)}) %all-gather.12.cloned.1.call-update) | async-done | bytes 2097168 | tf_op jit(solution)/shard_map/weights/all_gather | solution.py:202
  65.1 81.1 %all-gather.20.cloned.1.call-done = bf16[2,1,1024,1024]{3,2,1,0:T(8,128)(2,1)} async-done(((bf16[2,1,256,1024]{3,2,1,0:T(8,128)(2,1)}), bf16[2,1,1024,1024]{3,2,1,0:T(8,128)(2,1)}) %all-gather.20.cloned.1.call-update) | async-done | bytes 4194320 | tf_op jit(solution)/shard_map/group_inputs/all_gather | solution.py:234
  146.2 3.0 convert_reduce_fusion.1
  153.5 2.8 fusion.73
  156.3 15.9 %all-gather.10.cloned.1.call-done = bf16[1024,3,256]{2,0,1:T(8,128)(2,1)} async-done(((bf16[128,3,256]{2,0,1:T(8,128)(2,1)}), bf16[1024,3,256]{2,0,1:T(8,128)(2,1)}) %all-gather.10.cloned.1.call-update) | async-done | bytes 1572880 | tf_op jit(solution)/shard_map/weights/all_gather | solution.py:226
  172.2 3.2 fusion.128
  176.9 10.5 %all_gather.34 = bf16[1024,256]{1,0:T(8,128)(2,1)S(1)} all-gather(bf16[128,256]{1,0:T(8,128)(2,1)S(1)} %copy-done.58), channel_id=1, replica_groups=mesh['dp'=4,'frame'=2,'tensor'=4] {'dp','frame'}, dimensions={0}, use_global_device_ids=true | all-gather | bytes 589824 | tf_op jit(solution)/shard_map/weights/all_gather | solution.py:226
  189.5 21.1 %forward.2 = (bf16[1024,256]{1,0:T(8,128)(2,1)}, f32[1024,4]{1,0:T(8,128)}) custom-call(bf16[1024,256]{1,0:T(8,128)(2,1)} %get-tuple-element.159.q_ref, bf16[2048,256]{1,0:T(8,128)(2,1)} %maximum_bitcast_fusion.k_ref, bf16[2048,256]{1,0:T(8,128)(2,1)} %maximum_bitcast_fusion.1.v_ref), custom_call_target="tpu_custom_call" | custom-call | flops 2147483648 | bytes 3145728 | tf_op jit(solution)/shard_map/forward/pallas_call | solution.py:85
  210.6 3.2 convolution_convert_fusion.1
  213.8 4.8 all-to-all-start.1
  218.6 3.8 fusion.129
  227.4 21.1 %forward.3 = (bf16[1024,256]{1,0:T(8,128)(2,1)}, f32[1024,4]{1,0:T(8,128)}) custom-call(bf16[1024,256]{1,0:T(8,128)(2,1)} %get-tuple-element.162.q_ref, bf16[2048,256]{1,0:T(8,128)(2,1)} %maximum_bitcast_fusion.2.k_ref, bf16[2048,256]{1,0:T(8,128)(2,1)} %maximum_bitcast_fusion.3.v_ref), custom_call_target="tpu_custom_call" | custom-call | flops 2147483648 | bytes 3145728 | tf_op jit(solution)/shard_map/forward/pallas_call | solution.py:85
  248.5 3.1 convolution_convert_fusion
  251.6 15.7 %all-to-all-done.1 = bf16[1,4,256,1024]{3,2,0,1:T(8,128)(2,1)S(1)} async-done(((bf16[1,4,256,1024]{3,2,0,1:T(8,128)(2,1)}), bf16[1,4,256,1024]{3,2,0,1:T(8,128)(2,1)S(1)}, u32[]{:S(2)}, u32[]{:S(2)}) %all-to-all-start.1) | async-done | bytes 2097184 | tf_op jit(solution)/shard_map/forward/all_to_all | solution.py:264
  267.3 4.5 all-to-all-start.2
  273.3 3.6 convert_element_type.253
  282.2 37.5 %all-to-all-done.2 = bf16[1,4,256,1024]{3,2,0,1:T(8,128)(2,1)} async-done(((bf16[1,4,256,1024]{3,2,0,1:T(8,128)(2,1)}), bf16[1,4,256,1024]{3,2,0,1:T(8,128)(2,1)}, u32[]{:S(2)}, u32[]{:S(2)}) %all-to-all-start.2) | async-done | bytes 2097184 | tf_op jit(solution)/shard_map/forward/all_to_all | solution.py:264
  321.9 2.8 multiply_reduce_fusion.10
  341.4 3.9 fusion.244
  356.8 4.5 fusion.136
  374.9 2.7 reshape.943
  377.6 7.1 %fusion.60 = f32[512,4,512,1]{2,0,3,1:T(8,128)} fusion(bf16[512,4,256]{2,1,0:T(4,128)(2,1)} %reshape.943, bf16[4,4,1,256,512]{4,3,2,1,0:T(8,128)(2,1)} %copy-done.9), kind=kOutput, calls=%fused_computation.91 | convolution fusion | flops 2147483648 | bytes 9437184 | tf_op jit(solution)/shard_map/backward_ffn/crad,atdj->crtj/dot_general | solution.py:309
  387.1 9.0 %fusion.139 = bf16[1,512,1024]{2,1,0:T(8,128)(2,1)S(1)} fusion(bf16[1024,512,4]{1,0,2:T(8,128)(2,1)} %bitcast.617, f32[512,4,512,1]{2,0,3,1:T(8,128)} %fusion.60, f32[512,4,512,1]{2,0,3,1:T(8,128)} %copy-done.69), kind=kOutput, calls=%fused_computation.165 | convolution fusion | flops 2168979456 | bytes 13631488 | tf_op jit(solution)/shard_map/backward_ffn/crtj,atdj->crad/dot_general | solution.py:320
  396.2 6.1 fusion.75
  407.7 8.1 %fusion.43 = bf16[4,4,256,512]{3,2,0,1:T(8,128)(2,1)S(1)} fusion(f32[4,512,4,256]{1,3,2,0:T(8,128)} %fusion.75, f32[512,4,512,1]{2,0,3,1:T(8,128)} %copy-done.72, bf16[512,4,256]{0,2,1:T(8,128)(2,1)} %copy.280), kind=kOutput, calls=%fused_computation.62 | convolution fusion | flops 2161115136 | bytes 17825792 | tf_op jit(solution)/shard_map/backward_ffn/crad,crtj->atdj/dot_general | solution.py:312
  419.9 6.1 fusion.78
  426.0 6.7 fusion.42
  434.9 7.6 %pad_maximum_fusion = bf16[16,512,512]{2,1,0:T(8,128)(2,1)} fusion(bf16[16,256,512]{2,1,0:T(8,128)(2,1)} %bitcast.610, bf16[16,256,512]{2,1,0:T(8,128)(2,1)} %bitcast.612), kind=kLoop, calls=%fused_computation | loop fusion | flops 16777216 | bytes 16777216 | tf_op jit(solution)/shard_map/weight_grads/concatenate | solution.py:209
  443.6 3.1 fusion.145.g_ref
  446.7 32.5 %backward_attention.2 = (f32[1024,256]{1,0:T(8,128)}, f32[2048,256]{1,0:T(8,128)}, f32[2048,256]{1,0:T(8,128)}) custom-call(bf16[1024,256]{1,0:T(8,128)(2,1)} %get-tuple-element.159.q_ref, bf16[2048,256]{1,0:T(8,128)(2,1)} %maximum_bitcast_fusion.k_ref, bf16[2048,256]{1,0:T(8,128)(2,1)} %maximum_bitcast_fusion.1.v_ref, bf16[1024,256]{1,0:T(8,128)(2,1)} %fusion.145.g_ref, ...), custom_call_target="tpu_custom_call" | custom-call | flops 5368709120 | bytes 8912896 | tf_op jit(solution)/shard_map/backward_attention/pallas_call | solution.py:118
  484.2 3.1 bitcast_convert_fusion.1
  487.4 3.6 all-to-all-start.3
  491.1 3.2 fusion.148.g_ref
  494.3 32.3 %backward_attention.3 = (f32[1024,256]{1,0:T(8,128)}, f32[2048,256]{1,0:T(8,128)}, f32[2048,256]{1,0:T(8,128)}) custom-call(bf16[1024,256]{1,0:T(8,128)(2,1)} %get-tuple-element.162.q_ref, bf16[2048,256]{1,0:T(8,128)(2,1)} %maximum_bitcast_fusion.2.k_ref, bf16[2048,256]{1,0:T(8,128)(2,1)} %maximum_bitcast_fusion.3.v_ref, bf16[1024,256]{1,0:T(8,128)(2,1)} %fusion.148.g_ref, ...), custom_call_target="tpu_custom_call" | custom-call | flops 5368709120 | bytes 8912896 | tf_op jit(solution)/shard_map/backward_attention/pallas_call | solution.py:118
  526.6 24.0 %reduce-scatter.6.cloned.1.call-done = bf16[4,512,512]{2,1,0:T(8,128)(2,1)} async-done(((bf16[16,512,512]{2,1,0:T(8,128)(2,1)}), bf16[4,512,512]{2,1,0:T(8,128)(2,1)}) %reduce-scatter.6.cloned.1.call-update) | async-done | bytes 2097168 | tf_op jit(solution)/shard_map/weight_grads/reduce_scatter | solution.py:211
  556.3 3.2 bitcast_convert_fusion
  559.4 4.7 all-to-all-start.4
  576.8 2.8 convert_reduce_fusion.4
  579.8 60.7 %all-to-all-done.4 = bf16[1,4,256,1024]{3,2,0,1:T(8,128)(2,1)} async-done(((bf16[1,4,256,1024]{3,2,0,1:T(8,128)(2,1)}), bf16[1,4,256,1024]{3,2,0,1:T(8,128)(2,1)}, u32[]{:S(2)}, u32[]{:S(2)}) %all-to-all-start.4) | async-done | bytes 2097184 | tf_op jit(solution)/shard_map/backward_attention/all_to_all | solution.py:264
  640.6 2.7 convert_reduce_fusion.2
  646.4 3.4 reshape.1158
  649.8 4.1 all-to-all-start.5
  655.4 3.5 add_convert_fusion.6
  662.4 16.8 %reduce-scatter.10.cloned.1.call-done = bf16[128,1024]{1,0:T(8,128)(2,1)} async-done(((bf16[1024,1024]{1,0:T(8,128)(2,1)}), bf16[128,1024]{1,0:T(8,128)(2,1)}) %reduce-scatter.10.cloned.1.call-update) | async-done | bytes 262160
  687.1 9.5 %all-gather.1 = f32[16,4,1,6,256]{4,1,0,3,2:T(4,128)S(1)} all-gather(f32[2,4,1,6,256]{4,1,0,3,2:T(4,128)S(1)} %bitcast.638), channel_id=3, replica_groups=mesh['dp'=4,'frame'=2,'tensor'=4] {'dp','frame'}, dimensions={0}, use_global_device_ids=true | all-gather | bytes 442368 | tf_op jit(solution)/shard_map/ada_grad/all_gather | solution.py:395
  (361 shorter events, 129.6 us)
Async XLA Ops:
  7.2 17.8 %copy-start = (bf16[128,6,256]{2,0,1:T(8,128)(2,1)S(1)}, bf16[128,6,256]{2,0,1:T(8,128)(2,1)}, u32[]{:S(2)}) copy-start(bf16[128,6,256]{2,0,1:T(8,128)(2,1)} %param.19) | copy-start | bytes 1179652
  7.2 57.9 %all-gather.12.cloned.1.call-start = ((), (), s32[]{:S(2)}) async-start(), calls=%async_computation.10 | async-start | bytes 2621440 | tf_op jit(solution)/shard_map/weights/all_gather | solution.py:202
  8.4 1.8 collective-permute-start.4
  10.1 1.4 collective-permute-start.3
  12.7 133.6 %all-gather.20.cloned.1.call-start = ((), (), s32[]{:S(2)}) async-start(), calls=%async_computation.16 | async-start | bytes 5242880 | tf_op jit(solution)/shard_map/group_inputs/all_gather | solution.py:234
  13.4 158.8 %all-gather.10.cloned.1.call-start = ((), (), s32[]{:S(2)}) async-start(), calls=%async_computation.9 | async-start | bytes 1769472 | tf_op jit(solution)/shard_map/weights/all_gather | solution.py:226
  14.1 327.2 %all-gather.14.cloned.1.call-start = ((), (), s32[]{:S(2)}) async-start(), calls=%async_computation.11 | async-start | bytes 10485760 | tf_op jit(solution)/shard_map/weights/all_gather | solution.py:203
  156.3 19.2 %copy-start.29 = (bf16[1024,1024,1]{1,0,2:T(8,128)(2,1)}, bf16[1024,1024,1]{1,0,2:T(8,128)(2,1)S(1)}, u32[]{:S(2)}) copy-start(bf16[1024,1024,1]{1,0,2:T(8,128)(2,1)S(1)} %get-tuple-element.145) | copy-start | bytes 6291460
  176.4 11.0 %collective-permute-start = (bf16[1,1024,256]{2,1,0:T(8,128)(2,1)S(1)}, bf16[1,1024,256]{2,1,0:T(8,128)(2,1)S(1)}, u32[]{:S(2)}, u32[]{:S(2)}) collective-permute-start(bf16[1,1024,256]{2,1,0:T(8,128)(2,1)S(1)} %get-tuple-element.158), channel_id=1, source_target_pairs={{0,4},{4,0},{1,5},{5,1},{2,6},{6,2},{3,7},{7,3},{8,12},{12,8},{9,1... | collective-permute-start | bytes 1572872 | tf_op jit(solution)/shard_map/forward/ppermute | solution.py:239
  176.6 11.9 %collective-permute-start.1 = (bf16[1,1024,256]{2,1,0:T(8,128)(2,1)S(1)}, bf16[1,1024,256]{2,1,0:T(8,128)(2,1)S(1)}, u32[]{:S(2)}, u32[]{:S(2)}) collective-permute-start(bf16[1,1024,256]{2,1,0:T(8,128)(2,1)S(1)} %get-tuple-element.157), channel_id=1, source_target_pairs={{0,4},{4,0},{1,5},{5,1},{2,6},{6,2},{3,7},{7,3},{8,12},{12,8},{9,1... | collective-permute-start | bytes 1572872 | tf_op jit(solution)/shard_map/forward/ppermute | solution.py:239
  187.4 61.1 %copy-start.18 = (bf16[1024,256]{1,0:T(8,128)(2,1)}, bf16[1024,256]{1,0:T(8,128)(2,1)S(1)}, u32[]{:S(2)}) copy-start(bf16[1024,256]{1,0:T(8,128)(2,1)S(1)} %all_gather.34) | copy-start | bytes 1572868
  213.8 53.5 %all-to-all-start.1 = ((bf16[1,4,256,1024]{3,2,0,1:T(8,128)(2,1)}), bf16[1,4,256,1024]{3,2,0,1:T(8,128)(2,1)S(1)}, u32[]{:S(2)}, u32[]{:S(2)}) async-start(bf16[1,4,256,1024]{3,2,0,1:T(8,128)(2,1)} %bitcast.615), calls=%async_computation.1 | async-start | bytes 4194304 | tf_op jit(solution)/shard_map/forward/all_to_all | solution.py:264
  223.4 1.9 collective-permute-start.6
  223.4 2.9 collective-permute-start.7
  267.3 52.4 %all-to-all-start.2 = ((bf16[1,4,256,1024]{3,2,0,1:T(8,128)(2,1)}), bf16[1,4,256,1024]{3,2,0,1:T(8,128)(2,1)}, u32[]{:S(2)}, u32[]{:S(2)}) async-start(bf16[1,4,256,1024]{3,2,0,1:T(8,128)(2,1)} %bitcast.614), calls=%async_computation.2 | async-start | bytes 4194304 | tf_op jit(solution)/shard_map/forward/all_to_all | solution.py:264
  271.8 170.8 %all-gather.16.cloned.1.call-start = ((), (), s32[]{:S(2)}) async-start(), calls=%async_computation.12 | async-start | bytes 2621440 | tf_op jit(solution)/shard_map/backward_attention/all_gather | solution.py:258
  273.3 48.5 %copy-start.2 = (f32[2,1,256,1024]{3,2,1,0:T(8,128)}, f32[2,1,256,1024]{3,2,1,0:T(8,128)S(1)}, u32[]{:S(2)}) copy-start(f32[2,1,256,1024]{3,2,1,0:T(8,128)S(1)} %convert_element_type.285) | copy-start | bytes 6291460
  277.2 47.5 %copy-start.59 = (f32[256]{0:T(256)}, f32[256]{0:T(256)S(1)}, u32[]{:S(2)}) copy-start(f32[256]{0:T(256)S(1)} %get-tuple-element.191) | copy-start | bytes 3076
  277.2 47.5 %copy-start.61 = (f32[256]{0:T(256)}, f32[256]{0:T(256)S(1)}, u32[]{:S(2)}) copy-start(f32[256]{0:T(256)S(1)} %get-tuple-element.192) | copy-start | bytes 3076
  279.6 48.9 %collective-permute-start.10 = (bf16[1,256,1024]{2,1,0:T(8,128)(2,1)}, bf16[1,256,1024]{2,1,0:T(8,128)(2,1)}, u32[]{:S(2)}, u32[]{:S(2)}) collective-permute-start(bf16[1,256,1024]{2,1,0:T(8,128)(2,1)} %multiply_convert_fusion.3), channel_id=1, source_target_pairs={{0,4},{4,0},{1,5},{5,1},{2,6},{6,2},{3,7},{7,3},{8,12},{12,8},{9,1... | collective-permute-start | bytes 1572872 | tf_op jit(solution)/shard_map/backward_ffn/ppermute | solution.py:239
  326.7 6.1 collective-permute-start.2
  328.1 7.4 %collective-permute-start.8 = (bf16[1,256,1024]{2,1,0:T(8,128)(2,1)}, bf16[1,256,1024]{2,1,0:T(8,128)(2,1)}, u32[]{:S(2)}, u32[]{:S(2)}) collective-permute-start(bf16[1,256,1024]{2,1,0:T(8,128)(2,1)} %add_convert_fusion.10), channel_id=1, source_target_pairs={{0,4},{4,0},{1,5},{5,1},{2,6},{6,2},{3,7},{7,3},{8,12},{12,8},{9,1... | collective-permute-start | bytes 1572872 | tf_op jit(solution)/shard_map/forward/ppermute | solution.py:239
  356.6 8.3 %copy-start.23 = (bf16[1,512,1024]{2,1,0:T(8,128)(2,1)}, bf16[1,512,1024]{2,1,0:T(8,128)(2,1)S(1)}, u32[]{:S(2)}) copy-start(bf16[1,512,1024]{2,1,0:T(8,128)(2,1)S(1)} %fusion.130) | copy-start | bytes 3145732
  356.6 8.2 %collective-permute-start.5 = (bf16[1,256,1024]{2,1,0:T(8,128)(2,1)S(1)}, bf16[1,256,1024]{2,1,0:T(8,128)(2,1)S(1)}, u32[]{:S(2)}, u32[]{:S(2)}) collective-permute-start(bf16[1,256,1024]{2,1,0:T(8,128)(2,1)S(1)} %slice.292), channel_id=1, source_target_pairs={{0,4},{4,0},{1,5},{5,1},{2,6},{6,2},{3,7},{7,3},{8,12},{12,8},{9,1... | collective-permute-start | bytes 1572872 | tf_op jit(solution)/shard_map/forward/ppermute | solution.py:249
  361.3 2.9 collective-permute-start.11
  366.7 5.9 collective-permute-start.14
  371.2 31.8 %collective-permute-start.9 = (bf16[1,256,1024]{2,1,0:T(8,128)(2,1)}, bf16[1,256,1024]{2,1,0:T(8,128)(2,1)}, u32[]{:S(2)}, u32[]{:S(2)}) collective-permute-start(bf16[1,256,1024]{2,1,0:T(8,128)(2,1)} %slice.306), channel_id=1, source_target_pairs={{0,4},{4,0},{1,5},{5,1},{2,6},{6,2},{3,7},{7,3},{8,12},{12,8},{9,1... | collective-permute-start | bytes 1572872 | tf_op jit(solution)/shard_map/forward/ppermute | solution.py:249
  372.5 118.5 %all-gather.18.cloned.1.call-start = ((), (), s32[]{:S(2)}) async-start(), calls=%async_computation.13 | async-start | bytes 2621440 | tf_op jit(solution)/shard_map/backward_attention/all_gather | solution.py:258
  387.1 9.2 %copy-start.42 = (bf16[512,4,256]{0,2,1:T(8,128)(2,1)S(1)}, bf16[512,4,256]{0,2,1:T(8,128)(2,1)}, u32[]{:S(2)}) copy-start(bf16[512,4,256]{0,2,1:T(8,128)(2,1)} %copy.279) | copy-start | bytes 3145732
  387.1 9.2 %copy-start.70 = (f32[512,4,512,1]{2,0,3,1:T(8,128)S(1)}, f32[512,4,512,1]{2,0,3,1:T(8,128)}, u32[]{:S(2)}) copy-start(f32[512,4,512,1]{2,0,3,1:T(8,128)} %copy-done.69) | copy-start | bytes 12582916
  396.1 6.2 collective-permute-start.15
  407.5 143.1 %reduce-scatter.6.cloned.1.call-start = ((), (), s32[]{:S(2)}) async-start(), calls=%async_computation.14 | async-start | bytes 10485760 | tf_op jit(solution)/shard_map/weight_grads/reduce_scatter | solution.py:211
  407.7 10.7 %copy-start.76 = (f32[512,4,512,1]{2,0,3,1:T(8,128)S(1)}, f32[512,4,512,1]{2,0,3,1:T(8,128)}, u32[]{:S(2)}) copy-start(f32[512,4,512,1]{2,0,3,1:T(8,128)} %fusion.60) | copy-start | bytes 12582916
  481.4 2.0 collective-permute-start.13
  481.9 2.2 collective-permute-start.12
  487.4 72.0 %all-to-all-start.3 = ((bf16[1,4,256,1024]{3,2,0,1:T(8,128)(2,1)}), bf16[1,4,256,1024]{3,2,0,1:T(8,128)(2,1)S(1)}, u32[]{:S(2)}, u32[]{:S(2)}) async-start(bf16[1,4,256,1024]{3,2,0,1:T(8,128)(2,1)} %bitcast.622), calls=%async_computation.3 | async-start | bytes 4194304 | tf_op jit(solution)/shard_map/backward_attention/all_to_all | solution.py:264
  491.0 167.9 %reduce-scatter.8.cloned.1.call-start = ((), (), s32[]{:S(2)}) async-start(), calls=%async_computation.15 | async-start | bytes 2621440 | tf_op jit(solution)/shard_map/weight_grads/reduce_scatter | solution.py:212
  552.5 2.0 collective-permute-start.17
  553.0 2.3 collective-permute-start.16
  559.4 81.1 %all-to-all-start.4 = ((bf16[1,4,256,1024]{3,2,0,1:T(8,128)(2,1)}), bf16[1,4,256,1024]{3,2,0,1:T(8,128)(2,1)}, u32[]{:S(2)}, u32[]{:S(2)}) async-start(bf16[1,4,256,1024]{3,2,0,1:T(8,128)(2,1)} %bitcast.623), calls=%async_computation.4 | async-start | bytes 4194304 | tf_op jit(solution)/shard_map/backward_attention/all_to_all | solution.py:264
  564.1 115.0 %reduce-scatter.10.cloned.1.call-start = ((), (), s32[]{:S(2)}) async-start(), calls=%async_computation.17 | async-start | bytes 2359296
  576.8 67.4 %copy-start.3 = (f32[2,1,256,1024]{3,2,1,0:T(8,128)S(1)}, f32[2,1,256,1024]{3,2,1,0:T(8,128)}, u32[]{:S(2)}) copy-start(f32[2,1,256,1024]{3,2,1,0:T(8,128)} %copy-done.2) | copy-start | bytes 6291460
  576.8 67.4 %copy-start.56 = (f32[1,1,1,1024]{3,1,2,0:T(1,128)S(1)}, f32[1,1,1,1024]{3,1,2,0:T(1,128)}, u32[]{:S(2)}) copy-start(f32[1,1,1,1024]{3,1,2,0:T(1,128)} %get-tuple-element.184) | copy-start | bytes 12292
  576.8 67.4 %copy-start.60 = (f32[256]{0:T(256)S(1)}, f32[256]{0:T(256)}, u32[]{:S(2)}) copy-start(f32[256]{0:T(256)} %copy-done.59) | copy-start | bytes 3076
  576.8 67.4 %copy-start.62 = (f32[256]{0:T(256)S(1)}, f32[256]{0:T(256)}, u32[]{:S(2)}) copy-start(f32[256]{0:T(256)} %copy-done.61) | copy-start | bytes 3076
  649.8 33.1 %all-to-all-start.5 = ((f32[4,1,3072]{2,1,0:T(1,128)}), f32[4,1,3072]{2,1,0:T(1,128)}, u32[]{:S(2)}, u32[]{:S(2)}) async-start(f32[4,1,3072]{2,1,0:T(1,128)} %reshape.1158), calls=%async_computation.7 | async-start | bytes 98304 | tf_op jit(solution)/shard_map/ada_grad/all_to_all | solution.py:392
  660.0 36.6 %copy-start.55 = (bf16[8,2,4,128]{3,0,2,1:T(8,128)(2,1)S(1)}, bf16[8,2,4,128]{3,0,2,1:T(8,128)(2,1)}, u32[]{:S(2)}) copy-start(bf16[8,2,4,128]{3,0,2,1:T(8,128)(2,1)} %copy-done.54) | copy-start | bytes 49156
  660.0 38.1 %collective-permute-start.18 = (bf16[2,128,512]{2,1,0:T(8,128)(2,1)S(1)}, bf16[2,128,512]{2,1,0:T(8,128)(2,1)S(1)}, u32[]{:S(2)}, u32[]{:S(2)}) collective-permute-start(bf16[2,128,512]{2,1,0:T(8,128)(2,1)S(1)} %get-tuple-element.167), channel_id=1, source_target_pairs={{0,4},{4,0},{1,5},{5,1},{2,6},{6,2},{3,7},{7,3},{8,12},{12,8},{9,1... | collective-permute-start | bytes 786440 | tf_op jit(solution)/shard_map/weight_grads/ppermute | solution.py:216
  (62 other events, 211.6 us)
Sparse Core Ops, SparseCore 0:
  12.8 52.2 all-gather.11
  66.6 79.5 all-gather.19
  148.1 24.0 all-gather.9
  173.9 87.4 all-gather.13
  372.7 43.7 all-gather.15
  417.9 44.4 all-gather.17
  465.4 85.1 reduce-scatter.5
  552.9 69.9 reduce-scatter.7
  626.2 52.9 reduce-scatter.9

commit v16 on v11

--- a/solution.py
+++ b/solution.py
@@ -231,7 +231,13 @@
     residual = tokens[:, 0].astype(jnp.float32)
     upstream = out_grad[:, 0].astype(jnp.float32)
     with jax.named_scope("group_inputs"):
-        group_tokens = lax.all_gather(tokens[:, 0], "tensor", axis=1, tiled=True)
+        group_tokens = jnp.concatenate(
+            [
+                lax.all_gather(tokens[i : i + 1, 0], "tensor", axis=1, tiled=True)
+                for i in range(clips)
+            ],
+            axis=0,
+        )
         group_upstream = None
     def gather_halves(values):
         if halves != 2:

time: 712 us -> 708 us (level)
  blocking collectives: 57.8 us -> 49.4 us
    all_gather x1 -> x2, waiting for transfers between devices: 81.1 us -> 42.2 us  [on_device(): lax.all_gather(tokens[i:i + 1, 0], 'tensor', axis=1, tiled=True)]
    all_gather x1, waiting for transfers between devices: 11.5 us -> 42.3 us  [hidden_half(): gathered = lax.all_gather(joined, 'tensor', axis=0, tiled=True)]
    all_to_all x1 -> x0, blocking collectives: 10.9 us -> none  [on_device(): lax.all_to_all(partial_mod, ('dp', 'frame'), 0, 0, tiled=True)]
    all_gather x1, waiting for transfers between devices: 15.9 us -> 23.8 us  [on_device(): lax.all_gather(w, ('dp', 'frame'), axis=0, tiled=True)]
    unnamed x161 -> x165, local copies, waits for them, and re-layouts: 22.3 us -> 23.1 us
  transfers between devices with their start and end apart: 34 -> 36, of which waited for: 12 -> 12; matrix products, arithmetic and copies ran while one was open for 29% -> 30% of each run, Pallas kernels for 15% -> 15%
where the time goes in v16:
time: 708 us; the launch traced here: 703 us
  waiting for transfers between devices  258 us (36%)
  Pallas kernels  107 us (15%)
  matrix products  97.1 us (14%)
  other arithmetic  85 us (12%)
  local copies, waits for them, and re-layouts  57.7 us (8%)
  blocking collectives  49.4 us (7%)
  starting transfers between devices  32.6 us (5%)
  between operations  15.8 us (2%)
    reduce_scatter x2, waiting for transfers between devices, on_device(): lax.psum_scatter(total.astype(jnp.bfloat16), ('dp', 'frame'), scatter_dim...  66.6 us
    pallas_call x2, Pallas kernels, attention_backward(): pl.pallas_call(functools.partial(_backward_kernel, heads, HEAD_DIM ** (-0...  64.9 us
    all_to_all x4, waiting for transfers between devices, scatter_tokens(): received = lax.all_to_all(parts, 'tensor', 1, 1, tiled=True)  51.3 us
    all_gather x1, waiting for transfers between devices, hidden_half(): gathered = lax.all_gather(joined, 'tensor', axis=0, tiled=True)  42.3 us
    pallas_call x2, Pallas kernels, attention_forward(): pl.pallas_call(functools.partial(_forward_kernel, heads, HEAD_DIM ** (-0....  42.2 us
    all_gather x2, waiting for transfers between devices, on_device(): lax.all_gather(tokens[i:i + 1, 0], 'tensor', axis=1, tiled=True)  42.2 us
    reduce_scatter x1, waiting for transfers between devices, hidden_half_back(): summed = lax.psum_scatter(summed, 'tensor', scatter_dimension=0, tiled=True)  25.9 us
    all_gather x1, waiting for transfers between devices, on_device(): lax.all_gather(w, ('dp', 'frame'), axis=0, tiled=True)  23.8 us
  transfers between devices with their start and end apart: 36, of which 12 were waited for; matrix products, arithmetic and copies ran while one was open for 30% of the time, Pallas kernels for 15%

profile of v16, /device:TPU:0, one launch (start us, length us, event | category | flops | bytes accessed | tf_op | source)
XLA Modules:
  0.0 703.0 jit_solution(6397535129296578680)
XLA Ops:
  16.3 10.1 %all-gather.3 = s32[8,2,4]{2,1,0:T(2,128)S(1)} all-gather(s32[1,2,4]{2,1,0:T(2,128)S(1)} %bitcast.678), channel_id=1, replica_groups=mesh['dp'=4,'frame'=2,'tensor'=4] {'dp','frame'}, dimensions={0}, use_global_device_ids=true | all-gather | bytes 288 | tf_op jit(solution)/shard_map/modulation/all_gather | solution.py:168
  28.7 3.5 all-to-all-start
  32.2 12.7 %all_gather.37 = bf16[1024,256]{1,0:T(8,128)(2,1)S(1)} all-gather(bf16[128,256]{1,0:T(8,128)(2,1)S(1)} %copy-done.58), channel_id=1, replica_groups=mesh['dp'=4,'frame'=2,'tensor'=4] {'dp','frame'}, dimensions={0}, use_global_device_ids=true | all-gather | bytes 589824 | tf_op jit(solution)/shard_map/weights/all_gather | solution.py:226
  45.0 17.1 %all_gather.34 = f32[2,4,6,1024]{3,2,1,0:T(8,128)S(1)} all-gather(f32[2,4,6,256]{3,2,1,0:T(8,128)S(1)} %copy.301), channel_id=1, replica_groups=mesh['dp'=4,'frame'=2,'tensor'=4] {'tensor'}, dimensions={3}, use_global_device_ids=true | all-gather | bytes 245760 | tf_op jit(solution)/shard_map/modulation/all_gather | solution.py:181
  67.1 42.3 %all-gather.14.cloned.1.call-done = bf16[2048,512]{1,0:T(8,128)(2,1)} async-done(((bf16[512,512]{1,0:T(8,128)(2,1)}), bf16[2048,512]{1,0:T(8,128)(2,1)}) %all-gather.14.cloned.1.call-update) | async-done | bytes 2097168 | tf_op jit(solution)/shard_map/weights/all_gather | solution.py:202
  111.9 23.8 %all-gather.12.cloned.1.call-done = bf16[1024,3,256]{2,0,1:T(8,128)(2,1)} async-done(((bf16[128,3,256]{2,0,1:T(8,128)(2,1)}), bf16[1024,3,256]{2,0,1:T(8,128)(2,1)}) %all-gather.12.cloned.1.call-update) | async-done | bytes 1572880 | tf_op jit(solution)/shard_map/weights/all_gather | solution.py:226
  135.7 3.2 fusion.129
  141.2 42.2 %all-gather.22.cloned.1.call-done = bf16[1,1,1024,1024]{3,2,1,0:T(8,128)(2,1)} async-done(((bf16[1,1,256,1024]{3,2,1,0:T(8,128)(2,1)}), bf16[1,1,1024,1024]{3,2,1,0:T(8,128)(2,1)}) %all-gather.22.cloned.1.call-update) | async-done | bytes 2097168 | tf_op jit(solution)/shard_map/group_inputs/all_gather | solution.py:236
  188.5 21.1 %forward.3 = (bf16[1024,256]{1,0:T(8,128)(2,1)}, f32[1024,4]{1,0:T(8,128)}) custom-call(bf16[1024,256]{1,0:T(8,128)(2,1)} %get-tuple-element.156.q_ref, bf16[2048,256]{1,0:T(8,128)(2,1)} %maximum_bitcast_fusion.2.k_ref, bf16[2048,256]{1,0:T(8,128)(2,1)} %maximum_bitcast_fusion.3.v_ref), custom_call_target="tpu_custom_call" | custom-call | flops 2147483648 | bytes 3145728 | tf_op jit(solution)/shard_map/forward/pallas_call | solution.py:85
  209.6 3.3 convolution_convert_fusion
  212.9 4.8 all-to-all-start.2
  227.7 21.1 %forward.2 = (bf16[1024,256]{1,0:T(8,128)(2,1)}, f32[1024,4]{1,0:T(8,128)}) custom-call(bf16[1024,256]{1,0:T(8,128)(2,1)} %get-tuple-element.153.q_ref, bf16[2048,256]{1,0:T(8,128)(2,1)} %maximum_bitcast_fusion.k_ref, bf16[2048,256]{1,0:T(8,128)(2,1)} %maximum_bitcast_fusion.1.v_ref), custom_call_target="tpu_custom_call" | custom-call | flops 2147483648 | bytes 3145728 | tf_op jit(solution)/shard_map/forward/pallas_call | solution.py:85
  248.8 3.2 convolution_convert_fusion.1
  252.0 14.1 %all-to-all-done.2 = bf16[1,4,256,1024]{3,2,0,1:T(8,128)(2,1)} async-done(((bf16[1,4,256,1024]{3,2,0,1:T(8,128)(2,1)}), bf16[1,4,256,1024]{3,2,0,1:T(8,128)(2,1)}, u32[]{:S(2)}, u32[]{:S(2)}) %all-to-all-start.2) | async-done | bytes 2097184 | tf_op jit(solution)/shard_map/forward/all_to_all | solution.py:270
  266.1 4.4 all-to-all-start.1
  270.8 3.6 convert_element_type.262
  278.1 3.0 convert_reduce_fusion.6
  281.2 37.2 %all-to-all-done.1 = bf16[1,4,256,1024]{3,2,0,1:T(8,128)(2,1)} async-done(((bf16[1,4,256,1024]{3,2,0,1:T(8,128)(2,1)}), bf16[1,4,256,1024]{3,2,0,1:T(8,128)(2,1)}, u32[]{:S(2)}, u32[]{:S(2)}) %all-to-all-start.1) | async-done | bytes 2097184 | tf_op jit(solution)/shard_map/forward/all_to_all | solution.py:270
  320.5 2.8 multiply_reduce_fusion.10
  339.7 3.9 fusion.244
  355.0 4.6 fusion.136
  373.2 2.7 reshape.939
  375.9 7.1 %fusion.60 = f32[512,4,512,1]{2,0,3,1:T(8,128)} fusion(bf16[512,4,256]{2,1,0:T(4,128)(2,1)} %reshape.939, bf16[4,4,1,256,512]{4,3,2,1,0:T(8,128)(2,1)} %copy-done.10), kind=kOutput, calls=%fused_computation.91 | convolution fusion | flops 2147483648 | bytes 9437184 | tf_op jit(solution)/shard_map/backward_ffn/crad,atdj->crtj/dot_general | solution.py:315
  385.3 9.0 %fusion.139 = bf16[1,512,1024]{2,1,0:T(8,128)(2,1)S(1)} fusion(bf16[1024,512,4]{1,0,2:T(8,128)(2,1)} %bitcast.619, f32[512,4,512,1]{2,0,3,1:T(8,128)} %fusion.60, f32[512,4,512,1]{2,0,3,1:T(8,128)} %copy-done.70), kind=kOutput, calls=%fused_computation.164 | convolution fusion | flops 2168979456 | bytes 13631488 | tf_op jit(solution)/shard_map/backward_ffn/crtj,atdj->crad/dot_general | solution.py:326
  394.6 6.1 fusion.75
  406.2 8.1 %fusion.43 = bf16[4,4,256,512]{3,2,0,1:T(8,128)(2,1)S(1)} fusion(f32[4,512,4,256]{1,3,2,0:T(8,128)} %fusion.75, f32[512,4,512,1]{2,0,3,1:T(8,128)} %copy-done.73, bf16[512,4,256]{0,2,1:T(8,128)(2,1)} %copy.266), kind=kOutput, calls=%fused_computation.62 | convolution fusion | flops 2161115136 | bytes 17825792 | tf_op jit(solution)/shard_map/backward_ffn/crad,crtj->atdj/dot_general | solution.py:318
  418.4 6.1 fusion.78
  424.5 6.7 fusion.42
  433.4 7.6 %pad_maximum_fusion = bf16[16,512,512]{2,1,0:T(8,128)(2,1)} fusion(bf16[16,256,512]{2,1,0:T(8,128)(2,1)} %bitcast.610, bf16[16,256,512]{2,1,0:T(8,128)(2,1)} %bitcast.615), kind=kLoop, calls=%fused_computation | loop fusion | flops 16777216 | bytes 16777216 | tf_op jit(solution)/shard_map/weight_grads/concatenate | solution.py:209
  442.1 3.1 fusion.145.g_ref
  445.2 32.3 %backward_attention.2 = (f32[1024,256]{1,0:T(8,128)}, f32[2048,256]{1,0:T(8,128)}, f32[2048,256]{1,0:T(8,128)}) custom-call(bf16[1024,256]{1,0:T(8,128)(2,1)} %get-tuple-element.153.q_ref, bf16[2048,256]{1,0:T(8,128)(2,1)} %maximum_bitcast_fusion.k_ref, bf16[2048,256]{1,0:T(8,128)(2,1)} %maximum_bitcast_fusion.1.v_ref, bf16[1024,256]{1,0:T(8,128)(2,1)} %fusion.145.g_ref, ...), custom_call_target="tpu_custom_call" | custom-call | flops 5368709120 | bytes 8912896 | tf_op jit(solution)/shard_map/backward_attention/pallas_call | solution.py:118
  482.5 3.1 bitcast_convert_fusion.1
  485.7 3.7 all-to-all-start.3
  489.4 3.1 fusion.148.g_ref
  492.6 32.6 %backward_attention.3 = (f32[1024,256]{1,0:T(8,128)}, f32[2048,256]{1,0:T(8,128)}, f32[2048,256]{1,0:T(8,128)}) custom-call(bf16[1024,256]{1,0:T(8,128)(2,1)} %get-tuple-element.156.q_ref, bf16[2048,256]{1,0:T(8,128)(2,1)} %maximum_bitcast_fusion.2.k_ref, bf16[2048,256]{1,0:T(8,128)(2,1)} %maximum_bitcast_fusion.3.v_ref, bf16[1024,256]{1,0:T(8,128)(2,1)} %fusion.148.g_ref, ...), custom_call_target="tpu_custom_call" | custom-call | flops 5368709120 | bytes 8912896 | tf_op jit(solution)/shard_map/backward_attention/pallas_call | solution.py:118
  538.8 3.8 fusion.177
  542.7 3.2 add_convert_fusion.2
  545.9 4.7 bitcast_convert_fusion
  550.7 5.3 all-to-all-start.4
  557.9 29.4 %reduce-scatter.7.cloned.1.call-done = bf16[128,256]{1,0:T(8,128)(2,1)} async-done(((bf16[1024,256]{1,0:T(8,128)(2,1)}), bf16[128,256]{1,0:T(8,128)(2,1)}) %reduce-scatter.7.cloned.1.call-update) | async-done | bytes 65552 | tf_op jit(solution)/shard_map/weight_grads/reduce_scatter | solution.py:412
  588.8 2.7 convert_reduce_fusion.4
  591.6 37.2 %reduce-scatter.5.cloned.1.call-done = bf16[128,3,256]{2,0,1:T(8,128)(2,1)} async-done(((bf16[1024,3,256]{2,0,1:T(8,128)(2,1)}), bf16[128,3,256]{2,0,1:T(8,128)(2,1)}) %reduce-scatter.5.cloned.1.call-update) | async-done | bytes 196624 | tf_op jit(solution)/shard_map/weight_grads/reduce_scatter | solution.py:412
  630.5 2.7 convert_reduce_fusion.2
  636.3 3.6 reshape.1148
  639.9 4.8 all-to-all-start.5
  646.1 3.5 add_convert_fusion.6
  649.6 25.9 %reduce-scatter.11.cloned.1.call-done = bf16[1,512,512]{2,1,0:T(8,128)(2,1)} async-done(((bf16[4,512,512]{2,1,0:T(8,128)(2,1)}), bf16[1,512,512]{2,1,0:T(8,128)(2,1)}) %reduce-scatter.11.cloned.1.call-update) | async-done | bytes 524304 | tf_op jit(solution)/shard_map/weight_grads/reduce_scatter | solution.py:212
  682.3 9.5 %all-gather.2 = f32[16,4,1,6,256]{4,1,0,3,2:T(4,128)S(1)} all-gather(f32[2,4,1,6,256]{4,1,0,3,2:T(4,128)S(1)} %bitcast.638), channel_id=4, replica_groups=mesh['dp'=4,'frame'=2,'tensor'=4] {'dp','frame'}, dimensions={0}, use_global_device_ids=true | all-gather | bytes 442368 | tf_op jit(solution)/shard_map/ada_grad/all_gather | solution.py:401
  (369 shorter events, 137.5 us)
Async XLA Ops:
  7.2 55.7 %all-gather.24.cloned.1.call-start = ((), (), s32[]{:S(2)}) async-start(), calls=%async_computation.20 | async-start | bytes 2621440 | tf_op jit(solution)/shard_map/group_inputs/all_gather | solution.py:236
  9.5 99.9 %all-gather.14.cloned.1.call-start = ((), (), s32[]{:S(2)}) async-start(), calls=%async_computation.11 | async-start | bytes 2621440 | tf_op jit(solution)/shard_map/weights/all_gather | solution.py:202
  10.8 1.8 collective-permute-start.4
  12.5 1.4 collective-permute-start.3
  15.0 120.7 %all-gather.12.cloned.1.call-start = ((), (), s32[]{:S(2)}) async-start(), calls=%async_computation.10 | async-start | bytes 1769472 | tf_op jit(solution)/shard_map/weights/all_gather | solution.py:226
  15.8 167.6 %all-gather.22.cloned.1.call-start = ((), (), s32[]{:S(2)}) async-start(), calls=%async_computation.19 | async-start | bytes 2621440 | tf_op jit(solution)/shard_map/group_inputs/all_gather | solution.py:236
  28.7 16.2 %all-to-all-start = ((f32[8,2,4,6,256]{4,2,3,1,0:T(4,128)}), f32[8,2,4,6,256]{4,2,3,1,0:T(4,128)S(1)}, u32[]{:S(2)}, u32[]{:S(2)}) async-start(f32[8,2,4,6,256]{4,2,3,1,0:T(4,128)} %fusion.182), calls=%async_computation | async-start | bytes 786432 | tf_op jit(solution)/shard_map/modulation/all_to_all | solution.py:179
  32.1 307.5 %all-gather.16.cloned.1.call-start = ((), (), s32[]{:S(2)}) async-start(), calls=%async_computation.12 | async-start | bytes 10485760 | tf_op jit(solution)/shard_map/weights/all_gather | solution.py:203
  44.9 203.9 %copy-start.17 = (bf16[1024,256]{1,0:T(8,128)(2,1)}, bf16[1024,256]{1,0:T(8,128)(2,1)S(1)}, u32[]{:S(2)}) copy-start(bf16[1024,256]{1,0:T(8,128)(2,1)S(1)} %all_gather.37) | copy-start | bytes 1572868
  111.9 27.1 %copy-start.29 = (bf16[1024,1024,1]{1,0,2:T(8,128)(2,1)}, bf16[1024,1024,1]{1,0,2:T(8,128)(2,1)S(1)}, u32[]{:S(2)}) copy-start(bf16[1024,1024,1]{1,0,2:T(8,128)(2,1)S(1)} %fusion.72) | copy-start | bytes 6291460
  140.0 45.4 %collective-permute-start.6 = (bf16[1,1024,256]{2,1,0:T(8,128)(2,1)}, bf16[1,1024,256]{2,1,0:T(8,128)(2,1)S(1)}, u32[]{:S(2)}, u32[]{:S(2)}) collective-permute-start(bf16[1,1024,256]{2,1,0:T(8,128)(2,1)} %get-tuple-element.155), channel_id=1, source_target_pairs={{0,4},{4,0},{1,5},{5,1},{2,6},{6,2},{3,7},{7,3},{8,12},{12,8},{9,1... | collective-permute-start | bytes 1572872 | tf_op jit(solution)/shard_map/forward/ppermute | solution.py:245
  141.0 46.5 %collective-permute-start.7 = (bf16[1,1024,256]{2,1,0:T(8,128)(2,1)S(1)}, bf16[1,1024,256]{2,1,0:T(8,128)(2,1)S(1)}, u32[]{:S(2)}, u32[]{:S(2)}) collective-permute-start(bf16[1,1024,256]{2,1,0:T(8,128)(2,1)S(1)} %get-tuple-element.154), channel_id=1, source_target_pairs={{0,4},{4,0},{1,5},{5,1},{2,6},{6,2},{3,7},{7,3},{8,12},{12,8},{9,1... | collective-permute-start | bytes 1572872 | tf_op jit(solution)/shard_map/forward/ppermute | solution.py:245
  212.9 53.2 %all-to-all-start.2 = ((bf16[1,4,256,1024]{3,2,0,1:T(8,128)(2,1)}), bf16[1,4,256,1024]{3,2,0,1:T(8,128)(2,1)}, u32[]{:S(2)}, u32[]{:S(2)}) async-start(bf16[1,4,256,1024]{3,2,0,1:T(8,128)(2,1)} %bitcast.617), calls=%async_computation.2 | async-start | bytes 4194304 | tf_op jit(solution)/shard_map/forward/all_to_all | solution.py:270
  223.6 1.9 collective-permute-start
  223.6 3.0 collective-permute-start.1
  248.8 21.8 %copy-start.20 = (bf16[2,1,256,1024]{3,2,1,0:T(8,128)(2,1)S(1)}, bf16[2,1,256,1024]{3,2,1,0:T(8,128)(2,1)}, u32[]{:S(2)}) copy-start(bf16[2,1,256,1024]{3,2,1,0:T(8,128)(2,1)} %param.12) | copy-start | bytes 3145732
  266.1 52.3 %all-to-all-start.1 = ((bf16[1,4,256,1024]{3,2,0,1:T(8,128)(2,1)}), bf16[1,4,256,1024]{3,2,0,1:T(8,128)(2,1)}, u32[]{:S(2)}, u32[]{:S(2)}) async-start(bf16[1,4,256,1024]{3,2,0,1:T(8,128)(2,1)} %bitcast.23), calls=%async_computation.1 | async-start | bytes 4194304 | tf_op jit(solution)/shard_map/forward/all_to_all | solution.py:270
  270.5 170.5 %all-gather.18.cloned.1.call-start = ((), (), s32[]{:S(2)}) async-start(), calls=%async_computation.13 | async-start | bytes 2621440 | tf_op jit(solution)/shard_map/backward_attention/all_gather | solution.py:264
  270.8 49.6 %copy-start.2 = (f32[2,1,256,1024]{3,2,1,0:T(8,128)}, f32[2,1,256,1024]{3,2,1,0:T(8,128)S(1)}, u32[]{:S(2)}) copy-start(f32[2,1,256,1024]{3,2,1,0:T(8,128)S(1)} %convert_element_type.236) | copy-start | bytes 6291460
  274.6 48.6 %copy-start.59 = (f32[256]{0:T(256)}, f32[256]{0:T(256)S(1)}, u32[]{:S(2)}) copy-start(f32[256]{0:T(256)S(1)} %get-tuple-element.187) | copy-start | bytes 3076
  274.6 48.6 %copy-start.61 = (f32[256]{0:T(256)}, f32[256]{0:T(256)S(1)}, u32[]{:S(2)}) copy-start(f32[256]{0:T(256)S(1)} %get-tuple-element.188) | copy-start | bytes 3076
  276.9 50.2 %collective-permute-start.10 = (bf16[1,256,1024]{2,1,0:T(8,128)(2,1)}, bf16[1,256,1024]{2,1,0:T(8,128)(2,1)}, u32[]{:S(2)}, u32[]{:S(2)}) collective-permute-start(bf16[1,256,1024]{2,1,0:T(8,128)(2,1)} %multiply_convert_fusion.3), channel_id=1, source_target_pairs={{0,4},{4,0},{1,5},{5,1},{2,6},{6,2},{3,7},{7,3},{8,12},{12,8},{9,1... | collective-permute-start | bytes 1572872 | tf_op jit(solution)/shard_map/backward_ffn/ppermute | solution.py:245
  325.3 5.8 collective-permute-start.2
  326.6 7.1 %collective-permute-start.8 = (bf16[1,256,1024]{2,1,0:T(8,128)(2,1)}, bf16[1,256,1024]{2,1,0:T(8,128)(2,1)}, u32[]{:S(2)}, u32[]{:S(2)}) collective-permute-start(bf16[1,256,1024]{2,1,0:T(8,128)(2,1)} %add_convert_fusion.10), channel_id=1, source_target_pairs={{0,4},{4,0},{1,5},{5,1},{2,6},{6,2},{3,7},{7,3},{8,12},{12,8},{9,1... | collective-permute-start | bytes 1572872 | tf_op jit(solution)/shard_map/forward/ppermute | solution.py:245
  354.9 8.3 %collective-permute-start.5 = (bf16[1,256,1024]{2,1,0:T(8,128)(2,1)S(1)}, bf16[1,256,1024]{2,1,0:T(8,128)(2,1)S(1)}, u32[]{:S(2)}, u32[]{:S(2)}) collective-permute-start(bf16[1,256,1024]{2,1,0:T(8,128)(2,1)S(1)} %slice.287), channel_id=1, source_target_pairs={{0,4},{4,0},{1,5},{5,1},{2,6},{6,2},{3,7},{7,3},{8,12},{12,8},{9,1... | collective-permute-start | bytes 1572872 | tf_op jit(solution)/shard_map/forward/ppermute | solution.py:255
  359.7 2.9 collective-permute-start.11
  365.0 5.9 collective-permute-start.14
  369.5 31.7 %collective-permute-start.9 = (bf16[1,256,1024]{2,1,0:T(8,128)(2,1)}, bf16[1,256,1024]{2,1,0:T(8,128)(2,1)}, u32[]{:S(2)}, u32[]{:S(2)}) collective-permute-start(bf16[1,256,1024]{2,1,0:T(8,128)(2,1)} %slice.300), channel_id=1, source_target_pairs={{0,4},{4,0},{1,5},{5,1},{2,6},{6,2},{3,7},{7,3},{8,12},{12,8},{9,1... | collective-permute-start | bytes 1572872 | tf_op jit(solution)/shard_map/forward/ppermute | solution.py:255
  370.9 118.5 %all-gather.20.cloned.1.call-start = ((), (), s32[]{:S(2)}) async-start(), calls=%async_computation.14 | async-start | bytes 2621440 | tf_op jit(solution)/shard_map/backward_attention/all_gather | solution.py:264
  394.4 6.2 collective-permute-start.15
  405.8 150.2 %reduce-scatter.9.cloned.1.call-start = ((), (), s32[]{:S(2)}) async-start(), calls=%async_computation.17 | async-start | bytes 10485760 | tf_op jit(solution)/shard_map/weight_grads/reduce_scatter | solution.py:211
  479.4 2.2 collective-permute-start.13
  480.2 2.1 collective-permute-start.12
  485.7 65.0 %all-to-all-start.3 = ((bf16[1,4,256,1024]{3,2,0,1:T(8,128)(2,1)}), bf16[1,4,256,1024]{3,2,0,1:T(8,128)(2,1)S(1)}, u32[]{:S(2)}, u32[]{:S(2)}) async-start(bf16[1,4,256,1024]{3,2,0,1:T(8,128)(2,1)} %bitcast.624), calls=%async_computation.3 | async-start | bytes 4194304 | tf_op jit(solution)/shard_map/backward_attention/all_to_all | solution.py:270
  489.4 97.9 %reduce-scatter.7.cloned.1.call-start = ((), (), s32[]{:S(2)}) async-start(), calls=%async_computation.16 | async-start | bytes 589824 | tf_op jit(solution)/shard_map/weight_grads/reduce_scatter | solution.py:412
  527.9 7.4 %collective-permute-start.17 = (bf16[1,1024,256]{2,1,0:T(8,128)(2,1)}, bf16[1,1024,256]{2,1,0:T(8,128)(2,1)}, u32[]{:S(2)}, u32[]{:S(2)}) collective-permute-start(bf16[1,1024,256]{2,1,0:T(8,128)(2,1)} %slice.315), channel_id=1, source_target_pairs={{0,4},{4,0},{1,5},{5,1},{2,6},{6,2},{3,7},{7,3},{8,12},{12,8},{9,1... | collective-permute-start | bytes 1572872 | tf_op jit(solution)/shard_map/backward_attention/ppermute | solution.py:255
  530.0 6.5 collective-permute-start.16
  535.0 93.8 %reduce-scatter.5.cloned.1.call-start = ((), (), s32[]{:S(2)}) async-start(), calls=%async_computation.15 | async-start | bytes 1769472 | tf_op jit(solution)/shard_map/weight_grads/reduce_scatter | solution.py:412
  550.7 79.8 %all-to-all-start.4 = ((bf16[1,4,256,1024]{3,2,0,1:T(8,128)(2,1)}), bf16[1,4,256,1024]{3,2,0,1:T(8,128)(2,1)}, u32[]{:S(2)}, u32[]{:S(2)}) async-start(bf16[1,4,256,1024]{3,2,0,1:T(8,128)(2,1)} %bitcast.625), calls=%async_computation.4 | async-start | bytes 4194304 | tf_op jit(solution)/shard_map/backward_attention/all_to_all | solution.py:270
  556.0 35.5 %copy-start.57 = (f32[1,1,1,1024]{3,1,2,0:T(1,128)S(1)}, f32[1,1,1,1024]{3,1,2,0:T(1,128)}, u32[]{:S(2)}) copy-start(f32[1,1,1,1024]{3,1,2,0:T(1,128)} %get-tuple-element.176) | copy-start | bytes 12292
  556.0 119.5 %reduce-scatter.11.cloned.1.call-start = ((), (), s32[]{:S(2)}) async-start(), calls=%async_computation.18 | async-start | bytes 2621440 | tf_op jit(solution)/shard_map/weight_grads/reduce_scatter | solution.py:212
  557.8 76.3 %copy-start.3 = (f32[2,1,256,1024]{3,2,1,0:T(8,128)S(1)}, f32[2,1,256,1024]{3,2,1,0:T(8,128)}, u32[]{:S(2)}) copy-start(f32[2,1,256,1024]{3,2,1,0:T(8,128)} %copy-done.2) | copy-start | bytes 6291460
  557.8 76.3 %copy-start.56 = (f32[1,1,1,1024]{3,1,2,0:T(1,128)S(1)}, f32[1,1,1,1024]{3,1,2,0:T(1,128)}, u32[]{:S(2)}) copy-start(f32[1,1,1,1024]{3,1,2,0:T(1,128)} %get-tuple-element.180) | copy-start | bytes 12292
  557.9 76.3 %copy-start.60 = (f32[256]{0:T(256)S(1)}, f32[256]{0:T(256)}, u32[]{:S(2)}) copy-start(f32[256]{0:T(256)} %copy-done.59) | copy-start | bytes 3076
  557.9 76.3 %copy-start.62 = (f32[256]{0:T(256)S(1)}, f32[256]{0:T(256)}, u32[]{:S(2)}) copy-start(f32[256]{0:T(256)} %copy-done.61) | copy-start | bytes 3076
  639.9 39.1 %all-to-all-start.5 = ((f32[4,1,3072]{2,1,0:T(1,128)}), f32[4,1,3072]{2,1,0:T(1,128)S(1)}, u32[]{:S(2)}, u32[]{:S(2)}) async-start(f32[4,1,3072]{2,1,0:T(1,128)} %reshape.1148), calls=%async_computation.9 | async-start | bytes 98304 | tf_op jit(solution)/shard_map/ada_grad/all_to_all | solution.py:398
  649.6 42.2 %copy-start.55 = (bf16[8,2,4,128]{3,0,2,1:T(8,128)(2,1)S(1)}, bf16[8,2,4,128]{3,0,2,1:T(8,128)(2,1)}, u32[]{:S(2)}) copy-start(bf16[8,2,4,128]{3,0,2,1:T(8,128)(2,1)} %copy-done.54) | copy-start | bytes 49156
  676.6 16.7 %collective-permute-start.18 = (bf16[2,128,512]{2,1,0:T(8,128)(2,1)S(1)}, bf16[2,128,512]{2,1,0:T(8,128)(2,1)S(1)}, u32[]{:S(2)}, u32[]{:S(2)}) collective-permute-start(bf16[2,128,512]{2,1,0:T(8,128)(2,1)S(1)} %get-tuple-element.163), channel_id=1, source_target_pairs={{0,4},{4,0},{1,5},{5,1},{2,6},{6,2},{3,7},{7,3},{8,12},{12,8},{9,1... | collective-permute-start | bytes 786440 | tf_op jit(solution)/shard_map/weight_grads/ppermute | solution.py:216
  (66 other events, 308.4 us)
Sparse Core Ops, SparseCore 0:
  10.1 52.5 all-gather.23
  64.9 44.4 all-gather.13
  111.3 24.3 all-gather.11
  137.7 45.6 all-gather.21
  185.1 86.2 all-gather.15
  371.0 44.6 all-gather.17
  417.3 44.4 all-gather.19
  464.9 85.1 reduce-scatter.8
  553.1 34.1 reduce-scatter.6
  590.4 38.3 reduce-scatter.4
  631.1 44.4 reduce-scatter.10

commit v17 on v16

--- a/solution.py
+++ b/solution.py
@@ -375,7 +375,7 @@
             axis=1,
         )
         totals = (joint_total, mixer_total, up_total, down_total)
-        return output, grad_input.astype(jnp.bfloat16), grad_modulation, totals
+        return output, grad_input.astype(jnp.bfloat16), grad_modulation, totals, grad_one_all
 
     pieces = [
         clip_pass(
@@ -408,13 +408,17 @@
         )
 
     with jax.named_scope("weight_grads"):
+        up_total, down_total, _ = lax.optimization_barrier((up_total, down_total, pieces[-1][4]))
+        up_sum, down_sum = hidden_half_back((up_total, down_total))
+        joint_total, mixer_total, up_sum, down_sum = lax.optimization_barrier(
+            (joint_total, mixer_total, up_sum, down_sum)
+        )
         joint_sum, mixer_sum = (
             lax.psum_scatter(
                 total.astype(jnp.bfloat16), ("dp", "frame"), scatter_dimension=0, tiled=True
             ).astype(jnp.float32)
             for total in (joint_total, mixer_total)
         )
-        up_sum, down_sum = hidden_half_back((up_total, down_total))
         summed = (joint_sum, mixer_sum, up_sum, down_sum)
     result = output[:, None]
     input_grad = grad_input_low[:, None]

time: 708 us -> 767 us (1.083)
  waiting for transfers between devices: 258 us -> 323 us
  other arithmetic: 85 us -> 77.2 us
    all_to_all x4, waiting for transfers between devices: 51.3 us -> 111 us  [scatter_tokens(): received = lax.all_to_all(parts, 'tensor', 1, 1, tiled=True)]
    reduce_scatter x2, waiting for transfers between devices: 66.6 us -> 10.8 us  [on_device(): lax.psum_scatter(total.astype(jnp.bfloat16), ('dp', 'frame'), scatter_dim...]
    reduce_scatter x1, waiting for transfers between devices: 0.01 us -> 47.8 us  [hidden_half_back(): summed = lax.psum_scatter(blocks, 'dp', scatter_dimension=0, tiled=True)]
    all_gather x2, waiting for transfers between devices: 0.04 us -> 37.2 us  [gather_tokens(): return lax.all_gather(values, 'tensor', axis=1, tiled=True)]
    reduce_scatter x1, waiting for transfers between devices: 25.9 us -> 0.01 us  [hidden_half_back(): summed = lax.psum_scatter(summed, 'tensor', scatter_dimension=0, tiled=True)]
    another operation x8 -> x7, local copies, waits for them, and re-layouts: 11.5 us -> 20.5 us
    unnamed x165 -> x159, local copies, waits for them, and re-layouts: 23.1 us -> 18.6 us
  transfers between devices with their start and end apart: 36 -> 36, of which waited for: 12 -> 18; matrix products, arithmetic and copies ran while one was open for 30% -> 25% of each run, Pallas kernels for 15% -> 14%
where the time goes in v17:
time: 767 us; the launch traced here: 762 us
  waiting for transfers between devices  323 us (42%)
  Pallas kernels  107 us (14%)
  matrix products  101 us (13%)
  other arithmetic  77.2 us (10%)
  local copies, waits for them, and re-layouts  56.7 us (7%)
  blocking collectives  49.4 us (6%)
  starting transfers between devices  31.5 us (4%)
  between operations  15.4 us (2%)
    all_to_all x4, waiting for transfers between devices, scatter_tokens(): received = lax.all_to_all(parts, 'tensor', 1, 1, tiled=True)  111 us
    pallas_call x2, Pallas kernels, attention_backward(): pl.pallas_call(functools.partial(_backward_kernel, heads, HEAD_DIM ** (-0...  64.7 us
    reduce_scatter x1, waiting for transfers between devices, hidden_half_back(): summed = lax.psum_scatter(blocks, 'dp', scatter_dimension=0, tiled=True)  47.8 us
    all_gather x1, waiting for transfers between devices, hidden_half(): gathered = lax.all_gather(joined, 'tensor', axis=0, tiled=True)  42.3 us
    pallas_call x2, Pallas kernels, attention_forward(): pl.pallas_call(functools.partial(_forward_kernel, heads, HEAD_DIM ** (-0....  42.2 us
    all_gather x2, waiting for transfers between devices, on_device(): lax.all_gather(tokens[i:i + 1, 0], 'tensor', axis=1, tiled=True)  42.2 us
    all_gather x2, waiting for transfers between devices, gather_tokens(): return lax.all_gather(values, 'tensor', axis=1, tiled=True)  37.2 us
    all_gather x1, waiting for transfers between devices, on_device(): lax.all_gather(w, ('dp', 'frame'), axis=0, tiled=True)  23.8 us
  transfers between devices with their start and end apart: 36, of which 18 were waited for; matrix products, arithmetic and copies ran while one was open for 25% of the time, Pallas kernels for 14%

profile of v17, /device:TPU:0, one launch (start us, length us, event | category | flops | bytes accessed | tf_op | source)
XLA Modules:
  0.0 761.7 jit_solution(12183805857183981319)
XLA Ops:
  16.3 10.1 %all-gather.3 = s32[8,2,4]{2,1,0:T(2,128)S(1)} all-gather(s32[1,2,4]{2,1,0:T(2,128)S(1)} %bitcast.675), channel_id=1, replica_groups=mesh['dp'=4,'frame'=2,'tensor'=4] {'dp','frame'}, dimensions={0}, use_global_device_ids=true | all-gather | bytes 288 | tf_op jit(solution)/shard_map/modulation/all_gather | solution.py:168
  28.7 3.5 all-to-all-start
  32.2 12.7 %all_gather.37 = bf16[1024,256]{1,0:T(8,128)(2,1)S(1)} all-gather(bf16[128,256]{1,0:T(8,128)(2,1)S(1)} %copy-done.57), channel_id=1, replica_groups=mesh['dp'=4,'frame'=2,'tensor'=4] {'dp','frame'}, dimensions={0}, use_global_device_ids=true | all-gather | bytes 589824 | tf_op jit(solution)/shard_map/weights/all_gather | solution.py:226
  45.0 17.1 %all_gather.34 = f32[2,4,6,1024]{3,2,1,0:T(8,128)S(1)} all-gather(f32[2,4,6,256]{3,2,1,0:T(8,128)S(1)} %copy.349), channel_id=1, replica_groups=mesh['dp'=4,'frame'=2,'tensor'=4] {'tensor'}, dimensions={3}, use_global_device_ids=true | all-gather | bytes 245760 | tf_op jit(solution)/shard_map/modulation/all_gather | solution.py:181
  67.1 42.3 %all-gather.14.cloned.1.call-done = bf16[2048,512]{1,0:T(8,128)(2,1)} async-done(((bf16[512,512]{1,0:T(8,128)(2,1)}), bf16[2048,512]{1,0:T(8,128)(2,1)}) %all-gather.14.cloned.1.call-update) | async-done | bytes 2097168 | tf_op jit(solution)/shard_map/weights/all_gather | solution.py:202
  111.9 23.8 %all-gather.12.cloned.1.call-done = bf16[1024,3,256]{2,0,1:T(8,128)(2,1)} async-done(((bf16[128,3,256]{2,0,1:T(8,128)(2,1)}), bf16[1024,3,256]{2,0,1:T(8,128)(2,1)}) %all-gather.12.cloned.1.call-update) | async-done | bytes 1572880 | tf_op jit(solution)/shard_map/weights/all_gather | solution.py:226
  135.7 3.2 fusion.127
  141.2 42.2 %all-gather.22.cloned.1.call-done = bf16[1,1,1024,1024]{3,2,1,0:T(8,128)(2,1)} async-done(((bf16[1,1,256,1024]{3,2,1,0:T(8,128)(2,1)}), bf16[1,1,1024,1024]{3,2,1,0:T(8,128)(2,1)}) %all-gather.22.cloned.1.call-update) | async-done | bytes 2097168 | tf_op jit(solution)/shard_map/group_inputs/all_gather | solution.py:236
  188.5 21.1 %forward.3 = (bf16[1024,256]{1,0:T(8,128)(2,1)}, f32[1024,4]{1,0:T(8,128)}) custom-call(bf16[1024,256]{1,0:T(8,128)(2,1)} %get-tuple-element.168.q_ref, bf16[2048,256]{1,0:T(8,128)(2,1)} %maximum_bitcast_fusion.2.k_ref, bf16[2048,256]{1,0:T(8,128)(2,1)} %maximum_bitcast_fusion.3.v_ref), custom_call_target="tpu_custom_call" | custom-call | flops 2147483648 | bytes 3145728 | tf_op jit(solution)/shard_map/forward/pallas_call | solution.py:85
  209.6 3.2 convolution_convert_fusion
  212.8 4.7 all-to-all-start.2
  227.4 21.1 %forward.2 = (bf16[1024,256]{1,0:T(8,128)(2,1)}, f32[1024,4]{1,0:T(8,128)}) custom-call(bf16[1024,256]{1,0:T(8,128)(2,1)} %get-tuple-element.165.q_ref, bf16[2048,256]{1,0:T(8,128)(2,1)} %maximum_bitcast_fusion.k_ref, bf16[2048,256]{1,0:T(8,128)(2,1)} %maximum_bitcast_fusion.1.v_ref), custom_call_target="tpu_custom_call" | custom-call | flops 2147483648 | bytes 3145728 | tf_op jit(solution)/shard_map/forward/pallas_call | solution.py:85
  248.6 3.2 convolution_convert_fusion.1
  251.7 14.1 %all-to-all-done.2 = bf16[1,4,256,1024]{3,2,0,1:T(8,128)(2,1)} async-done(((bf16[1,4,256,1024]{3,2,0,1:T(8,128)(2,1)}), bf16[1,4,256,1024]{3,2,0,1:T(8,128)(2,1)}, u32[]{:S(2)}, u32[]{:S(2)}) %all-to-all-start.2) | async-done | bytes 2097184 | tf_op jit(solution)/shard_map/forward/all_to_all | solution.py:270
  265.9 4.5 all-to-all-start.1
  271.0 3.6 convert_element_type.262
  281.3 36.9 %all-to-all-done.1 = bf16[1,4,256,1024]{3,2,0,1:T(8,128)(2,1)} async-done(((bf16[1,4,256,1024]{3,2,0,1:T(8,128)(2,1)}), bf16[1,4,256,1024]{3,2,0,1:T(8,128)(2,1)}, u32[]{:S(2)}, u32[]{:S(2)}) %all-to-all-start.1) | async-done | bytes 2097184 | tf_op jit(solution)/shard_map/forward/all_to_all | solution.py:270
  333.6 3.9 fusion.242
  344.7 4.5 fusion.134
  356.4 4.4 fusion.62
  364.5 5.0 fusion.58
  369.5 4.6 fusion.137
  384.8 5.3 fusion.73
  390.2 4.8 add_bitcast_fusion
  395.0 10.2 %fusion.76 = f32[4,512,4,256]{3,1,2,0:T(8,128)} fusion(f32[512,4,512,1]{2,0,3,1:T(8,128)} %copy-done.74, f32[512,4,512,1]{2,0,3,1:T(8,128)S(1)} %copy-done.69, bf16[512,4,256]{2,1,0:T(4,128)(2,1)S(1)} %copy-done.43), kind=kOutput, calls=%fused_computation.109 | convolution fusion | flops 2168455168 | bytes 17825792 | tf_op jit(solution)/shard_map/backward_ffn/crad,crtj->atdj/dot_general | solution.py:323
  405.2 8.8 %add_bitcast_fusion.1 = bf16[4,4,256,512]{2,3,0,1:T(8,128)(2,1)} fusion(f32[4,512,4,256]{3,1,2,0:T(8,128)} %fusion.76, bf16[512,4,256,1]{0,2,1,3:T(8,128)(2,1)S(1)} %bitcast.629, f32[512,4,512,1]{2,0,3,1:T(8,128)S(1)} %copy-done.73, f32[512,4,512,1]{2,0,3,1:T(8,128)S(1)} %copy-done.71), kind=kOutput, calls=%fused_computation.2 | convolution fusion | flops 2172649472 | bytes 22020096 | tf_op jit(solution)/shard_map/backward_ffn/crad,crtj->atdj/dot_general | solution.py:323
  414.0 13.4 %all-gather.20.cloned.1.call-done = bf16[1,1024,1024]{2,1,0:T(8,128)(2,1)} async-done(((bf16[1,256,1024]{2,1,0:T(8,128)(2,1)}), bf16[1,1024,1024]{2,1,0:T(8,128)(2,1)}) %all-gather.20.cloned.1.call-update) | async-done | bytes 2097168 | tf_op jit(solution)/shard_map/backward_attention/all_gather | solution.py:264
  427.4 7.3 copy.305
  434.7 7.3 copy.304
  442.1 7.5 pad_maximum_fusion
  449.7 23.8 %all-gather.18.cloned.1.call-done = bf16[1,1024,1024]{2,1,0:T(8,128)(2,1)} async-done(((bf16[1,256,1024]{2,1,0:T(8,128)(2,1)}), bf16[1,1024,1024]{2,1,0:T(8,128)(2,1)}) %all-gather.18.cloned.1.call-update) | async-done | bytes 2097168 | tf_op jit(solution)/shard_map/backward_attention/all_gather | solution.py:264
  476.6 32.6 %backward_attention.2 = (f32[1024,256]{1,0:T(8,128)}, f32[2048,256]{1,0:T(8,128)}, f32[2048,256]{1,0:T(8,128)}) custom-call(bf16[1024,256]{1,0:T(8,128)(2,1)} %get-tuple-element.165.q_ref, bf16[2048,256]{1,0:T(8,128)(2,1)} %maximum_bitcast_fusion.k_ref, bf16[2048,256]{1,0:T(8,128)(2,1)} %maximum_bitcast_fusion.1.v_ref, bf16[1024,256]{1,0:T(8,128)(2,1)} %fusion.143.g_ref, ...), custom_call_target="tpu_custom_call" | custom-call | flops 5368709120 | bytes 8912896 | tf_op jit(solution)/shard_map/backward_attention/pallas_call | solution.py:118
  513.9 47.8 %reduce-scatter.5.cloned.1.call-done = bf16[4,512,512]{2,1,0:T(8,128)(2,1)} async-done(((bf16[16,512,512]{2,1,0:T(8,128)(2,1)}), bf16[4,512,512]{2,1,0:T(8,128)(2,1)}) %reduce-scatter.5.cloned.1.call-update) | async-done | bytes 2097168 | tf_op jit(solution)/shard_map/weight_grads/reduce_scatter | solution.py:211
  561.7 4.6 bitcast_convert_fusion.1
  566.3 4.8 all-to-all-start.3
  571.1 3.1 fusion.146.g_ref
  574.2 32.1 %backward_attention.3 = (f32[1024,256]{1,0:T(8,128)}, f32[2048,256]{1,0:T(8,128)}, f32[2048,256]{1,0:T(8,128)}) custom-call(bf16[1024,256]{1,0:T(8,128)(2,1)} %get-tuple-element.168.q_ref, bf16[2048,256]{1,0:T(8,128)(2,1)} %maximum_bitcast_fusion.2.k_ref, bf16[2048,256]{1,0:T(8,128)(2,1)} %maximum_bitcast_fusion.3.v_ref, bf16[1024,256]{1,0:T(8,128)(2,1)} %fusion.146.g_ref, ...), custom_call_target="tpu_custom_call" | custom-call | flops 5368709120 | bytes 8912896 | tf_op jit(solution)/shard_map/backward_attention/pallas_call | solution.py:118
  612.9 3.2 bitcast_convert_fusion
  616.1 35.5 %all-to-all-done.3 = bf16[1,4,256,1024]{3,2,0,1:T(8,128)(2,1)S(1)} async-done(((bf16[1,4,256,1024]{3,2,0,1:T(8,128)(2,1)}), bf16[1,4,256,1024]{3,2,0,1:T(8,128)(2,1)S(1)}, u32[]{:S(2)}, u32[]{:S(2)}) %all-to-all-start.3) | async-done | bytes 2097184 | tf_op jit(solution)/shard_map/backward_attention/all_to_all | solution.py:270
  651.6 4.6 all-to-all-start.4
  656.4 3.4 fusion.140
  659.8 5.6 fusion.175
  667.3 5.2 convolution_add_fusion
  680.0 24.8 %all-to-all-done.4 = bf16[1,4,256,1024]{3,2,0,1:T(8,128)(2,1)} async-done(((bf16[1,4,256,1024]{3,2,0,1:T(8,128)(2,1)}), bf16[1,4,256,1024]{3,2,0,1:T(8,128)(2,1)}, u32[]{:S(2)}, u32[]{:S(2)}) %all-to-all-start.4) | async-done | bytes 2097184 | tf_op jit(solution)/shard_map/backward_attention/all_to_all | solution.py:270
  710.7 3.4 reshape.1148
  714.1 3.9 all-to-all-start.5
  727.9 9.5 %all-gather.2 = f32[16,4,1,6,256]{4,1,0,3,2:T(4,128)S(1)} all-gather(f32[2,4,1,6,256]{4,1,0,3,2:T(4,128)S(1)} %bitcast.635), channel_id=4, replica_groups=mesh['dp'=4,'frame'=2,'tensor'=4] {'dp','frame'}, dimensions={0}, use_global_device_ids=true | all-gather | bytes 442368 | tf_op jit(solution)/shard_map/ada_grad/all_gather | solution.py:401
  742.4 10.8 %reduce-scatter.9.cloned.1.call-done = bf16[128,3,256]{2,0,1:T(8,128)(2,1)} async-done(((bf16[1024,3,256]{2,0,1:T(8,128)(2,1)}), bf16[128,3,256]{2,0,1:T(8,128)(2,1)}) %reduce-scatter.9.cloned.1.call-update) | async-done | bytes 196624 | tf_op jit(solution)/shard_map/weight_grads/reduce_scatter | solution.py:417
  (360 shorter events, 133.4 us)
Async XLA Ops:
  7.2 55.7 %all-gather.24.cloned.1.call-start = ((), (), s32[]{:S(2)}) async-start(), calls=%async_computation.20 | async-start | bytes 2621440 | tf_op jit(solution)/shard_map/group_inputs/all_gather | solution.py:236
  9.5 99.9 %all-gather.14.cloned.1.call-start = ((), (), s32[]{:S(2)}) async-start(), calls=%async_computation.11 | async-start | bytes 2621440 | tf_op jit(solution)/shard_map/weights/all_gather | solution.py:202
  10.8 1.8 collective-permute-start.4
  12.5 1.4 collective-permute-start.3
  15.0 120.7 %all-gather.12.cloned.1.call-start = ((), (), s32[]{:S(2)}) async-start(), calls=%async_computation.10 | async-start | bytes 1769472 | tf_op jit(solution)/shard_map/weights/all_gather | solution.py:226
  15.8 167.6 %all-gather.22.cloned.1.call-start = ((), (), s32[]{:S(2)}) async-start(), calls=%async_computation.19 | async-start | bytes 2621440 | tf_op jit(solution)/shard_map/group_inputs/all_gather | solution.py:236
  28.7 16.2 %all-to-all-start = ((f32[8,2,4,6,256]{4,2,3,1,0:T(4,128)}), f32[8,2,4,6,256]{4,2,3,1,0:T(4,128)S(1)}, u32[]{:S(2)}, u32[]{:S(2)}) async-start(f32[8,2,4,6,256]{4,2,3,1,0:T(4,128)} %fusion.180), calls=%async_computation | async-start | bytes 786432 | tf_op jit(solution)/shard_map/modulation/all_to_all | solution.py:179
  32.1 301.5 %all-gather.16.cloned.1.call-start = ((), (), s32[]{:S(2)}) async-start(), calls=%async_computation.12 | async-start | bytes 10485760 | tf_op jit(solution)/shard_map/weights/all_gather | solution.py:203
  44.9 203.6 %copy-start.16 = (bf16[1024,256]{1,0:T(8,128)(2,1)}, bf16[1024,256]{1,0:T(8,128)(2,1)S(1)}, u32[]{:S(2)}) copy-start(bf16[1024,256]{1,0:T(8,128)(2,1)S(1)} %all_gather.37) | copy-start | bytes 1572868
  111.9 27.1 %copy-start.30 = (bf16[1024,1024,1]{1,0,2:T(8,128)(2,1)}, bf16[1024,1024,1]{1,0,2:T(8,128)(2,1)S(1)}, u32[]{:S(2)}) copy-start(bf16[1024,1024,1]{1,0,2:T(8,128)(2,1)S(1)} %fusion.70) | copy-start | bytes 6291460
  140.0 45.3 %collective-permute-start.6 = (bf16[1,1024,256]{2,1,0:T(8,128)(2,1)}, bf16[1,1024,256]{2,1,0:T(8,128)(2,1)S(1)}, u32[]{:S(2)}, u32[]{:S(2)}) collective-permute-start(bf16[1,1024,256]{2,1,0:T(8,128)(2,1)} %get-tuple-element.167), channel_id=1, source_target_pairs={{0,4},{4,0},{1,5},{5,1},{2,6},{6,2},{3,7},{7,3},{8,12},{12,8},{9,1... | collective-permute-start | bytes 1572872 | tf_op jit(solution)/shard_map/forward/ppermute | solution.py:245
  141.0 46.5 %collective-permute-start.7 = (bf16[1,1024,256]{2,1,0:T(8,128)(2,1)S(1)}, bf16[1,1024,256]{2,1,0:T(8,128)(2,1)S(1)}, u32[]{:S(2)}, u32[]{:S(2)}) collective-permute-start(bf16[1,1024,256]{2,1,0:T(8,128)(2,1)S(1)} %get-tuple-element.166), channel_id=1, source_target_pairs={{0,4},{4,0},{1,5},{5,1},{2,6},{6,2},{3,7},{7,3},{8,12},{12,8},{9,1... | collective-permute-start | bytes 1572872 | tf_op jit(solution)/shard_map/forward/ppermute | solution.py:245
  212.8 53.0 %all-to-all-start.2 = ((bf16[1,4,256,1024]{3,2,0,1:T(8,128)(2,1)}), bf16[1,4,256,1024]{3,2,0,1:T(8,128)(2,1)}, u32[]{:S(2)}, u32[]{:S(2)}) async-start(bf16[1,4,256,1024]{3,2,0,1:T(8,128)(2,1)} %bitcast.615), calls=%async_computation.2 | async-start | bytes 4194304 | tf_op jit(solution)/shard_map/forward/all_to_all | solution.py:270
  223.4 1.9 collective-permute-start
  223.4 2.9 collective-permute-start.1
  265.9 52.3 %all-to-all-start.1 = ((bf16[1,4,256,1024]{3,2,0,1:T(8,128)(2,1)}), bf16[1,4,256,1024]{3,2,0,1:T(8,128)(2,1)}, u32[]{:S(2)}, u32[]{:S(2)}) async-start(bf16[1,4,256,1024]{3,2,0,1:T(8,128)(2,1)} %bitcast.23), calls=%async_computation.1 | async-start | bytes 4194304 | tf_op jit(solution)/shard_map/forward/all_to_all | solution.py:270
  270.3 157.1 %all-gather.20.cloned.1.call-start = ((), (), s32[]{:S(2)}) async-start(), calls=%async_computation.14 | async-start | bytes 2621440 | tf_op jit(solution)/shard_map/backward_attention/all_gather | solution.py:264
  271.0 49.2 %copy-start.2 = (f32[2,1,256,1024]{3,2,1,0:T(8,128)}, f32[2,1,256,1024]{3,2,1,0:T(8,128)S(1)}, u32[]{:S(2)}) copy-start(f32[2,1,256,1024]{3,2,1,0:T(8,128)S(1)} %convert_element_type.236) | copy-start | bytes 6291460
  274.8 48.3 %copy-start.58 = (f32[256]{0:T(256)}, f32[256]{0:T(256)S(1)}, u32[]{:S(2)}) copy-start(f32[256]{0:T(256)S(1)} %get-tuple-element.199) | copy-start | bytes 3076
  274.8 48.3 %copy-start.60 = (f32[256]{0:T(256)}, f32[256]{0:T(256)S(1)}, u32[]{:S(2)}) copy-start(f32[256]{0:T(256)S(1)} %get-tuple-element.200) | copy-start | bytes 3076
  277.1 48.5 %collective-permute-start.10 = (bf16[1,256,1024]{2,1,0:T(8,128)(2,1)}, bf16[1,256,1024]{2,1,0:T(8,128)(2,1)}, u32[]{:S(2)}, u32[]{:S(2)}) collective-permute-start(bf16[1,256,1024]{2,1,0:T(8,128)(2,1)} %multiply_convert_fusion.3), channel_id=1, source_target_pairs={{0,4},{4,0},{1,5},{5,1},{2,6},{6,2},{3,7},{7,3},{8,12},{12,8},{9,1... | collective-permute-start | bytes 1572872 | tf_op jit(solution)/shard_map/backward_ffn/ppermute | solution.py:245
  324.4 4.0 collective-permute-start.2
  325.0 5.9 collective-permute-start.8
  349.3 3.3 collective-permute-start.11
  352.0 2.1 collective-permute-start.5
  356.0 4.7 collective-permute-start.14
  374.1 3.3 collective-permute-start.15
  377.0 2.0 collective-permute-start.9
  382.6 90.9 %all-gather.18.cloned.1.call-start = ((), (), s32[]{:S(2)}) async-start(), calls=%async_computation.13 | async-start | bytes 2621440 | tf_op jit(solution)/shard_map/backward_attention/all_gather | solution.py:264
  384.8 176.9 %reduce-scatter.5.cloned.1.call-start = ((), (), s32[]{:S(2)}) async-start(), calls=%async_computation.15 | async-start | bytes 10485760 | tf_op jit(solution)/shard_map/weight_grads/reduce_scatter | solution.py:211
  449.6 215.9 %reduce-scatter.7.cloned.1.call-start = ((), (), s32[]{:S(2)}) async-start(), calls=%async_computation.16 | async-start | bytes 2621440 | tf_op jit(solution)/shard_map/weight_grads/reduce_scatter | solution.py:212
  511.0 2.0 collective-permute-start.13
  511.6 2.1 collective-permute-start.12
  513.2 53.1 %copy-start.45 = (bf16[1024,1,256]{2,0,1:T(8,128)(2,1)}, bf16[1024,1,256]{2,0,1:T(8,128)(2,1)S(1)}, u32[]{:S(2)}) copy-start(bf16[1024,1,256]{2,0,1:T(8,128)(2,1)S(1)} %fusion.177) | copy-start | bytes 1572868
  513.9 52.4 %copy-start.47 = (bf16[1024,1,256]{2,0,1:T(8,128)(2,1)}, bf16[1024,1,256]{2,0,1:T(8,128)(2,1)S(1)}, u32[]{:S(2)}) copy-start(bf16[1024,1,256]{2,0,1:T(8,128)(2,1)S(1)} %fusion.176) | copy-start | bytes 1572868
  566.3 85.2 %all-to-all-start.3 = ((bf16[1,4,256,1024]{3,2,0,1:T(8,128)(2,1)}), bf16[1,4,256,1024]{3,2,0,1:T(8,128)(2,1)S(1)}, u32[]{:S(2)}, u32[]{:S(2)}) async-start(bf16[1,4,256,1024]{3,2,0,1:T(8,128)(2,1)} %bitcast.623), calls=%async_computation.3 | async-start | bytes 4194304 | tf_op jit(solution)/shard_map/backward_attention/all_to_all | solution.py:270
  608.2 2.9 collective-permute-start.17
  608.7 2.6 collective-permute-start.16
  651.6 53.3 %all-to-all-start.4 = ((bf16[1,4,256,1024]{3,2,0,1:T(8,128)(2,1)}), bf16[1,4,256,1024]{3,2,0,1:T(8,128)(2,1)}, u32[]{:S(2)}, u32[]{:S(2)}) async-start(bf16[1,4,256,1024]{3,2,0,1:T(8,128)(2,1)} %bitcast.622), calls=%async_computation.4 | async-start | bytes 4194304 | tf_op jit(solution)/shard_map/backward_attention/all_to_all | solution.py:270
  656.1 84.8 %reduce-scatter.11.cloned.1.call-start = ((), (), s32[]{:S(2)}) async-start(), calls=%async_computation.18 | async-start | bytes 589824 | tf_op jit(solution)/shard_map/weight_grads/reduce_scatter | solution.py:417
  667.3 5.2 collective-permute-start.18
  675.8 77.4 %reduce-scatter.9.cloned.1.call-start = ((), (), s32[]{:S(2)}) async-start(), calls=%async_computation.17 | async-start | bytes 1769472 | tf_op jit(solution)/shard_map/weight_grads/reduce_scatter | solution.py:417
  677.0 31.6 %copy-start.3 = (f32[2,1,256,1024]{3,2,1,0:T(8,128)S(1)}, f32[2,1,256,1024]{3,2,1,0:T(8,128)}, u32[]{:S(2)}) copy-start(f32[2,1,256,1024]{3,2,1,0:T(8,128)} %copy-done.2) | copy-start | bytes 6291460
  677.0 31.6 %copy-start.55 = (f32[1,1,1,1024]{3,1,2,0:T(1,128)S(1)}, f32[1,1,1,1024]{3,1,2,0:T(1,128)}, u32[]{:S(2)}) copy-start(f32[1,1,1,1024]{3,1,2,0:T(1,128)} %get-tuple-element.192) | copy-start | bytes 12292
  677.0 31.6 %copy-start.59 = (f32[256]{0:T(256)S(1)}, f32[256]{0:T(256)}, u32[]{:S(2)}) copy-start(f32[256]{0:T(256)} %copy-done.58) | copy-start | bytes 3076
  677.0 31.6 %copy-start.61 = (f32[256]{0:T(256)S(1)}, f32[256]{0:T(256)}, u32[]{:S(2)}) copy-start(f32[256]{0:T(256)} %copy-done.60) | copy-start | bytes 3076
  714.1 9.7 %all-to-all-start.5 = ((f32[4,1,3072]{2,1,0:T(1,128)}), f32[4,1,3072]{2,1,0:T(1,128)}, u32[]{:S(2)}, u32[]{:S(2)}) async-start(f32[4,1,3072]{2,1,0:T(1,128)} %reshape.1148), calls=%async_computation.9 | async-start | bytes 98304 | tf_op jit(solution)/shard_map/ada_grad/all_to_all | solution.py:398
  722.1 32.8 %copy-start.1 = (bf16[128,6,256]{2,0,1:T(8,128)(2,1)S(1)}, bf16[128,6,256]{2,0,1:T(8,128)(2,1)}, u32[]{:S(2)}) copy-start(bf16[128,6,256]{2,0,1:T(8,128)(2,1)} %param.19) | copy-start | bytes 1179652
  (63 other events, 373.5 us)
Sparse Core Ops, SparseCore 0:
  10.1 52.5 all-gather.23
  64.9 44.4 all-gather.13
  111.3 24.3 all-gather.11
  137.7 45.6 all-gather.21
  185.1 86.2 all-gather.15
  382.7 44.7 all-gather.19
  429.0 44.4 all-gather.17
  476.6 85.1 reduce-scatter.4
  564.0 74.5 reduce-scatter.6
  675.9 35.5 reduce-scatter.10
  714.8 38.3 reduce-scatter.8

commit v18 on v16

--- a/solution.py
+++ b/solution.py
@@ -76,10 +76,12 @@
         dk_ref[:, cols] += _tn(grad_scores, q) * scaling
 
 
-def attention_forward(queries, keys, values, block_rows=256):
+def attention_forward(queries, keys, values, block_rows=None):
     rows, width = queries.shape
     length = keys.shape[0]
     heads = width // HEAD_DIM
+    if block_rows is None:
+        block_rows = 512 if length <= 2048 else 256
     block_rows = min(block_rows, rows)
     flops = 4 * rows * length * width
     return pl.pallas_call(
@@ -109,10 +111,12 @@
     )(queries, keys, values)
 
 
-def attention_backward(queries, keys, values, grad_out, lse, block_rows=256):
+def attention_backward(queries, keys, values, grad_out, lse, block_rows=None):
     rows, width = queries.shape
     length = keys.shape[0]
     heads = width // HEAD_DIM
+    if block_rows is None:
+        block_rows = 512 if length <= 2048 else 256
     block_rows = min(block_rows, rows)
     flops = 10 * rows * length * width
     return pl.pallas_call(

time: 708 us -> 710 us (level)
  transfers between devices with their start and end apart: 36 -> 36, of which waited for: 12 -> 13; matrix products, arithmetic and copies ran while one was open for 30% -> 30% of each run, Pallas kernels for 15% -> 14%
where the time goes in v18:
time: 710 us; the launch traced here: 701 us
  waiting for transfers between devices  263 us (37%)
  Pallas kernels  101 us (14%)
  matrix products  97.6 us (14%)
  other arithmetic  85.2 us (12%)
  local copies, waits for them, and re-layouts  57.8 us (8%)
  blocking collectives  49.2 us (7%)
  starting transfers between devices  31.2 us (4%)
  between operations  15.8 us (2%)
    reduce_scatter x2, waiting for transfers between devices, on_device(): lax.psum_scatter(total.astype(jnp.bfloat16), ('dp', 'frame'), scatter_dim...  70.5 us
    pallas_call x2, Pallas kernels, attention_backward(): pl.pallas_call(functools.partial(_backward_kernel, heads, HEAD_DIM ** (-0...  61.3 us
    all_to_all x4, waiting for transfers between devices, scatter_tokens(): received = lax.all_to_all(parts, 'tensor', 1, 1, tiled=True)  52 us
    all_gather x1, waiting for transfers between devices, hidden_half(): gathered = lax.all_gather(joined, 'tensor', axis=0, tiled=True)  42.4 us
    all_gather x2, waiting for transfers between devices, on_device(): lax.all_gather(tokens[i:i + 1, 0], 'tensor', axis=1, tiled=True)  42.2 us
    pallas_call x2, Pallas kernels, attention_forward(): pl.pallas_call(functools.partial(_forward_kernel, heads, HEAD_DIM ** (-0....  40.1 us
    reduce_scatter x1, waiting for transfers between devices, hidden_half_back(): summed = lax.psum_scatter(summed, 'tensor', scatter_dimension=0, tiled=True)  25.8 us
    all_gather x1, waiting for transfers between devices, on_device(): lax.all_gather(w, ('dp', 'frame'), axis=0, tiled=True)  23.8 us
  transfers between devices with their start and end apart: 36, of which 13 were waited for; matrix products, arithmetic and copies ran while one was open for 30% of the time, Pallas kernels for 14%

profile of v18, /device:TPU:0, one launch (start us, length us, event | category | flops | bytes accessed | tf_op | source)
XLA Modules:
  0.0 701.3 jit_solution(12635785780978043203)
XLA Ops:
  16.3 10.1 %all-gather.3 = s32[8,2,4]{2,1,0:T(2,128)S(1)} all-gather(s32[1,2,4]{2,1,0:T(2,128)S(1)} %bitcast.678), channel_id=1, replica_groups=mesh['dp'=4,'frame'=2,'tensor'=4] {'dp','frame'}, dimensions={0}, use_global_device_ids=true | all-gather | bytes 288 | tf_op jit(solution)/shard_map/modulation/all_gather | solution.py:172
  28.7 3.5 all-to-all-start
  32.2 12.7 %all_gather.37 = bf16[1024,256]{1,0:T(8,128)(2,1)S(1)} all-gather(bf16[128,256]{1,0:T(8,128)(2,1)S(1)} %copy-done.58), channel_id=1, replica_groups=mesh['dp'=4,'frame'=2,'tensor'=4] {'dp','frame'}, dimensions={0}, use_global_device_ids=true | all-gather | bytes 589824 | tf_op jit(solution)/shard_map/weights/all_gather | solution.py:230
  45.0 16.9 %all_gather.34 = f32[2,4,6,1024]{3,2,1,0:T(8,128)S(1)} all-gather(f32[2,4,6,256]{3,2,1,0:T(8,128)S(1)} %copy.301), channel_id=1, replica_groups=mesh['dp'=4,'frame'=2,'tensor'=4] {'tensor'}, dimensions={3}, use_global_device_ids=true | all-gather | bytes 245760 | tf_op jit(solution)/shard_map/modulation/all_gather | solution.py:185
  67.0 42.4 %all-gather.14.cloned.1.call-done = bf16[2048,512]{1,0:T(8,128)(2,1)} async-done(((bf16[512,512]{1,0:T(8,128)(2,1)}), bf16[2048,512]{1,0:T(8,128)(2,1)}) %all-gather.14.cloned.1.call-update) | async-done | bytes 2097168 | tf_op jit(solution)/shard_map/weights/all_gather | solution.py:206
  111.9 23.8 %all-gather.12.cloned.1.call-done = bf16[1024,3,256]{2,0,1:T(8,128)(2,1)} async-done(((bf16[128,3,256]{2,0,1:T(8,128)(2,1)}), bf16[1024,3,256]{2,0,1:T(8,128)(2,1)}) %all-gather.12.cloned.1.call-update) | async-done | bytes 1572880 | tf_op jit(solution)/shard_map/weights/all_gather | solution.py:230
  135.7 3.2 fusion.129
  141.2 42.2 %all-gather.22.cloned.1.call-done = bf16[1,1,1024,1024]{3,2,1,0:T(8,128)(2,1)} async-done(((bf16[1,1,256,1024]{3,2,1,0:T(8,128)(2,1)}), bf16[1,1,1024,1024]{3,2,1,0:T(8,128)(2,1)}) %all-gather.22.cloned.1.call-update) | async-done | bytes 2097168 | tf_op jit(solution)/shard_map/group_inputs/all_gather | solution.py:240
  188.5 20.0 %forward.3 = (bf16[1024,256]{1,0:T(8,128)(2,1)}, f32[1024,4]{1,0:T(8,128)}) custom-call(bf16[1024,256]{1,0:T(8,128)(2,1)} %get-tuple-element.156.q_ref, bf16[2048,256]{1,0:T(8,128)(2,1)} %maximum_bitcast_fusion.2.k_ref, bf16[2048,256]{1,0:T(8,128)(2,1)} %maximum_bitcast_fusion.3.v_ref), custom_call_target="tpu_custom_call" | custom-call | flops 2147483648 | bytes 3145728 | tf_op jit(solution)/shard_map/forward/pallas_call | solution.py:87
  208.4 3.3 convolution_convert_fusion
  211.7 4.4 all-to-all-start.2
  226.1 20.2 %forward.2 = (bf16[1024,256]{1,0:T(8,128)(2,1)}, f32[1024,4]{1,0:T(8,128)}) custom-call(bf16[1024,256]{1,0:T(8,128)(2,1)} %get-tuple-element.153.q_ref, bf16[2048,256]{1,0:T(8,128)(2,1)} %maximum_bitcast_fusion.k_ref, bf16[2048,256]{1,0:T(8,128)(2,1)} %maximum_bitcast_fusion.1.v_ref), custom_call_target="tpu_custom_call" | custom-call | flops 2147483648 | bytes 3145728 | tf_op jit(solution)/shard_map/forward/pallas_call | solution.py:87
  246.3 3.2 convolution_convert_fusion.1
  249.4 15.0 %all-to-all-done.2 = bf16[1,4,256,1024]{3,2,0,1:T(8,128)(2,1)} async-done(((bf16[1,4,256,1024]{3,2,0,1:T(8,128)(2,1)}), bf16[1,4,256,1024]{3,2,0,1:T(8,128)(2,1)}, u32[]{:S(2)}, u32[]{:S(2)}) %all-to-all-start.2) | async-done | bytes 2097184 | tf_op jit(solution)/shard_map/forward/all_to_all | solution.py:274
  264.5 4.4 all-to-all-start.1
  269.4 3.6 convert_element_type.262
  276.7 3.0 convert_reduce_fusion.6
  279.7 37.0 %all-to-all-done.1 = bf16[1,4,256,1024]{3,2,0,1:T(8,128)(2,1)} async-done(((bf16[1,4,256,1024]{3,2,0,1:T(8,128)(2,1)}), bf16[1,4,256,1024]{3,2,0,1:T(8,128)(2,1)}, u32[]{:S(2)}, u32[]{:S(2)}) %all-to-all-start.1) | async-done | bytes 2097184 | tf_op jit(solution)/shard_map/forward/all_to_all | solution.py:274
  318.9 2.8 multiply_reduce_fusion.10
  337.9 3.9 fusion.244
  353.2 4.7 fusion.136
  371.6 2.7 reshape.939
  374.3 7.1 %fusion.60 = f32[512,4,512,1]{2,0,3,1:T(8,128)} fusion(bf16[512,4,256]{2,1,0:T(4,128)(2,1)} %reshape.939, bf16[4,4,1,256,512]{4,3,2,1,0:T(8,128)(2,1)} %copy-done.10), kind=kOutput, calls=%fused_computation.91 | convolution fusion | flops 2147483648 | bytes 9437184 | tf_op jit(solution)/shard_map/backward_ffn/crad,atdj->crtj/dot_general | solution.py:319
  383.7 9.0 %fusion.139 = bf16[1,512,1024]{2,1,0:T(8,128)(2,1)S(1)} fusion(bf16[1024,512,4]{1,0,2:T(8,128)(2,1)} %bitcast.619, f32[512,4,512,1]{2,0,3,1:T(8,128)} %fusion.60, f32[512,4,512,1]{2,0,3,1:T(8,128)} %copy-done.70), kind=kOutput, calls=%fused_computation.164 | convolution fusion | flops 2168979456 | bytes 13631488 | tf_op jit(solution)/shard_map/backward_ffn/crtj,atdj->crad/dot_general | solution.py:330
  392.9 6.1 fusion.75
  404.4 8.1 %fusion.43 = bf16[4,4,256,512]{3,2,0,1:T(8,128)(2,1)S(1)} fusion(f32[4,512,4,256]{1,3,2,0:T(8,128)} %fusion.75, f32[512,4,512,1]{2,0,3,1:T(8,128)} %copy-done.73, bf16[512,4,256]{0,2,1:T(8,128)(2,1)} %copy.266), kind=kOutput, calls=%fused_computation.62 | convolution fusion | flops 2161115136 | bytes 17825792 | tf_op jit(solution)/shard_map/backward_ffn/crad,crtj->atdj/dot_general | solution.py:322
  416.5 6.1 fusion.78
  422.6 6.8 fusion.42
  431.7 7.6 %pad_maximum_fusion = bf16[16,512,512]{2,1,0:T(8,128)(2,1)} fusion(bf16[16,256,512]{2,1,0:T(8,128)(2,1)} %bitcast.610, bf16[16,256,512]{2,1,0:T(8,128)(2,1)} %bitcast.615), kind=kLoop, calls=%fused_computation | loop fusion | flops 16777216 | bytes 16777216 | tf_op jit(solution)/shard_map/weight_grads/concatenate | solution.py:213
  440.3 3.1 fusion.145.g_ref
  443.4 30.7 %backward_attention.2 = (f32[1024,256]{1,0:T(8,128)}, f32[2048,256]{1,0:T(8,128)}, f32[2048,256]{1,0:T(8,128)}) custom-call(bf16[1024,256]{1,0:T(8,128)(2,1)} %get-tuple-element.153.q_ref, bf16[2048,256]{1,0:T(8,128)(2,1)} %maximum_bitcast_fusion.k_ref, bf16[2048,256]{1,0:T(8,128)(2,1)} %maximum_bitcast_fusion.1.v_ref, bf16[1024,256]{1,0:T(8,128)(2,1)} %fusion.145.g_ref, ...), custom_call_target="tpu_custom_call" | custom-call | flops 5368709120 | bytes 8912896 | tf_op jit(solution)/shard_map/backward_attention/pallas_call | solution.py:122
  479.1 3.1 bitcast_convert_fusion.1
  482.2 3.6 all-to-all-start.3
  485.9 3.3 fusion.148.g_ref
  489.2 30.6 %backward_attention.3 = (f32[1024,256]{1,0:T(8,128)}, f32[2048,256]{1,0:T(8,128)}, f32[2048,256]{1,0:T(8,128)}) custom-call(bf16[1024,256]{1,0:T(8,128)(2,1)} %get-tuple-element.156.q_ref, bf16[2048,256]{1,0:T(8,128)(2,1)} %maximum_bitcast_fusion.2.k_ref, bf16[2048,256]{1,0:T(8,128)(2,1)} %maximum_bitcast_fusion.3.v_ref, bf16[1024,256]{1,0:T(8,128)(2,1)} %fusion.148.g_ref, ...), custom_call_target="tpu_custom_call" | custom-call | flops 5368709120 | bytes 8912896 | tf_op jit(solution)/shard_map/backward_attention/pallas_call | solution.py:122
  533.2 3.9 fusion.177
  537.1 3.2 add_convert_fusion.2
  540.4 4.7 bitcast_convert_fusion
  545.2 5.3 all-to-all-start.4
  552.3 33.3 %reduce-scatter.7.cloned.1.call-done = bf16[128,256]{1,0:T(8,128)(2,1)} async-done(((bf16[1024,256]{1,0:T(8,128)(2,1)}), bf16[128,256]{1,0:T(8,128)(2,1)}) %reduce-scatter.7.cloned.1.call-update) | async-done | bytes 65552 | tf_op jit(solution)/shard_map/weight_grads/reduce_scatter | solution.py:416
  587.2 2.7 convert_reduce_fusion.4
  590.0 37.2 %reduce-scatter.5.cloned.1.call-done = bf16[128,3,256]{2,0,1:T(8,128)(2,1)} async-done(((bf16[1024,3,256]{2,0,1:T(8,128)(2,1)}), bf16[128,3,256]{2,0,1:T(8,128)(2,1)}) %reduce-scatter.5.cloned.1.call-update) | async-done | bytes 196624 | tf_op jit(solution)/shard_map/weight_grads/reduce_scatter | solution.py:416
  628.9 2.7 convert_reduce_fusion.2
  635.0 3.5 reshape.1148
  638.5 4.6 all-to-all-start.5
  644.5 3.5 add_convert_fusion.6
  648.1 25.8 %reduce-scatter.11.cloned.1.call-done = bf16[1,512,512]{2,1,0:T(8,128)(2,1)} async-done(((bf16[4,512,512]{2,1,0:T(8,128)(2,1)}), bf16[1,512,512]{2,1,0:T(8,128)(2,1)}) %reduce-scatter.11.cloned.1.call-update) | async-done | bytes 524304 | tf_op jit(solution)/shard_map/weight_grads/reduce_scatter | solution.py:216
  680.7 9.5 %all-gather.2 = f32[16,4,1,6,256]{4,1,0,3,2:T(4,128)S(1)} all-gather(f32[2,4,1,6,256]{4,1,0,3,2:T(4,128)S(1)} %bitcast.638), channel_id=4, replica_groups=mesh['dp'=4,'frame'=2,'tensor'=4] {'dp','frame'}, dimensions={0}, use_global_device_ids=true | all-gather | bytes 442368 | tf_op jit(solution)/shard_map/ada_grad/all_gather | solution.py:405
  (369 shorter events, 137.3 us)
Async XLA Ops:
  7.2 55.6 %all-gather.24.cloned.1.call-start = ((), (), s32[]{:S(2)}) async-start(), calls=%async_computation.20 | async-start | bytes 2621440 | tf_op jit(solution)/shard_map/group_inputs/all_gather | solution.py:240
  9.5 99.9 %all-gather.14.cloned.1.call-start = ((), (), s32[]{:S(2)}) async-start(), calls=%async_computation.11 | async-start | bytes 2621440 | tf_op jit(solution)/shard_map/weights/all_gather | solution.py:206
  10.8 1.8 collective-permute-start.4
  12.5 1.4 collective-permute-start.3
  15.0 120.7 %all-gather.12.cloned.1.call-start = ((), (), s32[]{:S(2)}) async-start(), calls=%async_computation.10 | async-start | bytes 1769472 | tf_op jit(solution)/shard_map/weights/all_gather | solution.py:230
  15.8 167.6 %all-gather.22.cloned.1.call-start = ((), (), s32[]{:S(2)}) async-start(), calls=%async_computation.19 | async-start | bytes 2621440 | tf_op jit(solution)/shard_map/group_inputs/all_gather | solution.py:240
  28.7 16.2 %all-to-all-start = ((f32[8,2,4,6,256]{4,2,3,1,0:T(4,128)}), f32[8,2,4,6,256]{4,2,3,1,0:T(4,128)S(1)}, u32[]{:S(2)}, u32[]{:S(2)}) async-start(f32[8,2,4,6,256]{4,2,3,1,0:T(4,128)} %fusion.182), calls=%async_computation | async-start | bytes 786432 | tf_op jit(solution)/shard_map/modulation/all_to_all | solution.py:183
  32.1 305.7 %all-gather.16.cloned.1.call-start = ((), (), s32[]{:S(2)}) async-start(), calls=%async_computation.12 | async-start | bytes 10485760 | tf_op jit(solution)/shard_map/weights/all_gather | solution.py:207
  44.9 201.4 %copy-start.17 = (bf16[1024,256]{1,0:T(8,128)(2,1)}, bf16[1024,256]{1,0:T(8,128)(2,1)S(1)}, u32[]{:S(2)}) copy-start(bf16[1024,256]{1,0:T(8,128)(2,1)S(1)} %all_gather.37) | copy-start | bytes 1572868
  111.9 27.1 %copy-start.29 = (bf16[1024,1024,1]{1,0,2:T(8,128)(2,1)}, bf16[1024,1024,1]{1,0,2:T(8,128)(2,1)S(1)}, u32[]{:S(2)}) copy-start(bf16[1024,1024,1]{1,0,2:T(8,128)(2,1)S(1)} %fusion.72) | copy-start | bytes 6291460
  140.0 45.4 %collective-permute-start.6 = (bf16[1,1024,256]{2,1,0:T(8,128)(2,1)}, bf16[1,1024,256]{2,1,0:T(8,128)(2,1)S(1)}, u32[]{:S(2)}, u32[]{:S(2)}) collective-permute-start(bf16[1,1024,256]{2,1,0:T(8,128)(2,1)} %get-tuple-element.155), channel_id=1, source_target_pairs={{0,4},{4,0},{1,5},{5,1},{2,6},{6,2},{3,7},{7,3},{8,12},{12,8},{9,1... | collective-permute-start | bytes 1572872 | tf_op jit(solution)/shard_map/forward/ppermute | solution.py:249
  141.0 46.5 %collective-permute-start.7 = (bf16[1,1024,256]{2,1,0:T(8,128)(2,1)S(1)}, bf16[1,1024,256]{2,1,0:T(8,128)(2,1)S(1)}, u32[]{:S(2)}, u32[]{:S(2)}) collective-permute-start(bf16[1,1024,256]{2,1,0:T(8,128)(2,1)S(1)} %get-tuple-element.154), channel_id=1, source_target_pairs={{0,4},{4,0},{1,5},{5,1},{2,6},{6,2},{3,7},{7,3},{8,12},{12,8},{9,1... | collective-permute-start | bytes 1572872 | tf_op jit(solution)/shard_map/forward/ppermute | solution.py:249
  211.7 52.8 %all-to-all-start.2 = ((bf16[1,4,256,1024]{3,2,0,1:T(8,128)(2,1)}), bf16[1,4,256,1024]{3,2,0,1:T(8,128)(2,1)}, u32[]{:S(2)}, u32[]{:S(2)}) async-start(bf16[1,4,256,1024]{3,2,0,1:T(8,128)(2,1)} %bitcast.617), calls=%async_computation.2 | async-start | bytes 4194304 | tf_op jit(solution)/shard_map/forward/all_to_all | solution.py:274
  222.1 1.9 collective-permute-start
  222.1 3.0 collective-permute-start.1
  246.3 22.9 %copy-start.20 = (bf16[2,1,256,1024]{3,2,1,0:T(8,128)(2,1)S(1)}, bf16[2,1,256,1024]{3,2,1,0:T(8,128)(2,1)}, u32[]{:S(2)}) copy-start(bf16[2,1,256,1024]{3,2,1,0:T(8,128)(2,1)} %param.12) | copy-start | bytes 3145732
  264.5 52.3 %all-to-all-start.1 = ((bf16[1,4,256,1024]{3,2,0,1:T(8,128)(2,1)}), bf16[1,4,256,1024]{3,2,0,1:T(8,128)(2,1)}, u32[]{:S(2)}, u32[]{:S(2)}) async-start(bf16[1,4,256,1024]{3,2,0,1:T(8,128)(2,1)} %bitcast.23), calls=%async_computation.1 | async-start | bytes 4194304 | tf_op jit(solution)/shard_map/forward/all_to_all | solution.py:274
  268.9 170.4 %all-gather.18.cloned.1.call-start = ((), (), s32[]{:S(2)}) async-start(), calls=%async_computation.13 | async-start | bytes 2621440 | tf_op jit(solution)/shard_map/backward_attention/all_gather | solution.py:268
  269.4 49.5 %copy-start.2 = (f32[2,1,256,1024]{3,2,1,0:T(8,128)}, f32[2,1,256,1024]{3,2,1,0:T(8,128)S(1)}, u32[]{:S(2)}) copy-start(f32[2,1,256,1024]{3,2,1,0:T(8,128)S(1)} %convert_element_type.236) | copy-start | bytes 6291460
  273.2 48.4 %copy-start.59 = (f32[256]{0:T(256)}, f32[256]{0:T(256)S(1)}, u32[]{:S(2)}) copy-start(f32[256]{0:T(256)S(1)} %get-tuple-element.187) | copy-start | bytes 3076
  273.2 48.4 %copy-start.61 = (f32[256]{0:T(256)}, f32[256]{0:T(256)S(1)}, u32[]{:S(2)}) copy-start(f32[256]{0:T(256)S(1)} %get-tuple-element.188) | copy-start | bytes 3076
  275.5 50.1 %collective-permute-start.10 = (bf16[1,256,1024]{2,1,0:T(8,128)(2,1)}, bf16[1,256,1024]{2,1,0:T(8,128)(2,1)}, u32[]{:S(2)}, u32[]{:S(2)}) collective-permute-start(bf16[1,256,1024]{2,1,0:T(8,128)(2,1)} %multiply_convert_fusion.3), channel_id=1, source_target_pairs={{0,4},{4,0},{1,5},{5,1},{2,6},{6,2},{3,7},{7,3},{8,12},{12,8},{9,1... | collective-permute-start | bytes 1572872 | tf_op jit(solution)/shard_map/backward_ffn/ppermute | solution.py:249
  323.7 5.7 collective-permute-start.2
  325.0 7.0 collective-permute-start.8
  353.1 8.4 %collective-permute-start.5 = (bf16[1,256,1024]{2,1,0:T(8,128)(2,1)S(1)}, bf16[1,256,1024]{2,1,0:T(8,128)(2,1)S(1)}, u32[]{:S(2)}, u32[]{:S(2)}) collective-permute-start(bf16[1,256,1024]{2,1,0:T(8,128)(2,1)S(1)} %slice.287), channel_id=1, source_target_pairs={{0,4},{4,0},{1,5},{5,1},{2,6},{6,2},{3,7},{7,3},{8,12},{12,8},{9,1... | collective-permute-start | bytes 1572872 | tf_op jit(solution)/shard_map/forward/ppermute | solution.py:259
  358.1 2.9 collective-permute-start.11
  363.4 5.9 collective-permute-start.14
  367.9 31.7 %collective-permute-start.9 = (bf16[1,256,1024]{2,1,0:T(8,128)(2,1)}, bf16[1,256,1024]{2,1,0:T(8,128)(2,1)}, u32[]{:S(2)}, u32[]{:S(2)}) collective-permute-start(bf16[1,256,1024]{2,1,0:T(8,128)(2,1)} %slice.300), channel_id=1, source_target_pairs={{0,4},{4,0},{1,5},{5,1},{2,6},{6,2},{3,7},{7,3},{8,12},{12,8},{9,1... | collective-permute-start | bytes 1572872 | tf_op jit(solution)/shard_map/forward/ppermute | solution.py:259
  369.3 116.7 %all-gather.20.cloned.1.call-start = ((), (), s32[]{:S(2)}) async-start(), calls=%async_computation.14 | async-start | bytes 2621440 | tf_op jit(solution)/shard_map/backward_attention/all_gather | solution.py:268
  392.8 6.2 collective-permute-start.15
  404.1 146.3 %reduce-scatter.9.cloned.1.call-start = ((), (), s32[]{:S(2)}) async-start(), calls=%async_computation.17 | async-start | bytes 10485760 | tf_op jit(solution)/shard_map/weight_grads/reduce_scatter | solution.py:215
  476.2 2.0 collective-permute-start.13
  476.8 2.2 collective-permute-start.12
  482.2 62.9 %all-to-all-start.3 = ((bf16[1,4,256,1024]{3,2,0,1:T(8,128)(2,1)}), bf16[1,4,256,1024]{3,2,0,1:T(8,128)(2,1)S(1)}, u32[]{:S(2)}, u32[]{:S(2)}) async-start(bf16[1,4,256,1024]{3,2,0,1:T(8,128)(2,1)} %bitcast.624), calls=%async_computation.3 | async-start | bytes 4194304 | tf_op jit(solution)/shard_map/backward_attention/all_to_all | solution.py:274
  485.9 99.8 %reduce-scatter.7.cloned.1.call-start = ((), (), s32[]{:S(2)}) async-start(), calls=%async_computation.16 | async-start | bytes 589824 | tf_op jit(solution)/shard_map/weight_grads/reduce_scatter | solution.py:416
  522.6 7.0 collective-permute-start.17
  524.6 6.2 collective-permute-start.16
  529.5 97.7 %reduce-scatter.5.cloned.1.call-start = ((), (), s32[]{:S(2)}) async-start(), calls=%async_computation.15 | async-start | bytes 1769472 | tf_op jit(solution)/shard_map/weight_grads/reduce_scatter | solution.py:416
  545.2 83.7 %all-to-all-start.4 = ((bf16[1,4,256,1024]{3,2,0,1:T(8,128)(2,1)}), bf16[1,4,256,1024]{3,2,0,1:T(8,128)(2,1)}, u32[]{:S(2)}, u32[]{:S(2)}) async-start(bf16[1,4,256,1024]{3,2,0,1:T(8,128)(2,1)} %bitcast.625), calls=%async_computation.4 | async-start | bytes 4194304 | tf_op jit(solution)/shard_map/backward_attention/all_to_all | solution.py:274
  550.5 39.4 %copy-start.57 = (f32[1,1,1,1024]{3,1,2,0:T(1,128)S(1)}, f32[1,1,1,1024]{3,1,2,0:T(1,128)}, u32[]{:S(2)}) copy-start(f32[1,1,1,1024]{3,1,2,0:T(1,128)} %get-tuple-element.176) | copy-start | bytes 12292
  550.5 123.5 %reduce-scatter.11.cloned.1.call-start = ((), (), s32[]{:S(2)}) async-start(), calls=%async_computation.18 | async-start | bytes 2621440 | tf_op jit(solution)/shard_map/weight_grads/reduce_scatter | solution.py:216
  552.3 80.3 %copy-start.3 = (f32[2,1,256,1024]{3,2,1,0:T(8,128)S(1)}, f32[2,1,256,1024]{3,2,1,0:T(8,128)}, u32[]{:S(2)}) copy-start(f32[2,1,256,1024]{3,2,1,0:T(8,128)} %copy-done.2) | copy-start | bytes 6291460
  552.3 80.3 %copy-start.56 = (f32[1,1,1,1024]{3,1,2,0:T(1,128)S(1)}, f32[1,1,1,1024]{3,1,2,0:T(1,128)}, u32[]{:S(2)}) copy-start(f32[1,1,1,1024]{3,1,2,0:T(1,128)} %get-tuple-element.180) | copy-start | bytes 12292
  552.3 80.3 %copy-start.60 = (f32[256]{0:T(256)S(1)}, f32[256]{0:T(256)}, u32[]{:S(2)}) copy-start(f32[256]{0:T(256)} %copy-done.59) | copy-start | bytes 3076
  552.3 80.3 %copy-start.62 = (f32[256]{0:T(256)S(1)}, f32[256]{0:T(256)}, u32[]{:S(2)}) copy-start(f32[256]{0:T(256)} %copy-done.61) | copy-start | bytes 3076
  638.5 38.9 %all-to-all-start.5 = ((f32[4,1,3072]{2,1,0:T(1,128)}), f32[4,1,3072]{2,1,0:T(1,128)S(1)}, u32[]{:S(2)}, u32[]{:S(2)}) async-start(f32[4,1,3072]{2,1,0:T(1,128)} %reshape.1148), calls=%async_computation.9 | async-start | bytes 98304 | tf_op jit(solution)/shard_map/ada_grad/all_to_all | solution.py:402
  648.1 42.1 %copy-start.55 = (bf16[8,2,4,128]{3,0,2,1:T(8,128)(2,1)S(1)}, bf16[8,2,4,128]{3,0,2,1:T(8,128)(2,1)}, u32[]{:S(2)}) copy-start(bf16[8,2,4,128]{3,0,2,1:T(8,128)(2,1)} %copy-done.54) | copy-start | bytes 49156
  675.0 16.7 %collective-permute-start.18 = (bf16[2,128,512]{2,1,0:T(8,128)(2,1)S(1)}, bf16[2,128,512]{2,1,0:T(8,128)(2,1)S(1)}, u32[]{:S(2)}, u32[]{:S(2)}) collective-permute-start(bf16[2,128,512]{2,1,0:T(8,128)(2,1)S(1)} %get-tuple-element.163), channel_id=1, source_target_pairs={{0,4},{4,0},{1,5},{5,1},{2,6},{6,2},{3,7},{7,3},{8,12},{12,8},{9,1... | collective-permute-start | bytes 786440 | tf_op jit(solution)/shard_map/weight_grads/ppermute | solution.py:220
  (66 other events, 309.1 us)
Sparse Core Ops, SparseCore 0:
  10.1 52.5 all-gather.23
  64.9 44.4 all-gather.13
  111.3 24.3 all-gather.11
  137.7 45.6 all-gather.21
  185.1 86.2 all-gather.15
  369.4 44.6 all-gather.17
  415.7 44.4 all-gather.19
  463.3 85.1 reduce-scatter.8
  551.5 34.1 reduce-scatter.6
  588.8 38.3 reduce-scatter.4
  629.5 44.4 reduce-scatter.10

commit v19 on v16

--- a/solution.py
+++ b/solution.py
@@ -226,7 +226,7 @@
             lax.all_gather(w, ("dp", "frame"), axis=0, tiled=True)
             for w in (qkv_weight, out_weight)
         )
-        upward_weight, downward_weight = hidden_half((up_weight, down_weight))
+        ffn_cache = {}
 
     residual = tokens[:, 0].astype(jnp.float32)
     upstream = out_grad[:, 0].astype(jnp.float32)
@@ -289,6 +289,10 @@
             values_all = gather_halves(projected[:, :, 2])
             attended, log_totals = attention_forward(queries[0], keys_all[0], values_all[0])
             attended = attended[None]
+            if not ffn_cache:
+                up_in, down_in, attended = lax.optimization_barrier((up_weight, down_weight, attended))
+                ffn_cache["weights"] = hidden_half((up_in, down_in))
+            upward_weight, downward_weight = ffn_cache["weights"]
             partial_one = jnp.einsum(
                 "crh,oh->cro", attended, mixer_weight, preferred_element_type=jnp.float32
             )

time: 708 us -> 728 us (1.028)
  waiting for transfers between devices: 258 us -> 269 us
  starting transfers between devices: 32.6 us -> 40.8 us
    all_to_all x4, waiting for transfers between devices: 51.3 us -> 74.8 us  [scatter_tokens(): received = lax.all_to_all(parts, 'tensor', 1, 1, tiled=True)]
    all_gather x2, waiting for transfers between devices: 42.2 us -> 24.5 us  [on_device(): lax.all_gather(tokens[i:i + 1, 0], 'tensor', axis=1, tiled=True)]
    all_gather x2, starting transfers between devices: 0.08 us -> 10 us  [gather_tokens(): return lax.all_gather(values, 'tensor', axis=1, tiled=True)]
    all_to_all x1, waiting for transfers between devices: 0.01 us -> 7.46 us  [on_device(): lax.all_to_all(partial_mod, ('dp', 'frame'), 0, 0, tiled=True)]
    unnamed x165 -> x169, local copies, waits for them, and re-layouts: 23.1 us -> 20.9 us
  transfers between devices with their start and end apart: 36 -> 36, of which waited for: 12 -> 15; matrix products, arithmetic and copies ran while one was open for 30% -> 28% of each run, Pallas kernels for 15% -> 15%
where the time goes in v19:
time: 728 us; the launch traced here: 717 us
  waiting for transfers between devices  269 us (37%)
  Pallas kernels  107 us (15%)
  matrix products  96.5 us (13%)
  other arithmetic  83.9 us (12%)
  local copies, waits for them, and re-layouts  55.5 us (8%)
  blocking collectives  48.7 us (7%)
  starting transfers between devices  40.8 us (6%)
  between operations  15.5 us (2%)
    all_to_all x4, waiting for transfers between devices, scatter_tokens(): received = lax.all_to_all(parts, 'tensor', 1, 1, tiled=True)  74.8 us
    reduce_scatter x2, waiting for transfers between devices, on_device(): lax.psum_scatter(total.astype(jnp.bfloat16), ('dp', 'frame'), scatter_dim...  66.3 us
    pallas_call x2, Pallas kernels, attention_backward(): pl.pallas_call(functools.partial(_backward_kernel, heads, HEAD_DIM ** (-0...  64.9 us
    all_gather x1, waiting for transfers between devices, hidden_half(): gathered = lax.all_gather(joined, 'tensor', axis=0, tiled=True)  44.4 us
    pallas_call x2, Pallas kernels, attention_forward(): pl.pallas_call(functools.partial(_forward_kernel, heads, HEAD_DIM ** (-0....  42.4 us
    reduce_scatter x1, waiting for transfers between devices, hidden_half_back(): summed = lax.psum_scatter(summed, 'tensor', scatter_dimension=0, tiled=True)  25.9 us
    all_gather x2, waiting for transfers between devices, on_device(): lax.all_gather(tokens[i:i + 1, 0], 'tensor', axis=1, tiled=True)  24.5 us
    unnamed x169, local copies, waits for them, and re-layouts  20.9 us
  transfers between devices with their start and end apart: 36, of which 15 were waited for; matrix products, arithmetic and copies ran while one was open for 28% of the time, Pallas kernels for 15%

profile of v19, /device:TPU:0, one launch (start us, length us, event | category | flops | bytes accessed | tf_op | source)
XLA Modules:
  0.0 717.2 jit_solution(11960581671276694077)
XLA Ops:
  10.3 10.6 %all-gather.3 = s32[8,2,4]{2,1,0:T(2,128)S(1)} all-gather(s32[1,2,4]{2,1,0:T(2,128)} %bitcast.685), channel_id=1, replica_groups=mesh['dp'=4,'frame'=2,'tensor'=4] {'dp','frame'}, dimensions={0}, use_global_device_ids=true | all-gather | bytes 288 | tf_op jit(solution)/shard_map/modulation/all_gather | solution.py:168
  23.1 3.5 all-to-all-start
  27.3 7.5 %all-to-all-done = f32[8,2,4,6,256]{4,2,3,1,0:T(4,128)S(1)} async-done(((f32[8,2,4,6,256]{4,2,3,1,0:T(4,128)}), f32[8,2,4,6,256]{4,2,3,1,0:T(4,128)S(1)}, u32[]{:S(2)}, u32[]{:S(2)}) %all-to-all-start) | async-done | bytes 393248 | tf_op jit(solution)/shard_map/modulation/all_to_all | solution.py:179
  34.9 16.7 %all_gather.34 = f32[2,4,6,1024]{3,2,1,0:T(8,128)S(1)} all-gather(f32[2,4,6,256]{3,2,1,0:T(8,128)S(1)} %copy.301), channel_id=1, replica_groups=mesh['dp'=4,'frame'=2,'tensor'=4] {'tensor'}, dimensions={3}, use_global_device_ids=true | all-gather | bytes 245760 | tf_op jit(solution)/shard_map/modulation/all_gather | solution.py:181
  52.4 10.3 %all-gather.22.cloned.1.call-done = bf16[1,1,1024,1024]{3,2,1,0:T(8,128)(2,1)} async-done(((bf16[1,1,256,1024]{3,2,1,0:T(8,128)(2,1)}), bf16[1,1,1024,1024]{3,2,1,0:T(8,128)(2,1)}) %all-gather.22.cloned.1.call-update) | async-done | bytes 2097168 | tf_op jit(solution)/shard_map/group_inputs/all_gather | solution.py:236
  69.4 19.6 %all-gather.12.cloned.1.call-done = bf16[1024,3,256]{2,0,1:T(8,128)(2,1)} async-done(((bf16[128,3,256]{2,0,1:T(8,128)(2,1)}), bf16[1024,3,256]{2,0,1:T(8,128)(2,1)}) %all-gather.12.cloned.1.call-update) | async-done | bytes 1572880 | tf_op jit(solution)/shard_map/weights/all_gather | solution.py:226
  89.1 3.2 fusion.128
  97.2 21.3 %forward.2 = (bf16[1024,256]{1,0:T(8,128)(2,1)}, f32[1024,4]{1,0:T(8,128)}) custom-call(bf16[1024,256]{1,0:T(8,128)(2,1)} %get-tuple-element.159.q_ref, bf16[2048,256]{1,0:T(8,128)(2,1)} %maximum_bitcast_fusion.k_ref, bf16[2048,256]{1,0:T(8,128)(2,1)} %maximum_bitcast_fusion.1.v_ref), custom_call_target="tpu_custom_call" | custom-call | flops 2147483648 | bytes 3145728 | tf_op jit(solution)/shard_map/forward/pallas_call | solution.py:85
  122.8 14.1 %all-gather.24.cloned.1.call-done = bf16[1,1,1024,1024]{3,2,1,0:T(8,128)(2,1)} async-done(((bf16[1,1,256,1024]{3,2,1,0:T(8,128)(2,1)}), bf16[1,1,1024,1024]{3,2,1,0:T(8,128)(2,1)}) %all-gather.24.cloned.1.call-update) | async-done | bytes 2097168 | tf_op jit(solution)/shard_map/group_inputs/all_gather | solution.py:236
  139.0 44.4 %all-gather.14.cloned.1.call-done = bf16[2048,512]{1,0:T(8,128)(2,1)} async-done(((bf16[512,512]{1,0:T(8,128)(2,1)}), bf16[2048,512]{1,0:T(8,128)(2,1)}) %all-gather.14.cloned.1.call-update) | async-done | bytes 2097168 | tf_op jit(solution)/shard_map/forward/all_gather | solution.py:202
  189.8 11.9 %all_gather.37 = bf16[1024,256]{1,0:T(8,128)(2,1)S(1)} all-gather(bf16[128,256]{1,0:T(8,128)(2,1)S(1)} %copy-done.62), channel_id=1, replica_groups=mesh['dp'=4,'frame'=2,'tensor'=4] {'dp','frame'}, dimensions={0}, use_global_device_ids=true | all-gather | bytes 589824 | tf_op jit(solution)/shard_map/weights/all_gather | solution.py:226
  203.9 21.1 %forward.3 = (bf16[1024,256]{1,0:T(8,128)(2,1)}, f32[1024,4]{1,0:T(8,128)}) custom-call(bf16[1024,256]{1,0:T(8,128)(2,1)} %get-tuple-element.162.q_ref, bf16[2048,256]{1,0:T(8,128)(2,1)} %maximum_bitcast_fusion.2.k_ref, bf16[2048,256]{1,0:T(8,128)(2,1)} %maximum_bitcast_fusion.3.v_ref), custom_call_target="tpu_custom_call" | custom-call | flops 2147483648 | bytes 3145728 | tf_op jit(solution)/shard_map/forward/pallas_call | solution.py:85
  225.0 3.3 convolution_convert_fusion
  228.3 3.6 all-to-all-start.2
  234.0 46.8 %all-to-all-done.2 = bf16[1,4,256,1024]{3,2,0,1:T(8,128)(2,1)S(1)} async-done(((bf16[1,4,256,1024]{3,2,0,1:T(8,128)(2,1)}), bf16[1,4,256,1024]{3,2,0,1:T(8,128)(2,1)S(1)}, u32[]{:S(2)}, u32[]{:S(2)}) %all-to-all-start.2) | async-done | bytes 2097184 | tf_op jit(solution)/shard_map/forward/all_to_all | solution.py:270
  280.9 4.4 all-to-all-start.1
  285.4 10.0 %all-gather.18.cloned.1.call-start = ((), (), s32[]{:S(2)}) async-start(), calls=%async_computation.13 | async-start | bytes 2621440 | tf_op jit(solution)/shard_map/backward_attention/all_gather | solution.py:264
  296.8 3.6 convert_element_type.262
  305.6 27.9 %all-to-all-done.1 = bf16[1,4,256,1024]{3,2,0,1:T(8,128)(2,1)} async-done(((bf16[1,4,256,1024]{3,2,0,1:T(8,128)(2,1)}), bf16[1,4,256,1024]{3,2,0,1:T(8,128)(2,1)}, u32[]{:S(2)}, u32[]{:S(2)}) %all-to-all-start.1) | async-done | bytes 2097184 | tf_op jit(solution)/shard_map/forward/all_to_all | solution.py:270
  335.7 2.8 multiply_reduce_fusion.10
  354.7 3.9 fusion.246
  370.1 4.7 fusion.136
  391.2 7.1 fusion.60
  400.7 9.0 %fusion.139 = bf16[1,512,1024]{2,1,0:T(8,128)(2,1)S(1)} fusion(bf16[1024,512,4]{1,0,2:T(8,128)(2,1)} %bitcast.624, f32[512,4,512,1]{2,0,3,1:T(8,128)} %fusion.60, f32[512,4,512,1]{2,0,3,1:T(8,128)} %copy-done.73), kind=kOutput, calls=%fused_computation.164 | convolution fusion | flops 2168979456 | bytes 13631488 | tf_op jit(solution)/shard_map/backward_ffn/crtj,atdj->crad/dot_general | solution.py:330
  409.9 6.1 fusion.75
  421.3 8.1 %fusion.43 = bf16[4,4,256,512]{3,2,0,1:T(8,128)(2,1)S(1)} fusion(f32[4,512,4,256]{1,3,2,0:T(8,128)} %fusion.75, f32[512,4,512,1]{2,0,3,1:T(8,128)} %copy-done.76, bf16[512,4,256]{0,2,1:T(8,128)(2,1)} %copy.266), kind=kOutput, calls=%fused_computation.62 | convolution fusion | flops 2161115136 | bytes 17825792 | tf_op jit(solution)/shard_map/backward_ffn/crad,crtj->atdj/dot_general | solution.py:322
  433.5 6.1 fusion.78
  439.6 6.7 fusion.42
  448.5 7.6 %pad_maximum_fusion = bf16[16,512,512]{2,1,0:T(8,128)(2,1)} fusion(bf16[16,256,512]{2,1,0:T(8,128)(2,1)} %bitcast.614, bf16[16,256,512]{2,1,0:T(8,128)(2,1)} %bitcast.619), kind=kLoop, calls=%fused_computation | loop fusion | flops 16777216 | bytes 16777216 | tf_op jit(solution)/shard_map/weight_grads/concatenate | solution.py:209
  457.1 3.1 fusion.145.g_ref
  460.3 32.3 %backward_attention.2 = (f32[1024,256]{1,0:T(8,128)}, f32[2048,256]{1,0:T(8,128)}, f32[2048,256]{1,0:T(8,128)}) custom-call(bf16[1024,256]{1,0:T(8,128)(2,1)} %get-tuple-element.159.q_ref, bf16[2048,256]{1,0:T(8,128)(2,1)} %maximum_bitcast_fusion.k_ref, bf16[2048,256]{1,0:T(8,128)(2,1)} %maximum_bitcast_fusion.1.v_ref, bf16[1024,256]{1,0:T(8,128)(2,1)} %fusion.145.g_ref, ...), custom_call_target="tpu_custom_call" | custom-call | flops 5368709120 | bytes 8912896 | tf_op jit(solution)/shard_map/backward_attention/pallas_call | solution.py:118
  497.5 3.2 bitcast_convert_fusion.1
  500.7 3.6 all-to-all-start.3
  504.4 3.3 fusion.148.g_ref
  507.7 32.5 %backward_attention.3 = (f32[1024,256]{1,0:T(8,128)}, f32[2048,256]{1,0:T(8,128)}, f32[2048,256]{1,0:T(8,128)}) custom-call(bf16[1024,256]{1,0:T(8,128)(2,1)} %get-tuple-element.162.q_ref, bf16[2048,256]{1,0:T(8,128)(2,1)} %maximum_bitcast_fusion.2.k_ref, bf16[2048,256]{1,0:T(8,128)(2,1)} %maximum_bitcast_fusion.3.v_ref, bf16[1024,256]{1,0:T(8,128)(2,1)} %fusion.148.g_ref, ...), custom_call_target="tpu_custom_call" | custom-call | flops 5368709120 | bytes 8912896 | tf_op jit(solution)/shard_map/backward_attention/pallas_call | solution.py:118
  553.8 3.7 fusion.177
  557.6 3.2 add_convert_fusion.2
  560.8 4.8 bitcast_convert_fusion
  565.6 5.2 all-to-all-start.4
  572.7 29.1 %reduce-scatter.7.cloned.1.call-done = bf16[128,256]{1,0:T(8,128)(2,1)} async-done(((bf16[1024,256]{1,0:T(8,128)(2,1)}), bf16[128,256]{1,0:T(8,128)(2,1)}) %reduce-scatter.7.cloned.1.call-update) | async-done | bytes 65552 | tf_op jit(solution)/shard_map/weight_grads/reduce_scatter | solution.py:416
  603.3 2.7 convert_reduce_fusion.4
  606.1 37.2 %reduce-scatter.5.cloned.1.call-done = bf16[128,3,256]{2,0,1:T(8,128)(2,1)} async-done(((bf16[1024,3,256]{2,0,1:T(8,128)(2,1)}), bf16[128,3,256]{2,0,1:T(8,128)(2,1)}) %reduce-scatter.5.cloned.1.call-update) | async-done | bytes 196624 | tf_op jit(solution)/shard_map/weight_grads/reduce_scatter | solution.py:416
  645.0 2.7 convert_reduce_fusion.2
  650.9 3.6 reshape.1149
  654.5 4.7 all-to-all-start.5
  660.6 3.5 add_convert_fusion.6
  664.2 25.9 %reduce-scatter.11.cloned.1.call-done = bf16[1,512,512]{2,1,0:T(8,128)(2,1)} async-done(((bf16[4,512,512]{2,1,0:T(8,128)(2,1)}), bf16[1,512,512]{2,1,0:T(8,128)(2,1)}) %reduce-scatter.11.cloned.1.call-update) | async-done | bytes 524304 | tf_op jit(solution)/shard_map/weight_grads/reduce_scatter | solution.py:212
  696.8 9.5 %all-gather.2 = f32[16,4,1,6,256]{4,1,0,3,2:T(4,128)S(1)} all-gather(f32[2,4,1,6,256]{4,1,0,3,2:T(4,128)S(1)} %bitcast.645), channel_id=4, replica_groups=mesh['dp'=4,'frame'=2,'tensor'=4] {'dp','frame'}, dimensions={0}, use_global_device_ids=true | all-gather | bytes 442368 | tf_op jit(solution)/shard_map/ada_grad/all_gather | solution.py:405
  (375 shorter events, 141.6 us)
Async XLA Ops:
  7.2 55.6 %all-gather.22.cloned.1.call-start = ((), (), s32[]{:S(2)}) async-start(), calls=%async_computation.19 | async-start | bytes 2621440 | tf_op jit(solution)/shard_map/group_inputs/all_gather | solution.py:236
  9.5 79.5 %all-gather.12.cloned.1.call-start = ((), (), s32[]{:S(2)}) async-start(), calls=%async_computation.10 | async-start | bytes 1769472 | tf_op jit(solution)/shard_map/weights/all_gather | solution.py:226
  23.1 11.7 %all-to-all-start = ((f32[8,2,4,6,256]{4,2,3,1,0:T(4,128)}), f32[8,2,4,6,256]{4,2,3,1,0:T(4,128)S(1)}, u32[]{:S(2)}, u32[]{:S(2)}) async-start(f32[8,2,4,6,256]{4,2,3,1,0:T(4,128)} %fusion.184), calls=%async_computation | async-start | bytes 786432 | tf_op jit(solution)/shard_map/modulation/all_to_all | solution.py:179
  26.6 110.3 %all-gather.24.cloned.1.call-start = ((), (), s32[]{:S(2)}) async-start(), calls=%async_computation.20 | async-start | bytes 2621440 | tf_op jit(solution)/shard_map/group_inputs/all_gather | solution.py:236
  27.3 156.1 %all-gather.14.cloned.1.call-start = ((), (), s32[]{:S(2)}) async-start(), calls=%async_computation.11 | async-start | bytes 2621440 | tf_op jit(solution)/shard_map/forward/all_gather | solution.py:202
  69.4 22.8 %copy-start.30 = (bf16[1024,1024,1]{1,0,2:T(8,128)(2,1)}, bf16[1024,1024,1]{1,0,2:T(8,128)(2,1)S(1)}, u32[]{:S(2)}) copy-start(bf16[1024,1024,1]{1,0,2:T(8,128)(2,1)S(1)} %fusion.73) | copy-start | bytes 6291460
  93.2 1.9 collective-permute-start
  93.4 2.7 collective-permute-start.1
  118.7 1.4 collective-permute-start.4
  119.2 1.4 collective-permute-start.3
  121.7 233.0 %all-gather.16.cloned.1.call-start = ((), (), s32[]{:S(2)}) async-start(), calls=%async_computation.12 | async-start | bytes 10485760 | tf_op jit(solution)/shard_map/forward/all_gather | solution.py:203
  136.9 46.5 %copy-start.7 = (bf16[1,1,1024,1024]{3,2,1,0:T(8,128)(2,1)S(1)}, bf16[1,1,1024,1024]{3,2,1,0:T(8,128)(2,1)}, u32[]{:S(2)}) copy-start(bf16[1,1,1024,1024]{3,2,1,0:T(8,128)(2,1)} %all-gather.24.cloned.1.call-done) | copy-start | bytes 6291460
  189.3 12.4 %collective-permute-start.6 = (bf16[1,1024,256]{2,1,0:T(8,128)(2,1)S(1)}, bf16[1,1024,256]{2,1,0:T(8,128)(2,1)S(1)}, u32[]{:S(2)}, u32[]{:S(2)}) collective-permute-start(bf16[1,1024,256]{2,1,0:T(8,128)(2,1)S(1)} %get-tuple-element.161), channel_id=1, source_target_pairs={{0,4},{4,0},{1,5},{5,1},{2,6},{6,2},{3,7},{7,3},{8,12},{12,8},{9,1... | collective-permute-start | bytes 1572872 | tf_op jit(solution)/shard_map/forward/ppermute | solution.py:245
  189.3 13.5 %collective-permute-start.7 = (bf16[1,1024,256]{2,1,0:T(8,128)(2,1)S(1)}, bf16[1,1024,256]{2,1,0:T(8,128)(2,1)S(1)}, u32[]{:S(2)}, u32[]{:S(2)}) collective-permute-start(bf16[1,1024,256]{2,1,0:T(8,128)(2,1)S(1)} %get-tuple-element.160), channel_id=1, source_target_pairs={{0,4},{4,0},{1,5},{5,1},{2,6},{6,2},{3,7},{7,3},{8,12},{12,8},{9,1... | collective-permute-start | bytes 1572872 | tf_op jit(solution)/shard_map/forward/ppermute | solution.py:245
  201.7 30.2 %copy-start.19 = (bf16[1024,256]{1,0:T(8,128)(2,1)}, bf16[1024,256]{1,0:T(8,128)(2,1)S(1)}, u32[]{:S(2)}) copy-start(bf16[1024,256]{1,0:T(8,128)(2,1)S(1)} %all_gather.37) | copy-start | bytes 1572868
  228.3 52.6 %all-to-all-start.2 = ((bf16[1,4,256,1024]{3,2,0,1:T(8,128)(2,1)}), bf16[1,4,256,1024]{3,2,0,1:T(8,128)(2,1)S(1)}, u32[]{:S(2)}, u32[]{:S(2)}) async-start(bf16[1,4,256,1024]{3,2,0,1:T(8,128)(2,1)} %bitcast.622), calls=%async_computation.2 | async-start | bytes 4194304 | tf_op jit(solution)/shard_map/forward/all_to_all | solution.py:270
  280.9 52.7 %all-to-all-start.1 = ((bf16[1,4,256,1024]{3,2,0,1:T(8,128)(2,1)}), bf16[1,4,256,1024]{3,2,0,1:T(8,128)(2,1)}, u32[]{:S(2)}, u32[]{:S(2)}) async-start(bf16[1,4,256,1024]{3,2,0,1:T(8,128)(2,1)} %bitcast.621), calls=%async_computation.1 | async-start | bytes 4194304 | tf_op jit(solution)/shard_map/forward/all_to_all | solution.py:270
  285.4 170.8 %all-gather.18.cloned.1.call-start = ((), (), s32[]{:S(2)}) async-start(), calls=%async_computation.13 | async-start | bytes 2621440 | tf_op jit(solution)/shard_map/backward_attention/all_gather | solution.py:264
  296.8 38.9 %copy-start.2 = (f32[2,1,256,1024]{3,2,1,0:T(8,128)}, f32[2,1,256,1024]{3,2,1,0:T(8,128)S(1)}, u32[]{:S(2)}) copy-start(f32[2,1,256,1024]{3,2,1,0:T(8,128)S(1)} %convert_element_type.236) | copy-start | bytes 6291460
  300.6 37.9 %copy-start.63 = (f32[256]{0:T(256)}, f32[256]{0:T(256)S(1)}, u32[]{:S(2)}) copy-start(f32[256]{0:T(256)S(1)} %get-tuple-element.195) | copy-start | bytes 3076
  300.6 37.9 %copy-start.65 = (f32[256]{0:T(256)}, f32[256]{0:T(256)S(1)}, u32[]{:S(2)}) copy-start(f32[256]{0:T(256)S(1)} %get-tuple-element.196) | copy-start | bytes 3076
  303.0 39.3 %collective-permute-start.10 = (bf16[1,256,1024]{2,1,0:T(8,128)(2,1)}, bf16[1,256,1024]{2,1,0:T(8,128)(2,1)}, u32[]{:S(2)}, u32[]{:S(2)}) collective-permute-start(bf16[1,256,1024]{2,1,0:T(8,128)(2,1)} %multiply_convert_fusion.3), channel_id=1, source_target_pairs={{0,4},{4,0},{1,5},{5,1},{2,6},{6,2},{3,7},{7,3},{8,12},{12,8},{9,1... | collective-permute-start | bytes 1572872 | tf_op jit(solution)/shard_map/backward_ffn/ppermute | solution.py:245
  340.5 5.7 collective-permute-start.2
  341.9 7.0 collective-permute-start.8
  370.0 8.4 %collective-permute-start.5 = (bf16[1,256,1024]{2,1,0:T(8,128)(2,1)S(1)}, bf16[1,256,1024]{2,1,0:T(8,128)(2,1)S(1)}, u32[]{:S(2)}, u32[]{:S(2)}) collective-permute-start(bf16[1,256,1024]{2,1,0:T(8,128)(2,1)S(1)} %slice.287), channel_id=1, source_target_pairs={{0,4},{4,0},{1,5},{5,1},{2,6},{6,2},{3,7},{7,3},{8,12},{12,8},{9,1... | collective-permute-start | bytes 1572872 | tf_op jit(solution)/shard_map/forward/ppermute | solution.py:255
  374.9 2.9 collective-permute-start.11
  380.3 5.9 collective-permute-start.14
  384.8 31.8 %collective-permute-start.9 = (bf16[1,256,1024]{2,1,0:T(8,128)(2,1)}, bf16[1,256,1024]{2,1,0:T(8,128)(2,1)}, u32[]{:S(2)}, u32[]{:S(2)}) collective-permute-start(bf16[1,256,1024]{2,1,0:T(8,128)(2,1)} %slice.300), channel_id=1, source_target_pairs={{0,4},{4,0},{1,5},{5,1},{2,6},{6,2},{3,7},{7,3},{8,12},{12,8},{9,1... | collective-permute-start | bytes 1572872 | tf_op jit(solution)/shard_map/forward/ppermute | solution.py:255
  386.2 118.2 %all-gather.20.cloned.1.call-start = ((), (), s32[]{:S(2)}) async-start(), calls=%async_computation.14 | async-start | bytes 2621440 | tf_op jit(solution)/shard_map/backward_attention/all_gather | solution.py:264
  409.8 6.2 collective-permute-start.15
  421.1 149.7 %reduce-scatter.9.cloned.1.call-start = ((), (), s32[]{:S(2)}) async-start(), calls=%async_computation.17 | async-start | bytes 10485760 | tf_op jit(solution)/shard_map/weight_grads/reduce_scatter | solution.py:211
  494.5 2.1 collective-permute-start.13
  495.2 2.1 collective-permute-start.12
  500.7 64.9 %all-to-all-start.3 = ((bf16[1,4,256,1024]{3,2,0,1:T(8,128)(2,1)}), bf16[1,4,256,1024]{3,2,0,1:T(8,128)(2,1)S(1)}, u32[]{:S(2)}, u32[]{:S(2)}) async-start(bf16[1,4,256,1024]{3,2,0,1:T(8,128)(2,1)} %bitcast.629), calls=%async_computation.3 | async-start | bytes 4194304 | tf_op jit(solution)/shard_map/backward_attention/all_to_all | solution.py:270
  504.3 97.4 %reduce-scatter.7.cloned.1.call-start = ((), (), s32[]{:S(2)}) async-start(), calls=%async_computation.16 | async-start | bytes 589824 | tf_op jit(solution)/shard_map/weight_grads/reduce_scatter | solution.py:416
  542.9 7.2 %collective-permute-start.17 = (bf16[1,1024,256]{2,1,0:T(8,128)(2,1)}, bf16[1,1024,256]{2,1,0:T(8,128)(2,1)}, u32[]{:S(2)}, u32[]{:S(2)}) collective-permute-start(bf16[1,1024,256]{2,1,0:T(8,128)(2,1)} %slice.315), channel_id=1, source_target_pairs={{0,4},{4,0},{1,5},{5,1},{2,6},{6,2},{3,7},{7,3},{8,12},{12,8},{9,1... | collective-permute-start | bytes 1572872 | tf_op jit(solution)/shard_map/backward_attention/ppermute | solution.py:255
  545.0 6.5 collective-permute-start.16
  549.9 93.4 %reduce-scatter.5.cloned.1.call-start = ((), (), s32[]{:S(2)}) async-start(), calls=%async_computation.15 | async-start | bytes 1769472 | tf_op jit(solution)/shard_map/weight_grads/reduce_scatter | solution.py:416
  565.6 79.4 %all-to-all-start.4 = ((bf16[1,4,256,1024]{3,2,0,1:T(8,128)(2,1)}), bf16[1,4,256,1024]{3,2,0,1:T(8,128)(2,1)}, u32[]{:S(2)}, u32[]{:S(2)}) async-start(bf16[1,4,256,1024]{3,2,0,1:T(8,128)(2,1)} %bitcast.630), calls=%async_computation.4 | async-start | bytes 4194304 | tf_op jit(solution)/shard_map/backward_attention/all_to_all | solution.py:270
  570.8 35.2 %copy-start.61 = (f32[1,1,1,1024]{3,1,2,0:T(1,128)S(1)}, f32[1,1,1,1024]{3,1,2,0:T(1,128)}, u32[]{:S(2)}) copy-start(f32[1,1,1,1024]{3,1,2,0:T(1,128)} %get-tuple-element.182) | copy-start | bytes 12292
  570.8 119.3 %reduce-scatter.11.cloned.1.call-start = ((), (), s32[]{:S(2)}) async-start(), calls=%async_computation.18 | async-start | bytes 2621440 | tf_op jit(solution)/shard_map/weight_grads/reduce_scatter | solution.py:212
  572.6 76.0 %copy-start.3 = (f32[2,1,256,1024]{3,2,1,0:T(8,128)S(1)}, f32[2,1,256,1024]{3,2,1,0:T(8,128)}, u32[]{:S(2)}) copy-start(f32[2,1,256,1024]{3,2,1,0:T(8,128)} %copy-done.2) | copy-start | bytes 6291460
  572.6 76.0 %copy-start.60 = (f32[1,1,1,1024]{3,1,2,0:T(1,128)S(1)}, f32[1,1,1,1024]{3,1,2,0:T(1,128)}, u32[]{:S(2)}) copy-start(f32[1,1,1,1024]{3,1,2,0:T(1,128)} %get-tuple-element.186) | copy-start | bytes 12292
  572.6 76.0 %copy-start.64 = (f32[256]{0:T(256)S(1)}, f32[256]{0:T(256)}, u32[]{:S(2)}) copy-start(f32[256]{0:T(256)} %copy-done.63) | copy-start | bytes 3076
  572.7 76.0 %copy-start.66 = (f32[256]{0:T(256)S(1)}, f32[256]{0:T(256)}, u32[]{:S(2)}) copy-start(f32[256]{0:T(256)} %copy-done.65) | copy-start | bytes 3076
  654.5 39.0 %all-to-all-start.5 = ((f32[4,1,3072]{2,1,0:T(1,128)}), f32[4,1,3072]{2,1,0:T(1,128)S(1)}, u32[]{:S(2)}, u32[]{:S(2)}) async-start(f32[4,1,3072]{2,1,0:T(1,128)} %reshape.1149), calls=%async_computation.9 | async-start | bytes 98304 | tf_op jit(solution)/shard_map/ada_grad/all_to_all | solution.py:402
  664.2 42.2 %copy-start.59 = (bf16[8,2,4,128]{3,0,2,1:T(8,128)(2,1)S(1)}, bf16[8,2,4,128]{3,0,2,1:T(8,128)(2,1)}, u32[]{:S(2)}) copy-start(bf16[8,2,4,128]{3,0,2,1:T(8,128)(2,1)} %copy-done.58) | copy-start | bytes 49156
  691.1 16.7 %collective-permute-start.18 = (bf16[2,128,512]{2,1,0:T(8,128)(2,1)S(1)}, bf16[2,128,512]{2,1,0:T(8,128)(2,1)S(1)}, u32[]{:S(2)}, u32[]{:S(2)}) collective-permute-start(bf16[2,128,512]{2,1,0:T(8,128)(2,1)S(1)} %get-tuple-element.169), channel_id=1, source_target_pairs={{0,4},{4,0},{1,5},{5,1},{2,6},{6,2},{3,7},{7,3},{8,12},{12,8},{9,1... | collective-permute-start | bytes 786440 | tf_op jit(solution)/shard_map/weight_grads/ppermute | solution.py:216
  (69 other events, 329.2 us)
Sparse Core Ops, SparseCore 0:
  10.1 52.5 all-gather.21
  64.7 24.3 all-gather.11
  91.2 45.6 all-gather.23
  138.9 44.4 all-gather.13
  185.1 86.7 all-gather.15
  386.3 43.9 all-gather.17
  431.8 44.4 all-gather.19
  479.4 85.1 reduce-scatter.8
  567.6 34.1 reduce-scatter.6
  604.9 38.3 reduce-scatter.4
  645.6 44.4 reduce-scatter.10

commit v20 on v15

v20 whole, which is shorter than its diff:
```python
import functools
import math

import jax
import jax.numpy as jnp
from jax import lax
from jax.experimental import pallas as pl
from jax.experimental.pallas import tpu as pltpu
from jax.sharding import PartitionSpec as P


HEAD_DIM = 64


epsilon = 1e-06
highest = lax.Precision.HIGHEST


def normalize(values):
    center = values - jnp.mean(values, axis=-1, keepdims=True)
    spread = jnp.mean(center * center, axis=-1, keepdims=True)
    inverse = lax.rsqrt(spread + epsilon)
    return (center * inverse, inverse)


def norm_back(upstream, normed, inverse):
    upstream_mean = jnp.mean(upstream, axis=-1, keepdims=True)
    product_mean = jnp.mean(upstream * normed, axis=-1, keepdims=True)
    return inverse * (upstream - upstream_mean - normed * product_mean)


def level_embedding(levels, model_width):
    halfway = model_width // 2
    frequency = jnp.exp(-math.log(10000.0) * jnp.arange(halfway, dtype=jnp.float32) / halfway)
    angles = levels.astype(jnp.float32)[..., None] * frequency
    return jnp.concatenate([jnp.cos(angles), jnp.sin(angles)], axis=-1)


def _nt(a, b):
    return lax.dot_general(a, b, (((1,), (1,)), ((), ())), preferred_element_type=jnp.float32)


def _tn(a, b):
    return lax.dot_general(a, b, (((0,), (0,)), ((), ())), preferred_element_type=jnp.float32)


def _forward_kernel(heads, scaling, q_ref, k_ref, v_ref, o_ref, lse_ref):
    for h in range(heads):
        cols = slice(h * HEAD_DIM, (h + 1) * HEAD_DIM)
        scores = _nt(q_ref[:, cols], k_ref[:, cols]) * scaling
        largest = jnp.max(scores, axis=1, keepdims=True)
        raised = jnp.exp(scores - largest)
        total = jnp.sum(raised, axis=1, keepdims=True)
        probs_low = (raised / total).astype(jnp.bfloat16)
        out = jnp.dot(probs_low, v_ref[:, cols], preferred_element_type=jnp.float32)
        o_ref[:, cols] = out.astype(o_ref.dtype)
        lse_ref[:, h : h + 1] = largest + jnp.log(total)


def _backward_kernel(heads, scaling, q_ref, k_ref, v_ref, g_ref, lse_ref, dq_ref, dk_ref, dv_ref):
    @pl.when(pl.program_id(0) == 0)
    def _():
        dk_ref[...] = jnp.zeros_like(dk_ref)
        dv_ref[...] = jnp.zeros_like(dv_ref)

    for h in range(heads):
        cols = slice(h * HEAD_DIM, (h + 1) * HEAD_DIM)
        q = q_ref[:, cols]
        g = g_ref[:, cols]
        scores = _nt(q, k_ref[:, cols]) * scaling
        probs = jnp.exp(scores - lse_ref[:, h : h + 1])
        grad_probs = _nt(g, v_ref[:, cols])
        dv_ref[:, cols] += _tn(probs.astype(jnp.bfloat16), g)
        row_terms = jnp.sum(probs * grad_probs, axis=1, keepdims=True)
        grad_scores = (probs * (grad_probs - row_terms)).astype(jnp.bfloat16)
        dq_ref[:, cols] = jnp.dot(grad_scores, k_ref[:, cols], preferred_element_type=jnp.float32) * scaling
        dk_ref[:, cols] += _tn(grad_scores, q) * scaling


def attention_forward(queries, keys, values, block_rows=256):
    rows, width = queries.shape
    length = keys.shape[0]
    heads = width // HEAD_DIM
    block_rows = min(block_rows, rows)
    flops = 4 * rows * length * width
    return pl.pallas_call(
        functools.partial(_forward_kernel, heads, HEAD_DIM ** (-0.5)),
        out_shape=(
            jax.ShapeDtypeStruct((rows, width), jnp.bfloat16),
            jax.ShapeDtypeStruct((rows, heads), jnp.float32),
        ),
        grid=(rows // block_rows,),
        in_specs=[
            pl.BlockSpec((block_rows, width), lambda i: (i, 0)),
            pl.BlockSpec((length, width), lambda i: (0, 0)),
            pl.BlockSpec((length, width), lambda i: (0, 0)),
        ],
        out_specs=[
            pl.BlockSpec((block_rows, width), lambda i: (i, 0)),
            pl.BlockSpec((block_rows, heads), lambda i: (i, 0)),
        ],
        compiler_params=pltpu.CompilerParams(
            dimension_semantics=("arbitrary",), vmem_limit_bytes=56 * 1024 * 1024
        ),
        cost_estimate=pl.CostEstimate(
            flops=flops,
            transcendentals=rows * length * heads,
            bytes_accessed=2 * (2 * rows * width + 2 * length * width),
        ),
    )(queries, keys, values)


def attention_backward(queries, keys, values, grad_out, lse, block_rows=256):
    rows, width = queries.shape
    length = keys.shape[0]
    heads = width // HEAD_DIM
    block_rows = min(block_rows, rows)
    flops = 10 * rows * length * width
    return pl.pallas_call(
        functools.partial(_backward_kernel, heads, HEAD_DIM ** (-0.5)),
        out_shape=(
            jax.ShapeDtypeStruct((rows, width), jnp.float32),
            jax.ShapeDtypeStruct((length, width), jnp.float32),
            jax.ShapeDtypeStruct((length, width), jnp.float32),
        ),
        grid=(rows // block_rows,),
        in_specs=[
            pl.BlockSpec((block_rows, width), lambda i: (i, 0)),
            pl.BlockSpec((length, width), lambda i: (0, 0)),
            pl.BlockSpec((length, width), lambda i: (0, 0)),
            pl.BlockSpec((block_rows, width), lambda i: (i, 0)),
            pl.BlockSpec((block_rows, heads), lambda i: (i, 0)),
        ],
        out_specs=[
            pl.BlockSpec((block_rows, width), lambda i: (i, 0)),
            pl.BlockSpec((length, width), lambda i: (0, 0)),
            pl.BlockSpec((length, width), lambda i: (0, 0)),
        ],
        compiler_params=pltpu.CompilerParams(
            dimension_semantics=("arbitrary",), vmem_limit_bytes=56 * 1024 * 1024
        ),
        cost_estimate=pl.CostEstimate(
            flops=flops,
            transcendentals=rows * length * heads,
            bytes_accessed=2 * (3 * rows * width + 2 * length * width) + 4 * (rows + 2 * length) * width,
        ),
    )(queries, keys, values, grad_out, lse)


def gelu_tanh(values):
    return jax.nn.gelu(values, approximate=True)


def block_body(
    tokens, out_grad, noise_index, qkv_weight, out_weight, up_weight, down_weight, ada_weight
):
    clips = tokens.shape[0]
    model_width = tokens.shape[-1]
    local_width = qkv_weight.shape[2]
    rows_here = qkv_weight.shape[0]
    groups = lax.axis_size("tensor")
    halves = lax.axis_size("frame")
    replicas = lax.axis_size("dp")

    levels_all = lax.all_gather(noise_index, ("dp", "frame"), axis=0, tiled=True)
    levels_all = levels_all.reshape(replicas * halves, clips, groups)
    condition_all = jax.nn.silu(level_embedding(levels_all, model_width)).astype(jnp.bfloat16)
    row_block = lax.axis_index("dp") * halves + lax.axis_index("frame")
    my_condition = lax.dynamic_slice_in_dim(condition_all, row_block * rows_here, rows_here, axis=3)
    partial_mod = jnp.einsum(
        "acgd,dkw->acgkw", my_condition, ada_weight, preferred_element_type=jnp.float32
    )
    summed_mod = jnp.sum(
        lax.all_to_all(partial_mod, ("dp", "frame"), 0, 0, tiled=True), axis=0
    )
    group_mod = lax.all_gather(summed_mod, "tensor", axis=3, tiled=True)
    group_mod = jnp.swapaxes(group_mod, 1, 2)[:, :, :, None, :]
    group_index = lax.axis_index("tensor")
    modulation = lax.dynamic_index_in_dim(group_mod, group_index, axis=2, keepdims=False)

    frame_index = lax.axis_index("frame")

    def order_by_half(mine, other):
        both = jnp.stack([mine, other])
        return jnp.where(frame_index == 0, both, both[::-1])

    def hidden_half(weights):
        half = weights[0].shape[1] // halves
        pieces = []
        for weight in weights:
            blocks = weight.reshape(rows_here, halves, half)
            mine = jnp.take(blocks, frame_index, axis=1)
            sent = jnp.take(blocks, 1 - frame_index, axis=1)
            received = lax.ppermute(sent, "frame", [(0, 1), (1, 0)])
            pieces.append(order_by_half(mine, received).reshape(halves * rows_here, half))
        joined = jnp.concatenate(pieces, axis=0)
        gathered = lax.all_gather(joined, "tensor", axis=0, tiled=True)
        gathered = lax.all_gather(gathered, "dp", axis=0, tiled=True)
        gathered = gathered.reshape(replicas, groups, len(weights), halves * rows_here, half)
        return tuple(gathered[:, :, k] for k in range(len(weights)))

    def hidden_half_back(totals):
        half = totals[0].shape[-1]
        blocks = jnp.concatenate(totals, axis=2).astype(jnp.bfloat16)
        blocks = blocks.reshape(replicas * groups, len(totals) * halves * rows_here, half)
        summed = lax.psum_scatter(blocks, "dp", scatter_dimension=0, tiled=True)
        summed = lax.psum_scatter(summed, "tensor", scatter_dimension=0, tiled=True)
        summed = summed.reshape(len(totals), halves, rows_here, half)
        mine = jnp.take(summed, frame_index, axis=1).astype(jnp.float32)
        sent = jnp.take(summed, 1 - frame_index, axis=1)
        received = lax.ppermute(sent, "frame", [(0, 1), (1, 0)]).astype(jnp.float32)
        both = jnp.stack([mine, received], axis=1)
        ordered = jnp.where(frame_index == 0, both, both[:, ::-1])
        return tuple(
            jnp.swapaxes(ordered[k], 0, 1).reshape(rows_here, halves * half)
            for k in range(len(totals))
        )

    joint_weight, mixer_weight = (
        lax.all_gather(w, ("dp", "frame"), axis=0, tiled=True)
        for w in (qkv_weight, out_weight)
    )
    upward_weight, downward_weight = hidden_half((up_weight, down_weight))

    residual = tokens[:, 0].astype(jnp.float32)
    upstream = out_grad[:, 0].astype(jnp.float32)
    gathered_tokens = []
    for i in range(clips):
        gathered_tokens.append(lax.all_gather(tokens[i : i + 1, 0], "tensor", axis=1, tiled=True))
    group_tokens = jnp.concatenate(gathered_tokens, axis=0)

    def gather_halves(values):
        if halves != 2:
            return lax.all_gather(values, "frame", axis=1, tiled=True)
        other = lax.ppermute(values, "frame", [(0, 1), (1, 0)])
        return jnp.concatenate([values, other], axis=1)

    def scatter_halves(values):
        if halves != 2:
            return lax.psum_scatter(
                values.astype(jnp.bfloat16), "frame", scatter_dimension=1, tiled=True
            ).astype(jnp.float32)
        count = values.shape[1] // 2
        mine = values[:, :count]
        other = lax.ppermute(values[:, count:].astype(jnp.bfloat16), "frame", [(0, 1), (1, 0)])
        return mine.astype(jnp.bfloat16).astype(jnp.float32) + other.astype(jnp.float32)

    def clip_pass(residual, upstream, modulation, group_tokens, group_mod):
        clips = residual.shape[0]
        patches = residual.shape[1]
        scale1, gate1 = modulation[:, 1], modulation[:, 2]
        shift2, scale2, gate2 = modulation[:, 3], modulation[:, 4], modulation[:, 5]

        def gather_tokens(values):
            return lax.all_gather(values, "tensor", axis=1, tiled=True)

        def scatter_tokens(values):
            parts = values.astype(jnp.bfloat16).reshape(
                values.shape[0], groups, -1, values.shape[-1]
            )
            received = lax.all_to_all(parts, "tensor", 1, 1, tiled=True)
            return jnp.sum(received.astype(jnp.float32), axis=1)

        normed_one, inverse_one = normalize(residual)
        group_normed, _ = normalize(
            group_tokens.astype(jnp.float32).reshape(clips, groups, patches, model_width)
        )
        flat_one = (
            (group_normed * (1.0 + group_mod[:, 1]) + group_mod[:, 0])
            .astype(jnp.bfloat16)
            .reshape(clips, groups * patches, model_width)
        )
        projected = jnp.einsum(
            "crd,dkh->crkh", flat_one, joint_weight, preferred_element_type=jnp.float32
        ).astype(jnp.bfloat16)
        queries = projected[:, :, 0]
        keys_all = gather_halves(projected[:, :, 1])
        values_all = gather_halves(projected[:, :, 2])
        attended, log_totals = attention_forward(queries[0], keys_all[0], values_all[0])
        attended = attended[None]
        partial_one = jnp.einsum(
            "crh,oh->cro", attended, mixer_weight, preferred_element_type=jnp.float32
        )
        branch_one = scatter_tokens(partial_one)
        middle = residual + gate1 * branch_one
        normed_two, inverse_two = normalize(middle)
        entering_two = (normed_two * (1.0 + scale2) + shift2).astype(jnp.bfloat16)
        flat_two = gather_halves(entering_two)
        blocked_two = flat_two.reshape(clips, -1, replicas, halves * rows_here)
        up_values = jnp.einsum(
            "crad,atdj->crtj", blocked_two, upward_weight, preferred_element_type=jnp.float32
        )
        hidden = gelu_tanh(up_values).astype(jnp.bfloat16)
        partial_two = jnp.einsum(
            "crtj,atdj->crad", hidden, downward_weight, preferred_element_type=jnp.float32
        ).reshape(clips, -1, model_width)
        branch_two = scatter_halves(partial_two)
        output = (middle + gate2 * branch_two).astype(jnp.bfloat16)

        grad_gate_two = jnp.sum(upstream * branch_two, axis=1)
        grad_two_all = gather_halves((gate2 * upstream).astype(jnp.bfloat16))
        blocked_grad = grad_two_all.reshape(clips, -1, replicas, halves * rows_here)
        grad_hidden = jnp.einsum(
            "crad,atdj->crtj", blocked_grad, downward_weight, preferred_element_type=jnp.float32
        )
        down_total = jnp.einsum(
            "crad,crtj->atdj", blocked_grad, hidden, preferred_element_type=jnp.float32
        )
        _, gelu_pullback = jax.vjp(gelu_tanh, up_values)
        grad_up = gelu_pullback(grad_hidden)[0].astype(jnp.bfloat16)
        up_total = jnp.einsum(
            "crad,crtj->atdj", blocked_two, grad_up, preferred_element_type=jnp.float32
        )
        partial_back_two = jnp.einsum(
            "crtj,atdj->crad", grad_up, upward_weight, preferred_element_type=jnp.float32
        ).reshape(clips, -1, model_width)
        grad_entering_two = scatter_halves(partial_back_two)
        grad_shift_two = jnp.sum(grad_entering_two, axis=1)
        grad_scale_two = jnp.sum(grad_entering_two * normed_two, axis=1)
        grad_middle = upstream + norm_back(
            grad_entering_two * (1.0 + scale2), normed_two, inverse_two
        )
        grad_gate_one = jnp.sum(grad_middle * branch_one, axis=1)

        grad_branch_one = (gate1 * grad_middle).astype(jnp.bfloat16)
        grad_one_all = gather_tokens(grad_branch_one)
        grad_attended = jnp.einsum(
            "cro,oh->crh", grad_one_all, mixer_weight, preferred_element_type=jnp.float32
        ).astype(jnp.bfloat16)
        mixer_total = jnp.einsum(
            "cro,crh->oh", grad_one_all, attended, preferred_element_type=jnp.float32
        )
        query_grads, key_grads, value_grads = attention_backward(
            queries[0], keys_all[0], values_all[0], grad_attended[0], log_totals
        )
        query_grads = query_grads[None]
        key_grads = key_grads[None]
        value_grads = value_grads[None]
        key_own, value_own = (
            scatter_halves(grads.reshape(clips, -1, local_width))
            for grads in (key_grads, value_grads)
        )
        grad_projected = jnp.stack([query_grads, key_own, value_own], axis=2).astype(jnp.bfloat16)
        joint_total = jnp.einsum(
            "crd,crkh->dkh", flat_one, grad_projected, preferred_element_type=jnp.float32
        )
        partial_back_one = jnp.einsum(
            "crkh,dkh->crd", grad_projected, joint_weight, preferred_element_type=jnp.float32
        )
        grad_entering_one = scatter_tokens(partial_back_one)
        grad_shift_one = jnp.sum(grad_entering_one, axis=1)
        grad_scale_one = jnp.sum(grad_entering_one * normed_one, axis=1)
        grad_input = grad_middle + norm_back(
            grad_entering_one * (1.0 + scale1), normed_one, inverse_one
        )


        grad_modulation = jnp.stack(
            [grad_shift_one, grad_scale_one, grad_gate_one, grad_shift_two, grad_scale_two, grad_gate_two],
            axis=1,
        )
        totals = (joint_total, mixer_total, up_total, down_total)
        return output, grad_input.astype(jnp.bfloat16), grad_modulation, totals

    pieces = []
    for i in range(clips):
        pieces.append(
            clip_pass(
                residual[i : i + 1],
                upstream[i : i + 1],
                modulation[i : i + 1],
                group_tokens[i : i + 1],
                group_mod[i : i + 1],
            )
        )
    output = jnp.concatenate([p[0] for p in pieces], axis=0)
    grad_input_low = jnp.concatenate([p[1] for p in pieces], axis=0)
    grad_modulation = jnp.concatenate([p[2] for p in pieces], axis=0)
    joint_total, mixer_total, up_total, down_total = (
        sum(p[3][k] for p in pieces[1:]) + pieces[0][3][k] for k in range(4)
    )
    grad_columns = lax.all_to_all(
        grad_modulation.reshape(clips, 1, 6, model_width), "tensor", 3, 1, tiled=True
    )
    grad_all = lax.all_gather(grad_columns, ("dp", "frame"), axis=0, tiled=True)
    grad_all = grad_all.reshape(replicas * halves, clips, groups, 6, local_width)
    adaptive_total = jnp.einsum(
        "acgd,acgkw->dkw",
        my_condition.astype(jnp.float32),
        grad_all,
        precision=highest,
    )

    joint_sum, mixer_sum = (
        lax.psum_scatter(
            total.astype(jnp.bfloat16), ("dp", "frame"), scatter_dimension=0, tiled=True
        ).astype(jnp.float32)
        for total in (joint_total, mixer_total)
    )
    up_sum, down_sum = hidden_half_back((up_total, down_total))
    summed = (joint_sum, mixer_sum, up_sum, down_sum)
    result = output[:, None]
    input_grad = grad_input_low[:, None]
    return (result, input_grad, summed[0], summed[1], summed[2], summed[3], adaptive_total)


def solution(mesh):
    return jax.shard_map(
        block_body,
        mesh=mesh,
        in_specs=(
            P("dp", ("frame", "tensor"), None, None),
            P("dp", ("frame", "tensor"), None, None),
            P("dp", "frame"),
            P(("dp", "frame"), None, "tensor"),
            P(("dp", "frame"), "tensor"),
            P(("dp", "frame"), "tensor"),
            P(("dp", "frame"), "tensor"),
            P(("dp", "frame"), None, "tensor"),
        ),
        out_specs=(
            P("dp", ("frame", "tensor"), None, None),
            P("dp", ("frame", "tensor"), None, None),
            P(("dp", "frame"), None, "tensor"),
            P(("dp", "frame"), "tensor"),
            P(("dp", "frame"), "tensor"),
            P(("dp", "frame"), "tensor"),
            P(("dp", "frame"), None, "tensor"),
        ),
        check_vma=False,
    )
```

time: 715 us -> 708 us (level)
  waiting for transfers between devices: 271 us -> 258 us
  other arithmetic: 75.7 us -> 85 us
  blocking collectives: 57.8 us -> 49.4 us
    reduce_scatter x0 -> x2, waiting for transfers between devices: none -> 66.6 us  [block_body(): lax.psum_scatter(total.astype(jnp.bfloat16), ('dp', 'frame'), scatter_dim...]
    all_to_all x4, waiting for transfers between devices: 114 us -> 51.3 us  [scatter_tokens(): received = lax.all_to_all(parts, 'tensor', 1, 1, tiled=True)]
    all_gather x2 -> x3, waiting for transfers between devices: 97.1 us -> 66 us  [the longest x2 42.2 us: block_body(): lax.all_gather(tokens[i:i + 1, 0], 'tensor', axis=1, tiled=True)]
    all_gather x1, waiting for transfers between devices: 11.5 us -> 42.3 us  [hidden_half(): gathered = lax.all_gather(joined, 'tensor', axis=0, tiled=True)]
    reduce_scatter x1, waiting for transfers between devices: 0.01 us -> 25.9 us  [hidden_half_back(): summed = lax.psum_scatter(summed, 'tensor', scatter_dimension=0, tiled=True)]
    reduce_scatter x1, waiting for transfers between devices: 24 us -> 0.01 us  [hidden_half_back(): summed = lax.psum_scatter(blocks, 'dp', scatter_dimension=0, tiled=True)]
    unnamed x10 -> x11, waiting for transfers between devices: 18.3 us -> 2.02 us
    all_to_all x1 -> x0, blocking collectives: 10.9 us -> none  [on_device(): lax.all_to_all(partial_mod, ('dp', 'frame'), 0, 0, tiled=True)]
  transfers between devices with their start and end apart: 33 -> 36, of which waited for: 14 -> 12; matrix products, arithmetic and copies ran while one was open for 28% -> 30% of each run, Pallas kernels for 15% -> 15%
where the time goes in v20:
time: 708 us; the launch traced here: 703 us
  waiting for transfers between devices  258 us (36%)
  Pallas kernels  107 us (15%)
  matrix products  97.1 us (14%)
  other arithmetic  85 us (12%)
  local copies, waits for them, and re-layouts  57.7 us (8%)
  blocking collectives  49.4 us (7%)
  starting transfers between devices  32.6 us (5%)
  between operations  15.8 us (2%)
    reduce_scatter x2, waiting for transfers between devices, block_body(): lax.psum_scatter(total.astype(jnp.bfloat16), ('dp', 'frame'), scatter_dim...  66.6 us
    pallas_call x2, Pallas kernels, attention_backward(): pl.pallas_call(functools.partial(_backward_kernel, heads, HEAD_DIM ** (-0...  64.9 us
    all_to_all x4, waiting for transfers between devices, scatter_tokens(): received = lax.all_to_all(parts, 'tensor', 1, 1, tiled=True)  51.3 us
    all_gather x1, waiting for transfers between devices, hidden_half(): gathered = lax.all_gather(joined, 'tensor', axis=0, tiled=True)  42.3 us
    pallas_call x2, Pallas kernels, attention_forward(): pl.pallas_call(functools.partial(_forward_kernel, heads, HEAD_DIM ** (-0....  42.2 us
    all_gather x2, waiting for transfers between devices, block_body(): lax.all_gather(tokens[i:i + 1, 0], 'tensor', axis=1, tiled=True)  42.2 us
    reduce_scatter x1, waiting for transfers between devices, hidden_half_back(): summed = lax.psum_scatter(summed, 'tensor', scatter_dimension=0, tiled=True)  25.9 us
    all_gather x1, waiting for transfers between devices, block_body(): lax.all_gather(w, ('dp', 'frame'), axis=0, tiled=True)  23.8 us
  transfers between devices with their start and end apart: 36, of which 12 were waited for; matrix products, arithmetic and copies ran while one was open for 30% of the time, Pallas kernels for 15%

profile of v20, /device:TPU:0, one launch (start us, length us, event | category | flops | bytes accessed | tf_op | source)
XLA Modules:
  0.0 703.0 jit_solution(6397535129296578680)
XLA Ops:
  16.3 10.1 %all-gather.3 = s32[8,2,4]{2,1,0:T(2,128)S(1)} all-gather(s32[1,2,4]{2,1,0:T(2,128)S(1)} %bitcast.678), channel_id=1, replica_groups=mesh['dp'=4,'frame'=2,'tensor'=4] {'dp','frame'}, dimensions={0}, use_global_device_ids=true | all-gather | bytes 288 | tf_op jit(solution)/shard_map/all_gather | solution.py:165
  28.7 3.5 all-to-all-start
  32.2 12.7 %all_gather.37 = bf16[1024,256]{1,0:T(8,128)(2,1)S(1)} all-gather(bf16[128,256]{1,0:T(8,128)(2,1)S(1)} %copy-done.58), channel_id=1, replica_groups=mesh['dp'=4,'frame'=2,'tensor'=4] {'dp','frame'}, dimensions={0}, use_global_device_ids=true | all-gather | bytes 589824 | tf_op jit(solution)/shard_map/all_gather | solution.py:220
  45.0 17.1 %all_gather.34 = f32[2,4,6,1024]{3,2,1,0:T(8,128)S(1)} all-gather(f32[2,4,6,256]{3,2,1,0:T(8,128)S(1)} %copy.301), channel_id=1, replica_groups=mesh['dp'=4,'frame'=2,'tensor'=4] {'tensor'}, dimensions={3}, use_global_device_ids=true | all-gather | bytes 245760 | tf_op jit(solution)/shard_map/all_gather | solution.py:176
  67.1 42.3 %all-gather.14.cloned.1.call-done = bf16[2048,512]{1,0:T(8,128)(2,1)} async-done(((bf16[512,512]{1,0:T(8,128)(2,1)}), bf16[2048,512]{1,0:T(8,128)(2,1)}) %all-gather.14.cloned.1.call-update) | async-done | bytes 2097168 | tf_op jit(solution)/shard_map/all_gather | solution.py:197
  111.9 23.8 %all-gather.12.cloned.1.call-done = bf16[1024,3,256]{2,0,1:T(8,128)(2,1)} async-done(((bf16[128,3,256]{2,0,1:T(8,128)(2,1)}), bf16[1024,3,256]{2,0,1:T(8,128)(2,1)}) %all-gather.12.cloned.1.call-update) | async-done | bytes 1572880 | tf_op jit(solution)/shard_map/all_gather | solution.py:220
  135.7 3.2 fusion.129
  141.2 42.2 %all-gather.22.cloned.1.call-done = bf16[1,1,1024,1024]{3,2,1,0:T(8,128)(2,1)} async-done(((bf16[1,1,256,1024]{3,2,1,0:T(8,128)(2,1)}), bf16[1,1,1024,1024]{3,2,1,0:T(8,128)(2,1)}) %all-gather.22.cloned.1.call-update) | async-done | bytes 2097168 | tf_op jit(solution)/shard_map/all_gather | solution.py:229
  188.5 21.1 %shard_map.136 = (bf16[1024,256]{1,0:T(8,128)(2,1)}, f32[1024,4]{1,0:T(8,128)}) custom-call(bf16[1024,256]{1,0:T(8,128)(2,1)} %get-tuple-element.156.q_ref, bf16[2048,256]{1,0:T(8,128)(2,1)} %maximum_bitcast_fusion.2.k_ref, bf16[2048,256]{1,0:T(8,128)(2,1)} %maximum_bitcast_fusion.3.v_ref), custom_call_target="tpu_custom_call" | custom-call | flops 2147483648 | bytes 3145728 | tf_op jit(solution)/shard_map/pallas_call | solution.py:86
  209.6 3.3 convolution_convert_fusion
  212.9 4.8 all-to-all-start.2
  227.7 21.1 %shard_map.135 = (bf16[1024,256]{1,0:T(8,128)(2,1)}, f32[1024,4]{1,0:T(8,128)}) custom-call(bf16[1024,256]{1,0:T(8,128)(2,1)} %get-tuple-element.153.q_ref, bf16[2048,256]{1,0:T(8,128)(2,1)} %maximum_bitcast_fusion.k_ref, bf16[2048,256]{1,0:T(8,128)(2,1)} %maximum_bitcast_fusion.1.v_ref), custom_call_target="tpu_custom_call" | custom-call | flops 2147483648 | bytes 3145728 | tf_op jit(solution)/shard_map/pallas_call | solution.py:86
  248.8 3.2 convolution_convert_fusion.1
  252.0 14.1 %all-to-all-done.2 = bf16[1,4,256,1024]{3,2,0,1:T(8,128)(2,1)} async-done(((bf16[1,4,256,1024]{3,2,0,1:T(8,128)(2,1)}), bf16[1,4,256,1024]{3,2,0,1:T(8,128)(2,1)}, u32[]{:S(2)}, u32[]{:S(2)}) %all-to-all-start.2) | async-done | bytes 2097184 | tf_op jit(solution)/shard_map/all_to_all | solution.py:261
  266.1 4.4 all-to-all-start.1
  270.8 3.6 convert_element_type.262
  278.1 3.0 convert_reduce_fusion.6
  281.2 37.2 %all-to-all-done.1 = bf16[1,4,256,1024]{3,2,0,1:T(8,128)(2,1)} async-done(((bf16[1,4,256,1024]{3,2,0,1:T(8,128)(2,1)}), bf16[1,4,256,1024]{3,2,0,1:T(8,128)(2,1)}, u32[]{:S(2)}, u32[]{:S(2)}) %all-to-all-start.1) | async-done | bytes 2097184 | tf_op jit(solution)/shard_map/all_to_all | solution.py:261
  320.5 2.8 multiply_reduce_fusion.10
  339.7 3.9 fusion.244
  355.0 4.6 fusion.136
  373.2 2.7 reshape.939
  375.9 7.1 %fusion.60 = f32[512,4,512,1]{2,0,3,1:T(8,128)} fusion(bf16[512,4,256]{2,1,0:T(4,128)(2,1)} %reshape.939, bf16[4,4,1,256,512]{4,3,2,1,0:T(8,128)(2,1)} %copy-done.10), kind=kOutput, calls=%fused_computation.91 | convolution fusion | flops 2147483648 | bytes 9437184 | tf_op jit(solution)/shard_map/crad,atdj->crtj/dot_general | solution.py:303
  385.3 9.0 %fusion.139 = bf16[1,512,1024]{2,1,0:T(8,128)(2,1)S(1)} fusion(bf16[1024,512,4]{1,0,2:T(8,128)(2,1)} %bitcast.619, f32[512,4,512,1]{2,0,3,1:T(8,128)} %fusion.60, f32[512,4,512,1]{2,0,3,1:T(8,128)} %copy-done.70), kind=kOutput, calls=%fused_computation.164 | convolution fusion | flops 2168979456 | bytes 13631488 | tf_op jit(solution)/shard_map/crtj,atdj->crad/dot_general | solution.py:314
  394.6 6.1 fusion.75
  406.2 8.1 %fusion.43 = bf16[4,4,256,512]{3,2,0,1:T(8,128)(2,1)S(1)} fusion(f32[4,512,4,256]{1,3,2,0:T(8,128)} %fusion.75, f32[512,4,512,1]{2,0,3,1:T(8,128)} %copy-done.73, bf16[512,4,256]{0,2,1:T(8,128)(2,1)} %copy.266), kind=kOutput, calls=%fused_computation.62 | convolution fusion | flops 2161115136 | bytes 17825792 | tf_op jit(solution)/shard_map/crad,crtj->atdj/dot_general | solution.py:306
  418.4 6.1 fusion.78
  424.5 6.7 fusion.42
  433.4 7.6 %pad_maximum_fusion = bf16[16,512,512]{2,1,0:T(8,128)(2,1)} fusion(bf16[16,256,512]{2,1,0:T(8,128)(2,1)} %bitcast.610, bf16[16,256,512]{2,1,0:T(8,128)(2,1)} %bitcast.615), kind=kLoop, calls=%fused_computation | loop fusion | flops 16777216 | bytes 16777216 | tf_op jit(solution)/shard_map/concatenate | solution.py:204
  442.1 3.1 fusion.145.g_ref
  445.2 32.3 %shard_map.137 = (f32[1024,256]{1,0:T(8,128)}, f32[2048,256]{1,0:T(8,128)}, f32[2048,256]{1,0:T(8,128)}) custom-call(bf16[1024,256]{1,0:T(8,128)(2,1)} %get-tuple-element.153.q_ref, bf16[2048,256]{1,0:T(8,128)(2,1)} %maximum_bitcast_fusion.k_ref, bf16[2048,256]{1,0:T(8,128)(2,1)} %maximum_bitcast_fusion.1.v_ref, bf16[1024,256]{1,0:T(8,128)(2,1)} %fusion.145.g_ref, ...), custom_call_target="tpu_custom_call" | custom-call | flops 5368709120 | bytes 8912896 | tf_op jit(solution)/shard_map/pallas_call | solution.py:119
  482.5 3.1 bitcast_convert_fusion.1
  485.7 3.7 all-to-all-start.3
  489.4 3.1 fusion.148.g_ref
  492.6 32.6 %shard_map.138 = (f32[1024,256]{1,0:T(8,128)}, f32[2048,256]{1,0:T(8,128)}, f32[2048,256]{1,0:T(8,128)}) custom-call(bf16[1024,256]{1,0:T(8,128)(2,1)} %get-tuple-element.156.q_ref, bf16[2048,256]{1,0:T(8,128)(2,1)} %maximum_bitcast_fusion.2.k_ref, bf16[2048,256]{1,0:T(8,128)(2,1)} %maximum_bitcast_fusion.3.v_ref, bf16[1024,256]{1,0:T(8,128)(2,1)} %fusion.148.g_ref, ...), custom_call_target="tpu_custom_call" | custom-call | flops 5368709120 | bytes 8912896 | tf_op jit(solution)/shard_map/pallas_call | solution.py:119
  538.8 3.8 fusion.177
  542.7 3.2 add_convert_fusion.2
  545.9 4.7 bitcast_convert_fusion
  550.7 5.3 all-to-all-start.4
  557.9 29.4 %reduce-scatter.7.cloned.1.call-done = bf16[128,256]{1,0:T(8,128)(2,1)} async-done(((bf16[1024,256]{1,0:T(8,128)(2,1)}), bf16[128,256]{1,0:T(8,128)(2,1)}) %reduce-scatter.7.cloned.1.call-update) | async-done | bytes 65552 | tf_op jit(solution)/shard_map/reduce_scatter | solution.py:395
  588.8 2.7 convert_reduce_fusion.4
  591.6 37.2 %reduce-scatter.5.cloned.1.call-done = bf16[128,3,256]{2,0,1:T(8,128)(2,1)} async-done(((bf16[1024,3,256]{2,0,1:T(8,128)(2,1)}), bf16[128,3,256]{2,0,1:T(8,128)(2,1)}) %reduce-scatter.5.cloned.1.call-update) | async-done | bytes 196624 | tf_op jit(solution)/shard_map/reduce_scatter | solution.py:395
  630.5 2.7 convert_reduce_fusion.2
  636.3 3.6 reshape.1148
  639.9 4.8 all-to-all-start.5
  646.1 3.5 add_convert_fusion.6
  649.6 25.9 %reduce-scatter.11.cloned.1.call-done = bf16[1,512,512]{2,1,0:T(8,128)(2,1)} async-done(((bf16[4,512,512]{2,1,0:T(8,128)(2,1)}), bf16[1,512,512]{2,1,0:T(8,128)(2,1)}) %reduce-scatter.11.cloned.1.call-update) | async-done | bytes 524304 | tf_op jit(solution)/shard_map/reduce_scatter | solution.py:207
  682.3 9.5 %all-gather.2 = f32[16,4,1,6,256]{4,1,0,3,2:T(4,128)S(1)} all-gather(f32[2,4,1,6,256]{4,1,0,3,2:T(4,128)S(1)} %bitcast.638), channel_id=4, replica_groups=mesh['dp'=4,'frame'=2,'tensor'=4] {'dp','frame'}, dimensions={0}, use_global_device_ids=true | all-gather | bytes 442368 | tf_op jit(solution)/shard_map/all_gather | solution.py:385
  (369 shorter events, 137.5 us)
Async XLA Ops:
  7.2 55.7 %all-gather.24.cloned.1.call-start = ((), (), s32[]{:S(2)}) async-start(), calls=%async_computation.20 | async-start | bytes 2621440 | tf_op jit(solution)/shard_map/all_gather | solution.py:229
  9.5 99.9 %all-gather.14.cloned.1.call-start = ((), (), s32[]{:S(2)}) async-start(), calls=%async_computation.11 | async-start | bytes 2621440 | tf_op jit(solution)/shard_map/all_gather | solution.py:197
  10.8 1.8 collective-permute-start.4
  12.5 1.4 collective-permute-start.3
  15.0 120.7 %all-gather.12.cloned.1.call-start = ((), (), s32[]{:S(2)}) async-start(), calls=%async_computation.10 | async-start | bytes 1769472 | tf_op jit(solution)/shard_map/all_gather | solution.py:220
  15.8 167.6 %all-gather.22.cloned.1.call-start = ((), (), s32[]{:S(2)}) async-start(), calls=%async_computation.19 | async-start | bytes 2621440 | tf_op jit(solution)/shard_map/all_gather | solution.py:229
  28.7 16.2 %all-to-all-start = ((f32[8,2,4,6,256]{4,2,3,1,0:T(4,128)}), f32[8,2,4,6,256]{4,2,3,1,0:T(4,128)S(1)}, u32[]{:S(2)}, u32[]{:S(2)}) async-start(f32[8,2,4,6,256]{4,2,3,1,0:T(4,128)} %fusion.182), calls=%async_computation | async-start | bytes 786432 | tf_op jit(solution)/shard_map/all_to_all | solution.py:174
  32.1 307.5 %all-gather.16.cloned.1.call-start = ((), (), s32[]{:S(2)}) async-start(), calls=%async_computation.12 | async-start | bytes 10485760 | tf_op jit(solution)/shard_map/all_gather | solution.py:198
  44.9 203.9 %copy-start.17 = (bf16[1024,256]{1,0:T(8,128)(2,1)}, bf16[1024,256]{1,0:T(8,128)(2,1)S(1)}, u32[]{:S(2)}) copy-start(bf16[1024,256]{1,0:T(8,128)(2,1)S(1)} %all_gather.37) | copy-start | bytes 1572868
  111.9 27.1 %copy-start.29 = (bf16[1024,1024,1]{1,0,2:T(8,128)(2,1)}, bf16[1024,1024,1]{1,0,2:T(8,128)(2,1)S(1)}, u32[]{:S(2)}) copy-start(bf16[1024,1024,1]{1,0,2:T(8,128)(2,1)S(1)} %fusion.72) | copy-start | bytes 6291460
  140.0 45.4 %collective-permute-start.6 = (bf16[1,1024,256]{2,1,0:T(8,128)(2,1)}, bf16[1,1024,256]{2,1,0:T(8,128)(2,1)S(1)}, u32[]{:S(2)}, u32[]{:S(2)}) collective-permute-start(bf16[1,1024,256]{2,1,0:T(8,128)(2,1)} %get-tuple-element.155), channel_id=1, source_target_pairs={{0,4},{4,0},{1,5},{5,1},{2,6},{6,2},{3,7},{7,3},{8,12},{12,8},{9,1... | collective-permute-start | bytes 1572872 | tf_op jit(solution)/shard_map/ppermute | solution.py:235
  141.0 46.5 %collective-permute-start.7 = (bf16[1,1024,256]{2,1,0:T(8,128)(2,1)S(1)}, bf16[1,1024,256]{2,1,0:T(8,128)(2,1)S(1)}, u32[]{:S(2)}, u32[]{:S(2)}) collective-permute-start(bf16[1,1024,256]{2,1,0:T(8,128)(2,1)S(1)} %get-tuple-element.154), channel_id=1, source_target_pairs={{0,4},{4,0},{1,5},{5,1},{2,6},{6,2},{3,7},{7,3},{8,12},{12,8},{9,1... | collective-permute-start | bytes 1572872 | tf_op jit(solution)/shard_map/ppermute | solution.py:235
  212.9 53.2 %all-to-all-start.2 = ((bf16[1,4,256,1024]{3,2,0,1:T(8,128)(2,1)}), bf16[1,4,256,1024]{3,2,0,1:T(8,128)(2,1)}, u32[]{:S(2)}, u32[]{:S(2)}) async-start(bf16[1,4,256,1024]{3,2,0,1:T(8,128)(2,1)} %bitcast.617), calls=%async_computation.2 | async-start | bytes 4194304 | tf_op jit(solution)/shard_map/all_to_all | solution.py:261
  223.6 1.9 collective-permute-start
  223.6 3.0 collective-permute-start.1
  248.8 21.8 %copy-start.20 = (bf16[2,1,256,1024]{3,2,1,0:T(8,128)(2,1)S(1)}, bf16[2,1,256,1024]{3,2,1,0:T(8,128)(2,1)}, u32[]{:S(2)}) copy-start(bf16[2,1,256,1024]{3,2,1,0:T(8,128)(2,1)} %param.12) | copy-start | bytes 3145732
  266.1 52.3 %all-to-all-start.1 = ((bf16[1,4,256,1024]{3,2,0,1:T(8,128)(2,1)}), bf16[1,4,256,1024]{3,2,0,1:T(8,128)(2,1)}, u32[]{:S(2)}, u32[]{:S(2)}) async-start(bf16[1,4,256,1024]{3,2,0,1:T(8,128)(2,1)} %bitcast.23), calls=%async_computation.1 | async-start | bytes 4194304 | tf_op jit(solution)/shard_map/all_to_all | solution.py:261
  270.5 170.5 %all-gather.18.cloned.1.call-start = ((), (), s32[]{:S(2)}) async-start(), calls=%async_computation.13 | async-start | bytes 2621440 | tf_op jit(solution)/shard_map/all_gather | solution.py:255
  270.8 49.6 %copy-start.2 = (f32[2,1,256,1024]{3,2,1,0:T(8,128)}, f32[2,1,256,1024]{3,2,1,0:T(8,128)S(1)}, u32[]{:S(2)}) copy-start(f32[2,1,256,1024]{3,2,1,0:T(8,128)S(1)} %convert_element_type.236) | copy-start | bytes 6291460
  274.6 48.6 %copy-start.59 = (f32[256]{0:T(256)}, f32[256]{0:T(256)S(1)}, u32[]{:S(2)}) copy-start(f32[256]{0:T(256)S(1)} %get-tuple-element.187) | copy-start | bytes 3076
  274.6 48.6 %copy-start.61 = (f32[256]{0:T(256)}, f32[256]{0:T(256)S(1)}, u32[]{:S(2)}) copy-start(f32[256]{0:T(256)S(1)} %get-tuple-element.188) | copy-start | bytes 3076
  276.9 50.2 %collective-permute-start.10 = (bf16[1,256,1024]{2,1,0:T(8,128)(2,1)}, bf16[1,256,1024]{2,1,0:T(8,128)(2,1)}, u32[]{:S(2)}, u32[]{:S(2)}) collective-permute-start(bf16[1,256,1024]{2,1,0:T(8,128)(2,1)} %multiply_convert_fusion.3), channel_id=1, source_target_pairs={{0,4},{4,0},{1,5},{5,1},{2,6},{6,2},{3,7},{7,3},{8,12},{12,8},{9,1... | collective-permute-start | bytes 1572872 | tf_op jit(solution)/shard_map/ppermute | solution.py:235
  325.3 5.8 collective-permute-start.2
  326.6 7.1 %collective-permute-start.8 = (bf16[1,256,1024]{2,1,0:T(8,128)(2,1)}, bf16[1,256,1024]{2,1,0:T(8,128)(2,1)}, u32[]{:S(2)}, u32[]{:S(2)}) collective-permute-start(bf16[1,256,1024]{2,1,0:T(8,128)(2,1)} %add_convert_fusion.10), channel_id=1, source_target_pairs={{0,4},{4,0},{1,5},{5,1},{2,6},{6,2},{3,7},{7,3},{8,12},{12,8},{9,1... | collective-permute-start | bytes 1572872 | tf_op jit(solution)/shard_map/ppermute | solution.py:235
  354.9 8.3 %collective-permute-start.5 = (bf16[1,256,1024]{2,1,0:T(8,128)(2,1)S(1)}, bf16[1,256,1024]{2,1,0:T(8,128)(2,1)S(1)}, u32[]{:S(2)}, u32[]{:S(2)}) collective-permute-start(bf16[1,256,1024]{2,1,0:T(8,128)(2,1)S(1)} %slice.287), channel_id=1, source_target_pairs={{0,4},{4,0},{1,5},{5,1},{2,6},{6,2},{3,7},{7,3},{8,12},{12,8},{9,1... | collective-permute-start | bytes 1572872 | tf_op jit(solution)/shard_map/ppermute | solution.py:245
  359.7 2.9 collective-permute-start.11
  365.0 5.9 collective-permute-start.14
  369.5 31.7 %collective-permute-start.9 = (bf16[1,256,1024]{2,1,0:T(8,128)(2,1)}, bf16[1,256,1024]{2,1,0:T(8,128)(2,1)}, u32[]{:S(2)}, u32[]{:S(2)}) collective-permute-start(bf16[1,256,1024]{2,1,0:T(8,128)(2,1)} %slice.300), channel_id=1, source_target_pairs={{0,4},{4,0},{1,5},{5,1},{2,6},{6,2},{3,7},{7,3},{8,12},{12,8},{9,1... | collective-permute-start | bytes 1572872 | tf_op jit(solution)/shard_map/ppermute | solution.py:245
  370.9 118.5 %all-gather.20.cloned.1.call-start = ((), (), s32[]{:S(2)}) async-start(), calls=%async_computation.14 | async-start | bytes 2621440 | tf_op jit(solution)/shard_map/all_gather | solution.py:255
  394.4 6.2 collective-permute-start.15
  405.8 150.2 %reduce-scatter.9.cloned.1.call-start = ((), (), s32[]{:S(2)}) async-start(), calls=%async_computation.17 | async-start | bytes 10485760 | tf_op jit(solution)/shard_map/reduce_scatter | solution.py:206
  479.4 2.2 collective-permute-start.13
  480.2 2.1 collective-permute-start.12
  485.7 65.0 %all-to-all-start.3 = ((bf16[1,4,256,1024]{3,2,0,1:T(8,128)(2,1)}), bf16[1,4,256,1024]{3,2,0,1:T(8,128)(2,1)S(1)}, u32[]{:S(2)}, u32[]{:S(2)}) async-start(bf16[1,4,256,1024]{3,2,0,1:T(8,128)(2,1)} %bitcast.624), calls=%async_computation.3 | async-start | bytes 4194304 | tf_op jit(solution)/shard_map/all_to_all | solution.py:261
  489.4 97.9 %reduce-scatter.7.cloned.1.call-start = ((), (), s32[]{:S(2)}) async-start(), calls=%async_computation.16 | async-start | bytes 589824 | tf_op jit(solution)/shard_map/reduce_scatter | solution.py:395
  527.9 7.4 %collective-permute-start.17 = (bf16[1,1024,256]{2,1,0:T(8,128)(2,1)}, bf16[1,1024,256]{2,1,0:T(8,128)(2,1)}, u32[]{:S(2)}, u32[]{:S(2)}) collective-permute-start(bf16[1,1024,256]{2,1,0:T(8,128)(2,1)} %slice.315), channel_id=1, source_target_pairs={{0,4},{4,0},{1,5},{5,1},{2,6},{6,2},{3,7},{7,3},{8,12},{12,8},{9,1... | collective-permute-start | bytes 1572872 | tf_op jit(solution)/shard_map/ppermute | solution.py:245
  530.0 6.5 collective-permute-start.16
  535.0 93.8 %reduce-scatter.5.cloned.1.call-start = ((), (), s32[]{:S(2)}) async-start(), calls=%async_computation.15 | async-start | bytes 1769472 | tf_op jit(solution)/shard_map/reduce_scatter | solution.py:395
  550.7 79.8 %all-to-all-start.4 = ((bf16[1,4,256,1024]{3,2,0,1:T(8,128)(2,1)}), bf16[1,4,256,1024]{3,2,0,1:T(8,128)(2,1)}, u32[]{:S(2)}, u32[]{:S(2)}) async-start(bf16[1,4,256,1024]{3,2,0,1:T(8,128)(2,1)} %bitcast.625), calls=%async_computation.4 | async-start | bytes 4194304 | tf_op jit(solution)/shard_map/all_to_all | solution.py:261
  556.0 35.5 %copy-start.57 = (f32[1,1,1,1024]{3,1,2,0:T(1,128)S(1)}, f32[1,1,1,1024]{3,1,2,0:T(1,128)}, u32[]{:S(2)}) copy-start(f32[1,1,1,1024]{3,1,2,0:T(1,128)} %get-tuple-element.176) | copy-start | bytes 12292
  556.0 119.5 %reduce-scatter.11.cloned.1.call-start = ((), (), s32[]{:S(2)}) async-start(), calls=%async_computation.18 | async-start | bytes 2621440 | tf_op jit(solution)/shard_map/reduce_scatter | solution.py:207
  557.8 76.3 %copy-start.3 = (f32[2,1,256,1024]{3,2,1,0:T(8,128)S(1)}, f32[2,1,256,1024]{3,2,1,0:T(8,128)}, u32[]{:S(2)}) copy-start(f32[2,1,256,1024]{3,2,1,0:T(8,128)} %copy-done.2) | copy-start | bytes 6291460
  557.8 76.3 %copy-start.56 = (f32[1,1,1,1024]{3,1,2,0:T(1,128)S(1)}, f32[1,1,1,1024]{3,1,2,0:T(1,128)}, u32[]{:S(2)}) copy-start(f32[1,1,1,1024]{3,1,2,0:T(1,128)} %get-tuple-element.180) | copy-start | bytes 12292
  557.9 76.3 %copy-start.60 = (f32[256]{0:T(256)S(1)}, f32[256]{0:T(256)}, u32[]{:S(2)}) copy-start(f32[256]{0:T(256)} %copy-done.59) | copy-start | bytes 3076
  557.9 76.3 %copy-start.62 = (f32[256]{0:T(256)S(1)}, f32[256]{0:T(256)}, u32[]{:S(2)}) copy-start(f32[256]{0:T(256)} %copy-done.61) | copy-start | bytes 3076
  639.9 39.1 %all-to-all-start.5 = ((f32[4,1,3072]{2,1,0:T(1,128)}), f32[4,1,3072]{2,1,0:T(1,128)S(1)}, u32[]{:S(2)}, u32[]{:S(2)}) async-start(f32[4,1,3072]{2,1,0:T(1,128)} %reshape.1148), calls=%async_computation.9 | async-start | bytes 98304 | tf_op jit(solution)/shard_map/all_to_all | solution.py:382
  649.6 42.2 %copy-start.55 = (bf16[8,2,4,128]{3,0,2,1:T(8,128)(2,1)S(1)}, bf16[8,2,4,128]{3,0,2,1:T(8,128)(2,1)}, u32[]{:S(2)}) copy-start(bf16[8,2,4,128]{3,0,2,1:T(8,128)(2,1)} %copy-done.54) | copy-start | bytes 49156
  676.6 16.7 %collective-permute-start.18 = (bf16[2,128,512]{2,1,0:T(8,128)(2,1)S(1)}, bf16[2,128,512]{2,1,0:T(8,128)(2,1)S(1)}, u32[]{:S(2)}, u32[]{:S(2)}) collective-permute-start(bf16[2,128,512]{2,1,0:T(8,128)(2,1)S(1)} %get-tuple-element.163), channel_id=1, source_target_pairs={{0,4},{4,0},{1,5},{5,1},{2,6},{6,2},{3,7},{7,3},{8,12},{12,8},{9,1... | collective-permute-start | bytes 786440 | tf_op jit(solution)/shard_map/ppermute | solution.py:211
  (66 other events, 308.4 us)
Sparse Core Ops, SparseCore 0:
  10.1 52.5 all-gather.23
  64.9 44.4 all-gather.13
  111.3 24.3 all-gather.11
  137.7 45.6 all-gather.21
  185.1 86.2 all-gather.15
  371.0 44.6 all-gather.17
  417.3 44.4 all-gather.19
  464.9 85.1 reduce-scatter.8
  553.1 34.1 reduce-scatter.6
  590.4 38.3 reduce-scatter.4
  631.1 44.4 reduce-scatter.10
